TPU v7x, 128 devices: a whole 4x4x4 slice. The times are simulated.
128 devices in a mesh: dp: 128 (over z, y, x, core).
Axes of the slice: x: 4, y: 4, z: 4, core: 2. Of those that a mesh axis runs over, the one named last changes fastest.
Arguments:
- grads: float32 [128, 4194304], P('dp')
- master: float32 [4194304], P('dp'), may hold values from -0.75 to 0.75
- m_old: float32 [128, 65536], P('dp'), may hold values from -6 to 6
- v_old: float32 [128, 65536], P('dp'), may hold values from 0.25 to 4
- old_bounds: int32 [129], replicated, may hold values from 0 to 4194304, as said below
Outputs:
- master_new: float32 [4194304], P('dp')
- m_new: float32 [4194304], P('dp')
- v_new: float32 [4194304], P('dp')
- params_full: bfloat16 [4194304], replicated
Inputs may be any that keep to these rules, and one draw needn't show every extreme that they name: old_bounds[0] = 0, the last entry is 4194304, entries never fall, and old_bounds[i] - i * 32768 lies between -16384 and 16384 for every i. Row k of m_old and v_old holds its span in its first old_bounds[k+1] - old_bounds[k] slots; later slots are unused. Some span has exactly 65536 entries in every draw.
All inputs are finite; a program needn't handle non-finite values.
Results may differ from a plain program's by a relative error of at most 0.0049.
Values may be sent and summed in bfloat16 or wider, within the bound.
No kernel may reach another device: no remote copies, remote signals or barrier semaphores. Data moves between devices by JAX's collectives and lax.ppermute only.
A program may use at most 128 MiB of HBM per device.

v0:
```python
import jax
import jax.numpy as jnp
from jax import lax
from jax.experimental import pallas as pl
from jax.experimental.pallas import tpu as pltpu
from jax.sharding import Mesh
from jax.sharding import PartitionSpec as P

DP = ("z", "y", "x", "core")
BF = jnp.bfloat16
F32 = jnp.float32


def coords(d):
    return d // 32, d // 8 % 4, d // 2 % 4, d % 2


def shard_of(z, y, x, c):
    return ((z * 4 + y) * 4 + x) * 2 + c


def perm(axis, s):
    pairs = []
    for d in range(128):
        z, y, x, c = coords(d)
        if axis == "core":
            c = 1 - c
        elif axis == "z":
            z = (z + s) % 4
        elif (axis == "a") == (c == 0):
            x = (x + s) % 4
        else:
            y = (y + s) % 4
        pairs.append((d, shard_of(z, y, x, c)))
    return pairs


def send(value, axis, s=1):
    return lax.ppermute(value, DP, perm(axis, s))


def table(c, z, y, x, s):
    i = jnp.arange(16, dtype=jnp.int32)
    rb, rz = i // 4, i % 4
    zz = (z + rz) % 4
    on_0 = shard_of(zz, (y + rb) % 4, (x + s) % 4, 0)
    on_1 = shard_of(zz, (y + s) % 4, (x + rb) % 4, 1)
    return jnp.where(c == 0, on_0, on_1).astype(jnp.int32)


def cost(flops, nbytes):
    return pl.CostEstimate(flops=flops, transcendentals=0, bytes_accessed=nbytes)


def call(body, t, operands, outs, scratch, flops, nbytes, aliases=None, spaces=None, limit=2):
    vmem = pl.BlockSpec(memory_space=pltpu.VMEM)
    hbm = pl.BlockSpec(memory_space=pltpu.HBM)
    spaces = spaces or [True] * len(operands)
    operands = [pltpu.with_memory_space_constraint(o, pltpu.VMEM if v else pltpu.HBM) for o, v in zip(operands, spaces)]
    return pl.pallas_call(
        body,
        grid_spec=pltpu.PrefetchScalarGridSpec(
            num_scalar_prefetch=1,
            grid=(1,),
            in_specs=[vmem if v else hbm for v in spaces],
            out_specs=[hbm if isinstance(o, jax.ShapeDtypeStruct) else vmem for o in outs],
            scratch_shapes=scratch,
        ),
        out_shape=outs,
        input_output_aliases=aliases or {},
        cost_estimate=cost(flops, nbytes),
        compiler_params=pltpu.CompilerParams(vmem_limit_bytes=limit * 2**20),
    )(t, *operands)


def fetch(t, g, dtype):
    _, rows, lanes = g.shape
    whole = dtype == g.dtype

    def body(t_ref, g_ref, *refs):
        outs, (*buf, sem) = refs[:4], refs[4:]
        to = [outs[i // 16].at[i % 16] if whole else buf[0].at[i] for i in range(64)]
        copies = [pltpu.make_async_copy(g_ref.at[t_ref[i]], to[i], sem.at[i]) for i in range(64)]
        for copy in copies:
            copy.start()
        for i, copy in enumerate(copies):
            copy.wait()
            if not whole:
                outs[i // 16][i % 16] = buf[0][i].astype(dtype)

    scratch = [] if whole else [pltpu.VMEM((64, rows, lanes), g.dtype)]
    n = 64 * rows * lanes
    return call(
        body,
        t,
        (g,),
        [pltpu.VMEM((16, rows, lanes), dtype)] * 4,
        scratch + [pltpu.SemaphoreType.DMA((64,))],
        n,
        6 * n,
        spaces=[False],
        limit=12,
    )


def sum_piece(parts, split=False):
    n, rows, lanes = parts[0].shape
    m = len(parts)

    def body(t_ref, *refs):
        ins, outs = refs[:m], refs[m:]
        each = n // len(outs)

        for q, o in enumerate(outs):

            @pl.loop(0, each)
            def _(i, q=q, o=o):
                value = ins[0][q * each + i].astype(F32)
                for r in ins[1:]:
                    value = value + r[q * each + i].astype(F32)
                o[i] = value.astype(o.dtype)

    if split:
        outs = [pltpu.VMEM((4, rows, lanes), F32)] + [pltpu.VMEM((4, rows, lanes), BF)] * 3
    else:
        outs = [pltpu.VMEM((16, rows, lanes), BF)]
    size = n * rows * lanes
    got = call(body, jnp.zeros((1,), jnp.int32), parts, outs, [], m * size, (6 + 2 * m) * size)
    return got if split else got[0]


def place(pairs, out):
    k = len(pairs)
    n, rows, lanes = pairs[0][1].shape

    def body(t_ref, *refs):
        o, sem = refs[-2:]
        copies = [
            pltpu.make_async_copy(refs[j].at[i], o.at[t_ref[j * n + i]], sem.at[j * n + i])
            for j in range(k)
            for i in range(n)
        ]
        for copy in copies:
            copy.start()
        for copy in copies:
            copy.wait()

    t = jnp.concatenate([p[0] for p in pairs])
    operands = [p[1] for p in pairs] + ([] if out is None else [out])
    nbytes = 4 * k * n * rows * lanes
    return call(
        body,
        t,
        operands,
        [jax.ShapeDtypeStruct((128, rows, lanes), BF)],
        [pltpu.SemaphoreType.DMA((k * n,))],
        nbytes,
        nbytes,
        {} if out is None else {k + 1: 0},
        [True] * k + [False] * (0 if out is None else 1),
    )[0]


def shifted(value, steps):
    leading, last = (max(0, -steps), min(128, 128 - steps))
    return lax.ppermute(value, DP, [(source, source + steps) for source in range(leading, last)])


def window(buffer, offset, width):
    padded = jnp.pad(buffer, ((0, 0), (2 * width, width)))
    return lax.dynamic_slice_in_dim(padded, offset + 2 * width, width, 1)


def old_moments(m_old, v_old, old_bounds, device, width, after):
    packed = jnp.stack([m_old[0], v_old[0]])
    sent, _ = lax.optimization_barrier((packed.astype(BF), after))
    from_before = shifted(sent, 1).astype(packed.dtype)
    from_after = shifted(sent, -1).astype(packed.dtype)
    start = device * width
    bound_before = old_bounds[jnp.maximum(device - 1, 0)]
    bound_here = old_bounds[device]
    bound_after = old_bounds[device + 1]
    part_before = window(from_before, start - bound_before, width)
    part_here = window(packed, start - bound_here, width)
    part_after = window(from_after, start - bound_after, width)
    positions = start + jnp.arange(width, dtype=jnp.int32)
    moments = jnp.where(
        positions[None, :] < bound_here,
        part_before,
        jnp.where(positions[None, :] >= bound_after, part_after, part_here),
    )
    return moments[0], moments[1]


def step(grads, master, m_old, v_old, old_bounds):
    count = 128
    width = master.shape[0]
    rows = width // 128
    device = lax.axis_index(DP)
    z, y, x, c = coords(device)
    mine = [table(c, z, y, x, s) for s in range(4)]
    theirs = [table(1 - c, z, y, x, s) for s in range(4)]
    g = grads[0].reshape(128, rows, 128)

    order = (2, 1, 3, 0)
    given = fetch(jnp.concatenate([theirs[s] for s in order]), g, BF)
    swapped = {s: send(v, "core") for s, v in zip(order, given)}
    kept = fetch(jnp.concatenate([mine[s] for s in order]), g, F32)
    kept = dict(zip(order, kept))
    ringed = {}
    for s in (2, 1, 3):
        piece = sum_piece((kept[s], swapped[s]))
        ringed[s] = send(piece, "a", s)
    m_prev, v_prev = old_moments(m_old, v_old, old_bounds, device, width, piece)
    ringed[3], m_prev, v_prev = lax.optimization_barrier((ringed[3], m_prev, v_prev))
    own, q1, q2, q3 = sum_piece((kept[0], swapped[0], ringed[1], ringed[2], ringed[3]), split=True)
    q2, q1, q3 = send(q2, "b", 2), send(q1, "b", 1), send(q3, "b", 3)
    partial = own + (q1.astype(F32) + q3.astype(F32)) + q2.astype(F32)
    w = [partial[s].astype(BF) for s in range(4)]
    w2, w1, w3 = send(w[2], "z", 2), send(w[1], "z", 1), send(w[3], "z", 3)
    gradient = partial[0] + (w1.astype(F32) + w3.astype(F32)) + w2.astype(F32)

    squares = jnp.sum(gradient * gradient)
    total = jnp.sum(lax.all_to_all(jnp.broadcast_to(squares, (count,)), DP, 0, 0, tiled=True))
    clip = jnp.minimum(1.0, jnp.sqrt(jnp.float32(count * width)) / (jnp.sqrt(total) + 1e-06))
    clipped = clip * gradient.reshape(width)
    m_new = 0.5 * m_prev + 0.5 * clipped
    v_new = 0.95 * v_prev + 0.05 * clipped * clipped
    direction = m_new / (1.0 - 0.5**20) / (jnp.sqrt(v_new / (1.0 - 0.95**20)) + 1e-08)
    master_new = master - 0.05 * (direction + 0.1 * master)

    piece = master_new.astype(BF).reshape(1, rows, 128)
    for axis in ("z", "b"):
        got = {s: send(piece, axis, s) for s in (2, 1, 3)}
        piece = jnp.concatenate([piece, got[3], got[2], got[1]])
    got = {0: piece}
    for s in (2, 1, 3):
        got[(4 - s) % 4] = send(piece, "a", s)
    other = {0: send(got[0], "core")}
    out = place([(mine[0], got[0]), (theirs[0], other[0])], None)
    got[2], out = lax.optimization_barrier((got[2], out))
    other[2] = send(got[2], "core")
    out = place([(mine[2], got[2]), (theirs[2], other[2])], out)
    got[3], out = lax.optimization_barrier((got[3], out))
    other[3] = send(got[3], "core")
    other[1] = send(got[1], "core")
    out = place([(mine[3], got[3]), (mine[1], got[1]), (theirs[3], other[3])], out)
    out = place([(theirs[1], other[1])], out)
    return (master_new, m_new, v_new, out.reshape(count * width))


def solution(mesh):
    finer = Mesh(mesh.devices.reshape(4, 4, 4, 2), DP)
    placed = (P(DP, None), P(DP), P(DP, None), P(DP, None), P())
    return jax.shard_map(
        step, mesh=finer, in_specs=placed, out_specs=(P(DP), P(DP), P(DP), P()), check_vma=False
    )
```

profile of v0, /device:TPU:1, one launch (start us, length us, event | category | flops | bytes accessed | tf_op | source)
XLA Modules:
  0.0 159.9 jit_solution(4314823656956807628)
XLA Ops:
  1.0 6.6 %shard_map.85 = (bf16[16,256,128]{2,1,0:T(8,128)(2,1)}, bf16[16,256,128]{2,1,0:T(8,128)(2,1)}, bf16[16,256,128]{2,1,0:T(8,128)(2,1)}, bf16[16,256,128]{2,1,0:T(8,128)(2,1)}) custom-call(s32[64]{0:T(128)S(1)} %get-tuple-element.70.t_ref, f32[128,256,128]{2,1,0:T(8,128)} %bitcast.33), custom_call_target="tpu_custom_call" | custom-call | flops 2097152 | bytes 12582912 | tf_op jit(solution)/shard_map/pallas_call | solution.py:60
  7.6 1.5 collective-permute-start
  9.6 1.3 pad_maximum_fusion
  14.0 4.6 %shard_map.84 = (f32[16,256,128]{2,1,0:T(8,128)S(1)}, f32[16,256,128]{2,1,0:T(8,128)S(1)}, f32[16,256,128]{2,1,0:T(8,128)S(1)}, f32[16,256,128]{2,1,0:T(8,128)S(1)}) custom-call(s32[64]{0:T(128)S(1)} %get-tuple-element.69.t_ref, f32[128,256,128]{2,1,0:T(8,128)} %bitcast.34), custom_call_target="tpu_custom_call" | custom-call | flops 2097152 | bytes 12582912 | tf_op jit(solution)/shard_map/pallas_call | solution.py:60
  18.6 1.6 shard_map.86
  20.1 3.5 %collective-permute-start.2 = (bf16[2,65536]{1,0:T(2,128)(2,1)S(1)}, bf16[2,65536]{1,0:T(2,128)(2,1)S(1)}, u32[]{:S(2)}, u32[]{:S(2)}) collective-permute-start(bf16[2,65536]{1,0:T(2,128)(2,1)S(1)} %fusion.14), channel_id=1, source_target_pairs={{0,1},{1,2},{2,3},{3,4},{4,5},{5,6},{6,7},{7,8},{8,9},{9,10},{10,1... | collective-permute-start | bytes 786440 | tf_op jit(solution)/shard_map/ppermute | solution.py:166
  23.7 1.9 %collective-permute-start.3 = (bf16[2,65536]{1,0:T(2,128)(2,1)S(1)}, bf16[2,65536]{1,0:T(2,128)(2,1)S(1)}, u32[]{:S(2)}, u32[]{:S(2)}) collective-permute-start(bf16[2,65536]{1,0:T(2,128)(2,1)S(1)} %fusion.14), channel_id=1, source_target_pairs={{1,0},{2,1},{3,2},{4,3},{5,4},{6,5},{7,6},{8,7},{9,8},{10,9},{11,1... | collective-permute-start | bytes 786440 | tf_op jit(solution)/shard_map/ppermute | solution.py:166
  25.6 1.3 fusion.5
  27.0 2.8 %collective-permute-start.1 = (bf16[16,256,128]{2,1,0:T(8,128)(2,1)S(1)}, bf16[16,256,128]{2,1,0:T(8,128)(2,1)S(1)}, u32[]{:S(2)}, u32[]{:S(2)}) collective-permute-start(bf16[16,256,128]{2,1,0:T(8,128)(2,1)S(1)} %shard_map.86), channel_id=1, source_target_pairs={{0,6},{1,25},{2,0},{3,27},{4,2},{5,29},{6,4},{7,31},{8,14},{9,1},{... | collective-permute-start | bytes 3145736 | tf_op jit(solution)/shard_map/ppermute | solution.py:39
  30.5 1.7 %collective-permute-start.8 = (bf16[16,256,128]{2,1,0:T(8,128)(2,1)S(1)}, bf16[16,256,128]{2,1,0:T(8,128)(2,1)S(1)}, u32[]{:S(2)}, u32[]{:S(2)}) collective-permute-start(bf16[16,256,128]{2,1,0:T(8,128)(2,1)S(1)} %shard_map.88), channel_id=1, source_target_pairs={{0,4},{1,17},{2,6},{3,19},{4,0},{5,21},{6,2},{7,23},{8,12},{9,25},... | collective-permute-start | bytes 3145736 | tf_op jit(solution)/shard_map/ppermute | solution.py:39
  32.2 2.1 %fusion.1 = f32[2,32768]{1,0:T(2,128)S(1)} fusion(s32[]{:T(128)S(6)} %select_n.255, f32[2,65536]{1,0:T(2,128)S(1)} %copy-done, pred[32768]{0:T(1024)(128)(4,1)S(1)} %get-tuple-element.71, pred[32768]{0:T(1024)(128)(4,1)S(1)} %get-tuple-element.72, s32[]{:T(128)S(6)} %select_n.252, bf16[2,65536]{1,0:T(2,128)(2,1)S(1)} %collective-permute-done.2, ...), kind=kLoop, calls=%fused_computation.7 | loop fusion | flops 262144 | bytes 1376268 | tf_op jit(solution)/shard_map/jit(_where)/select_n | solution.py:187
  34.5 18.2 %collective-permute-done.1.refs_4_ = bf16[16,256,128]{2,1,0:T(8,128)(2,1)S(1)} collective-permute-done((bf16[16,256,128]{2,1,0:T(8,128)(2,1)S(1)}, bf16[16,256,128]{2,1,0:T(8,128)(2,1)S(1)}, u32[]{:S(2)}, u32[]{:S(2)}) %collective-permute-start.1) | collective-permute-done | bytes 1048608 | tf_op jit(solution)/shard_map/ppermute | solution.py:39
  52.8 3.8 %collective-permute-done.6.refs_2_ = bf16[16,256,128]{2,1,0:T(8,128)(2,1)S(1)} collective-permute-done((bf16[16,256,128]{2,1,0:T(8,128)(2,1)S(1)}, bf16[16,256,128]{2,1,0:T(8,128)(2,1)S(1)}, u32[]{:S(2)}, u32[]{:S(2)}) %collective-permute-start.6) | collective-permute-done | bytes 1048608 | tf_op jit(solution)/shard_map/ppermute | solution.py:39
  56.5 0.8 shard_map.89
  57.3 2.3 %collective-permute-start.10 = (bf16[4,256,128]{2,1,0:T(8,128)(2,1)S(1)}, bf16[4,256,128]{2,1,0:T(8,128)(2,1)S(1)}, u32[]{:S(2)}, u32[]{:S(2)}) collective-permute-start(bf16[4,256,128]{2,1,0:T(8,128)(2,1)S(1)} %get-tuple-element.37), channel_id=1, source_target_pairs={{0,24},{1,7},{2,26},{3,1},{4,28},{5,3},{6,30},{7,5},{8,0},{9,15},{... | collective-permute-start | bytes 786440 | tf_op jit(solution)/shard_map/ppermute | solution.py:39
  60.4 5.3 %collective-permute-done.10 = bf16[4,256,128]{2,1,0:T(8,128)(2,1)S(1)} collective-permute-done((bf16[4,256,128]{2,1,0:T(8,128)(2,1)S(1)}, bf16[4,256,128]{2,1,0:T(8,128)(2,1)S(1)}, u32[]{:S(2)}, u32[]{:S(2)}) %collective-permute-start.10) | collective-permute-done | bytes 262176 | tf_op jit(solution)/shard_map/ppermute | solution.py:39
  65.7 0.9 collective-permute-done.11
  66.6 2.8 %collective-permute-done.9 = bf16[4,256,128]{2,1,0:T(8,128)(2,1)S(1)} collective-permute-done((bf16[4,256,128]{2,1,0:T(8,128)(2,1)S(1)}, bf16[4,256,128]{2,1,0:T(8,128)(2,1)S(1)}, u32[]{:S(2)}, u32[]{:S(2)}) %collective-permute-start.9) | collective-permute-done | bytes 262176 | tf_op jit(solution)/shard_map/ppermute | solution.py:39
  69.6 1.9 %collective-permute-start.12 = (bf16[256,128]{1,0:T(8,128)(2,1)S(1)}, bf16[256,128]{1,0:T(8,128)(2,1)S(1)}, u32[]{:S(2)}, u32[]{:S(2)}) collective-permute-start(bf16[256,128]{1,0:T(8,128)(2,1)S(1)} %get-tuple-element.54), channel_id=1, source_target_pairs={{0,32},{1,33},{2,34},{3,35},{4,36},{5,37},{6,38},{7,39},{8,40},{9,... | collective-permute-start | bytes 196616 | tf_op jit(solution)/shard_map/ppermute | solution.py:39
  71.5 1.3 collective-permute-start.13
  72.8 1.9 %collective-permute-start.14 = (bf16[256,128]{1,0:T(8,128)(2,1)S(1)}, bf16[256,128]{1,0:T(8,128)(2,1)S(1)}, u32[]{:S(2)}, u32[]{:S(2)}) collective-permute-start(bf16[256,128]{1,0:T(8,128)(2,1)S(1)} %get-tuple-element.55), channel_id=1, source_target_pairs={{0,64},{1,65},{2,66},{3,67},{4,68},{5,69},{6,70},{7,71},{8,72},{9,... | collective-permute-start | bytes 196616 | tf_op jit(solution)/shard_map/ppermute | solution.py:39
  74.7 2.7 %collective-permute-done.14 = bf16[256,128]{1,0:T(8,128)(2,1)S(1)} collective-permute-done((bf16[256,128]{1,0:T(8,128)(2,1)S(1)}, bf16[256,128]{1,0:T(8,128)(2,1)S(1)}, u32[]{:S(2)}, u32[]{:S(2)}) %collective-permute-start.14) | collective-permute-done | bytes 65568 | tf_op jit(solution)/shard_map/ppermute | solution.py:39
  78.0 0.7 broadcast_in_dim.20
  78.7 18.8 %all_to_all.6 = f32[128,1,1]{2,1,0:T(1,128)S(1)} all-to-all(f32[128,1,1]{2,1,0:T(1,128)S(1)} %broadcast_in_dim.20), channel_id=1, replica_groups=mesh['z'=4,'y'=4,'x'=4,'core'=2] {'z','y','x','core'}, dimensions={0} | all-to-all | bytes 1024 | tf_op jit(solution)/shard_map/all_to_all | solution.py:224
  97.5 0.7 reduce_sum.19
  98.9 0.8 constant_dynamic-update-slice_fusion.6
  100.0 1.7 %collective-permute-start.16 = (bf16[1,256,128]{2,1,0:T(8,128)(2,1)S(1)}, bf16[1,256,128]{2,1,0:T(8,128)(2,1)S(1)}, u32[]{:S(2)}, u32[]{:S(2)}) collective-permute-start(bf16[1,256,128]{2,1,0:T(8,128)(2,1)S(1)} %get-tuple-element.45), channel_id=1, source_target_pairs={{0,64},{1,65},{2,66},{3,67},{4,68},{5,69},{6,70},{7,71},{8,72},{9,... | collective-permute-start | bytes 196616 | tf_op jit(solution)/shard_map/ppermute | solution.py:39
  101.8 1.0 collective-permute-done.15
  102.9 1.8 %collective-permute-done.16 = bf16[1,256,128]{2,1,0:T(8,128)(2,1)S(1)} collective-permute-done((bf16[1,256,128]{2,1,0:T(8,128)(2,1)S(1)}, bf16[1,256,128]{2,1,0:T(8,128)(2,1)S(1)}, u32[]{:S(2)}, u32[]{:S(2)}) %collective-permute-start.16) | collective-permute-done | bytes 65568 | tf_op jit(solution)/shard_map/ppermute | solution.py:39
  104.7 2.1 %collective-permute-done.17 = bf16[1,256,128]{2,1,0:T(8,128)(2,1)S(1)} collective-permute-done((bf16[1,256,128]{2,1,0:T(8,128)(2,1)S(1)}, bf16[1,256,128]{2,1,0:T(8,128)(2,1)S(1)}, u32[]{:S(2)}, u32[]{:S(2)}) %collective-permute-start.17) | collective-permute-done | bytes 65568 | tf_op jit(solution)/shard_map/ppermute | solution.py:39
  106.8 1.6 collective-permute-start.18
  108.4 0.7 collective-permute-start.19
  109.1 5.4 %collective-permute-done.18 = bf16[4,256,128]{2,1,0:T(8,128)(2,1)S(1)} collective-permute-done((bf16[4,256,128]{2,1,0:T(8,128)(2,1)S(1)}, bf16[4,256,128]{2,1,0:T(8,128)(2,1)S(1)}, u32[]{:S(2)}, u32[]{:S(2)}) %collective-permute-start.18) | collective-permute-done | bytes 262176 | tf_op jit(solution)/shard_map/ppermute | solution.py:39
  114.5 0.9 collective-permute-done.19
  115.5 2.7 %collective-permute-done.20 = bf16[4,256,128]{2,1,0:T(8,128)(2,1)S(1)} collective-permute-done((bf16[4,256,128]{2,1,0:T(8,128)(2,1)S(1)}, bf16[4,256,128]{2,1,0:T(8,128)(2,1)S(1)}, u32[]{:S(2)}, u32[]{:S(2)}) %collective-permute-start.20) | collective-permute-done | bytes 262176 | tf_op jit(solution)/shard_map/ppermute | solution.py:39
  118.2 2.6 %collective-permute-start.25 = (bf16[16,256,128]{2,1,0:T(8,128)(2,1)S(1)}, bf16[16,256,128]{2,1,0:T(8,128)(2,1)S(1)}, u32[]{:S(2)}, u32[]{:S(2)}) collective-permute-start(bf16[16,256,128]{2,1,0:T(8,128)(2,1)S(1)} %constant_dynamic-update-slice_fusion.refs_0_), channel_id=1, source_target_pairs={{0,1},{1,0},{2,3},{3,2},{4,5},{5,4},{6,7},{7,6},{8,9},{9,8},{10,11... | collective-permute-start | bytes 3145736 | tf_op jit(solution)/shard_map/ppermute | solution.py:39
  120.8 1.4 collective-permute-start.24
  122.2 0.8 collective-permute-done.25.refs_1_
  123.1 2.1 %shard_map.90.refs_2_ = bf16[128,256,128]{2,1,0:T(8,128)(2,1)} custom-call(s32[32]{0:T(128)S(1)} %pad_add_fusion.4.t_ref, bf16[16,256,128]{2,1,0:T(8,128)(2,1)S(1)} %constant_dynamic-update-slice_fusion.refs_0_, bf16[16,256,128]{2,1,0:T(8,128)(2,1)S(1)} %collective-permute-done.25.refs_1_), custom_call_target="tpu_custom_call" | custom-call | flops 4194304 | bytes 4194304 | tf_op jit(solution)/shard_map/pallas_call | solution.py:60
  125.2 11.0 %collective-permute-done.24.refs_0_ = bf16[16,256,128]{2,1,0:T(8,128)(2,1)S(1)} collective-permute-done((bf16[16,256,128]{2,1,0:T(8,128)(2,1)S(1)}, bf16[16,256,128]{2,1,0:T(8,128)(2,1)S(1)}, u32[]{:S(2)}, u32[]{:S(2)}) %collective-permute-start.24) | collective-permute-done | bytes 1048608 | tf_op jit(solution)/shard_map/ppermute | solution.py:39
  136.3 0.9 collective-permute-start.26
  137.2 2.7 %collective-permute-start.21 = (bf16[16,256,128]{2,1,0:T(8,128)(2,1)S(1)}, bf16[16,256,128]{2,1,0:T(8,128)(2,1)S(1)}, u32[]{:S(2)}, u32[]{:S(2)}) collective-permute-start(bf16[16,256,128]{2,1,0:T(8,128)(2,1)S(1)} %constant_dynamic-update-slice_fusion.refs_0_), channel_id=1, source_target_pairs={{0,6},{1,25},{2,0},{3,27},{4,2},{5,29},{6,4},{7,31},{8,14},{9,1},{... | collective-permute-start | bytes 3145736 | tf_op jit(solution)/shard_map/ppermute | solution.py:39
  140.0 2.1 %shard_map.91.refs_3_ = bf16[128,256,128]{2,1,0:T(8,128)(2,1)} custom-call(s32[32]{0:T(128)S(1)} %pad_add_fusion.3.t_ref, bf16[16,256,128]{2,1,0:T(8,128)(2,1)S(1)} %collective-permute-done.24.refs_0_, bf16[16,256,128]{2,1,0:T(8,128)(2,1)S(1)} %collective-permute-done.26.refs_1_, ...), custom_call_target="tpu_custom_call", output_to_operand_aliasing={{}: (3, {})} | custom-call | flops 4194304 | bytes 4194304 | tf_op jit(solution)/shard_map/pallas_call | solution.py:60
  142.1 10.3 %collective-permute-done.23.refs_0_ = bf16[16,256,128]{2,1,0:T(8,128)(2,1)S(1)} collective-permute-done((bf16[16,256,128]{2,1,0:T(8,128)(2,1)S(1)}, bf16[16,256,128]{2,1,0:T(8,128)(2,1)S(1)}, u32[]{:S(2)}, u32[]{:S(2)}) %collective-permute-start.23) | collective-permute-done | bytes 1048608 | tf_op jit(solution)/shard_map/ppermute | solution.py:39
  152.4 0.9 collective-permute-start.27
  154.0 1.5 collective-permute-done.27.refs_2_
  155.5 2.6 %shard_map.92.refs_1_ = bf16[128,256,128]{2,1,0:T(8,128)(2,1)} custom-call(s32[48]{0:T(128)S(1)} %pad_add_fusion.2.t_ref, bf16[16,256,128]{2,1,0:T(8,128)(2,1)S(1)} %collective-permute-done.23.refs_0_, bf16[16,256,128]{2,1,0:T(8,128)(2,1)S(1)} %collective-permute-done.21.refs_1_, ...), custom_call_target="tpu_custom_call", output_to_operand_aliasing={{}: (4, {})} | custom-call | flops 6291456 | bytes 6291456 | tf_op jit(solution)/shard_map/pallas_call | solution.py:60
  158.1 1.6 %shard_map.93 = bf16[128,256,128]{2,1,0:T(8,128)(2,1)} custom-call(s32[16]{0:T(128)S(1)} %get-tuple-element.62.t_ref, bf16[16,256,128]{2,1,0:T(8,128)(2,1)S(1)} %collective-permute-done.22.refs_0_, bf16[128,256,128]{2,1,0:T(8,128)(2,1)} %shard_map.92.refs_1_), custom_call_target="tpu_custom_call", output_to_operand_aliasing={{}: (2, {})} | custom-call | flops 2097152 | bytes 2097152 | tf_op jit(solution)/shard_map/pallas_call | solution.py:60
  (55 shorter events, 5.8 us)
Async XLA Ops:
  1.0 8.7 %copy-start.1 = (f32[1,65536]{1,0:T(1,128)S(1)}, f32[1,65536]{1,0:T(1,128)}, u32[]{:S(2)}) copy-start(f32[1,65536]{1,0:T(1,128)} %param.8) | copy-start | bytes 786436
  1.0 8.7 %copy-start.2 = (f32[1,65536]{1,0:T(1,128)S(1)}, f32[1,65536]{1,0:T(1,128)}, u32[]{:S(2)}) copy-start(f32[1,65536]{1,0:T(1,128)} %param.7) | copy-start | bytes 786436
  1.0 10.4 %copy-start.4 = (s32[129]{0:T(256)S(1)}, s32[129]{0:T(256)}, u32[]{:S(2)}) copy-start(s32[129]{0:T(256)} %param.9) | copy-start | bytes 1552
  7.6 11.0 %collective-permute-start = (bf16[16,256,128]{2,1,0:T(8,128)(2,1)}, bf16[16,256,128]{2,1,0:T(8,128)(2,1)}, u32[]{:S(2)}, u32[]{:S(2)}) collective-permute-start(bf16[16,256,128]{2,1,0:T(8,128)(2,1)} %get-tuple-element.25), channel_id=1, source_target_pairs={{0,1},{1,0},{2,3},{3,2},{4,5},{5,4},{6,7},{7,6},{8,9},{9,8},{10,11... | collective-permute-start | bytes 3145736 | tf_op jit(solution)/shard_map/ppermute | solution.py:39
  9.0 17.9 %collective-permute-start.5 = (bf16[16,256,128]{2,1,0:T(8,128)(2,1)}, bf16[16,256,128]{2,1,0:T(8,128)(2,1)S(1)}, u32[]{:S(2)}, u32[]{:S(2)}) collective-permute-start(bf16[16,256,128]{2,1,0:T(8,128)(2,1)} %get-tuple-element.31), channel_id=1, source_target_pairs={{0,1},{1,0},{2,3},{3,2},{4,5},{5,4},{6,7},{7,6},{8,9},{9,8},{10,11... | collective-permute-start | bytes 3145736 | tf_op jit(solution)/shard_map/ppermute | solution.py:39
  9.1 21.0 %collective-permute-start.7 = (bf16[16,256,128]{2,1,0:T(8,128)(2,1)}, bf16[16,256,128]{2,1,0:T(8,128)(2,1)S(1)}, u32[]{:S(2)}, u32[]{:S(2)}) collective-permute-start(bf16[16,256,128]{2,1,0:T(8,128)(2,1)} %get-tuple-element.33), channel_id=1, source_target_pairs={{0,1},{1,0},{2,3},{3,2},{4,5},{5,4},{6,7},{7,6},{8,9},{9,8},{10,11... | collective-permute-start | bytes 3145736 | tf_op jit(solution)/shard_map/ppermute | solution.py:39
  9.5 43.2 %collective-permute-start.4 = (bf16[16,256,128]{2,1,0:T(8,128)(2,1)}, bf16[16,256,128]{2,1,0:T(8,128)(2,1)S(1)}, u32[]{:S(2)}, u32[]{:S(2)}) collective-permute-start(bf16[16,256,128]{2,1,0:T(8,128)(2,1)} %get-tuple-element.29), channel_id=1, source_target_pairs={{0,1},{1,0},{2,3},{3,2},{4,5},{5,4},{6,7},{7,6},{8,9},{9,8},{10,11... | collective-permute-start | bytes 3145736 | tf_op jit(solution)/shard_map/ppermute | solution.py:39
  18.5 13.7 %copy-start = (f32[2,65536]{1,0:T(2,128)S(1)}, f32[2,65536]{1,0:T(2,128)}, u32[]{:S(2)}) copy-start(f32[2,65536]{1,0:T(2,128)} %pad_maximum_fusion) | copy-start | bytes 1572868
  20.1 10.3 %collective-permute-start.2 = (bf16[2,65536]{1,0:T(2,128)(2,1)S(1)}, bf16[2,65536]{1,0:T(2,128)(2,1)S(1)}, u32[]{:S(2)}, u32[]{:S(2)}) collective-permute-start(bf16[2,65536]{1,0:T(2,128)(2,1)S(1)} %fusion.14), channel_id=1, source_target_pairs={{0,1},{1,2},{2,3},{3,4},{4,5},{5,6},{6,7},{7,8},{8,9},{9,10},{10,1... | collective-permute-start | bytes 786440 | tf_op jit(solution)/shard_map/ppermute | solution.py:166
  23.7 8.5 %collective-permute-start.3 = (bf16[2,65536]{1,0:T(2,128)(2,1)S(1)}, bf16[2,65536]{1,0:T(2,128)(2,1)S(1)}, u32[]{:S(2)}, u32[]{:S(2)}) collective-permute-start(bf16[2,65536]{1,0:T(2,128)(2,1)S(1)} %fusion.14), channel_id=1, source_target_pairs={{1,0},{2,1},{3,2},{4,3},{5,4},{6,5},{7,6},{8,7},{9,8},{10,9},{11,1... | collective-permute-start | bytes 786440 | tf_op jit(solution)/shard_map/ppermute | solution.py:166
  27.0 25.8 %collective-permute-start.1 = (bf16[16,256,128]{2,1,0:T(8,128)(2,1)S(1)}, bf16[16,256,128]{2,1,0:T(8,128)(2,1)S(1)}, u32[]{:S(2)}, u32[]{:S(2)}) collective-permute-start(bf16[16,256,128]{2,1,0:T(8,128)(2,1)S(1)} %shard_map.86), channel_id=1, source_target_pairs={{0,6},{1,25},{2,0},{3,27},{4,2},{5,29},{6,4},{7,31},{8,14},{9,1},{... | collective-permute-start | bytes 3145736 | tf_op jit(solution)/shard_map/ppermute | solution.py:39
  30.1 68.9 %copy-start.3 = (f32[32768]{0:T(1024)S(1)}, f32[32768]{0:T(1024)}, u32[]{:S(2)}) copy-start(f32[32768]{0:T(1024)} %param.6) | copy-start | bytes 393220
  30.1 26.5 %collective-permute-start.6 = (bf16[16,256,128]{2,1,0:T(8,128)(2,1)S(1)}, bf16[16,256,128]{2,1,0:T(8,128)(2,1)S(1)}, u32[]{:S(2)}, u32[]{:S(2)}) collective-permute-start(bf16[16,256,128]{2,1,0:T(8,128)(2,1)S(1)} %shard_map.87), channel_id=1, source_target_pairs={{0,2},{1,9},{2,4},{3,11},{4,6},{5,13},{6,0},{7,15},{8,10},{9,17},{... | collective-permute-start | bytes 3145736 | tf_op jit(solution)/shard_map/ppermute | solution.py:39
  30.5 26.1 %collective-permute-start.8 = (bf16[16,256,128]{2,1,0:T(8,128)(2,1)S(1)}, bf16[16,256,128]{2,1,0:T(8,128)(2,1)S(1)}, u32[]{:S(2)}, u32[]{:S(2)}) collective-permute-start(bf16[16,256,128]{2,1,0:T(8,128)(2,1)S(1)} %shard_map.88), channel_id=1, source_target_pairs={{0,4},{1,17},{2,6},{3,19},{4,0},{5,21},{6,2},{7,23},{8,12},{9,25},... | collective-permute-start | bytes 3145736 | tf_op jit(solution)/shard_map/ppermute | solution.py:39
  57.3 8.4 %collective-permute-start.10 = (bf16[4,256,128]{2,1,0:T(8,128)(2,1)S(1)}, bf16[4,256,128]{2,1,0:T(8,128)(2,1)S(1)}, u32[]{:S(2)}, u32[]{:S(2)}) collective-permute-start(bf16[4,256,128]{2,1,0:T(8,128)(2,1)S(1)} %get-tuple-element.37), channel_id=1, source_target_pairs={{0,24},{1,7},{2,26},{3,1},{4,28},{5,3},{6,30},{7,5},{8,0},{9,15},{... | collective-permute-start | bytes 786440 | tf_op jit(solution)/shard_map/ppermute | solution.py:39
  59.6 7.1 %collective-permute-start.11 = (bf16[4,256,128]{2,1,0:T(8,128)(2,1)S(1)}, bf16[4,256,128]{2,1,0:T(8,128)(2,1)S(1)}, u32[]{:S(2)}, u32[]{:S(2)}) collective-permute-start(bf16[4,256,128]{2,1,0:T(8,128)(2,1)S(1)} %get-tuple-element.38), channel_id=1, source_target_pairs={{0,16},{1,5},{2,18},{3,7},{4,20},{5,1},{6,22},{7,3},{8,24},{9,13},... | collective-permute-start | bytes 786440 | tf_op jit(solution)/shard_map/ppermute | solution.py:39
  60.1 9.3 %collective-permute-start.9 = (bf16[4,256,128]{2,1,0:T(8,128)(2,1)S(1)}, bf16[4,256,128]{2,1,0:T(8,128)(2,1)S(1)}, u32[]{:S(2)}, u32[]{:S(2)}) collective-permute-start(bf16[4,256,128]{2,1,0:T(8,128)(2,1)S(1)} %get-tuple-element.36), channel_id=1, source_target_pairs={{0,8},{1,3},{2,10},{3,5},{4,12},{5,7},{6,14},{7,1},{8,16},{9,11},{... | collective-permute-start | bytes 786440 | tf_op jit(solution)/shard_map/ppermute | solution.py:39
  69.6 5.1 %collective-permute-start.12 = (bf16[256,128]{1,0:T(8,128)(2,1)S(1)}, bf16[256,128]{1,0:T(8,128)(2,1)S(1)}, u32[]{:S(2)}, u32[]{:S(2)}) collective-permute-start(bf16[256,128]{1,0:T(8,128)(2,1)S(1)} %get-tuple-element.54), channel_id=1, source_target_pairs={{0,32},{1,33},{2,34},{3,35},{4,36},{5,37},{6,38},{7,39},{8,40},{9,... | collective-permute-start | bytes 196616 | tf_op jit(solution)/shard_map/ppermute | solution.py:39
  71.5 3.2 %collective-permute-start.13 = (bf16[256,128]{1,0:T(8,128)(2,1)S(1)}, bf16[256,128]{1,0:T(8,128)(2,1)S(1)}, u32[]{:S(2)}, u32[]{:S(2)}) collective-permute-start(bf16[256,128]{1,0:T(8,128)(2,1)S(1)} %get-tuple-element.56), channel_id=1, source_target_pairs={{0,96},{1,97},{2,98},{3,99},{4,100},{5,101},{6,102},{7,103},{8,104... | collective-permute-start | bytes 196616 | tf_op jit(solution)/shard_map/ppermute | solution.py:39
  72.8 4.6 %collective-permute-start.14 = (bf16[256,128]{1,0:T(8,128)(2,1)S(1)}, bf16[256,128]{1,0:T(8,128)(2,1)S(1)}, u32[]{:S(2)}, u32[]{:S(2)}) collective-permute-start(bf16[256,128]{1,0:T(8,128)(2,1)S(1)} %get-tuple-element.55), channel_id=1, source_target_pairs={{0,64},{1,65},{2,66},{3,67},{4,68},{5,69},{6,70},{7,71},{8,72},{9,... | collective-permute-start | bytes 196616 | tf_op jit(solution)/shard_map/ppermute | solution.py:39
  99.7 3.1 %collective-permute-start.15 = (bf16[1,256,128]{2,1,0:T(8,128)(2,1)S(1)}, bf16[1,256,128]{2,1,0:T(8,128)(2,1)S(1)}, u32[]{:S(2)}, u32[]{:S(2)}) collective-permute-start(bf16[1,256,128]{2,1,0:T(8,128)(2,1)S(1)} %get-tuple-element.45), channel_id=1, source_target_pairs={{0,96},{1,97},{2,98},{3,99},{4,100},{5,101},{6,102},{7,103},{8,104... | collective-permute-start | bytes 196616 | tf_op jit(solution)/shard_map/ppermute | solution.py:39
  100.0 4.6 %collective-permute-start.16 = (bf16[1,256,128]{2,1,0:T(8,128)(2,1)S(1)}, bf16[1,256,128]{2,1,0:T(8,128)(2,1)S(1)}, u32[]{:S(2)}, u32[]{:S(2)}) collective-permute-start(bf16[1,256,128]{2,1,0:T(8,128)(2,1)S(1)} %get-tuple-element.45), channel_id=1, source_target_pairs={{0,64},{1,65},{2,66},{3,67},{4,68},{5,69},{6,70},{7,71},{8,72},{9,... | collective-permute-start | bytes 196616 | tf_op jit(solution)/shard_map/ppermute | solution.py:39
  101.8 5.0 %collective-permute-start.17 = (bf16[1,256,128]{2,1,0:T(8,128)(2,1)S(1)}, bf16[1,256,128]{2,1,0:T(8,128)(2,1)S(1)}, u32[]{:S(2)}, u32[]{:S(2)}) collective-permute-start(bf16[1,256,128]{2,1,0:T(8,128)(2,1)S(1)} %get-tuple-element.45), channel_id=1, source_target_pairs={{0,32},{1,33},{2,34},{3,35},{4,36},{5,37},{6,38},{7,39},{8,40},{9,... | collective-permute-start | bytes 196616 | tf_op jit(solution)/shard_map/ppermute | solution.py:39
  106.8 7.7 %collective-permute-start.18 = (bf16[4,256,128]{2,1,0:T(8,128)(2,1)S(1)}, bf16[4,256,128]{2,1,0:T(8,128)(2,1)S(1)}, u32[]{:S(2)}, u32[]{:S(2)}) collective-permute-start(bf16[4,256,128]{2,1,0:T(8,128)(2,1)S(1)} %pad_maximum_fusion.1), channel_id=1, source_target_pairs={{0,24},{1,7},{2,26},{3,1},{4,28},{5,3},{6,30},{7,5},{8,0},{9,15},{... | collective-permute-start | bytes 786440 | tf_op jit(solution)/shard_map/ppermute | solution.py:39
  108.4 7.1 %collective-permute-start.19 = (bf16[4,256,128]{2,1,0:T(8,128)(2,1)S(1)}, bf16[4,256,128]{2,1,0:T(8,128)(2,1)S(1)}, u32[]{:S(2)}, u32[]{:S(2)}) collective-permute-start(bf16[4,256,128]{2,1,0:T(8,128)(2,1)S(1)} %pad_maximum_fusion.1), channel_id=1, source_target_pairs={{0,16},{1,5},{2,18},{3,7},{4,20},{5,1},{6,22},{7,3},{8,24},{9,13},... | collective-permute-start | bytes 786440 | tf_op jit(solution)/shard_map/ppermute | solution.py:39
  109.1 9.1 %collective-permute-start.20 = (bf16[4,256,128]{2,1,0:T(8,128)(2,1)S(1)}, bf16[4,256,128]{2,1,0:T(8,128)(2,1)S(1)}, u32[]{:S(2)}, u32[]{:S(2)}) collective-permute-start(bf16[4,256,128]{2,1,0:T(8,128)(2,1)S(1)} %pad_maximum_fusion.1), channel_id=1, source_target_pairs={{0,8},{1,3},{2,10},{3,5},{4,12},{5,7},{6,14},{7,1},{8,16},{9,11},{... | collective-permute-start | bytes 786440 | tf_op jit(solution)/shard_map/ppermute | solution.py:39
  118.2 4.8 %collective-permute-start.25 = (bf16[16,256,128]{2,1,0:T(8,128)(2,1)S(1)}, bf16[16,256,128]{2,1,0:T(8,128)(2,1)S(1)}, u32[]{:S(2)}, u32[]{:S(2)}) collective-permute-start(bf16[16,256,128]{2,1,0:T(8,128)(2,1)S(1)} %constant_dynamic-update-slice_fusion.refs_0_), channel_id=1, source_target_pairs={{0,1},{1,0},{2,3},{3,2},{4,5},{5,4},{6,7},{7,6},{8,9},{9,8},{10,11... | collective-permute-start | bytes 3145736 | tf_op jit(solution)/shard_map/ppermute | solution.py:39
  120.8 15.4 %collective-permute-start.24 = (bf16[16,256,128]{2,1,0:T(8,128)(2,1)S(1)}, bf16[16,256,128]{2,1,0:T(8,128)(2,1)S(1)}, u32[]{:S(2)}, u32[]{:S(2)}) collective-permute-start(bf16[16,256,128]{2,1,0:T(8,128)(2,1)S(1)} %constant_dynamic-update-slice_fusion.refs_0_), channel_id=1, source_target_pairs={{0,4},{1,17},{2,6},{3,19},{4,0},{5,21},{6,2},{7,23},{8,12},{9,25},... | collective-permute-start | bytes 3145736 | tf_op jit(solution)/shard_map/ppermute | solution.py:39
  136.3 3.7 %collective-permute-start.26 = (bf16[16,256,128]{2,1,0:T(8,128)(2,1)S(1)}, bf16[16,256,128]{2,1,0:T(8,128)(2,1)S(1)}, u32[]{:S(2)}, u32[]{:S(2)}) collective-permute-start(bf16[16,256,128]{2,1,0:T(8,128)(2,1)S(1)} %collective-permute-done.24.refs_0_), channel_id=1, source_target_pairs={{0,1},{1,0},{2,3},{3,2},{4,5},{5,4},{6,7},{7,6},{8,9},{9,8},{10,11... | collective-permute-start | bytes 3145736 | tf_op jit(solution)/shard_map/ppermute | solution.py:39
  137.2 15.2 %collective-permute-start.23 = (bf16[16,256,128]{2,1,0:T(8,128)(2,1)S(1)}, bf16[16,256,128]{2,1,0:T(8,128)(2,1)S(1)}, u32[]{:S(2)}, u32[]{:S(2)}) collective-permute-start(bf16[16,256,128]{2,1,0:T(8,128)(2,1)S(1)} %constant_dynamic-update-slice_fusion.refs_0_), channel_id=1, source_target_pairs={{0,2},{1,9},{2,4},{3,11},{4,6},{5,13},{6,0},{7,15},{8,10},{9,17},{... | collective-permute-start | bytes 3145736 | tf_op jit(solution)/shard_map/ppermute | solution.py:39
  137.2 16.0 %collective-permute-start.21 = (bf16[16,256,128]{2,1,0:T(8,128)(2,1)S(1)}, bf16[16,256,128]{2,1,0:T(8,128)(2,1)S(1)}, u32[]{:S(2)}, u32[]{:S(2)}) collective-permute-start(bf16[16,256,128]{2,1,0:T(8,128)(2,1)S(1)} %constant_dynamic-update-slice_fusion.refs_0_), channel_id=1, source_target_pairs={{0,6},{1,25},{2,0},{3,27},{4,2},{5,29},{6,4},{7,31},{8,14},{9,1},{... | collective-permute-start | bytes 3145736 | tf_op jit(solution)/shard_map/ppermute | solution.py:39
  152.4 3.1 %collective-permute-start.27 = (bf16[16,256,128]{2,1,0:T(8,128)(2,1)S(1)}, bf16[16,256,128]{2,1,0:T(8,128)(2,1)S(1)}, u32[]{:S(2)}, u32[]{:S(2)}) collective-permute-start(bf16[16,256,128]{2,1,0:T(8,128)(2,1)S(1)} %collective-permute-done.23.refs_0_), channel_id=1, source_target_pairs={{0,1},{1,0},{2,3},{3,2},{4,5},{5,4},{6,7},{7,6},{8,9},{9,8},{10,11... | collective-permute-start | bytes 3145736 | tf_op jit(solution)/shard_map/ppermute | solution.py:39
  153.2 4.9 %collective-permute-start.22 = (bf16[16,256,128]{2,1,0:T(8,128)(2,1)S(1)}, bf16[16,256,128]{2,1,0:T(8,128)(2,1)S(1)}, u32[]{:S(2)}, u32[]{:S(2)}) collective-permute-start(bf16[16,256,128]{2,1,0:T(8,128)(2,1)S(1)} %collective-permute-done.21.refs_1_), channel_id=1, source_target_pairs={{0,1},{1,0},{2,3},{3,2},{4,5},{5,4},{6,7},{7,6},{8,9},{9,8},{10,11... | collective-permute-start | bytes 3145736 | tf_op jit(solution)/shard_map/ppermute | solution.py:39
where the time goes:
time: 160 us
  waiting for transfers between devices  71.3 us (45%)
  starting transfers between devices  33.1 us (21%)
  Pallas kernels  22.5 us (14%)
  blocking collectives  18.8 us (12%)
  other arithmetic  8.54 us (5%)
  between operations  3.95 us (2%)
  local copies, waits for them, and re-layouts  1.67 us (1%)
    ppermute x26, waiting for transfers between devices, send(): return lax.ppermute(value, DP, perm(axis, s))  71.3 us
    ppermute x26, starting transfers between devices, send(): return lax.ppermute(value, DP, perm(axis, s))  27.7 us
    pallas_call x10, Pallas kernels, call(): pl.pallas_call(body, grid_spec=pltpu.PrefetchScalarGridSpec(num_scalar_pr...  22.5 us
    all_to_all x1, blocking collectives, step(): lax.all_to_all(jnp.broadcast_to(squares, (count,)), DP, 0, 0, tiled=True)  18.8 us
    ppermute x2, starting transfers between devices, shifted(): lax.ppermute(value, DP, [(source, source + steps) for source in range(lea...  5.45 us
  transfers between devices with their start and end apart: 28, of which 16 were waited for; matrix products, arithmetic and copies ran while one was open for 4% of the time, Pallas kernels for 8%

commit v1 on v0

--- a/solution.py
+++ b/solution.py
@@ -52,7 +52,7 @@
     return pl.CostEstimate(flops=flops, transcendentals=0, bytes_accessed=nbytes)
 
 
-def call(body, t, operands, outs, scratch, flops, nbytes, aliases=None, spaces=None, limit=2):
+def call(body, t, operands, outs, scratch, flops, nbytes, aliases=None, spaces=None, limit=8):
     vmem = pl.BlockSpec(memory_space=pltpu.VMEM)
     hbm = pl.BlockSpec(memory_space=pltpu.HBM)
     spaces = spaces or [True] * len(operands)
@@ -99,7 +99,7 @@
         n,
         6 * n,
         spaces=[False],
-        limit=12,
+        limit=2 if whole else 10,
     )
 
 
@@ -121,9 +121,9 @@
                 o[i] = value.astype(o.dtype)
 
     if split:
-        outs = [pltpu.VMEM((4, rows, lanes), F32)] + [pltpu.VMEM((4, rows, lanes), BF)] * 3
+        outs = [pltpu.VMEM((n // 4, rows, lanes), F32)] + [pltpu.VMEM((n // 4, rows, lanes), BF)] * 3
     else:
-        outs = [pltpu.VMEM((16, rows, lanes), BF)]
+        outs = [pltpu.VMEM((n, rows, lanes), BF)]
     size = n * rows * lanes
     got = call(body, jnp.zeros((1,), jnp.int32), parts, outs, [], m * size, (6 + 2 * m) * size)
     return got if split else got[0]
@@ -161,35 +161,130 @@
     )[0]
 
 
+def total_piece(own, from1, from2, from3, copies):
+    n, rows, lanes = own.shape
+
+    def body(t_ref, w, x1, x2, x3, g, squares):
+        sums = []
+        for r in range(n):
+
+            def step(i, acc, r=r):
+                at = pl.ds(i * 16, 16)
+                even = w[r, at].astype(F32) + x2[(r + 2) % n, at].astype(F32)
+                odd = x1[(r + 1) % n, at].astype(F32) + x3[(r + 3) % n, at].astype(F32)
+                value = even + odd
+                g[r, at] = value
+                return acc + value * value
+
+            sums.append(lax.fori_loop(0, rows // 16, step, jnp.zeros((16, lanes), F32)))
+        acc = (sums[0] + sums[2]) + (sums[1] + sums[3])
+        squares[...] = jnp.broadcast_to(jnp.sum(acc), squares.shape)
+
+    size = n * rows * lanes
+    outs = [pltpu.VMEM((n, rows, lanes), F32), pltpu.VMEM((copies, 8, lanes), F32)]
+    return call(body, jnp.zeros((1,), jnp.int32), (own, from1, from2, from3), outs, [], 6 * size, 12 * size)
+
+
+def adam(master, m_prev, v_prev, gradient, clip):
+    clipped = clip * gradient
+    m_new = 0.5 * m_prev + 0.5 * clipped
+    v_new = 0.95 * v_prev + 0.05 * clipped * clipped
+    direction = m_new / (1.0 - 0.5**20) / (jnp.sqrt(v_new / (1.0 - 0.95**20)) + 1e-08)
+    return master - 0.05 * (direction + 0.1 * master), m_new, v_new
+
+
+def updated_piece(gradient, states, squares, flat):
+    n, rows, lanes = gradient.shape
+
+    def body(t_ref, g, *refs):
+        state, part, piece, clip_ref = refs[:n], refs[n], refs[n + 1], refs[n + 2]
+        total = part[0]
+        for i in range(1, part.shape[0]):
+            total = total + part[i]
+        clip = jnp.minimum(1.0, jnp.sqrt(jnp.float32(flat)) / (jnp.sqrt(total) + 1e-06))
+        clip_ref[...] = clip
+        clip = jnp.concatenate([clip, clip])
+        for r in range(n):
+
+            @pl.loop(0, rows // 16)
+            def _(i, r=r):
+                at = pl.ds(i * 16, 16)
+                high, low, m, v = (state[r][k, at].astype(F32) for k in range(4))
+                piece[r, at] = adam(high + low, m, v, g[r, at], clip)[0].astype(BF)
+
+    size = n * rows * lanes
+    outs = [pltpu.VMEM((n, rows, lanes), BF), pltpu.VMEM((8, lanes), F32)]
+    return call(body, jnp.zeros((1,), jnp.int32), (gradient, *states, squares), outs, [], 20 * size, 14 * size)
+
+
+def packed_moments(m_old, v_old):
+    def body(t_ref, m, v, o):
+        o[0] = m[...].astype(BF)
+        o[1] = v[...].astype(BF)
+
+    n = 2 * m_old.size
+    outs = [pltpu.VMEM((2, *m_old.shape), BF)]
+    return call(body, jnp.zeros((1,), jnp.int32), (m_old, v_old), outs, [], n, 6 * n)[0]
+
+
+def old_moments(device, old_bounds, m_old, v_old, before, after, master):
+    rows, lanes = master.shape
+    top = 392
+    reach = top + m_old.shape[0] + rows // 2 + 8
+    where = jnp.concatenate([old_bounds, device[None].astype(jnp.int32)])
+    last = old_bounds.shape[0]
+
+    def body(t_ref, m, v, b, a, w, m_out, v_out, state, buf):
+        d = t_ref[last]
+        start = d * (rows * lanes)
+        first = t_ref[d]
+        end = t_ref[d + 1]
+        starts = (t_ref[jnp.maximum(d - 1, 0)], first, end)
+        offsets = [start - s + top * lanes for s in starts]
+        for k, (old, out) in enumerate(((m, m_out), (v, v_out))):
+            held = pl.ds(top, m_old.shape[0])
+            buf[0, held] = b[k].astype(F32)
+            buf[1, held] = old[...]
+            buf[2, held] = a[k].astype(F32)
+
+            @pl.loop(0, rows // 32)
+            def _(i, k=k, out=out):
+                lane = lax.broadcasted_iota(jnp.int32, (32, lanes), 1)
+                row = lax.broadcasted_iota(jnp.int32, (32, lanes), 0)
+                position = start + i * (32 * lanes) + row * lanes + lane
+                parts = []
+                for j, offset in enumerate(offsets):
+                    q = offset // lanes + i * 32
+                    r = offset % lanes
+                    back = (lanes - r) % lanes
+                    here = pltpu.roll(buf[j, pl.ds(q, 32)], back, 1)
+                    then = pltpu.roll(buf[j, pl.ds(q + 1, 32)], back, 1)
+                    parts.append(jnp.where(lane < lanes - r, here, then))
+                value = jnp.where(position < first, parts[0], jnp.where(position >= end, parts[2], parts[1]))
+                at = pl.ds(i * 32, 32)
+                out[at] = value
+                state[2 + k, at] = value.astype(BF)
+
+        high = w[...].astype(BF)
+        state[0] = high
+        state[1] = (w[...] - high.astype(F32)).astype(BF)
+
+    size = rows * lanes
+    outs = [pltpu.VMEM((rows, lanes), F32)] * 2 + [pltpu.VMEM((4, rows, lanes), BF)]
+    return call(
+        body,
+        where,
+        (m_old, v_old, before, after, master),
+        outs,
+        [pltpu.VMEM((3, reach, lanes), F32)],
+        40 * size,
+        40 * size,
+    )
+
+
 def shifted(value, steps):
     leading, last = (max(0, -steps), min(128, 128 - steps))
     return lax.ppermute(value, DP, [(source, source + steps) for source in range(leading, last)])
-
-
-def window(buffer, offset, width):
-    padded = jnp.pad(buffer, ((0, 0), (2 * width, width)))
-    return lax.dynamic_slice_in_dim(padded, offset + 2 * width, width, 1)
-
-
-def old_moments(m_old, v_old, old_bounds, device, width, after):
-    packed = jnp.stack([m_old[0], v_old[0]])
-    sent, _ = lax.optimization_barrier((packed.astype(BF), after))
-    from_before = shifted(sent, 1).astype(packed.dtype)
-    from_after = shifted(sent, -1).astype(packed.dtype)
-    start = device * width
-    bound_before = old_bounds[jnp.maximum(device - 1, 0)]
-    bound_here = old_bounds[device]
-    bound_after = old_bounds[device + 1]
-    part_before = window(from_before, start - bound_before, width)
-    part_here = window(packed, start - bound_here, width)
-    part_after = window(from_after, start - bound_after, width)
-    positions = start + jnp.arange(width, dtype=jnp.int32)
-    moments = jnp.where(
-        positions[None, :] < bound_here,
-        part_before,
-        jnp.where(positions[None, :] >= bound_after, part_after, part_here),
-    )
-    return moments[0], moments[1]
 
 
 def step(grads, master, m_old, v_old, old_bounds):
@@ -208,31 +303,31 @@
     kept = fetch(jnp.concatenate([mine[s] for s in order]), g, F32)
     kept = dict(zip(order, kept))
     ringed = {}
+    pieces = {}
     for s in (2, 1, 3):
-        piece = sum_piece((kept[s], swapped[s]))
-        ringed[s] = send(piece, "a", s)
-    m_prev, v_prev = old_moments(m_old, v_old, old_bounds, device, width, piece)
-    ringed[3], m_prev, v_prev = lax.optimization_barrier((ringed[3], m_prev, v_prev))
+        pieces[s] = sum_piece((kept[s], swapped[s]))
+        ringed[s] = send(pieces[s], "a", s)
+    master_tiles = master.reshape(rows, 128)
+    m_tiles, v_tiles = m_old[0].reshape(-1, 128), v_old[0].reshape(-1, 128)
+    packed = packed_moments(m_tiles, v_tiles)
+    before = shifted(packed, 1)
+    after = shifted(packed, -1)
+    m_prev, v_prev, state = old_moments(device, old_bounds, m_tiles, v_tiles, before, after, master_tiles)
+    states = [state] + [None] * 3
+    for s in (2, 1, 3):
+        states[4 - s] = send(state, "z", s)
     own, q1, q2, q3 = sum_piece((kept[0], swapped[0], ringed[1], ringed[2], ringed[3]), split=True)
     q2, q1, q3 = send(q2, "b", 2), send(q1, "b", 1), send(q3, "b", 3)
-    partial = own + (q1.astype(F32) + q3.astype(F32)) + q2.astype(F32)
-    w = [partial[s].astype(BF) for s in range(4)]
-    w2, w1, w3 = send(w[2], "z", 2), send(w[1], "z", 1), send(w[3], "z", 3)
-    gradient = partial[0] + (w1.astype(F32) + w3.astype(F32)) + w2.astype(F32)
-
-    squares = jnp.sum(gradient * gradient)
-    total = jnp.sum(lax.all_to_all(jnp.broadcast_to(squares, (count,)), DP, 0, 0, tiled=True))
-    clip = jnp.minimum(1.0, jnp.sqrt(jnp.float32(count * width)) / (jnp.sqrt(total) + 1e-06))
-    clipped = clip * gradient.reshape(width)
-    m_new = 0.5 * m_prev + 0.5 * clipped
-    v_new = 0.95 * v_prev + 0.05 * clipped * clipped
-    direction = m_new / (1.0 - 0.5**20) / (jnp.sqrt(v_new / (1.0 - 0.95**20)) + 1e-08)
-    master_new = master - 0.05 * (direction + 0.1 * master)
-
-    piece = master_new.astype(BF).reshape(1, rows, 128)
-    for axis in ("z", "b"):
-        got = {s: send(piece, axis, s) for s in (2, 1, 3)}
-        piece = jnp.concatenate([piece, got[3], got[2], got[1]])
+    partial = sum_piece((own, q1, q2, q3))
+    w2, w1, w3 = send(partial, "z", 2), send(partial, "z", 1), send(partial, "z", 3)
+    gradient, squares = total_piece(partial, w1, w2, w3, 32)
+    squares = lax.all_to_all(squares, ("y", "x", "core"), 0, 0, tiled=True)
+    piece, clip = updated_piece(gradient, states, squares, count * width)
+    new = adam(master_tiles, m_prev, v_prev, gradient[0], clip[0, 0])
+    master_new, m_new, v_new = (value.reshape(width) for value in new)
+
+    got = {s: send(piece, "b", s) for s in (2, 1, 3)}
+    piece = jnp.concatenate([piece, got[3], got[2], got[1]])
     got = {0: piece}
     for s in (2, 1, 3):
         got[(4 - s) % 4] = send(piece, "a", s)
@@ -244,14 +339,12 @@
     got[3], out = lax.optimization_barrier((got[3], out))
     other[3] = send(got[3], "core")
     other[1] = send(got[1], "core")
-    out = place([(mine[3], got[3]), (mine[1], got[1]), (theirs[3], other[3])], out)
-    out = place([(theirs[1], other[1])], out)
+    out = place([(mine[3], got[3]), (mine[1], got[1])], out)
+    out = place([(theirs[3], other[3]), (theirs[1], other[1])], out)
     return (master_new, m_new, v_new, out.reshape(count * width))
 
 
 def solution(mesh):
     finer = Mesh(mesh.devices.reshape(4, 4, 4, 2), DP)
     placed = (P(DP, None), P(DP), P(DP, None), P(DP, None), P())
-    return jax.shard_map(
-        step, mesh=finer, in_specs=placed, out_specs=(P(DP), P(DP), P(DP), P()), check_vma=False
-    )
+    return jax.shard_map(step, mesh=finer, in_specs=placed, out_specs=(P(DP), P(DP), P(DP), P()), check_vma=False)

time: 160 us -> 143 us (0.89)
  blocking collectives: 18.8 us -> 0 us
  starting transfers between devices: 33.1 us -> 47.2 us
  other arithmetic: 8.54 us -> 1.96 us
  waiting for transfers between devices: 71.3 us -> 66.8 us
  between operations: 3.95 us -> 1.09 us
  Pallas kernels: 22.5 us -> 24.5 us
    all_to_all x1 -> x0, blocking collectives: 18.8 us -> none  [step(): lax.all_to_all(jnp.broadcast_to(squares, (count,)), DP, 0, 0, tiled=True)]
    ppermute x26, waiting for transfers between devices: 71.3 us -> 61.7 us  [send(): return lax.ppermute(value, DP, perm(axis, s))]
    all_to_all x0 -> x1, starting transfers between devices: none -> 8.14 us  [step(): squares = lax.all_to_all(squares, ('y', 'x', 'core'), 0, 0, tiled=True)]
    all_to_all x0 -> x1, waiting for transfers between devices: none -> 5.14 us  [step(): squares = lax.all_to_all(squares, ('y', 'x', 'core'), 0, 0, tiled=True)]
    ppermute x26, starting transfers between devices: 27.7 us -> 30.9 us  [send(): return lax.ppermute(value, DP, perm(axis, s))]
    ppermute x2, starting transfers between devices: 5.45 us -> 8.2 us  [shifted(): lax.ppermute(value, DP, [(source, source + steps) for source in range(lea...]
    select_n x1 -> x0, other arithmetic: 2.1 us -> none  [old_moments(): jnp.where(positions[None, :] < bound_here, part_before, jnp.where(positio...]
    pallas_call x10 -> x15, Pallas kernels: 22.5 us -> 24.5 us  [call(): pl.pallas_call(body, grid_spec=pltpu.PrefetchScalarGridSpec(num_scalar_pr...]
  transfers between devices with their start and end apart: 28 -> 29, of which waited for: 16 -> 11; matrix products, arithmetic and copies ran while one was open for 4% -> 2% of each run, Pallas kernels for 8% -> 11%
where the time goes in v1:
time: 143 us; the launch traced here: 142 us
  waiting for transfers between devices  66.8 us (47%)
  starting transfers between devices  47.2 us (33%)
  Pallas kernels  24.5 us (17%)
  other arithmetic  1.96 us (1%)
    ppermute x26, waiting for transfers between devices, send(): return lax.ppermute(value, DP, perm(axis, s))  61.7 us
    ppermute x26, starting transfers between devices, send(): return lax.ppermute(value, DP, perm(axis, s))  30.9 us
    pallas_call x15, Pallas kernels, call(): pl.pallas_call(body, grid_spec=pltpu.PrefetchScalarGridSpec(num_scalar_pr...  24.5 us
    ppermute x2, starting transfers between devices, shifted(): lax.ppermute(value, DP, [(source, source + steps) for source in range(lea...  8.2 us
    all_to_all x1, starting transfers between devices, step(): squares = lax.all_to_all(squares, ('y', 'x', 'core'), 0, 0, tiled=True)  8.14 us
    all_to_all x1, waiting for transfers between devices, step(): squares = lax.all_to_all(squares, ('y', 'x', 'core'), 0, 0, tiled=True)  5.14 us
  transfers between devices with their start and end apart: 29, of which 11 were waited for; matrix products, arithmetic and copies ran while one was open for 2% of the time, Pallas kernels for 11%

profile of v1, /device:TPU:1, one launch (start us, length us, event | category | flops | bytes accessed | tf_op | source)
XLA Modules:
  0.0 142.3 jit_solution(2175285880184463617)
XLA Ops:
  1.0 4.6 %shard_map.87 = (bf16[16,256,128]{2,1,0:T(8,128)(2,1)S(1)}, bf16[16,256,128]{2,1,0:T(8,128)(2,1)S(1)}, bf16[16,256,128]{2,1,0:T(8,128)(2,1)S(1)}, bf16[16,256,128]{2,1,0:T(8,128)(2,1)S(1)}) custom-call(s32[64]{0:T(128)S(1)} %get-tuple-element.63.t_ref, f32[128,256,128]{2,1,0:T(8,128)} %bitcast.31), custom_call_target="tpu_custom_call" | custom-call | flops 2097152 | bytes 12582912 | tf_op jit(solution)/shard_map/pallas_call | solution.py:60
  5.5 1.5 %collective-permute-start.3 = (bf16[16,256,128]{2,1,0:T(8,128)(2,1)S(1)}, bf16[16,256,128]{2,1,0:T(8,128)(2,1)S(1)}, u32[]{:S(2)}, u32[]{:S(2)}) collective-permute-start(bf16[16,256,128]{2,1,0:T(8,128)(2,1)S(1)} %get-tuple-element.31), channel_id=1, source_target_pairs={{0,1},{1,0},{2,3},{3,2},{4,5},{5,4},{6,7},{7,6},{8,9},{9,8},{10,11... | collective-permute-start | bytes 3145736 | tf_op jit(solution)/shard_map/ppermute | solution.py:39
  7.1 0.4 collective-permute-start.7
  7.6 4.6 %shard_map.86 = (f32[16,256,128]{2,1,0:T(8,128)S(1)}, f32[16,256,128]{2,1,0:T(8,128)S(1)}, f32[16,256,128]{2,1,0:T(8,128)S(1)}, f32[16,256,128]{2,1,0:T(8,128)S(1)}) custom-call(s32[64]{0:T(128)S(1)} %get-tuple-element.62.t_ref, f32[128,256,128]{2,1,0:T(8,128)} %bitcast.32), custom_call_target="tpu_custom_call" | custom-call | flops 2097152 | bytes 12582912 | tf_op jit(solution)/shard_map/pallas_call | solution.py:60
  12.2 0.3 shard_map.88
  12.5 1.5 %collective-permute-start.4 = (bf16[16,256,128]{2,1,0:T(8,128)(2,1)S(1)}, bf16[16,256,128]{2,1,0:T(8,128)(2,1)S(1)}, u32[]{:S(2)}, u32[]{:S(2)}) collective-permute-start(bf16[16,256,128]{2,1,0:T(8,128)(2,1)S(1)} %shard_map.88), channel_id=1, source_target_pairs={{0,2},{1,9},{2,4},{3,11},{4,6},{5,13},{6,0},{7,15},{8,10},{9,17},{... | collective-permute-start | bytes 3145736 | tf_op jit(solution)/shard_map/ppermute | solution.py:39
  14.2 2.7 %collective-permute-start.6 = (bf16[16,256,128]{2,1,0:T(8,128)(2,1)S(1)}, bf16[16,256,128]{2,1,0:T(8,128)(2,1)S(1)}, u32[]{:S(2)}, u32[]{:S(2)}) collective-permute-start(bf16[16,256,128]{2,1,0:T(8,128)(2,1)S(1)} %shard_map.89), channel_id=1, source_target_pairs={{0,4},{1,17},{2,6},{3,19},{4,0},{5,21},{6,2},{7,23},{8,12},{9,25},... | collective-permute-start | bytes 3145736 | tf_op jit(solution)/shard_map/ppermute | solution.py:39
  17.2 1.1 collective-permute-start.8
  18.3 9.6 %collective-permute-done.4.refs_2_ = bf16[16,256,128]{2,1,0:T(8,128)(2,1)S(1)} collective-permute-done((bf16[16,256,128]{2,1,0:T(8,128)(2,1)S(1)}, bf16[16,256,128]{2,1,0:T(8,128)(2,1)S(1)}, u32[]{:S(2)}, u32[]{:S(2)}) %collective-permute-start.4) | collective-permute-done | bytes 1048608 | tf_op jit(solution)/shard_map/ppermute | solution.py:39
  27.9 12.4 %collective-permute-done.6.refs_3_ = bf16[16,256,128]{2,1,0:T(8,128)(2,1)S(1)} collective-permute-done((bf16[16,256,128]{2,1,0:T(8,128)(2,1)S(1)}, bf16[16,256,128]{2,1,0:T(8,128)(2,1)S(1)}, u32[]{:S(2)}, u32[]{:S(2)}) %collective-permute-start.6) | collective-permute-done | bytes 1048608 | tf_op jit(solution)/shard_map/ppermute | solution.py:39
  40.3 0.7 shard_map.91
  41.0 2.6 %collective-permute-start.10 = (bf16[4,256,128]{2,1,0:T(8,128)(2,1)S(1)}, bf16[4,256,128]{2,1,0:T(8,128)(2,1)S(1)}, u32[]{:S(2)}, u32[]{:S(2)}) collective-permute-start(bf16[4,256,128]{2,1,0:T(8,128)(2,1)S(1)} %get-tuple-element.38), channel_id=1, source_target_pairs={{0,16},{1,5},{2,18},{3,7},{4,20},{5,1},{6,22},{7,3},{8,24},{9,13},... | collective-permute-start | bytes 786440 | tf_op jit(solution)/shard_map/ppermute | solution.py:39
  43.6 0.9 collective-permute-start.11
  44.5 0.6 collective-permute-start.9
  45.1 6.3 %collective-permute-start = (bf16[2,512,128]{2,1,0:T(8,128)(2,1)S(1)}, bf16[2,512,128]{2,1,0:T(8,128)(2,1)S(1)}, u32[]{:S(2)}, u32[]{:S(2)}) collective-permute-start(bf16[2,512,128]{2,1,0:T(8,128)(2,1)S(1)} %shard_map.84), channel_id=1, source_target_pairs={{0,1},{1,2},{2,3},{3,4},{4,5},{5,6},{6,7},{7,8},{8,9},{9,10},{10,1... | collective-permute-start | bytes 786440 | tf_op jit(solution)/shard_map/ppermute | solution.py:287
  51.4 1.9 %collective-permute-start.1 = (bf16[2,512,128]{2,1,0:T(8,128)(2,1)S(1)}, bf16[2,512,128]{2,1,0:T(8,128)(2,1)S(1)}, u32[]{:S(2)}, u32[]{:S(2)}) collective-permute-start(bf16[2,512,128]{2,1,0:T(8,128)(2,1)S(1)} %shard_map.84), channel_id=1, source_target_pairs={{1,0},{2,1},{3,2},{4,3},{5,4},{6,5},{7,6},{8,7},{9,8},{10,9},{11,1... | collective-permute-start | bytes 786440 | tf_op jit(solution)/shard_map/ppermute | solution.py:287
  53.5 1.7 %collective-permute-start.12 = (bf16[4,256,128]{2,1,0:T(8,128)(2,1)S(1)}, bf16[4,256,128]{2,1,0:T(8,128)(2,1)S(1)}, u32[]{:S(2)}, u32[]{:S(2)}) collective-permute-start(bf16[4,256,128]{2,1,0:T(8,128)(2,1)S(1)} %shard_map.92.w), channel_id=1, source_target_pairs={{0,32},{1,33},{2,34},{3,35},{4,36},{5,37},{6,38},{7,39},{8,40},{9,... | collective-permute-start | bytes 786440 | tf_op jit(solution)/shard_map/ppermute | solution.py:39
  55.2 3.3 %collective-permute-start.13 = (bf16[4,256,128]{2,1,0:T(8,128)(2,1)S(1)}, bf16[4,256,128]{2,1,0:T(8,128)(2,1)S(1)}, u32[]{:S(2)}, u32[]{:S(2)}) collective-permute-start(bf16[4,256,128]{2,1,0:T(8,128)(2,1)S(1)} %shard_map.92.w), channel_id=1, source_target_pairs={{0,64},{1,65},{2,66},{3,67},{4,68},{5,69},{6,70},{7,71},{8,72},{9,... | collective-permute-start | bytes 786440 | tf_op jit(solution)/shard_map/ppermute | solution.py:39
  58.5 0.7 collective-permute-start.14
  59.4 2.2 %shard_map.85 = (f32[256,128]{1,0:T(8,128)S(1)}, f32[256,128]{1,0:T(8,128)S(1)}, bf16[4,256,128]{2,1,0:T(8,128)(2,1)S(1)}) custom-call(s32[130]{0:T(256)S(1)} %pad_add_fusion.t_ref, f32[512,128]{1,0:T(8,128)S(1)} %bitcast.26, f32[512,128]{1,0:T(8,128)S(1)} %bitcast.28, bf16[2,512,128]{2,1,0:T(8,128)(2,1)S(1)} %collective-permute-done.b, ...), custom_call_target="tpu_custom_call" | custom-call | flops 1310720 | bytes 1310720 | tf_op jit(solution)/shard_map/pallas_call | solution.py:60
  61.6 3.6 %collective-permute-start.15 = (bf16[4,256,128]{2,1,0:T(8,128)(2,1)S(1)}, bf16[4,256,128]{2,1,0:T(8,128)(2,1)S(1)}, u32[]{:S(2)}, u32[]{:S(2)}) collective-permute-start(bf16[4,256,128]{2,1,0:T(8,128)(2,1)S(1)} %get-tuple-element.41.refs_0_), channel_id=1, source_target_pairs={{0,96},{1,97},{2,98},{3,99},{4,100},{5,101},{6,102},{7,103},{8,104... | collective-permute-start | bytes 786440 | tf_op jit(solution)/shard_map/ppermute | solution.py:39
  65.2 0.7 collective-permute-start.17
  65.9 6.3 %collective-permute-done.13.x2 = bf16[4,256,128]{2,1,0:T(8,128)(2,1)S(1)} collective-permute-done((bf16[4,256,128]{2,1,0:T(8,128)(2,1)S(1)}, bf16[4,256,128]{2,1,0:T(8,128)(2,1)S(1)}, u32[]{:S(2)}, u32[]{:S(2)}) %collective-permute-start.13) | collective-permute-done | bytes 262176 | tf_op jit(solution)/shard_map/ppermute | solution.py:39
  72.2 1.4 shard_map.93
  73.5 8.1 %all-to-all-start = ((f32[32,8,128]{2,1,0:T(8,128)}), f32[32,8,128]{2,1,0:T(8,128)S(1)}, u32[]{:S(2)}, u32[]{:S(2)}) async-start(f32[32,8,128]{2,1,0:T(8,128)} %get-tuple-element.42), calls=%async_computation | async-start | bytes 262144 | tf_op jit(solution)/shard_map/all_to_all | solution.py:324
  81.7 2.4 %collective-permute-done.17.refs_3_ = bf16[4,256,128]{2,1,0:T(8,128)(2,1)S(1)} collective-permute-done((bf16[4,256,128]{2,1,0:T(8,128)(2,1)S(1)}, bf16[4,256,128]{2,1,0:T(8,128)(2,1)S(1)}, u32[]{:S(2)}, u32[]{:S(2)}) %collective-permute-start.17) | collective-permute-done | bytes 262176 | tf_op jit(solution)/shard_map/ppermute | solution.py:39
  84.1 5.1 %all-to-all-done.refs_4_ = f32[32,8,128]{2,1,0:T(8,128)S(1)} async-done(((f32[32,8,128]{2,1,0:T(8,128)}), f32[32,8,128]{2,1,0:T(8,128)S(1)}, u32[]{:S(2)}, u32[]{:S(2)}) %all-to-all-start) | async-done | bytes 131104 | tf_op jit(solution)/shard_map/all_to_all | solution.py:324
  89.3 1.8 %shard_map.94 = (bf16[4,256,128]{2,1,0:T(8,128)(2,1)S(1)}, f32[8,128]{1,0:T(8,128)S(1)}) custom-call(s32[1]{0:T(128)} %constant.267.clone.1.t_ref, f32[4,256,128]{2,1,0:T(8,128)S(1)} %get-tuple-element.40.g, bf16[4,256,128]{2,1,0:T(8,128)(2,1)S(1)} %get-tuple-element.41.refs_0_, bf16[4,256,128]{2,1,0:T(8,128)(2,1)S(1)} %collective-permute-done.15.refs_1_, ...), custom_call_target="tpu_custom_call" | custom-call | flops 2621440 | bytes 1835008 | tf_op jit(solution)/shard_map/pallas_call | solution.py:60
  91.0 1.1 collective-permute-start.18
  92.1 1.2 collective-permute-start.19
  93.3 3.3 %collective-permute-done.18 = bf16[4,256,128]{2,1,0:T(8,128)(2,1)S(1)} collective-permute-done((bf16[4,256,128]{2,1,0:T(8,128)(2,1)S(1)}, bf16[4,256,128]{2,1,0:T(8,128)(2,1)S(1)}, u32[]{:S(2)}, u32[]{:S(2)}) %collective-permute-start.18) | collective-permute-done | bytes 262176 | tf_op jit(solution)/shard_map/ppermute | solution.py:39
  96.7 2.5 %collective-permute-done.19 = bf16[4,256,128]{2,1,0:T(8,128)(2,1)S(1)} collective-permute-done((bf16[4,256,128]{2,1,0:T(8,128)(2,1)S(1)}, bf16[4,256,128]{2,1,0:T(8,128)(2,1)S(1)}, u32[]{:S(2)}, u32[]{:S(2)}) %collective-permute-start.19) | collective-permute-done | bytes 262176 | tf_op jit(solution)/shard_map/ppermute | solution.py:39
  99.2 2.7 %collective-permute-done.20 = bf16[4,256,128]{2,1,0:T(8,128)(2,1)S(1)} collective-permute-done((bf16[4,256,128]{2,1,0:T(8,128)(2,1)S(1)}, bf16[4,256,128]{2,1,0:T(8,128)(2,1)S(1)}, u32[]{:S(2)}, u32[]{:S(2)}) %collective-permute-start.20) | collective-permute-done | bytes 262176 | tf_op jit(solution)/shard_map/ppermute | solution.py:39
  102.0 1.5 %collective-permute-start.23 = (bf16[16,256,128]{2,1,0:T(8,128)(2,1)S(1)}, bf16[16,256,128]{2,1,0:T(8,128)(2,1)S(1)}, u32[]{:S(2)}, u32[]{:S(2)}) collective-permute-start(bf16[16,256,128]{2,1,0:T(8,128)(2,1)S(1)} %constant_dynamic-update-slice_fusion.refs_0_), channel_id=1, source_target_pairs={{0,1},{1,0},{2,3},{3,2},{4,5},{5,4},{6,7},{7,6},{8,9},{9,8},{10,11... | collective-permute-start | bytes 3145736 | tf_op jit(solution)/shard_map/ppermute | solution.py:39
  103.5 1.3 collective-permute-start.22
  104.8 0.9 collective-permute-start.26
  105.7 2.1 %shard_map.95.refs_2_ = bf16[128,256,128]{2,1,0:T(8,128)(2,1)} custom-call(s32[32]{0:T(128)S(1)} %pad_add_fusion.5.t_ref, bf16[16,256,128]{2,1,0:T(8,128)(2,1)S(1)} %constant_dynamic-update-slice_fusion.refs_0_, bf16[16,256,128]{2,1,0:T(8,128)(2,1)S(1)} %collective-permute-done.23.refs_1_), custom_call_target="tpu_custom_call" | custom-call | flops 4194304 | bytes 4194304 | tf_op jit(solution)/shard_map/pallas_call | solution.py:60
  107.9 11.0 %collective-permute-done.22.refs_0_ = bf16[16,256,128]{2,1,0:T(8,128)(2,1)S(1)} collective-permute-done((bf16[16,256,128]{2,1,0:T(8,128)(2,1)S(1)}, bf16[16,256,128]{2,1,0:T(8,128)(2,1)S(1)}, u32[]{:S(2)}, u32[]{:S(2)}) %collective-permute-start.22) | collective-permute-done | bytes 1048608 | tf_op jit(solution)/shard_map/ppermute | solution.py:39
  118.9 0.9 collective-permute-start.24
  119.9 8.2 %collective-permute-done.26.refs_1_ = bf16[16,256,128]{2,1,0:T(8,128)(2,1)S(1)} collective-permute-done((bf16[16,256,128]{2,1,0:T(8,128)(2,1)S(1)}, bf16[16,256,128]{2,1,0:T(8,128)(2,1)S(1)}, u32[]{:S(2)}, u32[]{:S(2)}) %collective-permute-start.26) | collective-permute-done | bytes 1048608 | tf_op jit(solution)/shard_map/ppermute | solution.py:39
  128.1 1.7 %collective-permute-start.27 = (bf16[16,256,128]{2,1,0:T(8,128)(2,1)S(1)}, bf16[16,256,128]{2,1,0:T(8,128)(2,1)S(1)}, u32[]{:S(2)}, u32[]{:S(2)}) collective-permute-start(bf16[16,256,128]{2,1,0:T(8,128)(2,1)S(1)} %collective-permute-done.26.refs_1_), channel_id=1, source_target_pairs={{0,1},{1,0},{2,3},{3,2},{4,5},{5,4},{6,7},{7,6},{8,9},{9,8},{10,11... | collective-permute-start | bytes 3145736 | tf_op jit(solution)/shard_map/ppermute | solution.py:39
  129.8 2.1 %shard_map.96.refs_2_ = bf16[128,256,128]{2,1,0:T(8,128)(2,1)} custom-call(s32[32]{0:T(128)S(1)} %pad_add_fusion.4.t_ref, bf16[16,256,128]{2,1,0:T(8,128)(2,1)S(1)} %collective-permute-done.22.refs_0_, bf16[16,256,128]{2,1,0:T(8,128)(2,1)S(1)} %collective-permute-done.24.refs_1_, ...), custom_call_target="tpu_custom_call", output_to_operand_aliasing={{}: (3, {})} | custom-call | flops 4194304 | bytes 4194304 | tf_op jit(solution)/shard_map/pallas_call | solution.py:60
  131.9 3.1 %collective-permute-done.21.refs_0_ = bf16[16,256,128]{2,1,0:T(8,128)(2,1)S(1)} collective-permute-done((bf16[16,256,128]{2,1,0:T(8,128)(2,1)S(1)}, bf16[16,256,128]{2,1,0:T(8,128)(2,1)S(1)}, u32[]{:S(2)}, u32[]{:S(2)}) %collective-permute-start.21) | collective-permute-done | bytes 1048608 | tf_op jit(solution)/shard_map/ppermute | solution.py:39
  135.0 0.9 collective-permute-start.25
  136.0 0.5 slice.6
  136.6 1.5 %fusion.1 = (f32[32768]{0:T(1024)}, f32[32768]{0:T(1024)}, f32[32768]{0:T(1024)}) fusion(f32[4,256,128]{2,1,0:T(8,128)S(1)} %get-tuple-element.40.g, f32[]{:T(128)} %bitcast.5, f32[256,128]{1,0:T(8,128)S(1)} %get-tuple-element.44, f32[256,128]{1,0:T(8,128)S(1)} %get-tuple-element.27, f32[32768]{0:T(1024)S(1)} %copy-done.2), kind=kLoop, calls=%fused_computation.6 | loop fusion | flops 491520 | bytes 917508 | tf_op jit(solution)/shard_map/reshape | solution.py:327
  138.0 2.1 %shard_map.97.refs_2_ = bf16[128,256,128]{2,1,0:T(8,128)(2,1)} custom-call(s32[32]{0:T(128)S(1)} %pad_add_fusion.6.t_ref, bf16[16,256,128]{2,1,0:T(8,128)(2,1)S(1)} %collective-permute-done.21.refs_0_, bf16[16,256,128]{2,1,0:T(8,128)(2,1)S(1)} %collective-permute-done.26.refs_1_, ...), custom_call_target="tpu_custom_call", output_to_operand_aliasing={{}: (3, {})} | custom-call | flops 4194304 | bytes 4194304 | tf_op jit(solution)/shard_map/pallas_call | solution.py:60
  140.2 2.1 %shard_map.98 = bf16[128,256,128]{2,1,0:T(8,128)(2,1)} custom-call(s32[32]{0:T(128)S(1)} %pad_add_fusion.3.t_ref, bf16[16,256,128]{2,1,0:T(8,128)(2,1)S(1)} %collective-permute-done.25.refs_0_, bf16[16,256,128]{2,1,0:T(8,128)(2,1)S(1)} %collective-permute-done.27.refs_1_, bf16[128,256,128]{2,1,0:T(8,128)(2,1)} %shard_map.97.refs_2_), custom_call_target="tpu_custom_call", output_to_operand_aliasing={{}: (3, {})} | custom-call | flops 4194304 | bytes 4194304 | tf_op jit(solution)/shard_map/pallas_call | solution.py:60
  (47 shorter events, 1.5 us)
Async XLA Ops:
  5.5 6.6 %collective-permute-start.3 = (bf16[16,256,128]{2,1,0:T(8,128)(2,1)S(1)}, bf16[16,256,128]{2,1,0:T(8,128)(2,1)S(1)}, u32[]{:S(2)}, u32[]{:S(2)}) collective-permute-start(bf16[16,256,128]{2,1,0:T(8,128)(2,1)S(1)} %get-tuple-element.31), channel_id=1, source_target_pairs={{0,1},{1,0},{2,3},{3,2},{4,5},{5,4},{6,7},{7,6},{8,9},{9,8},{10,11... | collective-permute-start | bytes 3145736 | tf_op jit(solution)/shard_map/ppermute | solution.py:39
  7.0 6.9 %collective-permute-start.5 = (bf16[16,256,128]{2,1,0:T(8,128)(2,1)S(1)}, bf16[16,256,128]{2,1,0:T(8,128)(2,1)S(1)}, u32[]{:S(2)}, u32[]{:S(2)}) collective-permute-start(bf16[16,256,128]{2,1,0:T(8,128)(2,1)S(1)} %get-tuple-element.33), channel_id=1, source_target_pairs={{0,1},{1,0},{2,3},{3,2},{4,5},{5,4},{6,7},{7,6},{8,9},{9,8},{10,11... | collective-permute-start | bytes 3145736 | tf_op jit(solution)/shard_map/ppermute | solution.py:39
  7.1 9.8 %collective-permute-start.7 = (bf16[16,256,128]{2,1,0:T(8,128)(2,1)S(1)}, bf16[16,256,128]{2,1,0:T(8,128)(2,1)S(1)}, u32[]{:S(2)}, u32[]{:S(2)}) collective-permute-start(bf16[16,256,128]{2,1,0:T(8,128)(2,1)S(1)} %get-tuple-element.35), channel_id=1, source_target_pairs={{0,1},{1,0},{2,3},{3,2},{4,5},{5,4},{6,7},{7,6},{8,9},{9,8},{10,11... | collective-permute-start | bytes 3145736 | tf_op jit(solution)/shard_map/ppermute | solution.py:39
  7.5 10.8 %collective-permute-start.2 = (bf16[16,256,128]{2,1,0:T(8,128)(2,1)S(1)}, bf16[16,256,128]{2,1,0:T(8,128)(2,1)S(1)}, u32[]{:S(2)}, u32[]{:S(2)}) collective-permute-start(bf16[16,256,128]{2,1,0:T(8,128)(2,1)S(1)} %get-tuple-element.29), channel_id=1, source_target_pairs={{0,1},{1,0},{2,3},{3,2},{4,5},{5,4},{6,7},{7,6},{8,9},{9,8},{10,11... | collective-permute-start | bytes 3145736 | tf_op jit(solution)/shard_map/ppermute | solution.py:39
  12.5 32.6 %copy-start = (f32[1,65536]{1,0:T(1,128)S(1)}, f32[1,65536]{1,0:T(1,128)}, u32[]{:S(2)}) copy-start(f32[1,65536]{1,0:T(1,128)} %param.7) | copy-start | bytes 786436
  12.5 32.6 %copy-start.1 = (f32[1,65536]{1,0:T(1,128)S(1)}, f32[1,65536]{1,0:T(1,128)}, u32[]{:S(2)}) copy-start(f32[1,65536]{1,0:T(1,128)} %param.8) | copy-start | bytes 786436
  12.5 15.4 %collective-permute-start.4 = (bf16[16,256,128]{2,1,0:T(8,128)(2,1)S(1)}, bf16[16,256,128]{2,1,0:T(8,128)(2,1)S(1)}, u32[]{:S(2)}, u32[]{:S(2)}) collective-permute-start(bf16[16,256,128]{2,1,0:T(8,128)(2,1)S(1)} %shard_map.88), channel_id=1, source_target_pairs={{0,2},{1,9},{2,4},{3,11},{4,6},{5,13},{6,0},{7,15},{8,10},{9,17},{... | collective-permute-start | bytes 3145736 | tf_op jit(solution)/shard_map/ppermute | solution.py:39
  14.0 45.3 %copy-start.3 = (s32[129]{0:T(256)S(1)}, s32[129]{0:T(256)}, u32[]{:S(2)}) copy-start(s32[129]{0:T(256)} %param.9) | copy-start | bytes 1552
  14.0 45.4 %copy-start.2 = (f32[32768]{0:T(1024)S(1)}, f32[32768]{0:T(1024)}, u32[]{:S(2)}) copy-start(f32[32768]{0:T(1024)} %param.6) | copy-start | bytes 393220
  14.2 26.1 %collective-permute-start.6 = (bf16[16,256,128]{2,1,0:T(8,128)(2,1)S(1)}, bf16[16,256,128]{2,1,0:T(8,128)(2,1)S(1)}, u32[]{:S(2)}, u32[]{:S(2)}) collective-permute-start(bf16[16,256,128]{2,1,0:T(8,128)(2,1)S(1)} %shard_map.89), channel_id=1, source_target_pairs={{0,4},{1,17},{2,6},{3,19},{4,0},{5,21},{6,2},{7,23},{8,12},{9,25},... | collective-permute-start | bytes 3145736 | tf_op jit(solution)/shard_map/ppermute | solution.py:39
  17.2 23.1 %collective-permute-start.8 = (bf16[16,256,128]{2,1,0:T(8,128)(2,1)S(1)}, bf16[16,256,128]{2,1,0:T(8,128)(2,1)S(1)}, u32[]{:S(2)}, u32[]{:S(2)}) collective-permute-start(bf16[16,256,128]{2,1,0:T(8,128)(2,1)S(1)} %shard_map.90), channel_id=1, source_target_pairs={{0,6},{1,25},{2,0},{3,27},{4,2},{5,29},{6,4},{7,31},{8,14},{9,1},{... | collective-permute-start | bytes 3145736 | tf_op jit(solution)/shard_map/ppermute | solution.py:39
  41.0 12.4 %collective-permute-start.10 = (bf16[4,256,128]{2,1,0:T(8,128)(2,1)S(1)}, bf16[4,256,128]{2,1,0:T(8,128)(2,1)S(1)}, u32[]{:S(2)}, u32[]{:S(2)}) collective-permute-start(bf16[4,256,128]{2,1,0:T(8,128)(2,1)S(1)} %get-tuple-element.38), channel_id=1, source_target_pairs={{0,16},{1,5},{2,18},{3,7},{4,20},{5,1},{6,22},{7,3},{8,24},{9,13},... | collective-permute-start | bytes 786440 | tf_op jit(solution)/shard_map/ppermute | solution.py:39
  43.6 9.7 %collective-permute-start.11 = (bf16[4,256,128]{2,1,0:T(8,128)(2,1)S(1)}, bf16[4,256,128]{2,1,0:T(8,128)(2,1)S(1)}, u32[]{:S(2)}, u32[]{:S(2)}) collective-permute-start(bf16[4,256,128]{2,1,0:T(8,128)(2,1)S(1)} %get-tuple-element.39), channel_id=1, source_target_pairs={{0,24},{1,7},{2,26},{3,1},{4,28},{5,3},{6,30},{7,5},{8,0},{9,15},{... | collective-permute-start | bytes 786440 | tf_op jit(solution)/shard_map/ppermute | solution.py:39
  44.5 8.9 %collective-permute-start.9 = (bf16[4,256,128]{2,1,0:T(8,128)(2,1)S(1)}, bf16[4,256,128]{2,1,0:T(8,128)(2,1)S(1)}, u32[]{:S(2)}, u32[]{:S(2)}) collective-permute-start(bf16[4,256,128]{2,1,0:T(8,128)(2,1)S(1)} %get-tuple-element.37), channel_id=1, source_target_pairs={{0,8},{1,3},{2,10},{3,5},{4,12},{5,7},{6,14},{7,1},{8,16},{9,11},{... | collective-permute-start | bytes 786440 | tf_op jit(solution)/shard_map/ppermute | solution.py:39
  45.1 14.2 %collective-permute-start = (bf16[2,512,128]{2,1,0:T(8,128)(2,1)S(1)}, bf16[2,512,128]{2,1,0:T(8,128)(2,1)S(1)}, u32[]{:S(2)}, u32[]{:S(2)}) collective-permute-start(bf16[2,512,128]{2,1,0:T(8,128)(2,1)S(1)} %shard_map.84), channel_id=1, source_target_pairs={{0,1},{1,2},{2,3},{3,4},{4,5},{5,6},{6,7},{7,8},{8,9},{9,10},{10,1... | collective-permute-start | bytes 786440 | tf_op jit(solution)/shard_map/ppermute | solution.py:287
  51.4 7.9 %collective-permute-start.1 = (bf16[2,512,128]{2,1,0:T(8,128)(2,1)S(1)}, bf16[2,512,128]{2,1,0:T(8,128)(2,1)S(1)}, u32[]{:S(2)}, u32[]{:S(2)}) collective-permute-start(bf16[2,512,128]{2,1,0:T(8,128)(2,1)S(1)} %shard_map.84), channel_id=1, source_target_pairs={{1,0},{2,1},{3,2},{4,3},{5,4},{6,5},{7,6},{8,7},{9,8},{10,9},{11,1... | collective-permute-start | bytes 786440 | tf_op jit(solution)/shard_map/ppermute | solution.py:287
  53.5 11.6 %collective-permute-start.12 = (bf16[4,256,128]{2,1,0:T(8,128)(2,1)S(1)}, bf16[4,256,128]{2,1,0:T(8,128)(2,1)S(1)}, u32[]{:S(2)}, u32[]{:S(2)}) collective-permute-start(bf16[4,256,128]{2,1,0:T(8,128)(2,1)S(1)} %shard_map.92.w), channel_id=1, source_target_pairs={{0,32},{1,33},{2,34},{3,35},{4,36},{5,37},{6,38},{7,39},{8,40},{9,... | collective-permute-start | bytes 786440 | tf_op jit(solution)/shard_map/ppermute | solution.py:39
  55.2 16.9 %collective-permute-start.13 = (bf16[4,256,128]{2,1,0:T(8,128)(2,1)S(1)}, bf16[4,256,128]{2,1,0:T(8,128)(2,1)S(1)}, u32[]{:S(2)}, u32[]{:S(2)}) collective-permute-start(bf16[4,256,128]{2,1,0:T(8,128)(2,1)S(1)} %shard_map.92.w), channel_id=1, source_target_pairs={{0,64},{1,65},{2,66},{3,67},{4,68},{5,69},{6,70},{7,71},{8,72},{9,... | collective-permute-start | bytes 786440 | tf_op jit(solution)/shard_map/ppermute | solution.py:39
  58.5 13.6 %collective-permute-start.14 = (bf16[4,256,128]{2,1,0:T(8,128)(2,1)S(1)}, bf16[4,256,128]{2,1,0:T(8,128)(2,1)S(1)}, u32[]{:S(2)}, u32[]{:S(2)}) collective-permute-start(bf16[4,256,128]{2,1,0:T(8,128)(2,1)S(1)} %shard_map.92.w), channel_id=1, source_target_pairs={{0,96},{1,97},{2,98},{3,99},{4,100},{5,101},{6,102},{7,103},{8,104... | collective-permute-start | bytes 786440 | tf_op jit(solution)/shard_map/ppermute | solution.py:39
  61.6 20.1 %collective-permute-start.15 = (bf16[4,256,128]{2,1,0:T(8,128)(2,1)S(1)}, bf16[4,256,128]{2,1,0:T(8,128)(2,1)S(1)}, u32[]{:S(2)}, u32[]{:S(2)}) collective-permute-start(bf16[4,256,128]{2,1,0:T(8,128)(2,1)S(1)} %get-tuple-element.41.refs_0_), channel_id=1, source_target_pairs={{0,96},{1,97},{2,98},{3,99},{4,100},{5,101},{6,102},{7,103},{8,104... | collective-permute-start | bytes 786440 | tf_op jit(solution)/shard_map/ppermute | solution.py:39
  65.2 16.5 %collective-permute-start.16 = (bf16[4,256,128]{2,1,0:T(8,128)(2,1)S(1)}, bf16[4,256,128]{2,1,0:T(8,128)(2,1)S(1)}, u32[]{:S(2)}, u32[]{:S(2)}) collective-permute-start(bf16[4,256,128]{2,1,0:T(8,128)(2,1)S(1)} %get-tuple-element.41.refs_0_), channel_id=1, source_target_pairs={{0,64},{1,65},{2,66},{3,67},{4,68},{5,69},{6,70},{7,71},{8,72},{9,... | collective-permute-start | bytes 786440 | tf_op jit(solution)/shard_map/ppermute | solution.py:39
  65.2 19.0 %collective-permute-start.17 = (bf16[4,256,128]{2,1,0:T(8,128)(2,1)S(1)}, bf16[4,256,128]{2,1,0:T(8,128)(2,1)S(1)}, u32[]{:S(2)}, u32[]{:S(2)}) collective-permute-start(bf16[4,256,128]{2,1,0:T(8,128)(2,1)S(1)} %get-tuple-element.41.refs_0_), channel_id=1, source_target_pairs={{0,32},{1,33},{2,34},{3,35},{4,36},{5,37},{6,38},{7,39},{8,40},{9,... | collective-permute-start | bytes 786440 | tf_op jit(solution)/shard_map/ppermute | solution.py:39
  73.5 15.7 %all-to-all-start = ((f32[32,8,128]{2,1,0:T(8,128)}), f32[32,8,128]{2,1,0:T(8,128)S(1)}, u32[]{:S(2)}, u32[]{:S(2)}) async-start(f32[32,8,128]{2,1,0:T(8,128)} %get-tuple-element.42), calls=%async_computation | async-start | bytes 262144 | tf_op jit(solution)/shard_map/all_to_all | solution.py:324
  91.0 5.6 %collective-permute-start.18 = (bf16[4,256,128]{2,1,0:T(8,128)(2,1)S(1)}, bf16[4,256,128]{2,1,0:T(8,128)(2,1)S(1)}, u32[]{:S(2)}, u32[]{:S(2)}) collective-permute-start(bf16[4,256,128]{2,1,0:T(8,128)(2,1)S(1)} %get-tuple-element.45), channel_id=1, source_target_pairs={{0,24},{1,7},{2,26},{3,1},{4,28},{5,3},{6,30},{7,5},{8,0},{9,15},{... | collective-permute-start | bytes 786440 | tf_op jit(solution)/shard_map/ppermute | solution.py:39
  92.1 7.1 %collective-permute-start.19 = (bf16[4,256,128]{2,1,0:T(8,128)(2,1)S(1)}, bf16[4,256,128]{2,1,0:T(8,128)(2,1)S(1)}, u32[]{:S(2)}, u32[]{:S(2)}) collective-permute-start(bf16[4,256,128]{2,1,0:T(8,128)(2,1)S(1)} %get-tuple-element.45), channel_id=1, source_target_pairs={{0,16},{1,5},{2,18},{3,7},{4,20},{5,1},{6,22},{7,3},{8,24},{9,13},... | collective-permute-start | bytes 786440 | tf_op jit(solution)/shard_map/ppermute | solution.py:39
  93.3 8.7 %collective-permute-start.20 = (bf16[4,256,128]{2,1,0:T(8,128)(2,1)S(1)}, bf16[4,256,128]{2,1,0:T(8,128)(2,1)S(1)}, u32[]{:S(2)}, u32[]{:S(2)}) collective-permute-start(bf16[4,256,128]{2,1,0:T(8,128)(2,1)S(1)} %get-tuple-element.45), channel_id=1, source_target_pairs={{0,8},{1,3},{2,10},{3,5},{4,12},{5,7},{6,14},{7,1},{8,16},{9,11},{... | collective-permute-start | bytes 786440 | tf_op jit(solution)/shard_map/ppermute | solution.py:39
  102.0 3.7 %collective-permute-start.23 = (bf16[16,256,128]{2,1,0:T(8,128)(2,1)S(1)}, bf16[16,256,128]{2,1,0:T(8,128)(2,1)S(1)}, u32[]{:S(2)}, u32[]{:S(2)}) collective-permute-start(bf16[16,256,128]{2,1,0:T(8,128)(2,1)S(1)} %constant_dynamic-update-slice_fusion.refs_0_), channel_id=1, source_target_pairs={{0,1},{1,0},{2,3},{3,2},{4,5},{5,4},{6,7},{7,6},{8,9},{9,8},{10,11... | collective-permute-start | bytes 3145736 | tf_op jit(solution)/shard_map/ppermute | solution.py:39
  103.5 15.4 %collective-permute-start.22 = (bf16[16,256,128]{2,1,0:T(8,128)(2,1)S(1)}, bf16[16,256,128]{2,1,0:T(8,128)(2,1)S(1)}, u32[]{:S(2)}, u32[]{:S(2)}) collective-permute-start(bf16[16,256,128]{2,1,0:T(8,128)(2,1)S(1)} %constant_dynamic-update-slice_fusion.refs_0_), channel_id=1, source_target_pairs={{0,4},{1,17},{2,6},{3,19},{4,0},{5,21},{6,2},{7,23},{8,12},{9,25},... | collective-permute-start | bytes 3145736 | tf_op jit(solution)/shard_map/ppermute | solution.py:39
  104.8 23.3 %collective-permute-start.26 = (bf16[16,256,128]{2,1,0:T(8,128)(2,1)S(1)}, bf16[16,256,128]{2,1,0:T(8,128)(2,1)S(1)}, u32[]{:S(2)}, u32[]{:S(2)}) collective-permute-start(bf16[16,256,128]{2,1,0:T(8,128)(2,1)S(1)} %constant_dynamic-update-slice_fusion.refs_0_), channel_id=1, source_target_pairs={{0,6},{1,25},{2,0},{3,27},{4,2},{5,29},{6,4},{7,31},{8,14},{9,1},{... | collective-permute-start | bytes 3145736 | tf_op jit(solution)/shard_map/ppermute | solution.py:39
  118.9 10.9 %collective-permute-start.24 = (bf16[16,256,128]{2,1,0:T(8,128)(2,1)S(1)}, bf16[16,256,128]{2,1,0:T(8,128)(2,1)S(1)}, u32[]{:S(2)}, u32[]{:S(2)}) collective-permute-start(bf16[16,256,128]{2,1,0:T(8,128)(2,1)S(1)} %collective-permute-done.22.refs_0_), channel_id=1, source_target_pairs={{0,1},{1,0},{2,3},{3,2},{4,5},{5,4},{6,7},{7,6},{8,9},{9,8},{10,11... | collective-permute-start | bytes 3145736 | tf_op jit(solution)/shard_map/ppermute | solution.py:39
  119.9 15.2 %collective-permute-start.21 = (bf16[16,256,128]{2,1,0:T(8,128)(2,1)S(1)}, bf16[16,256,128]{2,1,0:T(8,128)(2,1)S(1)}, u32[]{:S(2)}, u32[]{:S(2)}) collective-permute-start(bf16[16,256,128]{2,1,0:T(8,128)(2,1)S(1)} %constant_dynamic-update-slice_fusion.refs_0_), channel_id=1, source_target_pairs={{0,2},{1,9},{2,4},{3,11},{4,6},{5,13},{6,0},{7,15},{8,10},{9,17},{... | collective-permute-start | bytes 3145736 | tf_op jit(solution)/shard_map/ppermute | solution.py:39
  128.1 12.1 %collective-permute-start.27 = (bf16[16,256,128]{2,1,0:T(8,128)(2,1)S(1)}, bf16[16,256,128]{2,1,0:T(8,128)(2,1)S(1)}, u32[]{:S(2)}, u32[]{:S(2)}) collective-permute-start(bf16[16,256,128]{2,1,0:T(8,128)(2,1)S(1)} %collective-permute-done.26.refs_1_), channel_id=1, source_target_pairs={{0,1},{1,0},{2,3},{3,2},{4,5},{5,4},{6,7},{7,6},{8,9},{9,8},{10,11... | collective-permute-start | bytes 3145736 | tf_op jit(solution)/shard_map/ppermute | solution.py:39
  135.0 5.1 %collective-permute-start.25 = (bf16[16,256,128]{2,1,0:T(8,128)(2,1)S(1)}, bf16[16,256,128]{2,1,0:T(8,128)(2,1)S(1)}, u32[]{:S(2)}, u32[]{:S(2)}) collective-permute-start(bf16[16,256,128]{2,1,0:T(8,128)(2,1)S(1)} %collective-permute-done.21.refs_0_), channel_id=1, source_target_pairs={{0,1},{1,0},{2,3},{3,2},{4,5},{5,4},{6,7},{7,6},{8,9},{9,8},{10,11... | collective-permute-start | bytes 3145736 | tf_op jit(solution)/shard_map/ppermute | solution.py:39

commit v2 on v1

--- a/solution.py
+++ b/solution.py
@@ -73,33 +73,41 @@
     )(t, *operands)
 
 
-def fetch(t, g, dtype):
+def fetch(g, *pieces):
     _, rows, lanes = g.shape
-    whole = dtype == g.dtype
+    n = 16
+    kept = [dtype == g.dtype for _, dtype in pieces]
+    m = len(pieces)
 
     def body(t_ref, g_ref, *refs):
-        outs, (*buf, sem) = refs[:4], refs[4:]
-        to = [outs[i // 16].at[i % 16] if whole else buf[0].at[i] for i in range(64)]
-        copies = [pltpu.make_async_copy(g_ref.at[t_ref[i]], to[i], sem.at[i]) for i in range(64)]
-        for copy in copies:
+        outs, rest = refs[:m], refs[m:]
+        sem, buf = rest[-1], rest[0]
+        copies = []
+        for k in range(m):
+            slot = sum(not v for v in kept[:k]) * n
+            for i in range(n):
+                to = outs[k].at[i] if kept[k] else buf.at[slot + i]
+                copies.append((k, i, slot + i, pltpu.make_async_copy(g_ref.at[t_ref[k * n + i]], to, sem.at[k * n + i])))
+        for *_, copy in copies:
             copy.start()
-        for i, copy in enumerate(copies):
+        for k, i, at, copy in copies:
             copy.wait()
-            if not whole:
-                outs[i // 16][i % 16] = buf[0][i].astype(dtype)
-
-    scratch = [] if whole else [pltpu.VMEM((64, rows, lanes), g.dtype)]
-    n = 64 * rows * lanes
+            if not kept[k]:
+                outs[k][i] = buf[at].astype(outs[k].dtype)
+
+    converted = m - sum(kept)
+    scratch = [pltpu.VMEM((converted * n, rows, lanes), g.dtype)] if converted else []
+    size = m * n * rows * lanes
     return call(
         body,
-        t,
+        jnp.concatenate([t for t, _ in pieces]),
         (g,),
-        [pltpu.VMEM((16, rows, lanes), dtype)] * 4,
-        scratch + [pltpu.SemaphoreType.DMA((64,))],
-        n,
-        6 * n,
+        [pltpu.VMEM((n, rows, lanes), dtype) for _, dtype in pieces],
+        scratch + [pltpu.SemaphoreType.DMA((m * n,))],
+        size,
+        6 * size,
         spaces=[False],
-        limit=2 if whole else 10,
+        limit=2 + 2 * converted,
     )
 
 
@@ -217,53 +225,78 @@
     return call(body, jnp.zeros((1,), jnp.int32), (gradient, *states, squares), outs, [], 20 * size, 14 * size)
 
 
-def packed_moments(m_old, v_old):
-    def body(t_ref, m, v, o):
-        o[0] = m[...].astype(BF)
-        o[1] = v[...].astype(BF)
-
-    n = 2 * m_old.size
-    outs = [pltpu.VMEM((2, *m_old.shape), BF)]
-    return call(body, jnp.zeros((1,), jnp.int32), (m_old, v_old), outs, [], n, 6 * n)[0]
-
-
-def old_moments(device, old_bounds, m_old, v_old, before, after, master):
+def moved_rows(end, half, lanes, total):
+    return jnp.minimum(jnp.maximum(end - half * lanes, 0) // lanes, total - half - 8)
+
+
+def packed_moments(where, m_old, v_old, half):
+    total, lanes = m_old.shape
+    last = where.shape[0] - 1
+
+    def body(t_ref, m, v, up, down):
+        d = t_ref[last]
+        q = moved_rows(t_ref[d + 1] - t_ref[d], half, lanes, total)
+        for k, old in enumerate((m, v)):
+            up[k] = old[pl.ds(q, half + 8)].astype(BF)
+            down[k] = old[pl.ds(0, half)].astype(BF)
+
+    n = 4 * half * lanes
+    outs = [pltpu.VMEM((2, half + 8, lanes), BF), pltpu.VMEM((2, half, lanes), BF)]
+    return call(body, where, (m_old, v_old), outs, [], n, 6 * n)
+
+
+def old_moments(where, m_old, v_old, before, after, passed, master):
     rows, lanes = master.shape
+    total = m_old.shape[0]
+    half = rows // 2
     top = 392
-    reach = top + m_old.shape[0] + rows // 2 + 8
-    where = jnp.concatenate([old_bounds, device[None].astype(jnp.int32)])
-    last = old_bounds.shape[0]
-
-    def body(t_ref, m, v, b, a, w, m_out, v_out, state, buf):
+    reach = top + total + half + 8
+    last = where.shape[0] - 1
+
+    def body(t_ref, m, v, b, a, p, w, m_out, v_out, state, buf):
         d = t_ref[last]
         start = d * (rows * lanes)
         first = t_ref[d]
         end = t_ref[d + 1]
-        starts = (t_ref[jnp.maximum(d - 1, 0)], first, end)
-        offsets = [start - s + top * lanes for s in starts]
+        ahead = t_ref[jnp.maximum(d - 1, 0)]
+        q = moved_rows(first - ahead, half, lanes, total)
+        offsets = [start - s + top * lanes for s in (ahead + q * lanes, first, end)]
         for k, (old, out) in enumerate(((m, m_out), (v, v_out))):
-            held = pl.ds(top, m_old.shape[0])
-            buf[0, held] = b[k].astype(F32)
-            buf[1, held] = old[...]
-            buf[2, held] = a[k].astype(F32)
-
-            @pl.loop(0, rows // 32)
-            def _(i, k=k, out=out):
+            buf[0, pl.ds(top, half + 8)] = b[k].astype(F32)
+            buf[1, pl.ds(top, total)] = old[...]
+
+            @pl.when(d % 2 == 0)
+            def _(k=k):
+                buf[2, pl.ds(top, half)] = a[k].astype(F32)
+
+            @pl.when(d % 2 == 1)
+            def _(k=k):
+                buf[2, pl.ds(top, half)] = p[k].astype(F32)
+
+            def part(j, i):
                 lane = lax.broadcasted_iota(jnp.int32, (32, lanes), 1)
-                row = lax.broadcasted_iota(jnp.int32, (32, lanes), 0)
-                position = start + i * (32 * lanes) + row * lanes + lane
-                parts = []
-                for j, offset in enumerate(offsets):
-                    q = offset // lanes + i * 32
-                    r = offset % lanes
-                    back = (lanes - r) % lanes
-                    here = pltpu.roll(buf[j, pl.ds(q, 32)], back, 1)
-                    then = pltpu.roll(buf[j, pl.ds(q + 1, 32)], back, 1)
-                    parts.append(jnp.where(lane < lanes - r, here, then))
-                value = jnp.where(position < first, parts[0], jnp.where(position >= end, parts[2], parts[1]))
-                at = pl.ds(i * 32, 32)
-                out[at] = value
-                state[2 + k, at] = value.astype(BF)
+                at = offsets[j] // lanes + i * 32
+                r = offsets[j] % lanes
+                back = (lanes - r) % lanes
+                here = pltpu.roll(buf[j, pl.ds(at, 32)], back, 1)
+                then = pltpu.roll(buf[j, pl.ds(at + 1, 32)], back, 1)
+                return jnp.where(lane < lanes - r, here, then)
+
+            for low in (True, False):
+
+                @pl.loop(0, half // 32)
+                def _(step, k=k, out=out, low=low):
+                    i = step if low else step + half // 32
+                    lane = lax.broadcasted_iota(jnp.int32, (32, lanes), 1)
+                    row = lax.broadcasted_iota(jnp.int32, (32, lanes), 0)
+                    position = start + i * (32 * lanes) + row * lanes + lane
+                    if low:
+                        value = jnp.where(position < first, part(0, i), part(1, i))
+                    else:
+                        value = jnp.where(position >= end, part(2, i), part(1, i))
+                    at = pl.ds(i * 32, 32)
+                    out[at] = value
+                    state[2 + k, at] = value.astype(BF)
 
         high = w[...].astype(BF)
         state[0] = high
@@ -274,17 +307,12 @@
     return call(
         body,
         where,
-        (m_old, v_old, before, after, master),
+        (m_old, v_old, before, after, passed, master),
         outs,
         [pltpu.VMEM((3, reach, lanes), F32)],
         40 * size,
         40 * size,
     )
-
-
-def shifted(value, steps):
-    leading, last = (max(0, -steps), min(128, 128 - steps))
-    return lax.ppermute(value, DP, [(source, source + steps) for source in range(leading, last)])
 
 
 def step(grads, master, m_old, v_old, old_bounds):
@@ -297,22 +325,26 @@
     theirs = [table(1 - c, z, y, x, s) for s in range(4)]
     g = grads[0].reshape(128, rows, 128)
 
-    order = (2, 1, 3, 0)
-    given = fetch(jnp.concatenate([theirs[s] for s in order]), g, BF)
-    swapped = {s: send(v, "core") for s, v in zip(order, given)}
-    kept = fetch(jnp.concatenate([mine[s] for s in order]), g, F32)
-    kept = dict(zip(order, kept))
-    ringed = {}
-    pieces = {}
+    given, kept, swapped, pieces, ringed = {}, {}, {}, {}, {}
+    (given[2],) = fetch(g, (theirs[2], BF))
+    swapped[2] = send(given[2], "core")
+    kept[2], given[1], given[3] = fetch(g, (mine[2], F32), (theirs[1], BF), (theirs[3], BF))
+    swapped[1] = send(given[1], "core")
+    swapped[3] = send(given[3], "core")
+    kept[1], kept[3] = fetch(g, (mine[1], F32), (mine[3], F32))
+    given[0], kept[0] = fetch(g, (theirs[0], BF), (mine[0], F32))
+    swapped[0] = send(given[0], "core")
     for s in (2, 1, 3):
         pieces[s] = sum_piece((kept[s], swapped[s]))
         ringed[s] = send(pieces[s], "a", s)
     master_tiles = master.reshape(rows, 128)
     m_tiles, v_tiles = m_old[0].reshape(-1, 128), v_old[0].reshape(-1, 128)
-    packed = packed_moments(m_tiles, v_tiles)
-    before = shifted(packed, 1)
-    after = shifted(packed, -1)
-    m_prev, v_prev, state = old_moments(device, old_bounds, m_tiles, v_tiles, before, after, master_tiles)
+    where = jnp.concatenate([old_bounds, device[None].astype(jnp.int32)])
+    up, down = packed_moments(where, m_tiles, v_tiles, rows // 2)
+    before = lax.ppermute(up, DP, [(d, d + 1) for d in range(127)])
+    after = send(down, "core")
+    passed = lax.ppermute(after, DP, [(d, d - 2) for d in range(3, 128, 2)])
+    m_prev, v_prev, state = old_moments(where, m_tiles, v_tiles, before, after, passed, master_tiles)
     states = [state] + [None] * 3
     for s in (2, 1, 3):
         states[4 - s] = send(state, "z", s)

time: 143 us -> 148 us (1.035)
  waiting for transfers between devices: 66.8 us -> 71.2 us
  Pallas kernels: 24.5 us -> 27.9 us
  starting transfers between devices: 47.2 us -> 45.5 us
    ppermute x2, waiting for transfers between devices: 0.01 us -> 4 us  [the longest x1 3.97 us: step(): passed = lax.ppermute(after, DP, [(d, d - 2) for d in range(3, 128, 2)])]
    pallas_call x15 -> x17, Pallas kernels: 24.5 us -> 27.9 us  [call(): pl.pallas_call(body, grid_spec=pltpu.PrefetchScalarGridSpec(num_scalar_pr...]
    ppermute x2, starting transfers between devices: 8.2 us -> 5.19 us  [the longest x1 3.9 us: step(): before = lax.ppermute(up, DP, [(d, d + 1) for d in range(127)])]
    ppermute x26 -> x27, starting transfers between devices: 30.9 us -> 33.9 us  [send(): return lax.ppermute(value, DP, perm(axis, s))]
    ppermute x26 -> x27, waiting for transfers between devices: 61.7 us -> 64.3 us  [send(): return lax.ppermute(value, DP, perm(axis, s))]
    all_to_all x1, waiting for transfers between devices: 5.14 us -> 2.91 us  [step(): squares = lax.all_to_all(squares, ('y', 'x', 'core'), 0, 0, tiled=True)]
    all_to_all x1, starting transfers between devices: 8.14 us -> 6.41 us  [step(): squares = lax.all_to_all(squares, ('y', 'x', 'core'), 0, 0, tiled=True)]
  transfers between devices with their start and end apart: 29 -> 30, of which waited for: 11 -> 15; matrix products, arithmetic and copies ran while one was open for 2% -> 2% of each run, Pallas kernels for 11% -> 13%
where the time goes in v2:
time: 148 us
  waiting for transfers between devices  71.2 us (48%)
  starting transfers between devices  45.5 us (31%)
  Pallas kernels  27.9 us (19%)
  other arithmetic  1.8 us (1%)
    ppermute x27, waiting for transfers between devices, send(): return lax.ppermute(value, DP, perm(axis, s))  64.3 us
    ppermute x27, starting transfers between devices, send(): return lax.ppermute(value, DP, perm(axis, s))  33.9 us
    pallas_call x17, Pallas kernels, call(): pl.pallas_call(body, grid_spec=pltpu.PrefetchScalarGridSpec(num_scalar_pr...  27.9 us
    all_to_all x1, starting transfers between devices, step(): squares = lax.all_to_all(squares, ('y', 'x', 'core'), 0, 0, tiled=True)  6.41 us
    ppermute x1, waiting for transfers between devices, step(): passed = lax.ppermute(after, DP, [(d, d - 2) for d in range(3, 128, 2)])  3.97 us
    ppermute x1, starting transfers between devices, step(): before = lax.ppermute(up, DP, [(d, d + 1) for d in range(127)])  3.9 us
  transfers between devices with their start and end apart: 30, of which 15 were waited for; matrix products, arithmetic and copies ran while one was open for 2% of the time, Pallas kernels for 13%

profile of v2, /device:TPU:1, one launch (start us, length us, event | category | flops | bytes accessed | tf_op | source)
XLA Modules:
  0.0 148.1 jit_solution(2126890677124079187)
XLA Ops:
  1.0 3.8 %shard_map.88 = (f32[16,256,128]{2,1,0:T(8,128)S(1)}, bf16[16,256,128]{2,1,0:T(8,128)(2,1)S(1)}, bf16[16,256,128]{2,1,0:T(8,128)(2,1)S(1)}) custom-call(s32[48]{0:T(128)S(1)} %pad_add_fusion.3.t_ref, f32[128,256,128]{2,1,0:T(8,128)} %bitcast.30), custom_call_target="tpu_custom_call" | custom-call | flops 1572864 | bytes 9437184 | tf_op jit(solution)/shard_map/pallas_call | solution.py:60
  4.8 1.5 collective-permute-start.4
  6.4 2.3 %shard_map.90 = bf16[16,256,128]{2,1,0:T(8,128)(2,1)S(1)} custom-call(s32[16]{0:T(128)S(1)} %get-tuple-element.52.t_ref, f32[128,256,128]{2,1,0:T(8,128)} %bitcast.31), custom_call_target="tpu_custom_call" | custom-call | flops 524288 | bytes 3145728 | tf_op jit(solution)/shard_map/pallas_call | solution.py:60
  9.2 3.1 %shard_map.86 = (bf16[16,256,128]{2,1,0:T(8,128)(2,1)S(1)}, f32[16,256,128]{2,1,0:T(8,128)S(1)}) custom-call(s32[32]{0:T(128)S(1)} %get-tuple-element.60.t_ref, f32[128,256,128]{2,1,0:T(8,128)} %bitcast.32), custom_call_target="tpu_custom_call" | custom-call | flops 1048576 | bytes 6291456 | tf_op jit(solution)/shard_map/pallas_call | solution.py:60
  12.5 3.1 %shard_map.87 = (f32[16,256,128]{2,1,0:T(8,128)S(1)}, f32[16,256,128]{2,1,0:T(8,128)S(1)}) custom-call(s32[32]{0:T(128)S(1)} %get-tuple-element.68.t_ref, f32[128,256,128]{2,1,0:T(8,128)} %bitcast.33), custom_call_target="tpu_custom_call" | custom-call | flops 1048576 | bytes 6291456 | tf_op jit(solution)/shard_map/pallas_call | solution.py:60
  15.8 1.5 collective-permute-start.5
  17.6 1.5 %collective-permute-start.9 = (bf16[16,256,128]{2,1,0:T(8,128)(2,1)S(1)}, bf16[16,256,128]{2,1,0:T(8,128)(2,1)S(1)}, u32[]{:S(2)}, u32[]{:S(2)}) collective-permute-start(bf16[16,256,128]{2,1,0:T(8,128)(2,1)S(1)} %shard_map.92), channel_id=1, source_target_pairs={{0,6},{1,25},{2,0},{3,27},{4,2},{5,29},{6,4},{7,31},{8,14},{9,1},{... | collective-permute-start | bytes 3145736 | tf_op jit(solution)/shard_map/ppermute | solution.py:39
  19.4 1.7 %collective-permute-start.7 = (bf16[16,256,128]{2,1,0:T(8,128)(2,1)S(1)}, bf16[16,256,128]{2,1,0:T(8,128)(2,1)S(1)}, u32[]{:S(2)}, u32[]{:S(2)}) collective-permute-start(bf16[16,256,128]{2,1,0:T(8,128)(2,1)S(1)} %shard_map.91), channel_id=1, source_target_pairs={{0,4},{1,17},{2,6},{3,19},{4,0},{5,21},{6,2},{7,23},{8,12},{9,25},... | collective-permute-start | bytes 3145736 | tf_op jit(solution)/shard_map/ppermute | solution.py:39
  21.1 10.2 %collective-permute-done.5.refs_2_ = bf16[16,256,128]{2,1,0:T(8,128)(2,1)S(1)} collective-permute-done((bf16[16,256,128]{2,1,0:T(8,128)(2,1)S(1)}, bf16[16,256,128]{2,1,0:T(8,128)(2,1)S(1)}, u32[]{:S(2)}, u32[]{:S(2)}) %collective-permute-start.5) | collective-permute-done | bytes 1048608 | tf_op jit(solution)/shard_map/ppermute | solution.py:39
  31.6 12.1 %collective-permute-done.7.refs_3_ = bf16[16,256,128]{2,1,0:T(8,128)(2,1)S(1)} collective-permute-done((bf16[16,256,128]{2,1,0:T(8,128)(2,1)S(1)}, bf16[16,256,128]{2,1,0:T(8,128)(2,1)S(1)}, u32[]{:S(2)}, u32[]{:S(2)}) %collective-permute-start.7) | collective-permute-done | bytes 1048608 | tf_op jit(solution)/shard_map/ppermute | solution.py:39
  44.3 1.0 collective-permute-start.10
  45.3 2.7 %collective-permute-start.11 = (bf16[4,256,128]{2,1,0:T(8,128)(2,1)S(1)}, bf16[4,256,128]{2,1,0:T(8,128)(2,1)S(1)}, u32[]{:S(2)}, u32[]{:S(2)}) collective-permute-start(bf16[4,256,128]{2,1,0:T(8,128)(2,1)S(1)} %get-tuple-element.40), channel_id=1, source_target_pairs={{0,16},{1,5},{2,18},{3,7},{4,20},{5,1},{6,22},{7,3},{8,24},{9,13},... | collective-permute-start | bytes 786440 | tf_op jit(solution)/shard_map/ppermute | solution.py:39
  48.1 0.9 collective-permute-start.12
  48.9 2.2 %collective-permute-done.10.refs_1_ = bf16[4,256,128]{2,1,0:T(8,128)(2,1)S(1)} collective-permute-done((bf16[4,256,128]{2,1,0:T(8,128)(2,1)S(1)}, bf16[4,256,128]{2,1,0:T(8,128)(2,1)S(1)}, u32[]{:S(2)}, u32[]{:S(2)}) %collective-permute-start.10) | collective-permute-done | bytes 262176 | tf_op jit(solution)/shard_map/ppermute | solution.py:39
  51.1 3.8 %collective-permute-done.11.refs_2_ = bf16[4,256,128]{2,1,0:T(8,128)(2,1)S(1)} collective-permute-done((bf16[4,256,128]{2,1,0:T(8,128)(2,1)S(1)}, bf16[4,256,128]{2,1,0:T(8,128)(2,1)S(1)}, u32[]{:S(2)}, u32[]{:S(2)}) %collective-permute-start.11) | collective-permute-done | bytes 262176 | tf_op jit(solution)/shard_map/ppermute | solution.py:39
  55.1 1.7 %collective-permute-start.13 = (bf16[4,256,128]{2,1,0:T(8,128)(2,1)S(1)}, bf16[4,256,128]{2,1,0:T(8,128)(2,1)S(1)}, u32[]{:S(2)}, u32[]{:S(2)}) collective-permute-start(bf16[4,256,128]{2,1,0:T(8,128)(2,1)S(1)} %shard_map.94.w), channel_id=1, source_target_pairs={{0,32},{1,33},{2,34},{3,35},{4,36},{5,37},{6,38},{7,39},{8,40},{9,... | collective-permute-start | bytes 786440 | tf_op jit(solution)/shard_map/ppermute | solution.py:39
  57.4 2.5 %collective-permute-start.1 = (bf16[2,128,128]{2,1,0:T(8,128)(2,1)S(1)}, bf16[2,128,128]{2,1,0:T(8,128)(2,1)S(1)}, u32[]{:S(2)}, u32[]{:S(2)}) collective-permute-start(bf16[2,128,128]{2,1,0:T(8,128)(2,1)S(1)} %get-tuple-element.29), channel_id=1, source_target_pairs={{0,1},{1,0},{2,3},{3,2},{4,5},{5,4},{6,7},{7,6},{8,9},{9,8},{10,11... | collective-permute-start | bytes 196616 | tf_op jit(solution)/shard_map/ppermute | solution.py:39
  59.9 3.3 %collective-permute-start.14 = (bf16[4,256,128]{2,1,0:T(8,128)(2,1)S(1)}, bf16[4,256,128]{2,1,0:T(8,128)(2,1)S(1)}, u32[]{:S(2)}, u32[]{:S(2)}) collective-permute-start(bf16[4,256,128]{2,1,0:T(8,128)(2,1)S(1)} %shard_map.94.w), channel_id=1, source_target_pairs={{0,64},{1,65},{2,66},{3,67},{4,68},{5,69},{6,70},{7,71},{8,72},{9,... | collective-permute-start | bytes 786440 | tf_op jit(solution)/shard_map/ppermute | solution.py:39
  63.9 3.9 %collective-permute-start = (bf16[2,136,128]{2,1,0:T(8,128)(2,1)S(1)}, bf16[2,136,128]{2,1,0:T(8,128)(2,1)S(1)}, u32[]{:S(2)}, u32[]{:S(2)}) collective-permute-start(bf16[2,136,128]{2,1,0:T(8,128)(2,1)S(1)} %get-tuple-element.28), channel_id=1, source_target_pairs={{0,1},{1,2},{2,3},{3,4},{4,5},{5,6},{6,7},{7,8},{8,9},{9,10},{10,1... | collective-permute-start | bytes 208904 | tf_op jit(solution)/shard_map/ppermute | solution.py:344
  67.9 1.3 collective-permute-start.2
  69.2 4.0 %collective-permute-done.2.p = bf16[2,128,128]{2,1,0:T(8,128)(2,1)S(1)} collective-permute-done((bf16[2,128,128]{2,1,0:T(8,128)(2,1)S(1)}, bf16[2,128,128]{2,1,0:T(8,128)(2,1)S(1)}, u32[]{:S(2)}, u32[]{:S(2)}) %collective-permute-start.2) | collective-permute-done | bytes 65568 | tf_op jit(solution)/shard_map/ppermute | solution.py:346
  73.2 2.0 %shard_map.85 = (f32[256,128]{1,0:T(8,128)S(1)}, f32[256,128]{1,0:T(8,128)S(1)}, bf16[4,256,128]{2,1,0:T(8,128)(2,1)S(1)}) custom-call(s32[130]{0:T(256)S(1)} %pad_add_fusion.t_ref, f32[512,128]{1,0:T(8,128)S(1)} %bitcast.26, f32[512,128]{1,0:T(8,128)S(1)} %bitcast.28, bf16[2,136,128]{2,1,0:T(8,128)(2,1)S(1)} %collective-permute-done.b, ...), custom_call_target="tpu_custom_call" | custom-call | flops 1310720 | bytes 1310720 | tf_op jit(solution)/shard_map/pallas_call | solution.py:60
  75.2 1.9 %collective-permute-start.16 = (bf16[4,256,128]{2,1,0:T(8,128)(2,1)S(1)}, bf16[4,256,128]{2,1,0:T(8,128)(2,1)S(1)}, u32[]{:S(2)}, u32[]{:S(2)}) collective-permute-start(bf16[4,256,128]{2,1,0:T(8,128)(2,1)S(1)} %get-tuple-element.43.refs_0_), channel_id=1, source_target_pairs={{0,96},{1,97},{2,98},{3,99},{4,100},{5,101},{6,102},{7,103},{8,104... | collective-permute-start | bytes 786440 | tf_op jit(solution)/shard_map/ppermute | solution.py:39
  77.1 2.8 %collective-permute-start.17 = (bf16[4,256,128]{2,1,0:T(8,128)(2,1)S(1)}, bf16[4,256,128]{2,1,0:T(8,128)(2,1)S(1)}, u32[]{:S(2)}, u32[]{:S(2)}) collective-permute-start(bf16[4,256,128]{2,1,0:T(8,128)(2,1)S(1)} %get-tuple-element.43.refs_0_), channel_id=1, source_target_pairs={{0,64},{1,65},{2,66},{3,67},{4,68},{5,69},{6,70},{7,71},{8,72},{9,... | collective-permute-start | bytes 786440 | tf_op jit(solution)/shard_map/ppermute | solution.py:39
  79.9 1.4 shard_map.95
  81.3 6.4 %all-to-all-start = ((f32[32,8,128]{2,1,0:T(8,128)}), f32[32,8,128]{2,1,0:T(8,128)S(1)}, u32[]{:S(2)}, u32[]{:S(2)}) async-start(f32[32,8,128]{2,1,0:T(8,128)} %get-tuple-element.44), calls=%async_computation | async-start | bytes 262144 | tf_op jit(solution)/shard_map/all_to_all | solution.py:356
  87.8 4.7 %collective-permute-done.18.refs_3_ = bf16[4,256,128]{2,1,0:T(8,128)(2,1)S(1)} collective-permute-done((bf16[4,256,128]{2,1,0:T(8,128)(2,1)S(1)}, bf16[4,256,128]{2,1,0:T(8,128)(2,1)S(1)}, u32[]{:S(2)}, u32[]{:S(2)}) %collective-permute-start.18) | collective-permute-done | bytes 262176 | tf_op jit(solution)/shard_map/ppermute | solution.py:39
  92.4 2.9 %all-to-all-done.refs_4_ = f32[32,8,128]{2,1,0:T(8,128)S(1)} async-done(((f32[32,8,128]{2,1,0:T(8,128)}), f32[32,8,128]{2,1,0:T(8,128)S(1)}, u32[]{:S(2)}, u32[]{:S(2)}) %all-to-all-start) | async-done | bytes 131104 | tf_op jit(solution)/shard_map/all_to_all | solution.py:356
  95.3 1.8 %shard_map.96 = (bf16[4,256,128]{2,1,0:T(8,128)(2,1)S(1)}, f32[8,128]{1,0:T(8,128)S(1)}) custom-call(s32[1]{0:T(128)} %constant.267.clone.1.t_ref, f32[4,256,128]{2,1,0:T(8,128)S(1)} %get-tuple-element.42.g, bf16[4,256,128]{2,1,0:T(8,128)(2,1)S(1)} %get-tuple-element.43.refs_0_, bf16[4,256,128]{2,1,0:T(8,128)(2,1)S(1)} %collective-permute-done.16.refs_1_, ...), custom_call_target="tpu_custom_call" | custom-call | flops 2621440 | bytes 1835008 | tf_op jit(solution)/shard_map/pallas_call | solution.py:60
  97.1 1.1 collective-permute-start.19
  98.2 1.2 collective-permute-start.20
  99.4 3.3 %collective-permute-done.19 = bf16[4,256,128]{2,1,0:T(8,128)(2,1)S(1)} collective-permute-done((bf16[4,256,128]{2,1,0:T(8,128)(2,1)S(1)}, bf16[4,256,128]{2,1,0:T(8,128)(2,1)S(1)}, u32[]{:S(2)}, u32[]{:S(2)}) %collective-permute-start.19) | collective-permute-done | bytes 262176 | tf_op jit(solution)/shard_map/ppermute | solution.py:39
  102.7 2.5 %collective-permute-done.20 = bf16[4,256,128]{2,1,0:T(8,128)(2,1)S(1)} collective-permute-done((bf16[4,256,128]{2,1,0:T(8,128)(2,1)S(1)}, bf16[4,256,128]{2,1,0:T(8,128)(2,1)S(1)}, u32[]{:S(2)}, u32[]{:S(2)}) %collective-permute-start.20) | collective-permute-done | bytes 262176 | tf_op jit(solution)/shard_map/ppermute | solution.py:39
  105.3 2.7 %collective-permute-done.21 = bf16[4,256,128]{2,1,0:T(8,128)(2,1)S(1)} collective-permute-done((bf16[4,256,128]{2,1,0:T(8,128)(2,1)S(1)}, bf16[4,256,128]{2,1,0:T(8,128)(2,1)S(1)}, u32[]{:S(2)}, u32[]{:S(2)}) %collective-permute-start.21) | collective-permute-done | bytes 262176 | tf_op jit(solution)/shard_map/ppermute | solution.py:39
  108.0 1.5 collective-permute-start.24
  109.5 1.3 collective-permute-start.23
  110.8 0.9 collective-permute-start.27
  111.8 2.1 %shard_map.97.refs_2_ = bf16[128,256,128]{2,1,0:T(8,128)(2,1)} custom-call(s32[32]{0:T(128)S(1)} %get-tuple-element.59.t_ref, bf16[16,256,128]{2,1,0:T(8,128)(2,1)S(1)} %constant_dynamic-update-slice_fusion.refs_0_, bf16[16,256,128]{2,1,0:T(8,128)(2,1)S(1)} %collective-permute-done.24.refs_1_), custom_call_target="tpu_custom_call" | custom-call | flops 4194304 | bytes 4194304 | tf_op jit(solution)/shard_map/pallas_call | solution.py:60
  113.9 11.0 %collective-permute-done.23.refs_0_ = bf16[16,256,128]{2,1,0:T(8,128)(2,1)S(1)} collective-permute-done((bf16[16,256,128]{2,1,0:T(8,128)(2,1)S(1)}, bf16[16,256,128]{2,1,0:T(8,128)(2,1)S(1)}, u32[]{:S(2)}, u32[]{:S(2)}) %collective-permute-start.23) | collective-permute-done | bytes 1048608 | tf_op jit(solution)/shard_map/ppermute | solution.py:39
  125.0 0.9 collective-permute-start.25
  126.0 8.2 %collective-permute-done.27.refs_1_ = bf16[16,256,128]{2,1,0:T(8,128)(2,1)S(1)} collective-permute-done((bf16[16,256,128]{2,1,0:T(8,128)(2,1)S(1)}, bf16[16,256,128]{2,1,0:T(8,128)(2,1)S(1)}, u32[]{:S(2)}, u32[]{:S(2)}) %collective-permute-start.27) | collective-permute-done | bytes 1048608 | tf_op jit(solution)/shard_map/ppermute | solution.py:39
  134.1 1.7 %collective-permute-start.28 = (bf16[16,256,128]{2,1,0:T(8,128)(2,1)S(1)}, bf16[16,256,128]{2,1,0:T(8,128)(2,1)S(1)}, u32[]{:S(2)}, u32[]{:S(2)}) collective-permute-start(bf16[16,256,128]{2,1,0:T(8,128)(2,1)S(1)} %collective-permute-done.27.refs_1_), channel_id=1, source_target_pairs={{0,1},{1,0},{2,3},{3,2},{4,5},{5,4},{6,7},{7,6},{8,9},{9,8},{10,11... | collective-permute-start | bytes 3145736 | tf_op jit(solution)/shard_map/ppermute | solution.py:39
  135.8 2.1 %shard_map.98.refs_2_ = bf16[128,256,128]{2,1,0:T(8,128)(2,1)} custom-call(s32[32]{0:T(128)S(1)} %pad_add_fusion.5.t_ref, bf16[16,256,128]{2,1,0:T(8,128)(2,1)S(1)} %collective-permute-done.23.refs_0_, bf16[16,256,128]{2,1,0:T(8,128)(2,1)S(1)} %collective-permute-done.25.refs_1_, ...), custom_call_target="tpu_custom_call", output_to_operand_aliasing={{}: (3, {})} | custom-call | flops 4194304 | bytes 4194304 | tf_op jit(solution)/shard_map/pallas_call | solution.py:60
  137.9 3.1 %collective-permute-done.22.refs_0_ = bf16[16,256,128]{2,1,0:T(8,128)(2,1)S(1)} collective-permute-done((bf16[16,256,128]{2,1,0:T(8,128)(2,1)S(1)}, bf16[16,256,128]{2,1,0:T(8,128)(2,1)S(1)}, u32[]{:S(2)}, u32[]{:S(2)}) %collective-permute-start.22) | collective-permute-done | bytes 1048608 | tf_op jit(solution)/shard_map/ppermute | solution.py:39
  141.1 0.9 collective-permute-start.26
  142.5 1.4 fusion.1
  143.9 2.1 %shard_map.99.refs_2_ = bf16[128,256,128]{2,1,0:T(8,128)(2,1)} custom-call(s32[32]{0:T(128)S(1)} %get-tuple-element.69.t_ref, bf16[16,256,128]{2,1,0:T(8,128)(2,1)S(1)} %collective-permute-done.22.refs_0_, bf16[16,256,128]{2,1,0:T(8,128)(2,1)S(1)} %collective-permute-done.27.refs_1_, ...), custom_call_target="tpu_custom_call", output_to_operand_aliasing={{}: (3, {})} | custom-call | flops 4194304 | bytes 4194304 | tf_op jit(solution)/shard_map/pallas_call | solution.py:60
  146.0 2.1 %shard_map.100 = bf16[128,256,128]{2,1,0:T(8,128)(2,1)} custom-call(s32[32]{0:T(128)S(1)} %pad_add_fusion.4.t_ref, bf16[16,256,128]{2,1,0:T(8,128)(2,1)S(1)} %collective-permute-done.26.refs_0_, bf16[16,256,128]{2,1,0:T(8,128)(2,1)S(1)} %collective-permute-done.28.refs_1_, bf16[128,256,128]{2,1,0:T(8,128)(2,1)} %shard_map.99.refs_2_), custom_call_target="tpu_custom_call", output_to_operand_aliasing={{}: (3, {})} | custom-call | flops 4194304 | bytes 4194304 | tf_op jit(solution)/shard_map/pallas_call | solution.py:60
  (50 shorter events, 5.2 us)
Async XLA Ops:
  4.8 10.7 %collective-permute-start.4 = (bf16[16,256,128]{2,1,0:T(8,128)(2,1)S(1)}, bf16[16,256,128]{2,1,0:T(8,128)(2,1)S(1)}, u32[]{:S(2)}, u32[]{:S(2)}) collective-permute-start(bf16[16,256,128]{2,1,0:T(8,128)(2,1)S(1)} %get-tuple-element.34), channel_id=1, source_target_pairs={{0,1},{1,0},{2,3},{3,2},{4,5},{5,4},{6,7},{7,6},{8,9},{9,8},{10,11... | collective-permute-start | bytes 3145736 | tf_op jit(solution)/shard_map/ppermute | solution.py:39
  6.3 11.0 %collective-permute-start.8 = (bf16[16,256,128]{2,1,0:T(8,128)(2,1)S(1)}, bf16[16,256,128]{2,1,0:T(8,128)(2,1)S(1)}, u32[]{:S(2)}, u32[]{:S(2)}) collective-permute-start(bf16[16,256,128]{2,1,0:T(8,128)(2,1)S(1)} %get-tuple-element.37), channel_id=1, source_target_pairs={{0,1},{1,0},{2,3},{3,2},{4,5},{5,4},{6,7},{7,6},{8,9},{9,8},{10,11... | collective-permute-start | bytes 3145736 | tf_op jit(solution)/shard_map/ppermute | solution.py:39
  8.7 10.5 %collective-permute-start.6 = (bf16[16,256,128]{2,1,0:T(8,128)(2,1)S(1)}, bf16[16,256,128]{2,1,0:T(8,128)(2,1)S(1)}, u32[]{:S(2)}, u32[]{:S(2)}) collective-permute-start(bf16[16,256,128]{2,1,0:T(8,128)(2,1)S(1)} %shard_map.90), channel_id=1, source_target_pairs={{0,1},{1,0},{2,3},{3,2},{4,5},{5,4},{6,7},{7,6},{8,9},{9,8},{10,11... | collective-permute-start | bytes 3145736 | tf_op jit(solution)/shard_map/ppermute | solution.py:39
  12.3 8.8 %collective-permute-start.3 = (bf16[16,256,128]{2,1,0:T(8,128)(2,1)S(1)}, bf16[16,256,128]{2,1,0:T(8,128)(2,1)S(1)}, u32[]{:S(2)}, u32[]{:S(2)}) collective-permute-start(bf16[16,256,128]{2,1,0:T(8,128)(2,1)S(1)} %get-tuple-element.32), channel_id=1, source_target_pairs={{0,1},{1,0},{2,3},{3,2},{4,5},{5,4},{6,7},{7,6},{8,9},{9,8},{10,11... | collective-permute-start | bytes 3145736 | tf_op jit(solution)/shard_map/ppermute | solution.py:39
  15.8 41.0 %copy-start.3 = (s32[129]{0:T(256)S(1)}, s32[129]{0:T(256)}, u32[]{:S(2)}) copy-start(s32[129]{0:T(256)} %param.9) | copy-start | bytes 1552
  15.8 41.0 %copy-start = (f32[1,65536]{1,0:T(1,128)S(1)}, f32[1,65536]{1,0:T(1,128)}, u32[]{:S(2)}) copy-start(f32[1,65536]{1,0:T(1,128)} %param.7) | copy-start | bytes 786436
  15.8 41.0 %copy-start.1 = (f32[1,65536]{1,0:T(1,128)S(1)}, f32[1,65536]{1,0:T(1,128)}, u32[]{:S(2)}) copy-start(f32[1,65536]{1,0:T(1,128)} %param.8) | copy-start | bytes 786436
  15.8 15.4 %collective-permute-start.5 = (bf16[16,256,128]{2,1,0:T(8,128)(2,1)S(1)}, bf16[16,256,128]{2,1,0:T(8,128)(2,1)S(1)}, u32[]{:S(2)}, u32[]{:S(2)}) collective-permute-start(bf16[16,256,128]{2,1,0:T(8,128)(2,1)S(1)} %shard_map.89), channel_id=1, source_target_pairs={{0,2},{1,9},{2,4},{3,11},{4,6},{5,13},{6,0},{7,15},{8,10},{9,17},{... | collective-permute-start | bytes 3145736 | tf_op jit(solution)/shard_map/ppermute | solution.py:39
  17.3 55.9 %copy-start.2 = (f32[32768]{0:T(1024)S(1)}, f32[32768]{0:T(1024)}, u32[]{:S(2)}) copy-start(f32[32768]{0:T(1024)} %param.6) | copy-start | bytes 393220
  17.6 14.0 %collective-permute-start.9 = (bf16[16,256,128]{2,1,0:T(8,128)(2,1)S(1)}, bf16[16,256,128]{2,1,0:T(8,128)(2,1)S(1)}, u32[]{:S(2)}, u32[]{:S(2)}) collective-permute-start(bf16[16,256,128]{2,1,0:T(8,128)(2,1)S(1)} %shard_map.92), channel_id=1, source_target_pairs={{0,6},{1,25},{2,0},{3,27},{4,2},{5,29},{6,4},{7,31},{8,14},{9,1},{... | collective-permute-start | bytes 3145736 | tf_op jit(solution)/shard_map/ppermute | solution.py:39
  19.4 24.3 %collective-permute-start.7 = (bf16[16,256,128]{2,1,0:T(8,128)(2,1)S(1)}, bf16[16,256,128]{2,1,0:T(8,128)(2,1)S(1)}, u32[]{:S(2)}, u32[]{:S(2)}) collective-permute-start(bf16[16,256,128]{2,1,0:T(8,128)(2,1)S(1)} %shard_map.91), channel_id=1, source_target_pairs={{0,4},{1,17},{2,6},{3,19},{4,0},{5,21},{6,2},{7,23},{8,12},{9,25},... | collective-permute-start | bytes 3145736 | tf_op jit(solution)/shard_map/ppermute | solution.py:39
  44.3 6.8 %collective-permute-start.10 = (bf16[4,256,128]{2,1,0:T(8,128)(2,1)S(1)}, bf16[4,256,128]{2,1,0:T(8,128)(2,1)S(1)}, u32[]{:S(2)}, u32[]{:S(2)}) collective-permute-start(bf16[4,256,128]{2,1,0:T(8,128)(2,1)S(1)} %get-tuple-element.39), channel_id=1, source_target_pairs={{0,8},{1,3},{2,10},{3,5},{4,12},{5,7},{6,14},{7,1},{8,16},{9,11},{... | collective-permute-start | bytes 786440 | tf_op jit(solution)/shard_map/ppermute | solution.py:39
  45.3 9.6 %collective-permute-start.11 = (bf16[4,256,128]{2,1,0:T(8,128)(2,1)S(1)}, bf16[4,256,128]{2,1,0:T(8,128)(2,1)S(1)}, u32[]{:S(2)}, u32[]{:S(2)}) collective-permute-start(bf16[4,256,128]{2,1,0:T(8,128)(2,1)S(1)} %get-tuple-element.40), channel_id=1, source_target_pairs={{0,16},{1,5},{2,18},{3,7},{4,20},{5,1},{6,22},{7,3},{8,24},{9,13},... | collective-permute-start | bytes 786440 | tf_op jit(solution)/shard_map/ppermute | solution.py:39
  48.1 6.9 %collective-permute-start.12 = (bf16[4,256,128]{2,1,0:T(8,128)(2,1)S(1)}, bf16[4,256,128]{2,1,0:T(8,128)(2,1)S(1)}, u32[]{:S(2)}, u32[]{:S(2)}) collective-permute-start(bf16[4,256,128]{2,1,0:T(8,128)(2,1)S(1)} %get-tuple-element.41), channel_id=1, source_target_pairs={{0,24},{1,7},{2,26},{3,1},{4,28},{5,3},{6,30},{7,5},{8,0},{9,15},{... | collective-permute-start | bytes 786440 | tf_op jit(solution)/shard_map/ppermute | solution.py:39
  55.1 24.9 %collective-permute-start.13 = (bf16[4,256,128]{2,1,0:T(8,128)(2,1)S(1)}, bf16[4,256,128]{2,1,0:T(8,128)(2,1)S(1)}, u32[]{:S(2)}, u32[]{:S(2)}) collective-permute-start(bf16[4,256,128]{2,1,0:T(8,128)(2,1)S(1)} %shard_map.94.w), channel_id=1, source_target_pairs={{0,32},{1,33},{2,34},{3,35},{4,36},{5,37},{6,38},{7,39},{8,40},{9,... | collective-permute-start | bytes 786440 | tf_op jit(solution)/shard_map/ppermute | solution.py:39
  57.4 10.4 %collective-permute-start.1 = (bf16[2,128,128]{2,1,0:T(8,128)(2,1)S(1)}, bf16[2,128,128]{2,1,0:T(8,128)(2,1)S(1)}, u32[]{:S(2)}, u32[]{:S(2)}) collective-permute-start(bf16[2,128,128]{2,1,0:T(8,128)(2,1)S(1)} %get-tuple-element.29), channel_id=1, source_target_pairs={{0,1},{1,0},{2,3},{3,2},{4,5},{5,4},{6,7},{7,6},{8,9},{9,8},{10,11... | collective-permute-start | bytes 196616 | tf_op jit(solution)/shard_map/ppermute | solution.py:39
  59.9 20.0 %collective-permute-start.14 = (bf16[4,256,128]{2,1,0:T(8,128)(2,1)S(1)}, bf16[4,256,128]{2,1,0:T(8,128)(2,1)S(1)}, u32[]{:S(2)}, u32[]{:S(2)}) collective-permute-start(bf16[4,256,128]{2,1,0:T(8,128)(2,1)S(1)} %shard_map.94.w), channel_id=1, source_target_pairs={{0,64},{1,65},{2,66},{3,67},{4,68},{5,69},{6,70},{7,71},{8,72},{9,... | collective-permute-start | bytes 786440 | tf_op jit(solution)/shard_map/ppermute | solution.py:39
  63.2 16.7 %collective-permute-start.15 = (bf16[4,256,128]{2,1,0:T(8,128)(2,1)S(1)}, bf16[4,256,128]{2,1,0:T(8,128)(2,1)S(1)}, u32[]{:S(2)}, u32[]{:S(2)}) collective-permute-start(bf16[4,256,128]{2,1,0:T(8,128)(2,1)S(1)} %shard_map.94.w), channel_id=1, source_target_pairs={{0,96},{1,97},{2,98},{3,99},{4,100},{5,101},{6,102},{7,103},{8,104... | collective-permute-start | bytes 786440 | tf_op jit(solution)/shard_map/ppermute | solution.py:39
  63.9 5.3 %collective-permute-start = (bf16[2,136,128]{2,1,0:T(8,128)(2,1)S(1)}, bf16[2,136,128]{2,1,0:T(8,128)(2,1)S(1)}, u32[]{:S(2)}, u32[]{:S(2)}) collective-permute-start(bf16[2,136,128]{2,1,0:T(8,128)(2,1)S(1)} %get-tuple-element.28), channel_id=1, source_target_pairs={{0,1},{1,2},{2,3},{3,4},{4,5},{5,6},{6,7},{7,8},{8,9},{9,10},{10,1... | collective-permute-start | bytes 208904 | tf_op jit(solution)/shard_map/ppermute | solution.py:344
  67.9 5.3 %collective-permute-start.2 = (bf16[2,128,128]{2,1,0:T(8,128)(2,1)S(1)}, bf16[2,128,128]{2,1,0:T(8,128)(2,1)S(1)}, u32[]{:S(2)}, u32[]{:S(2)}) collective-permute-start(bf16[2,128,128]{2,1,0:T(8,128)(2,1)S(1)} %collective-permute-done.1.a), channel_id=1, source_target_pairs={{3,1},{5,3},{7,5},{9,7},{11,9},{13,11},{15,13},{17,15},{19,17},{21... | collective-permute-start | bytes 196616 | tf_op jit(solution)/shard_map/ppermute | solution.py:346
  75.2 12.6 %collective-permute-start.16 = (bf16[4,256,128]{2,1,0:T(8,128)(2,1)S(1)}, bf16[4,256,128]{2,1,0:T(8,128)(2,1)S(1)}, u32[]{:S(2)}, u32[]{:S(2)}) collective-permute-start(bf16[4,256,128]{2,1,0:T(8,128)(2,1)S(1)} %get-tuple-element.43.refs_0_), channel_id=1, source_target_pairs={{0,96},{1,97},{2,98},{3,99},{4,100},{5,101},{6,102},{7,103},{8,104... | collective-permute-start | bytes 786440 | tf_op jit(solution)/shard_map/ppermute | solution.py:39
  77.1 10.6 %collective-permute-start.17 = (bf16[4,256,128]{2,1,0:T(8,128)(2,1)S(1)}, bf16[4,256,128]{2,1,0:T(8,128)(2,1)S(1)}, u32[]{:S(2)}, u32[]{:S(2)}) collective-permute-start(bf16[4,256,128]{2,1,0:T(8,128)(2,1)S(1)} %get-tuple-element.43.refs_0_), channel_id=1, source_target_pairs={{0,64},{1,65},{2,66},{3,67},{4,68},{5,69},{6,70},{7,71},{8,72},{9,... | collective-permute-start | bytes 786440 | tf_op jit(solution)/shard_map/ppermute | solution.py:39
  79.9 12.5 %collective-permute-start.18 = (bf16[4,256,128]{2,1,0:T(8,128)(2,1)S(1)}, bf16[4,256,128]{2,1,0:T(8,128)(2,1)S(1)}, u32[]{:S(2)}, u32[]{:S(2)}) collective-permute-start(bf16[4,256,128]{2,1,0:T(8,128)(2,1)S(1)} %get-tuple-element.43.refs_0_), channel_id=1, source_target_pairs={{0,32},{1,33},{2,34},{3,35},{4,36},{5,37},{6,38},{7,39},{8,40},{9,... | collective-permute-start | bytes 786440 | tf_op jit(solution)/shard_map/ppermute | solution.py:39
  81.3 14.0 %all-to-all-start = ((f32[32,8,128]{2,1,0:T(8,128)}), f32[32,8,128]{2,1,0:T(8,128)S(1)}, u32[]{:S(2)}, u32[]{:S(2)}) async-start(f32[32,8,128]{2,1,0:T(8,128)} %get-tuple-element.44), calls=%async_computation | async-start | bytes 262144 | tf_op jit(solution)/shard_map/all_to_all | solution.py:356
  97.1 5.6 %collective-permute-start.19 = (bf16[4,256,128]{2,1,0:T(8,128)(2,1)S(1)}, bf16[4,256,128]{2,1,0:T(8,128)(2,1)S(1)}, u32[]{:S(2)}, u32[]{:S(2)}) collective-permute-start(bf16[4,256,128]{2,1,0:T(8,128)(2,1)S(1)} %get-tuple-element.47), channel_id=1, source_target_pairs={{0,24},{1,7},{2,26},{3,1},{4,28},{5,3},{6,30},{7,5},{8,0},{9,15},{... | collective-permute-start | bytes 786440 | tf_op jit(solution)/shard_map/ppermute | solution.py:39
  98.2 7.1 %collective-permute-start.20 = (bf16[4,256,128]{2,1,0:T(8,128)(2,1)S(1)}, bf16[4,256,128]{2,1,0:T(8,128)(2,1)S(1)}, u32[]{:S(2)}, u32[]{:S(2)}) collective-permute-start(bf16[4,256,128]{2,1,0:T(8,128)(2,1)S(1)} %get-tuple-element.47), channel_id=1, source_target_pairs={{0,16},{1,5},{2,18},{3,7},{4,20},{5,1},{6,22},{7,3},{8,24},{9,13},... | collective-permute-start | bytes 786440 | tf_op jit(solution)/shard_map/ppermute | solution.py:39
  99.3 8.7 %collective-permute-start.21 = (bf16[4,256,128]{2,1,0:T(8,128)(2,1)S(1)}, bf16[4,256,128]{2,1,0:T(8,128)(2,1)S(1)}, u32[]{:S(2)}, u32[]{:S(2)}) collective-permute-start(bf16[4,256,128]{2,1,0:T(8,128)(2,1)S(1)} %get-tuple-element.47), channel_id=1, source_target_pairs={{0,8},{1,3},{2,10},{3,5},{4,12},{5,7},{6,14},{7,1},{8,16},{9,11},{... | collective-permute-start | bytes 786440 | tf_op jit(solution)/shard_map/ppermute | solution.py:39
  108.0 3.7 %collective-permute-start.24 = (bf16[16,256,128]{2,1,0:T(8,128)(2,1)S(1)}, bf16[16,256,128]{2,1,0:T(8,128)(2,1)S(1)}, u32[]{:S(2)}, u32[]{:S(2)}) collective-permute-start(bf16[16,256,128]{2,1,0:T(8,128)(2,1)S(1)} %constant_dynamic-update-slice_fusion.refs_0_), channel_id=1, source_target_pairs={{0,1},{1,0},{2,3},{3,2},{4,5},{5,4},{6,7},{7,6},{8,9},{9,8},{10,11... | collective-permute-start | bytes 3145736 | tf_op jit(solution)/shard_map/ppermute | solution.py:39
  109.5 15.4 %collective-permute-start.23 = (bf16[16,256,128]{2,1,0:T(8,128)(2,1)S(1)}, bf16[16,256,128]{2,1,0:T(8,128)(2,1)S(1)}, u32[]{:S(2)}, u32[]{:S(2)}) collective-permute-start(bf16[16,256,128]{2,1,0:T(8,128)(2,1)S(1)} %constant_dynamic-update-slice_fusion.refs_0_), channel_id=1, source_target_pairs={{0,4},{1,17},{2,6},{3,19},{4,0},{5,21},{6,2},{7,23},{8,12},{9,25},... | collective-permute-start | bytes 3145736 | tf_op jit(solution)/shard_map/ppermute | solution.py:39
  110.8 23.4 %collective-permute-start.27 = (bf16[16,256,128]{2,1,0:T(8,128)(2,1)S(1)}, bf16[16,256,128]{2,1,0:T(8,128)(2,1)S(1)}, u32[]{:S(2)}, u32[]{:S(2)}) collective-permute-start(bf16[16,256,128]{2,1,0:T(8,128)(2,1)S(1)} %constant_dynamic-update-slice_fusion.refs_0_), channel_id=1, source_target_pairs={{0,6},{1,25},{2,0},{3,27},{4,2},{5,29},{6,4},{7,31},{8,14},{9,1},{... | collective-permute-start | bytes 3145736 | tf_op jit(solution)/shard_map/ppermute | solution.py:39
  125.0 10.9 %collective-permute-start.25 = (bf16[16,256,128]{2,1,0:T(8,128)(2,1)S(1)}, bf16[16,256,128]{2,1,0:T(8,128)(2,1)S(1)}, u32[]{:S(2)}, u32[]{:S(2)}) collective-permute-start(bf16[16,256,128]{2,1,0:T(8,128)(2,1)S(1)} %collective-permute-done.23.refs_0_), channel_id=1, source_target_pairs={{0,1},{1,0},{2,3},{3,2},{4,5},{5,4},{6,7},{7,6},{8,9},{9,8},{10,11... | collective-permute-start | bytes 3145736 | tf_op jit(solution)/shard_map/ppermute | solution.py:39
  125.9 15.2 %collective-permute-start.22 = (bf16[16,256,128]{2,1,0:T(8,128)(2,1)S(1)}, bf16[16,256,128]{2,1,0:T(8,128)(2,1)S(1)}, u32[]{:S(2)}, u32[]{:S(2)}) collective-permute-start(bf16[16,256,128]{2,1,0:T(8,128)(2,1)S(1)} %constant_dynamic-update-slice_fusion.refs_0_), channel_id=1, source_target_pairs={{0,2},{1,9},{2,4},{3,11},{4,6},{5,13},{6,0},{7,15},{8,10},{9,17},{... | collective-permute-start | bytes 3145736 | tf_op jit(solution)/shard_map/ppermute | solution.py:39
  134.1 11.8 %collective-permute-start.28 = (bf16[16,256,128]{2,1,0:T(8,128)(2,1)S(1)}, bf16[16,256,128]{2,1,0:T(8,128)(2,1)S(1)}, u32[]{:S(2)}, u32[]{:S(2)}) collective-permute-start(bf16[16,256,128]{2,1,0:T(8,128)(2,1)S(1)} %collective-permute-done.27.refs_1_), channel_id=1, source_target_pairs={{0,1},{1,0},{2,3},{3,2},{4,5},{5,4},{6,7},{7,6},{8,9},{9,8},{10,11... | collective-permute-start | bytes 3145736 | tf_op jit(solution)/shard_map/ppermute | solution.py:39
  141.1 4.9 %collective-permute-start.26 = (bf16[16,256,128]{2,1,0:T(8,128)(2,1)S(1)}, bf16[16,256,128]{2,1,0:T(8,128)(2,1)S(1)}, u32[]{:S(2)}, u32[]{:S(2)}) collective-permute-start(bf16[16,256,128]{2,1,0:T(8,128)(2,1)S(1)} %collective-permute-done.22.refs_0_), channel_id=1, source_target_pairs={{0,1},{1,0},{2,3},{3,2},{4,5},{5,4},{6,7},{7,6},{8,9},{9,8},{10,11... | collective-permute-start | bytes 3145736 | tf_op jit(solution)/shard_map/ppermute | solution.py:39

commit v3 on v2

--- a/solution.py
+++ b/solution.py
@@ -111,30 +111,50 @@
     )
 
 
-def sum_piece(parts, split=False):
-    n, rows, lanes = parts[0].shape
-    m = len(parts)
+def sum_piece(parts, kinds):
+    rows, lanes = parts[0][0][0].shape[1:]
+    operands = [array for part in parts for array, _, _ in part]
+
+    def sources(base):
+        at = 0
+        for part in parts:
+            begin = 0
+            for k, (_, first, count) in enumerate(part):
+                if begin <= base < begin + count:
+                    yield at + k, first + base - begin
+                begin += count
+            at += len(part)
 
     def body(t_ref, *refs):
-        ins, outs = refs[:m], refs[m:]
-        each = n // len(outs)
-
-        for q, o in enumerate(outs):
-
-            @pl.loop(0, each)
-            def _(i, q=q, o=o):
-                value = ins[0][q * each + i].astype(F32)
-                for r in ins[1:]:
-                    value = value + r[q * each + i].astype(F32)
+        ins, outs = refs[: len(operands)], refs[len(operands) :]
+        base = 0
+        for o, (count, _) in zip(outs, kinds):
+            where = list(sources(base))
+
+            @pl.loop(0, count)
+            def _(i, o=o, where=where):
+                value = None
+                for k, first in where:
+                    term = ins[k][first + i].astype(F32)
+                    value = term if value is None else value + term
                 o[i] = value.astype(o.dtype)
 
-    if split:
-        outs = [pltpu.VMEM((n // 4, rows, lanes), F32)] + [pltpu.VMEM((n // 4, rows, lanes), BF)] * 3
-    else:
-        outs = [pltpu.VMEM((n, rows, lanes), BF)]
-    size = n * rows * lanes
-    got = call(body, jnp.zeros((1,), jnp.int32), parts, outs, [], m * size, (6 + 2 * m) * size)
-    return got if split else got[0]
+            base += count
+
+    size = sum(count for count, _ in kinds) * rows * lanes
+    outs = [pltpu.VMEM((count, rows, lanes), dtype) for count, dtype in kinds]
+    return call(body, jnp.zeros((1,), jnp.int32), operands, outs, [], len(parts) * size, (4 + 2 * len(parts)) * size)
+
+
+def joined(first, second):
+    def body(t_ref, a, b, o):
+        o[: a.shape[0]] = a[...]
+        o[a.shape[0] :] = b[...]
+
+    shape = (first.shape[0] + second.shape[0], *first.shape[1:])
+    n = first.size + second.size
+    outs = [pltpu.VMEM(shape, first.dtype)]
+    return call(body, jnp.zeros((1,), jnp.int32), (first, second), outs, [], n, 4 * n)[0]
 
 
 def place(pairs, out):
@@ -325,7 +345,7 @@
     theirs = [table(1 - c, z, y, x, s) for s in range(4)]
     g = grads[0].reshape(128, rows, 128)
 
-    given, kept, swapped, pieces, ringed = {}, {}, {}, {}, {}
+    given, kept, swapped = {}, {}, {}
     (given[2],) = fetch(g, (theirs[2], BF))
     swapped[2] = send(given[2], "core")
     kept[2], given[1], given[3] = fetch(g, (mine[2], F32), (theirs[1], BF), (theirs[3], BF))
@@ -334,9 +354,21 @@
     kept[1], kept[3] = fetch(g, (mine[1], F32), (mine[3], F32))
     given[0], kept[0] = fetch(g, (theirs[0], BF), (mine[0], F32))
     swapped[0] = send(given[0], "core")
-    for s in (2, 1, 3):
-        pieces[s] = sum_piece((kept[s], swapped[s]))
-        ringed[s] = send(pieces[s], "a", s)
+    low, high = (0, 8), (8, 8)
+
+    def local_sum(s, half, *more):
+        (value,) = sum_piece([[(kept[s], *half)], [(swapped[s], *half)]] + [[(v, 0, 8)] for v in more], [(8, BF)])
+        return value
+
+    two_low, two_high = sum_piece([[(kept[2], 0, 16)], [(swapped[2], 0, 16)]], [(8, BF)] * 2)
+    passing_low = send(two_low, "a", 1)
+    passing_high = send(two_high, "a", 3)
+    left_high = send(local_sum(1, high), "a", 1)
+    right_low = send(local_sum(3, low), "a", 3)
+    joined_low = local_sum(1, low, passing_low)
+    left_low = send(joined_low, "a", 1)
+    joined_high = local_sum(3, high, passing_high)
+    right_high = send(joined_high, "a", 3)
     master_tiles = master.reshape(rows, 128)
     m_tiles, v_tiles = m_old[0].reshape(-1, 128), v_old[0].reshape(-1, 128)
     where = jnp.concatenate([old_bounds, device[None].astype(jnp.int32)])
@@ -348,9 +380,17 @@
     states = [state] + [None] * 3
     for s in (2, 1, 3):
         states[4 - s] = send(state, "z", s)
-    own, q1, q2, q3 = sum_piece((kept[0], swapped[0], ringed[1], ringed[2], ringed[3]), split=True)
+    own, q1, q2, q3 = sum_piece(
+        [
+            [(kept[0], 0, 16)],
+            [(swapped[0], 0, 16)],
+            [(left_low, 0, 8), (left_high, 0, 8)],
+            [(right_low, 0, 8), (right_high, 0, 8)],
+        ],
+        [(4, F32)] + [(4, BF)] * 3,
+    )
     q2, q1, q3 = send(q2, "b", 2), send(q1, "b", 1), send(q3, "b", 3)
-    partial = sum_piece((own, q1, q2, q3))
+    (partial,) = sum_piece([[(v, 0, 4)] for v in (own, q1, q2, q3)], [(4, BF)])
     w2, w1, w3 = send(partial, "z", 2), send(partial, "z", 1), send(partial, "z", 3)
     gradient, squares = total_piece(partial, w1, w2, w3, 32)
     squares = lax.all_to_all(squares, ("y", "x", "core"), 0, 0, tiled=True)
@@ -358,21 +398,24 @@
     new = adam(master_tiles, m_prev, v_prev, gradient[0], clip[0, 0])
     master_new, m_new, v_new = (value.reshape(width) for value in new)
 
-    got = {s: send(piece, "b", s) for s in (2, 1, 3)}
-    piece = jnp.concatenate([piece, got[3], got[2], got[1]])
-    got = {0: piece}
-    for s in (2, 1, 3):
-        got[(4 - s) % 4] = send(piece, "a", s)
-    other = {0: send(got[0], "core")}
-    out = place([(mine[0], got[0]), (theirs[0], other[0])], None)
-    got[2], out = lax.optimization_barrier((got[2], out))
-    other[2] = send(got[2], "core")
-    out = place([(mine[2], got[2]), (theirs[2], other[2])], out)
-    got[3], out = lax.optimization_barrier((got[3], out))
-    other[3] = send(got[3], "core")
-    other[1] = send(got[1], "core")
-    out = place([(mine[3], got[3]), (mine[1], got[1])], out)
-    out = place([(theirs[3], other[3]), (theirs[1], other[1])], out)
+    got = {}
+    for s in (3, 2, 1):
+        got[s] = send(piece, "b", s)
+    halves = {}
+    halves[0, 0] = joined(piece, got[3])
+    halves[0, 1] = joined(got[2], got[1])
+    for h in range(2):
+        halves[3, h] = send(halves[0, h], "a", 1)
+        halves[1, h] = send(halves[0, h], "a", 3)
+    halves[2, 0] = send(halves[3, 0], "a", 1)
+    halves[2, 1] = send(halves[1, 1], "a", 3)
+    partner = {}
+    for r, h in halves:
+        partner[r, h] = send(halves[r, h], "core")
+    out = None
+    for keys in (((0, 0), (0, 1)), ((3, 0), (1, 0)), ((3, 1), (1, 1)), ((2, 0), (2, 1))):
+        for tables, values in ((mine, halves), (theirs, partner)):
+            out = place([(tables[r][8 * h : 8 * h + 8], values[r, h]) for r, h in keys], out)
     return (master_new, m_new, v_new, out.reshape(count * width))
 
 

time: 148 us -> 139 us (0.939)
  waiting for transfers between devices: 71.2 us -> 45.2 us
  starting transfers between devices: 45.5 us -> 56.5 us
  Pallas kernels: 27.9 us -> 32.8 us
    ppermute x27 -> x37, waiting for transfers between devices: 64.3 us -> 38.3 us  [send(): return lax.ppermute(value, DP, perm(axis, s))]
    ppermute x27 -> x37, starting transfers between devices: 33.9 us -> 46.9 us  [send(): return lax.ppermute(value, DP, perm(axis, s))]
    pallas_call x17 -> x25, Pallas kernels: 27.9 us -> 32.8 us  [call(): pl.pallas_call(body, grid_spec=pltpu.PrefetchScalarGridSpec(num_scalar_pr...]
    ppermute x1, starting transfers between devices: 3.9 us -> 1.91 us  [step(): before = lax.ppermute(up, DP, [(d, d + 1) for d in range(127)])]
  transfers between devices with their start and end apart: 30 -> 40, of which waited for: 15 -> 15; matrix products, arithmetic and copies ran while one was open for 2% -> 2% of each run, Pallas kernels for 13% -> 19%
where the time goes in v3:
time: 139 us
  starting transfers between devices  56.5 us (41%)
  waiting for transfers between devices  45.2 us (33%)
  Pallas kernels  32.8 us (24%)
  other arithmetic  2.04 us (1%)
    ppermute x37, starting transfers between devices, send(): return lax.ppermute(value, DP, perm(axis, s))  46.9 us
    ppermute x37, waiting for transfers between devices, send(): return lax.ppermute(value, DP, perm(axis, s))  38.3 us
    pallas_call x25, Pallas kernels, call(): pl.pallas_call(body, grid_spec=pltpu.PrefetchScalarGridSpec(num_scalar_pr...  32.8 us
    all_to_all x1, starting transfers between devices, step(): squares = lax.all_to_all(squares, ('y', 'x', 'core'), 0, 0, tiled=True)  6.41 us
    ppermute x1, waiting for transfers between devices, step(): passed = lax.ppermute(after, DP, [(d, d - 2) for d in range(3, 128, 2)])  3.97 us
    all_to_all x1, waiting for transfers between devices, step(): squares = lax.all_to_all(squares, ('y', 'x', 'core'), 0, 0, tiled=True)  2.9 us
  transfers between devices with their start and end apart: 40, of which 15 were waited for; matrix products, arithmetic and copies ran while one was open for 2% of the time, Pallas kernels for 19%

profile of v3, /device:TPU:1, one launch (start us, length us, event | category | flops | bytes accessed | tf_op | source)
XLA Modules:
  0.0 138.5 jit_solution(13343281197106458507)
XLA Ops:
  0.8 2.3 %shard_map.89 = bf16[16,256,128]{2,1,0:T(8,128)(2,1)S(1)} custom-call(s32[16]{0:T(128)S(1)} %get-tuple-element.48.t_ref, f32[128,256,128]{2,1,0:T(8,128)} %bitcast.31), custom_call_target="tpu_custom_call" | custom-call | flops 524288 | bytes 3145728 | tf_op jit(solution)/shard_map/pallas_call | solution.py:60
  3.1 1.5 %collective-permute-start.5 = (bf16[16,256,128]{2,1,0:T(8,128)(2,1)S(1)}, bf16[16,256,128]{2,1,0:T(8,128)(2,1)S(1)}, u32[]{:S(2)}, u32[]{:S(2)}) collective-permute-start(bf16[16,256,128]{2,1,0:T(8,128)(2,1)S(1)} %shard_map.89), channel_id=1, source_target_pairs={{0,1},{1,0},{2,3},{3,2},{4,5},{5,4},{6,7},{7,6},{8,9},{9,8},{10,11... | collective-permute-start | bytes 3145736 | tf_op jit(solution)/shard_map/ppermute | solution.py:39
  4.6 3.8 %shard_map.88 = (f32[16,256,128]{2,1,0:T(8,128)S(1)}, bf16[16,256,128]{2,1,0:T(8,128)(2,1)S(1)}, bf16[16,256,128]{2,1,0:T(8,128)(2,1)S(1)}) custom-call(s32[48]{0:T(128)S(1)} %pad_add_fusion.3.t_ref, f32[128,256,128]{2,1,0:T(8,128)} %bitcast.32), custom_call_target="tpu_custom_call" | custom-call | flops 1572864 | bytes 9437184 | tf_op jit(solution)/shard_map/pallas_call | solution.py:60
  9.1 3.1 %shard_map.86 = (bf16[16,256,128]{2,1,0:T(8,128)(2,1)S(1)}, f32[16,256,128]{2,1,0:T(8,128)S(1)}) custom-call(s32[32]{0:T(128)S(1)} %get-tuple-element.68.t_ref, f32[128,256,128]{2,1,0:T(8,128)} %bitcast.33), custom_call_target="tpu_custom_call" | custom-call | flops 1048576 | bytes 6291456 | tf_op jit(solution)/shard_map/pallas_call | solution.py:60
  12.5 2.9 %collective-permute-start.11 = (bf16[8,256,128]{2,1,0:T(8,128)(2,1)S(1)}, bf16[8,256,128]{2,1,0:T(8,128)(2,1)S(1)}, u32[]{:S(2)}, u32[]{:S(2)}) collective-permute-start(bf16[8,256,128]{2,1,0:T(8,128)(2,1)S(1)} %get-tuple-element.37), channel_id=1, source_target_pairs={{0,6},{1,25},{2,0},{3,27},{4,2},{5,29},{6,4},{7,31},{8,14},{9,1},{... | collective-permute-start | bytes 1572872 | tf_op jit(solution)/shard_map/ppermute | solution.py:39
  15.5 1.3 collective-permute-start.6
  16.8 3.1 %shard_map.87 = (f32[16,256,128]{2,1,0:T(8,128)S(1)}, f32[16,256,128]{2,1,0:T(8,128)S(1)}) custom-call(s32[32]{0:T(128)S(1)} %get-tuple-element.69.t_ref, f32[128,256,128]{2,1,0:T(8,128)} %bitcast.34), custom_call_target="tpu_custom_call" | custom-call | flops 1048576 | bytes 6291456 | tf_op jit(solution)/shard_map/pallas_call | solution.py:60
  20.0 1.5 %collective-permute-start.10 = (bf16[8,256,128]{2,1,0:T(8,128)(2,1)S(1)}, bf16[8,256,128]{2,1,0:T(8,128)(2,1)S(1)}, u32[]{:S(2)}, u32[]{:S(2)}) collective-permute-start(bf16[8,256,128]{2,1,0:T(8,128)(2,1)S(1)} %shard_map.93), channel_id=1, source_target_pairs={{0,6},{1,25},{2,0},{3,27},{4,2},{5,29},{6,4},{7,31},{8,14},{9,1},{... | collective-permute-start | bytes 1572872 | tf_op jit(solution)/shard_map/ppermute | solution.py:39
  22.0 3.2 %collective-permute-start.12 = (bf16[8,256,128]{2,1,0:T(8,128)(2,1)S(1)}, bf16[8,256,128]{2,1,0:T(8,128)(2,1)S(1)}, u32[]{:S(2)}, u32[]{:S(2)}) collective-permute-start(bf16[8,256,128]{2,1,0:T(8,128)(2,1)S(1)} %shard_map.94), channel_id=1, source_target_pairs={{0,6},{1,25},{2,0},{3,27},{4,2},{5,29},{6,4},{7,31},{8,14},{9,1},{... | collective-permute-start | bytes 1572872 | tf_op jit(solution)/shard_map/ppermute | solution.py:39
  25.5 2.9 %collective-permute-done.10.refs_4_ = bf16[8,256,128]{2,1,0:T(8,128)(2,1)S(1)} collective-permute-done((bf16[8,256,128]{2,1,0:T(8,128)(2,1)S(1)}, bf16[8,256,128]{2,1,0:T(8,128)(2,1)S(1)}, u32[]{:S(2)}, u32[]{:S(2)}) %collective-permute-start.10) | collective-permute-done | bytes 524320 | tf_op jit(solution)/shard_map/ppermute | solution.py:39
  28.4 2.9 %collective-permute-done.8.refs_3_ = bf16[8,256,128]{2,1,0:T(8,128)(2,1)S(1)} collective-permute-done((bf16[8,256,128]{2,1,0:T(8,128)(2,1)S(1)}, bf16[8,256,128]{2,1,0:T(8,128)(2,1)S(1)}, u32[]{:S(2)}, u32[]{:S(2)}) %collective-permute-start.8) | collective-permute-done | bytes 524320 | tf_op jit(solution)/shard_map/ppermute | solution.py:39
  31.3 2.7 %collective-permute-done.12.refs_5_ = bf16[8,256,128]{2,1,0:T(8,128)(2,1)S(1)} collective-permute-done((bf16[8,256,128]{2,1,0:T(8,128)(2,1)S(1)}, bf16[8,256,128]{2,1,0:T(8,128)(2,1)S(1)}, u32[]{:S(2)}, u32[]{:S(2)}) %collective-permute-start.12) | collective-permute-done | bytes 524320 | tf_op jit(solution)/shard_map/ppermute | solution.py:39
  34.1 2.9 %collective-permute-done.7.refs_2_ = bf16[8,256,128]{2,1,0:T(8,128)(2,1)S(1)} collective-permute-done((bf16[8,256,128]{2,1,0:T(8,128)(2,1)S(1)}, bf16[8,256,128]{2,1,0:T(8,128)(2,1)S(1)}, u32[]{:S(2)}, u32[]{:S(2)}) %collective-permute-start.7) | collective-permute-done | bytes 524320 | tf_op jit(solution)/shard_map/ppermute | solution.py:39
  38.4 2.5 %collective-permute-start.14 = (bf16[4,256,128]{2,1,0:T(8,128)(2,1)S(1)}, bf16[4,256,128]{2,1,0:T(8,128)(2,1)S(1)}, u32[]{:S(2)}, u32[]{:S(2)}) collective-permute-start(bf16[4,256,128]{2,1,0:T(8,128)(2,1)S(1)} %get-tuple-element.40), channel_id=1, source_target_pairs={{0,16},{1,5},{2,18},{3,7},{4,20},{5,1},{6,22},{7,3},{8,24},{9,13},... | collective-permute-start | bytes 786440 | tf_op jit(solution)/shard_map/ppermute | solution.py:39
  42.0 2.4 %collective-permute-done.13.refs_1_ = bf16[4,256,128]{2,1,0:T(8,128)(2,1)S(1)} collective-permute-done((bf16[4,256,128]{2,1,0:T(8,128)(2,1)S(1)}, bf16[4,256,128]{2,1,0:T(8,128)(2,1)S(1)}, u32[]{:S(2)}, u32[]{:S(2)}) %collective-permute-start.13) | collective-permute-done | bytes 262176 | tf_op jit(solution)/shard_map/ppermute | solution.py:39
  44.4 3.3 %collective-permute-done.14.refs_2_ = bf16[4,256,128]{2,1,0:T(8,128)(2,1)S(1)} collective-permute-done((bf16[4,256,128]{2,1,0:T(8,128)(2,1)S(1)}, bf16[4,256,128]{2,1,0:T(8,128)(2,1)S(1)}, u32[]{:S(2)}, u32[]{:S(2)}) %collective-permute-start.14) | collective-permute-done | bytes 262176 | tf_op jit(solution)/shard_map/ppermute | solution.py:39
  47.9 1.7 %collective-permute-start.16 = (bf16[4,256,128]{2,1,0:T(8,128)(2,1)S(1)}, bf16[4,256,128]{2,1,0:T(8,128)(2,1)S(1)}, u32[]{:S(2)}, u32[]{:S(2)}) collective-permute-start(bf16[4,256,128]{2,1,0:T(8,128)(2,1)S(1)} %shard_map.96.w), channel_id=1, source_target_pairs={{0,32},{1,33},{2,34},{3,35},{4,36},{5,37},{6,38},{7,39},{8,40},{9,... | collective-permute-start | bytes 786440 | tf_op jit(solution)/shard_map/ppermute | solution.py:39
  50.2 3.2 %collective-permute-start.1 = (bf16[2,128,128]{2,1,0:T(8,128)(2,1)S(1)}, bf16[2,128,128]{2,1,0:T(8,128)(2,1)S(1)}, u32[]{:S(2)}, u32[]{:S(2)}) collective-permute-start(bf16[2,128,128]{2,1,0:T(8,128)(2,1)S(1)} %get-tuple-element.27), channel_id=1, source_target_pairs={{0,1},{1,0},{2,3},{3,2},{4,5},{5,4},{6,7},{7,6},{8,9},{9,8},{10,11... | collective-permute-start | bytes 196616 | tf_op jit(solution)/shard_map/ppermute | solution.py:39
  53.5 3.3 %collective-permute-start.17 = (bf16[4,256,128]{2,1,0:T(8,128)(2,1)S(1)}, bf16[4,256,128]{2,1,0:T(8,128)(2,1)S(1)}, u32[]{:S(2)}, u32[]{:S(2)}) collective-permute-start(bf16[4,256,128]{2,1,0:T(8,128)(2,1)S(1)} %shard_map.96.w), channel_id=1, source_target_pairs={{0,64},{1,65},{2,66},{3,67},{4,68},{5,69},{6,70},{7,71},{8,72},{9,... | collective-permute-start | bytes 786440 | tf_op jit(solution)/shard_map/ppermute | solution.py:39
  57.5 1.9 %collective-permute-start = (bf16[2,136,128]{2,1,0:T(8,128)(2,1)S(1)}, bf16[2,136,128]{2,1,0:T(8,128)(2,1)S(1)}, u32[]{:S(2)}, u32[]{:S(2)}) collective-permute-start(bf16[2,136,128]{2,1,0:T(8,128)(2,1)S(1)} %get-tuple-element.26), channel_id=1, source_target_pairs={{0,1},{1,2},{2,3},{3,4},{4,5},{5,6},{6,7},{7,8},{8,9},{9,10},{10,1... | collective-permute-start | bytes 208904 | tf_op jit(solution)/shard_map/ppermute | solution.py:376
  59.4 1.3 collective-permute-start.2
  60.8 4.0 %collective-permute-done.2.p = bf16[2,128,128]{2,1,0:T(8,128)(2,1)S(1)} collective-permute-done((bf16[2,128,128]{2,1,0:T(8,128)(2,1)S(1)}, bf16[2,128,128]{2,1,0:T(8,128)(2,1)S(1)}, u32[]{:S(2)}, u32[]{:S(2)}) %collective-permute-start.2) | collective-permute-done | bytes 65568 | tf_op jit(solution)/shard_map/ppermute | solution.py:378
  64.8 2.0 %shard_map.85 = (f32[256,128]{1,0:T(8,128)S(1)}, f32[256,128]{1,0:T(8,128)S(1)}, bf16[4,256,128]{2,1,0:T(8,128)(2,1)S(1)}) custom-call(s32[130]{0:T(256)S(1)} %pad_add_fusion.t_ref, f32[512,128]{1,0:T(8,128)S(1)} %bitcast.26, f32[512,128]{1,0:T(8,128)S(1)} %bitcast.28, bf16[2,136,128]{2,1,0:T(8,128)(2,1)S(1)} %collective-permute-done.b, ...), custom_call_target="tpu_custom_call" | custom-call | flops 1310720 | bytes 1310720 | tf_op jit(solution)/shard_map/pallas_call | solution.py:60
  66.8 3.9 %collective-permute-start.19 = (bf16[4,256,128]{2,1,0:T(8,128)(2,1)S(1)}, bf16[4,256,128]{2,1,0:T(8,128)(2,1)S(1)}, u32[]{:S(2)}, u32[]{:S(2)}) collective-permute-start(bf16[4,256,128]{2,1,0:T(8,128)(2,1)S(1)} %get-tuple-element.43.refs_0_), channel_id=1, source_target_pairs={{0,96},{1,97},{2,98},{3,99},{4,100},{5,101},{6,102},{7,103},{8,104... | collective-permute-start | bytes 786440 | tf_op jit(solution)/shard_map/ppermute | solution.py:39
  70.7 2.8 %collective-permute-start.20 = (bf16[4,256,128]{2,1,0:T(8,128)(2,1)S(1)}, bf16[4,256,128]{2,1,0:T(8,128)(2,1)S(1)}, u32[]{:S(2)}, u32[]{:S(2)}) collective-permute-start(bf16[4,256,128]{2,1,0:T(8,128)(2,1)S(1)} %get-tuple-element.43.refs_0_), channel_id=1, source_target_pairs={{0,64},{1,65},{2,66},{3,67},{4,68},{5,69},{6,70},{7,71},{8,72},{9,... | collective-permute-start | bytes 786440 | tf_op jit(solution)/shard_map/ppermute | solution.py:39
  73.5 1.4 shard_map.97
  74.9 6.4 %all-to-all-start = ((f32[32,8,128]{2,1,0:T(8,128)}), f32[32,8,128]{2,1,0:T(8,128)S(1)}, u32[]{:S(2)}, u32[]{:S(2)}) async-start(f32[32,8,128]{2,1,0:T(8,128)} %get-tuple-element.44), calls=%async_computation | async-start | bytes 262144 | tf_op jit(solution)/shard_map/all_to_all | solution.py:396
  81.3 4.7 %collective-permute-done.21.refs_3_ = bf16[4,256,128]{2,1,0:T(8,128)(2,1)S(1)} collective-permute-done((bf16[4,256,128]{2,1,0:T(8,128)(2,1)S(1)}, bf16[4,256,128]{2,1,0:T(8,128)(2,1)S(1)}, u32[]{:S(2)}, u32[]{:S(2)}) %collective-permute-start.21) | collective-permute-done | bytes 262176 | tf_op jit(solution)/shard_map/ppermute | solution.py:39
  86.0 2.9 %all-to-all-done.refs_4_ = f32[32,8,128]{2,1,0:T(8,128)S(1)} async-done(((f32[32,8,128]{2,1,0:T(8,128)}), f32[32,8,128]{2,1,0:T(8,128)S(1)}, u32[]{:S(2)}, u32[]{:S(2)}) %all-to-all-start) | async-done | bytes 131104 | tf_op jit(solution)/shard_map/all_to_all | solution.py:396
  88.9 1.8 %shard_map.98 = (bf16[4,256,128]{2,1,0:T(8,128)(2,1)S(1)}, f32[8,128]{1,0:T(8,128)S(1)}) custom-call(s32[1]{0:T(128)} %constant.267.clone.1.t_ref, f32[4,256,128]{2,1,0:T(8,128)S(1)} %get-tuple-element.42.g, bf16[4,256,128]{2,1,0:T(8,128)(2,1)S(1)} %get-tuple-element.43.refs_0_, bf16[4,256,128]{2,1,0:T(8,128)(2,1)S(1)} %collective-permute-done.19.refs_1_, ...), custom_call_target="tpu_custom_call" | custom-call | flops 2621440 | bytes 1835008 | tf_op jit(solution)/shard_map/pallas_call | solution.py:60
  92.3 1.9 %collective-permute-start.22 = (bf16[4,256,128]{2,1,0:T(8,128)(2,1)S(1)}, bf16[4,256,128]{2,1,0:T(8,128)(2,1)S(1)}, u32[]{:S(2)}, u32[]{:S(2)}) collective-permute-start(bf16[4,256,128]{2,1,0:T(8,128)(2,1)S(1)} %get-tuple-element.47.a), channel_id=1, source_target_pairs={{0,24},{1,7},{2,26},{3,1},{4,28},{5,3},{6,30},{7,5},{8,0},{9,15},{... | collective-permute-start | bytes 786440 | tf_op jit(solution)/shard_map/ppermute | solution.py:39
  94.2 3.6 %collective-permute-done.26.a = bf16[4,256,128]{2,1,0:T(8,128)(2,1)S(1)} collective-permute-done((bf16[4,256,128]{2,1,0:T(8,128)(2,1)S(1)}, bf16[4,256,128]{2,1,0:T(8,128)(2,1)S(1)}, u32[]{:S(2)}, u32[]{:S(2)}) %collective-permute-start.26) | collective-permute-done | bytes 262176 | tf_op jit(solution)/shard_map/ppermute | solution.py:39
  97.8 2.8 %collective-permute-done.27.b = bf16[4,256,128]{2,1,0:T(8,128)(2,1)S(1)} collective-permute-done((bf16[4,256,128]{2,1,0:T(8,128)(2,1)S(1)}, bf16[4,256,128]{2,1,0:T(8,128)(2,1)S(1)}, u32[]{:S(2)}, u32[]{:S(2)}) %collective-permute-start.27) | collective-permute-done | bytes 262176 | tf_op jit(solution)/shard_map/ppermute | solution.py:39
  100.6 1.3 collective-permute-start.38
  102.7 2.0 %collective-permute-start.28 = (bf16[8,256,128]{2,1,0:T(8,128)(2,1)S(1)}, bf16[8,256,128]{2,1,0:T(8,128)(2,1)S(1)}, u32[]{:S(2)}, u32[]{:S(2)}) collective-permute-start(bf16[8,256,128]{2,1,0:T(8,128)(2,1)S(1)} %shard_map.100.refs_1_), channel_id=1, source_target_pairs={{0,6},{1,25},{2,0},{3,27},{4,2},{5,29},{6,4},{7,31},{8,14},{9,1},{... | collective-permute-start | bytes 1572872 | tf_op jit(solution)/shard_map/ppermute | solution.py:39
  104.9 1.4 %collective-permute-start.31 = (bf16[8,256,128]{2,1,0:T(8,128)(2,1)S(1)}, bf16[8,256,128]{2,1,0:T(8,128)(2,1)S(1)}, u32[]{:S(2)}, u32[]{:S(2)}) collective-permute-start(bf16[8,256,128]{2,1,0:T(8,128)(2,1)S(1)} %shard_map.100.refs_1_), channel_id=1, source_target_pairs={{0,2},{1,9},{2,4},{3,11},{4,6},{5,13},{6,0},{7,15},{8,10},{9,17},{... | collective-permute-start | bytes 1572872 | tf_op jit(solution)/shard_map/ppermute | solution.py:39
  106.4 5.2 %collective-permute-done.23.refs_0_ = bf16[8,256,128]{2,1,0:T(8,128)(2,1)S(1)} collective-permute-done((bf16[8,256,128]{2,1,0:T(8,128)(2,1)S(1)}, bf16[8,256,128]{2,1,0:T(8,128)(2,1)S(1)}, u32[]{:S(2)}, u32[]{:S(2)}) %collective-permute-start.23) | collective-permute-done | bytes 524320 | tf_op jit(solution)/shard_map/ppermute | solution.py:39
  112.7 2.5 %collective-permute-start.29 = (bf16[8,256,128]{2,1,0:T(8,128)(2,1)S(1)}, bf16[8,256,128]{2,1,0:T(8,128)(2,1)S(1)}, u32[]{:S(2)}, u32[]{:S(2)}) collective-permute-start(bf16[8,256,128]{2,1,0:T(8,128)(2,1)S(1)} %collective-permute-done.28.refs_1_), channel_id=1, source_target_pairs={{0,6},{1,25},{2,0},{3,27},{4,2},{5,29},{6,4},{7,31},{8,14},{9,1},{... | collective-permute-start | bytes 1572872 | tf_op jit(solution)/shard_map/ppermute | solution.py:39
  118.2 4.1 %collective-permute-done.29.refs_1_ = bf16[8,256,128]{2,1,0:T(8,128)(2,1)S(1)} collective-permute-done((bf16[8,256,128]{2,1,0:T(8,128)(2,1)S(1)}, bf16[8,256,128]{2,1,0:T(8,128)(2,1)S(1)}, u32[]{:S(2)}, u32[]{:S(2)}) %collective-permute-start.29) | collective-permute-done | bytes 524320 | tf_op jit(solution)/shard_map/ppermute | solution.py:39
  123.7 1.5 %fusion.1 = (f32[32768]{0:T(1024)}, f32[32768]{0:T(1024)}, f32[32768]{0:T(1024)}) fusion(f32[4,256,128]{2,1,0:T(8,128)S(1)} %get-tuple-element.42.g, f32[]{:T(128)} %bitcast.5, f32[256,128]{1,0:T(8,128)S(1)} %get-tuple-element.46, f32[256,128]{1,0:T(8,128)S(1)} %get-tuple-element.28, f32[32768]{0:T(1024)S(1)} %copy-done.2), kind=kLoop, calls=%fused_computation.6 | loop fusion | flops 491520 | bytes 917508 | tf_op jit(solution)/shard_map/reshape | solution.py:399
  125.2 1.6 %shard_map.101.refs_2_ = bf16[128,256,128]{2,1,0:T(8,128)(2,1)} custom-call(s32[16]{0:T(128)S(1)} %get-tuple-element.67.t_ref, bf16[8,256,128]{2,1,0:T(8,128)(2,1)S(1)} %shard_map.99.refs_0_, bf16[8,256,128]{2,1,0:T(8,128)(2,1)S(1)} %shard_map.100.refs_1_), custom_call_target="tpu_custom_call" | custom-call | flops 2097152 | bytes 2097152 | tf_op jit(solution)/shard_map/pallas_call | solution.py:60
  126.8 1.6 %shard_map.102.refs_2_ = bf16[128,256,128]{2,1,0:T(8,128)(2,1)} custom-call(s32[16]{0:T(128)S(1)} %get-tuple-element.64.t_ref, bf16[8,256,128]{2,1,0:T(8,128)(2,1)S(1)} %collective-permute-done.37.refs_0_, bf16[8,256,128]{2,1,0:T(8,128)(2,1)S(1)} %collective-permute-done.38.refs_1_, ...), custom_call_target="tpu_custom_call", output_to_operand_aliasing={{}: (3, {})} | custom-call | flops 2097152 | bytes 2097152 | tf_op jit(solution)/shard_map/pallas_call | solution.py:60
  128.5 1.6 %shard_map.103.refs_2_ = bf16[128,256,128]{2,1,0:T(8,128)(2,1)} custom-call(s32[16]{0:T(128)S(1)} %pad_add_fusion.7.t_ref, bf16[8,256,128]{2,1,0:T(8,128)(2,1)S(1)} %collective-permute-done.23.refs_0_, bf16[8,256,128]{2,1,0:T(8,128)(2,1)S(1)} %collective-permute-done.35.refs_1_, ...), custom_call_target="tpu_custom_call", output_to_operand_aliasing={{}: (3, {})} | custom-call | flops 2097152 | bytes 2097152 | tf_op jit(solution)/shard_map/pallas_call | solution.py:60
  130.1 1.6 %shard_map.104.refs_2_ = bf16[128,256,128]{2,1,0:T(8,128)(2,1)} custom-call(s32[16]{0:T(128)S(1)} %pad_add_fusion.6.t_ref, bf16[8,256,128]{2,1,0:T(8,128)(2,1)S(1)} %collective-permute-done.34.refs_0_, bf16[8,256,128]{2,1,0:T(8,128)(2,1)S(1)} %collective-permute-done.36.refs_1_, ...), custom_call_target="tpu_custom_call", output_to_operand_aliasing={{}: (3, {})} | custom-call | flops 2097152 | bytes 2097152 | tf_op jit(solution)/shard_map/pallas_call | solution.py:60
  131.8 1.6 %shard_map.105.refs_2_ = bf16[128,256,128]{2,1,0:T(8,128)(2,1)} custom-call(s32[16]{0:T(128)S(1)} %pad_add_fusion.5.t_ref, bf16[8,256,128]{2,1,0:T(8,128)(2,1)S(1)} %collective-permute-done.31.refs_0_, bf16[8,256,128]{2,1,0:T(8,128)(2,1)S(1)} %collective-permute-done.28.refs_1_, ...), custom_call_target="tpu_custom_call", output_to_operand_aliasing={{}: (3, {})} | custom-call | flops 2097152 | bytes 2097152 | tf_op jit(solution)/shard_map/pallas_call | solution.py:60
  133.4 1.6 %shard_map.106.refs_2_ = bf16[128,256,128]{2,1,0:T(8,128)(2,1)} custom-call(s32[16]{0:T(128)S(1)} %pad_add_fusion.4.t_ref, bf16[8,256,128]{2,1,0:T(8,128)(2,1)S(1)} %collective-permute-done.32.refs_0_, bf16[8,256,128]{2,1,0:T(8,128)(2,1)S(1)} %collective-permute-done.33.refs_1_, ...), custom_call_target="tpu_custom_call", output_to_operand_aliasing={{}: (3, {})} | custom-call | flops 2097152 | bytes 2097152 | tf_op jit(solution)/shard_map/pallas_call | solution.py:60
  135.1 1.6 %shard_map.107.refs_2_ = bf16[128,256,128]{2,1,0:T(8,128)(2,1)} custom-call(s32[16]{0:T(128)S(1)} %get-tuple-element.61.t_ref, bf16[8,256,128]{2,1,0:T(8,128)(2,1)S(1)} %collective-permute-done.24.refs_0_, bf16[8,256,128]{2,1,0:T(8,128)(2,1)S(1)} %collective-permute-done.29.refs_1_, ...), custom_call_target="tpu_custom_call", output_to_operand_aliasing={{}: (3, {})} | custom-call | flops 2097152 | bytes 2097152 | tf_op jit(solution)/shard_map/pallas_call | solution.py:60
  136.7 1.6 %shard_map.108 = bf16[128,256,128]{2,1,0:T(8,128)(2,1)} custom-call(s32[16]{0:T(128)S(1)} %get-tuple-element.48.t_ref, bf16[8,256,128]{2,1,0:T(8,128)(2,1)S(1)} %collective-permute-done.25.refs_0_, bf16[8,256,128]{2,1,0:T(8,128)(2,1)S(1)} %collective-permute-done.30.refs_1_, bf16[128,256,128]{2,1,0:T(8,128)(2,1)} %shard_map.107.refs_2_), custom_call_target="tpu_custom_call", output_to_operand_aliasing={{}: (3, {})} | custom-call | flops 2097152 | bytes 2097152 | tf_op jit(solution)/shard_map/pallas_call | solution.py:60
  (78 shorter events, 14.4 us)
Async XLA Ops:
  3.1 9.1 %collective-permute-start.5 = (bf16[16,256,128]{2,1,0:T(8,128)(2,1)S(1)}, bf16[16,256,128]{2,1,0:T(8,128)(2,1)S(1)}, u32[]{:S(2)}, u32[]{:S(2)}) collective-permute-start(bf16[16,256,128]{2,1,0:T(8,128)(2,1)S(1)} %shard_map.89), channel_id=1, source_target_pairs={{0,1},{1,0},{2,3},{3,2},{4,5},{5,4},{6,7},{7,6},{8,9},{9,8},{10,11... | collective-permute-start | bytes 3145736 | tf_op jit(solution)/shard_map/ppermute | solution.py:39
  8.5 11.4 %collective-permute-start.9 = (bf16[16,256,128]{2,1,0:T(8,128)(2,1)S(1)}, bf16[16,256,128]{2,1,0:T(8,128)(2,1)S(1)}, u32[]{:S(2)}, u32[]{:S(2)}) collective-permute-start(bf16[16,256,128]{2,1,0:T(8,128)(2,1)S(1)} %get-tuple-element.36), channel_id=1, source_target_pairs={{0,1},{1,0},{2,3},{3,2},{4,5},{5,4},{6,7},{7,6},{8,9},{9,8},{10,11... | collective-permute-start | bytes 3145736 | tf_op jit(solution)/shard_map/ppermute | solution.py:39
  8.6 12.9 %collective-permute-start.4 = (bf16[16,256,128]{2,1,0:T(8,128)(2,1)S(1)}, bf16[16,256,128]{2,1,0:T(8,128)(2,1)S(1)}, u32[]{:S(2)}, u32[]{:S(2)}) collective-permute-start(bf16[16,256,128]{2,1,0:T(8,128)(2,1)S(1)} %get-tuple-element.32), channel_id=1, source_target_pairs={{0,1},{1,0},{2,3},{3,2},{4,5},{5,4},{6,7},{7,6},{8,9},{9,8},{10,11... | collective-permute-start | bytes 3145736 | tf_op jit(solution)/shard_map/ppermute | solution.py:39
  12.5 9.3 %collective-permute-start.11 = (bf16[8,256,128]{2,1,0:T(8,128)(2,1)S(1)}, bf16[8,256,128]{2,1,0:T(8,128)(2,1)S(1)}, u32[]{:S(2)}, u32[]{:S(2)}) collective-permute-start(bf16[8,256,128]{2,1,0:T(8,128)(2,1)S(1)} %get-tuple-element.37), channel_id=1, source_target_pairs={{0,6},{1,25},{2,0},{3,27},{4,2},{5,29},{6,4},{7,31},{8,14},{9,1},{... | collective-permute-start | bytes 1572872 | tf_op jit(solution)/shard_map/ppermute | solution.py:39
  15.4 10.1 %collective-permute-start.3 = (bf16[16,256,128]{2,1,0:T(8,128)(2,1)S(1)}, bf16[16,256,128]{2,1,0:T(8,128)(2,1)S(1)}, u32[]{:S(2)}, u32[]{:S(2)}) collective-permute-start(bf16[16,256,128]{2,1,0:T(8,128)(2,1)S(1)} %get-tuple-element.30), channel_id=1, source_target_pairs={{0,1},{1,0},{2,3},{3,2},{4,5},{5,4},{6,7},{7,6},{8,9},{9,8},{10,11... | collective-permute-start | bytes 3145736 | tf_op jit(solution)/shard_map/ppermute | solution.py:39
  15.5 9.7 %collective-permute-start.6 = (bf16[8,256,128]{2,1,0:T(8,128)(2,1)S(1)}, bf16[8,256,128]{2,1,0:T(8,128)(2,1)S(1)}, u32[]{:S(2)}, u32[]{:S(2)}) collective-permute-start(bf16[8,256,128]{2,1,0:T(8,128)(2,1)S(1)} %get-tuple-element.34), channel_id=1, source_target_pairs={{0,2},{1,9},{2,4},{3,11},{4,6},{5,13},{6,0},{7,15},{8,10},{9,17},{... | collective-permute-start | bytes 1572872 | tf_op jit(solution)/shard_map/ppermute | solution.py:39
  20.0 8.4 %collective-permute-start.10 = (bf16[8,256,128]{2,1,0:T(8,128)(2,1)S(1)}, bf16[8,256,128]{2,1,0:T(8,128)(2,1)S(1)}, u32[]{:S(2)}, u32[]{:S(2)}) collective-permute-start(bf16[8,256,128]{2,1,0:T(8,128)(2,1)S(1)} %shard_map.93), channel_id=1, source_target_pairs={{0,6},{1,25},{2,0},{3,27},{4,2},{5,29},{6,4},{7,31},{8,14},{9,1},{... | collective-permute-start | bytes 1572872 | tf_op jit(solution)/shard_map/ppermute | solution.py:39
  21.7 27.9 %copy-start.3 = (s32[129]{0:T(256)S(1)}, s32[129]{0:T(256)}, u32[]{:S(2)}) copy-start(s32[129]{0:T(256)} %param.9) | copy-start | bytes 1552
  21.7 28.0 %copy-start = (f32[1,65536]{1,0:T(1,128)S(1)}, f32[1,65536]{1,0:T(1,128)}, u32[]{:S(2)}) copy-start(f32[1,65536]{1,0:T(1,128)} %param.7) | copy-start | bytes 786436
  21.7 28.0 %copy-start.1 = (f32[1,65536]{1,0:T(1,128)S(1)}, f32[1,65536]{1,0:T(1,128)}, u32[]{:S(2)}) copy-start(f32[1,65536]{1,0:T(1,128)} %param.8) | copy-start | bytes 786436
  21.7 43.0 %copy-start.2 = (f32[32768]{0:T(1024)S(1)}, f32[32768]{0:T(1024)}, u32[]{:S(2)}) copy-start(f32[32768]{0:T(1024)} %param.6) | copy-start | bytes 393220
  21.7 9.6 %collective-permute-start.8 = (bf16[8,256,128]{2,1,0:T(8,128)(2,1)S(1)}, bf16[8,256,128]{2,1,0:T(8,128)(2,1)S(1)}, u32[]{:S(2)}, u32[]{:S(2)}) collective-permute-start(bf16[8,256,128]{2,1,0:T(8,128)(2,1)S(1)} %shard_map.92), channel_id=1, source_target_pairs={{0,2},{1,9},{2,4},{3,11},{4,6},{5,13},{6,0},{7,15},{8,10},{9,17},{... | collective-permute-start | bytes 1572872 | tf_op jit(solution)/shard_map/ppermute | solution.py:39
  22.0 12.0 %collective-permute-start.12 = (bf16[8,256,128]{2,1,0:T(8,128)(2,1)S(1)}, bf16[8,256,128]{2,1,0:T(8,128)(2,1)S(1)}, u32[]{:S(2)}, u32[]{:S(2)}) collective-permute-start(bf16[8,256,128]{2,1,0:T(8,128)(2,1)S(1)} %shard_map.94), channel_id=1, source_target_pairs={{0,6},{1,25},{2,0},{3,27},{4,2},{5,29},{6,4},{7,31},{8,14},{9,1},{... | collective-permute-start | bytes 1572872 | tf_op jit(solution)/shard_map/ppermute | solution.py:39
  25.4 11.5 %collective-permute-start.7 = (bf16[8,256,128]{2,1,0:T(8,128)(2,1)S(1)}, bf16[8,256,128]{2,1,0:T(8,128)(2,1)S(1)}, u32[]{:S(2)}, u32[]{:S(2)}) collective-permute-start(bf16[8,256,128]{2,1,0:T(8,128)(2,1)S(1)} %shard_map.91), channel_id=1, source_target_pairs={{0,2},{1,9},{2,4},{3,11},{4,6},{5,13},{6,0},{7,15},{8,10},{9,17},{... | collective-permute-start | bytes 1572872 | tf_op jit(solution)/shard_map/ppermute | solution.py:39
  37.6 6.8 %collective-permute-start.13 = (bf16[4,256,128]{2,1,0:T(8,128)(2,1)S(1)}, bf16[4,256,128]{2,1,0:T(8,128)(2,1)S(1)}, u32[]{:S(2)}, u32[]{:S(2)}) collective-permute-start(bf16[4,256,128]{2,1,0:T(8,128)(2,1)S(1)} %get-tuple-element.39), channel_id=1, source_target_pairs={{0,8},{1,3},{2,10},{3,5},{4,12},{5,7},{6,14},{7,1},{8,16},{9,11},{... | collective-permute-start | bytes 786440 | tf_op jit(solution)/shard_map/ppermute | solution.py:39
  38.4 9.3 %collective-permute-start.14 = (bf16[4,256,128]{2,1,0:T(8,128)(2,1)S(1)}, bf16[4,256,128]{2,1,0:T(8,128)(2,1)S(1)}, u32[]{:S(2)}, u32[]{:S(2)}) collective-permute-start(bf16[4,256,128]{2,1,0:T(8,128)(2,1)S(1)} %get-tuple-element.40), channel_id=1, source_target_pairs={{0,16},{1,5},{2,18},{3,7},{4,20},{5,1},{6,22},{7,3},{8,24},{9,13},... | collective-permute-start | bytes 786440 | tf_op jit(solution)/shard_map/ppermute | solution.py:39
  40.8 6.9 %collective-permute-start.15 = (bf16[4,256,128]{2,1,0:T(8,128)(2,1)S(1)}, bf16[4,256,128]{2,1,0:T(8,128)(2,1)S(1)}, u32[]{:S(2)}, u32[]{:S(2)}) collective-permute-start(bf16[4,256,128]{2,1,0:T(8,128)(2,1)S(1)} %get-tuple-element.41), channel_id=1, source_target_pairs={{0,24},{1,7},{2,26},{3,1},{4,28},{5,3},{6,30},{7,5},{8,0},{9,15},{... | collective-permute-start | bytes 786440 | tf_op jit(solution)/shard_map/ppermute | solution.py:39
  47.9 25.6 %collective-permute-start.16 = (bf16[4,256,128]{2,1,0:T(8,128)(2,1)S(1)}, bf16[4,256,128]{2,1,0:T(8,128)(2,1)S(1)}, u32[]{:S(2)}, u32[]{:S(2)}) collective-permute-start(bf16[4,256,128]{2,1,0:T(8,128)(2,1)S(1)} %shard_map.96.w), channel_id=1, source_target_pairs={{0,32},{1,33},{2,34},{3,35},{4,36},{5,37},{6,38},{7,39},{8,40},{9,... | collective-permute-start | bytes 786440 | tf_op jit(solution)/shard_map/ppermute | solution.py:39
  50.2 9.2 %collective-permute-start.1 = (bf16[2,128,128]{2,1,0:T(8,128)(2,1)S(1)}, bf16[2,128,128]{2,1,0:T(8,128)(2,1)S(1)}, u32[]{:S(2)}, u32[]{:S(2)}) collective-permute-start(bf16[2,128,128]{2,1,0:T(8,128)(2,1)S(1)} %get-tuple-element.27), channel_id=1, source_target_pairs={{0,1},{1,0},{2,3},{3,2},{4,5},{5,4},{6,7},{7,6},{8,9},{9,8},{10,11... | collective-permute-start | bytes 196616 | tf_op jit(solution)/shard_map/ppermute | solution.py:39
  53.5 20.0 %collective-permute-start.17 = (bf16[4,256,128]{2,1,0:T(8,128)(2,1)S(1)}, bf16[4,256,128]{2,1,0:T(8,128)(2,1)S(1)}, u32[]{:S(2)}, u32[]{:S(2)}) collective-permute-start(bf16[4,256,128]{2,1,0:T(8,128)(2,1)S(1)} %shard_map.96.w), channel_id=1, source_target_pairs={{0,64},{1,65},{2,66},{3,67},{4,68},{5,69},{6,70},{7,71},{8,72},{9,... | collective-permute-start | bytes 786440 | tf_op jit(solution)/shard_map/ppermute | solution.py:39
  56.8 16.7 %collective-permute-start.18 = (bf16[4,256,128]{2,1,0:T(8,128)(2,1)S(1)}, bf16[4,256,128]{2,1,0:T(8,128)(2,1)S(1)}, u32[]{:S(2)}, u32[]{:S(2)}) collective-permute-start(bf16[4,256,128]{2,1,0:T(8,128)(2,1)S(1)} %shard_map.96.w), channel_id=1, source_target_pairs={{0,96},{1,97},{2,98},{3,99},{4,100},{5,101},{6,102},{7,103},{8,104... | collective-permute-start | bytes 786440 | tf_op jit(solution)/shard_map/ppermute | solution.py:39
  57.5 3.3 %collective-permute-start = (bf16[2,136,128]{2,1,0:T(8,128)(2,1)S(1)}, bf16[2,136,128]{2,1,0:T(8,128)(2,1)S(1)}, u32[]{:S(2)}, u32[]{:S(2)}) collective-permute-start(bf16[2,136,128]{2,1,0:T(8,128)(2,1)S(1)} %get-tuple-element.26), channel_id=1, source_target_pairs={{0,1},{1,2},{2,3},{3,4},{4,5},{5,6},{6,7},{7,8},{8,9},{9,10},{10,1... | collective-permute-start | bytes 208904 | tf_op jit(solution)/shard_map/ppermute | solution.py:376
  59.4 5.3 %collective-permute-start.2 = (bf16[2,128,128]{2,1,0:T(8,128)(2,1)S(1)}, bf16[2,128,128]{2,1,0:T(8,128)(2,1)S(1)}, u32[]{:S(2)}, u32[]{:S(2)}) collective-permute-start(bf16[2,128,128]{2,1,0:T(8,128)(2,1)S(1)} %collective-permute-done.1.a), channel_id=1, source_target_pairs={{3,1},{5,3},{7,5},{9,7},{11,9},{13,11},{15,13},{17,15},{19,17},{21... | collective-permute-start | bytes 196616 | tf_op jit(solution)/shard_map/ppermute | solution.py:378
  66.8 14.5 %collective-permute-start.19 = (bf16[4,256,128]{2,1,0:T(8,128)(2,1)S(1)}, bf16[4,256,128]{2,1,0:T(8,128)(2,1)S(1)}, u32[]{:S(2)}, u32[]{:S(2)}) collective-permute-start(bf16[4,256,128]{2,1,0:T(8,128)(2,1)S(1)} %get-tuple-element.43.refs_0_), channel_id=1, source_target_pairs={{0,96},{1,97},{2,98},{3,99},{4,100},{5,101},{6,102},{7,103},{8,104... | collective-permute-start | bytes 786440 | tf_op jit(solution)/shard_map/ppermute | solution.py:39
  70.7 10.6 %collective-permute-start.20 = (bf16[4,256,128]{2,1,0:T(8,128)(2,1)S(1)}, bf16[4,256,128]{2,1,0:T(8,128)(2,1)S(1)}, u32[]{:S(2)}, u32[]{:S(2)}) collective-permute-start(bf16[4,256,128]{2,1,0:T(8,128)(2,1)S(1)} %get-tuple-element.43.refs_0_), channel_id=1, source_target_pairs={{0,64},{1,65},{2,66},{3,67},{4,68},{5,69},{6,70},{7,71},{8,72},{9,... | collective-permute-start | bytes 786440 | tf_op jit(solution)/shard_map/ppermute | solution.py:39
  73.5 12.5 %collective-permute-start.21 = (bf16[4,256,128]{2,1,0:T(8,128)(2,1)S(1)}, bf16[4,256,128]{2,1,0:T(8,128)(2,1)S(1)}, u32[]{:S(2)}, u32[]{:S(2)}) collective-permute-start(bf16[4,256,128]{2,1,0:T(8,128)(2,1)S(1)} %get-tuple-element.43.refs_0_), channel_id=1, source_target_pairs={{0,32},{1,33},{2,34},{3,35},{4,36},{5,37},{6,38},{7,39},{8,40},{9,... | collective-permute-start | bytes 786440 | tf_op jit(solution)/shard_map/ppermute | solution.py:39
  74.9 14.0 %all-to-all-start = ((f32[32,8,128]{2,1,0:T(8,128)}), f32[32,8,128]{2,1,0:T(8,128)S(1)}, u32[]{:S(2)}, u32[]{:S(2)}) async-start(f32[32,8,128]{2,1,0:T(8,128)} %get-tuple-element.44), calls=%async_computation | async-start | bytes 262144 | tf_op jit(solution)/shard_map/all_to_all | solution.py:396
  90.7 7.1 %collective-permute-start.26 = (bf16[4,256,128]{2,1,0:T(8,128)(2,1)S(1)}, bf16[4,256,128]{2,1,0:T(8,128)(2,1)S(1)}, u32[]{:S(2)}, u32[]{:S(2)}) collective-permute-start(bf16[4,256,128]{2,1,0:T(8,128)(2,1)S(1)} %get-tuple-element.47.a), channel_id=1, source_target_pairs={{0,16},{1,5},{2,18},{3,7},{4,20},{5,1},{6,22},{7,3},{8,24},{9,13},... | collective-permute-start | bytes 786440 | tf_op jit(solution)/shard_map/ppermute | solution.py:39
  91.5 9.1 %collective-permute-start.27 = (bf16[4,256,128]{2,1,0:T(8,128)(2,1)S(1)}, bf16[4,256,128]{2,1,0:T(8,128)(2,1)S(1)}, u32[]{:S(2)}, u32[]{:S(2)}) collective-permute-start(bf16[4,256,128]{2,1,0:T(8,128)(2,1)S(1)} %get-tuple-element.47.a), channel_id=1, source_target_pairs={{0,8},{1,3},{2,10},{3,5},{4,12},{5,7},{6,14},{7,1},{8,16},{9,11},{... | collective-permute-start | bytes 786440 | tf_op jit(solution)/shard_map/ppermute | solution.py:39
  92.3 9.6 %collective-permute-start.22 = (bf16[4,256,128]{2,1,0:T(8,128)(2,1)S(1)}, bf16[4,256,128]{2,1,0:T(8,128)(2,1)S(1)}, u32[]{:S(2)}, u32[]{:S(2)}) collective-permute-start(bf16[4,256,128]{2,1,0:T(8,128)(2,1)S(1)} %get-tuple-element.47.a), channel_id=1, source_target_pairs={{0,24},{1,7},{2,26},{3,1},{4,28},{5,3},{6,30},{7,5},{8,0},{9,15},{... | collective-permute-start | bytes 786440 | tf_op jit(solution)/shard_map/ppermute | solution.py:39
  100.6 4.3 %collective-permute-start.38 = (bf16[8,256,128]{2,1,0:T(8,128)(2,1)S(1)}, bf16[8,256,128]{2,1,0:T(8,128)(2,1)S(1)}, u32[]{:S(2)}, u32[]{:S(2)}) collective-permute-start(bf16[8,256,128]{2,1,0:T(8,128)(2,1)S(1)} %shard_map.100.refs_1_), channel_id=1, source_target_pairs={{0,1},{1,0},{2,3},{3,2},{4,5},{5,4},{6,7},{7,6},{8,9},{9,8},{10,11... | collective-permute-start | bytes 1572872 | tf_op jit(solution)/shard_map/ppermute | solution.py:39
  102.0 9.6 %collective-permute-start.23 = (bf16[8,256,128]{2,1,0:T(8,128)(2,1)S(1)}, bf16[8,256,128]{2,1,0:T(8,128)(2,1)S(1)}, u32[]{:S(2)}, u32[]{:S(2)}) collective-permute-start(bf16[8,256,128]{2,1,0:T(8,128)(2,1)S(1)} %shard_map.99.refs_0_), channel_id=1, source_target_pairs={{0,2},{1,9},{2,4},{3,11},{4,6},{5,13},{6,0},{7,15},{8,10},{9,17},{... | collective-permute-start | bytes 1572872 | tf_op jit(solution)/shard_map/ppermute | solution.py:39
  102.1 10.4 %collective-permute-start.37 = (bf16[8,256,128]{2,1,0:T(8,128)(2,1)S(1)}, bf16[8,256,128]{2,1,0:T(8,128)(2,1)S(1)}, u32[]{:S(2)}, u32[]{:S(2)}) collective-permute-start(bf16[8,256,128]{2,1,0:T(8,128)(2,1)S(1)} %shard_map.99.refs_0_), channel_id=1, source_target_pairs={{0,1},{1,0},{2,3},{3,2},{4,5},{5,4},{6,7},{7,6},{8,9},{9,8},{10,11... | collective-permute-start | bytes 1572872 | tf_op jit(solution)/shard_map/ppermute | solution.py:39
  102.7 10.0 %collective-permute-start.28 = (bf16[8,256,128]{2,1,0:T(8,128)(2,1)S(1)}, bf16[8,256,128]{2,1,0:T(8,128)(2,1)S(1)}, u32[]{:S(2)}, u32[]{:S(2)}) collective-permute-start(bf16[8,256,128]{2,1,0:T(8,128)(2,1)S(1)} %shard_map.100.refs_1_), channel_id=1, source_target_pairs={{0,6},{1,25},{2,0},{3,27},{4,2},{5,29},{6,4},{7,31},{8,14},{9,1},{... | collective-permute-start | bytes 1572872 | tf_op jit(solution)/shard_map/ppermute | solution.py:39
  104.9 11.8 %collective-permute-start.35 = (bf16[8,256,128]{2,1,0:T(8,128)(2,1)S(1)}, bf16[8,256,128]{2,1,0:T(8,128)(2,1)S(1)}, u32[]{:S(2)}, u32[]{:S(2)}) collective-permute-start(bf16[8,256,128]{2,1,0:T(8,128)(2,1)S(1)} %shard_map.99.refs_0_), channel_id=1, source_target_pairs={{0,6},{1,25},{2,0},{3,27},{4,2},{5,29},{6,4},{7,31},{8,14},{9,1},{... | collective-permute-start | bytes 1572872 | tf_op jit(solution)/shard_map/ppermute | solution.py:39
  104.9 12.7 %collective-permute-start.31 = (bf16[8,256,128]{2,1,0:T(8,128)(2,1)S(1)}, bf16[8,256,128]{2,1,0:T(8,128)(2,1)S(1)}, u32[]{:S(2)}, u32[]{:S(2)}) collective-permute-start(bf16[8,256,128]{2,1,0:T(8,128)(2,1)S(1)} %shard_map.100.refs_1_), channel_id=1, source_target_pairs={{0,2},{1,9},{2,4},{3,11},{4,6},{5,13},{6,0},{7,15},{8,10},{9,17},{... | collective-permute-start | bytes 1572872 | tf_op jit(solution)/shard_map/ppermute | solution.py:39
  111.6 6.5 %collective-permute-start.34 = (bf16[8,256,128]{2,1,0:T(8,128)(2,1)S(1)}, bf16[8,256,128]{2,1,0:T(8,128)(2,1)S(1)}, u32[]{:S(2)}, u32[]{:S(2)}) collective-permute-start(bf16[8,256,128]{2,1,0:T(8,128)(2,1)S(1)} %collective-permute-done.23.refs_0_), channel_id=1, source_target_pairs={{0,1},{1,0},{2,3},{3,2},{4,5},{5,4},{6,7},{7,6},{8,9},{9,8},{10,11... | collective-permute-start | bytes 1572872 | tf_op jit(solution)/shard_map/ppermute | solution.py:39
  112.5 10.8 %collective-permute-start.24 = (bf16[8,256,128]{2,1,0:T(8,128)(2,1)S(1)}, bf16[8,256,128]{2,1,0:T(8,128)(2,1)S(1)}, u32[]{:S(2)}, u32[]{:S(2)}) collective-permute-start(bf16[8,256,128]{2,1,0:T(8,128)(2,1)S(1)} %collective-permute-done.23.refs_0_), channel_id=1, source_target_pairs={{0,2},{1,9},{2,4},{3,11},{4,6},{5,13},{6,0},{7,15},{8,10},{9,17},{... | collective-permute-start | bytes 1572872 | tf_op jit(solution)/shard_map/ppermute | solution.py:39
  112.7 9.6 %collective-permute-start.29 = (bf16[8,256,128]{2,1,0:T(8,128)(2,1)S(1)}, bf16[8,256,128]{2,1,0:T(8,128)(2,1)S(1)}, u32[]{:S(2)}, u32[]{:S(2)}) collective-permute-start(bf16[8,256,128]{2,1,0:T(8,128)(2,1)S(1)} %collective-permute-done.28.refs_1_), channel_id=1, source_target_pairs={{0,6},{1,25},{2,0},{3,27},{4,2},{5,29},{6,4},{7,31},{8,14},{9,1},{... | collective-permute-start | bytes 1572872 | tf_op jit(solution)/shard_map/ppermute | solution.py:39
  116.7 16.8 %collective-permute-start.33 = (bf16[8,256,128]{2,1,0:T(8,128)(2,1)S(1)}, bf16[8,256,128]{2,1,0:T(8,128)(2,1)S(1)}, u32[]{:S(2)}, u32[]{:S(2)}) collective-permute-start(bf16[8,256,128]{2,1,0:T(8,128)(2,1)S(1)} %collective-permute-done.28.refs_1_), channel_id=1, source_target_pairs={{0,1},{1,0},{2,3},{3,2},{4,5},{5,4},{6,7},{7,6},{8,9},{9,8},{10,11... | collective-permute-start | bytes 1572872 | tf_op jit(solution)/shard_map/ppermute | solution.py:39
  117.7 12.5 %collective-permute-start.36 = (bf16[8,256,128]{2,1,0:T(8,128)(2,1)S(1)}, bf16[8,256,128]{2,1,0:T(8,128)(2,1)S(1)}, u32[]{:S(2)}, u32[]{:S(2)}) collective-permute-start(bf16[8,256,128]{2,1,0:T(8,128)(2,1)S(1)} %collective-permute-done.35.refs_1_), channel_id=1, source_target_pairs={{0,1},{1,0},{2,3},{3,2},{4,5},{5,4},{6,7},{7,6},{8,9},{9,8},{10,11... | collective-permute-start | bytes 1572872 | tf_op jit(solution)/shard_map/ppermute | solution.py:39
  118.1 15.3 %collective-permute-start.32 = (bf16[8,256,128]{2,1,0:T(8,128)(2,1)S(1)}, bf16[8,256,128]{2,1,0:T(8,128)(2,1)S(1)}, u32[]{:S(2)}, u32[]{:S(2)}) collective-permute-start(bf16[8,256,128]{2,1,0:T(8,128)(2,1)S(1)} %collective-permute-done.31.refs_0_), channel_id=1, source_target_pairs={{0,1},{1,0},{2,3},{3,2},{4,5},{5,4},{6,7},{7,6},{8,9},{9,8},{10,11... | collective-permute-start | bytes 1572872 | tf_op jit(solution)/shard_map/ppermute | solution.py:39
  122.3 14.5 %collective-permute-start.30 = (bf16[8,256,128]{2,1,0:T(8,128)(2,1)S(1)}, bf16[8,256,128]{2,1,0:T(8,128)(2,1)S(1)}, u32[]{:S(2)}, u32[]{:S(2)}) collective-permute-start(bf16[8,256,128]{2,1,0:T(8,128)(2,1)S(1)} %collective-permute-done.29.refs_1_), channel_id=1, source_target_pairs={{0,1},{1,0},{2,3},{3,2},{4,5},{5,4},{6,7},{7,6},{8,9},{9,8},{10,11... | collective-permute-start | bytes 1572872 | tf_op jit(solution)/shard_map/ppermute | solution.py:39
  123.3 13.5 %collective-permute-start.25 = (bf16[8,256,128]{2,1,0:T(8,128)(2,1)S(1)}, bf16[8,256,128]{2,1,0:T(8,128)(2,1)S(1)}, u32[]{:S(2)}, u32[]{:S(2)}) collective-permute-start(bf16[8,256,128]{2,1,0:T(8,128)(2,1)S(1)} %collective-permute-done.24.refs_0_), channel_id=1, source_target_pairs={{0,1},{1,0},{2,3},{3,2},{4,5},{5,4},{6,7},{7,6},{8,9},{9,8},{10,11... | collective-permute-start | bytes 1572872 | tf_op jit(solution)/shard_map/ppermute | solution.py:39

commit v4 on v3

--- a/solution.py
+++ b/solution.py
@@ -39,9 +39,10 @@
     return lax.ppermute(value, DP, perm(axis, s))
 
 
-def table(c, z, y, x, s):
-    i = jnp.arange(16, dtype=jnp.int32)
-    rb, rz = i // 4, i % 4
+def table(z, y, x, core):
+    i = jnp.arange(128, dtype=jnp.int32)
+    c = (core + i // 64) % 2
+    s, rb, rz = i // 16 % 4, i // 4 % 4, i % 4
     zz = (z + rz) % 4
     on_0 = shard_of(zz, (y + rb) % 4, (x + s) % 4, 0)
     on_1 = shard_of(zz, (y + s) % 4, (x + rb) % 4, 1)
@@ -73,7 +74,7 @@
     )(t, *operands)
 
 
-def fetch(g, *pieces):
+def fetch(t, g, *pieces):
     _, rows, lanes = g.shape
     n = 16
     kept = [dtype == g.dtype for _, dtype in pieces]
@@ -87,7 +88,7 @@
             slot = sum(not v for v in kept[:k]) * n
             for i in range(n):
                 to = outs[k].at[i] if kept[k] else buf.at[slot + i]
-                copies.append((k, i, slot + i, pltpu.make_async_copy(g_ref.at[t_ref[k * n + i]], to, sem.at[k * n + i])))
+                copies.append((k, i, slot + i, pltpu.make_async_copy(g_ref.at[t_ref[pieces[k][0] + i]], to, sem.at[k * n + i])))
         for *_, copy in copies:
             copy.start()
         for k, i, at, copy in copies:
@@ -100,7 +101,7 @@
     size = m * n * rows * lanes
     return call(
         body,
-        jnp.concatenate([t for t, _ in pieces]),
+        t,
         (g,),
         [pltpu.VMEM((n, rows, lanes), dtype) for _, dtype in pieces],
         scratch + [pltpu.SemaphoreType.DMA((m * n,))],
@@ -157,31 +158,30 @@
     return call(body, jnp.zeros((1,), jnp.int32), (first, second), outs, [], n, 4 * n)[0]
 
 
-def place(pairs, out):
+def place(t, pairs, out):
     k = len(pairs)
-    n, rows, lanes = pairs[0][1].shape
+    rows, lanes = pairs[0][1].shape[1:]
+    counts = [piece.shape[0] for _, piece in pairs]
 
     def body(t_ref, *refs):
         o, sem = refs[-2:]
-        copies = [
-            pltpu.make_async_copy(refs[j].at[i], o.at[t_ref[j * n + i]], sem.at[j * n + i])
-            for j in range(k)
-            for i in range(n)
-        ]
+        copies = []
+        for j, (first, _) in enumerate(pairs):
+            for i in range(counts[j]):
+                copies.append(pltpu.make_async_copy(refs[j].at[i], o.at[t_ref[first + i]], sem.at[len(copies)]))
         for copy in copies:
             copy.start()
         for copy in copies:
             copy.wait()
 
-    t = jnp.concatenate([p[0] for p in pairs])
-    operands = [p[1] for p in pairs] + ([] if out is None else [out])
-    nbytes = 4 * k * n * rows * lanes
+    operands = [piece for _, piece in pairs] + ([] if out is None else [out])
+    nbytes = 4 * sum(counts) * rows * lanes
     return call(
         body,
         t,
         operands,
         [jax.ShapeDtypeStruct((128, rows, lanes), BF)],
-        [pltpu.SemaphoreType.DMA((k * n,))],
+        [pltpu.SemaphoreType.DMA((sum(counts),))],
         nbytes,
         nbytes,
         {} if out is None else {k + 1: 0},
@@ -341,18 +341,19 @@
     rows = width // 128
     device = lax.axis_index(DP)
     z, y, x, c = coords(device)
-    mine = [table(c, z, y, x, s) for s in range(4)]
-    theirs = [table(1 - c, z, y, x, s) for s in range(4)]
+    places = table(z, y, x, c)
+    mine = [16 * s for s in range(4)]
+    theirs = [64 + 16 * s for s in range(4)]
     g = grads[0].reshape(128, rows, 128)
 
     given, kept, swapped = {}, {}, {}
-    (given[2],) = fetch(g, (theirs[2], BF))
+    (given[2],) = fetch(places, g, (theirs[2], BF))
     swapped[2] = send(given[2], "core")
-    kept[2], given[1], given[3] = fetch(g, (mine[2], F32), (theirs[1], BF), (theirs[3], BF))
+    kept[2], given[1], given[3] = fetch(places, g, (mine[2], F32), (theirs[1], BF), (theirs[3], BF))
     swapped[1] = send(given[1], "core")
     swapped[3] = send(given[3], "core")
-    kept[1], kept[3] = fetch(g, (mine[1], F32), (mine[3], F32))
-    given[0], kept[0] = fetch(g, (theirs[0], BF), (mine[0], F32))
+    kept[1], kept[3] = fetch(places, g, (mine[1], F32), (mine[3], F32))
+    given[0], kept[0] = fetch(places, g, (theirs[0], BF), (mine[0], F32))
     swapped[0] = send(given[0], "core")
     low, high = (0, 8), (8, 8)
 
@@ -389,8 +390,10 @@
         ],
         [(4, F32)] + [(4, BF)] * 3,
     )
-    q2, q1, q3 = send(q2, "b", 2), send(q1, "b", 1), send(q3, "b", 3)
-    (partial,) = sum_piece([[(v, 0, 4)] for v in (own, q1, q2, q3)], [(4, BF)])
+    quarters = {2: q2, 1: q1, 3: q3}
+    for s in (2, 1, 3):
+        quarters[s] = send(quarters[s], "b", s)
+    (partial,) = sum_piece([[(v, 0, 4)] for v in (own, quarters[1], quarters[2], quarters[3])], [(4, BF)])
     w2, w1, w3 = send(partial, "z", 2), send(partial, "z", 1), send(partial, "z", 3)
     gradient, squares = total_piece(partial, w1, w2, w3, 32)
     squares = lax.all_to_all(squares, ("y", "x", "core"), 0, 0, tiled=True)
@@ -413,9 +416,10 @@
     for r, h in halves:
         partner[r, h] = send(halves[r, h], "core")
     out = None
-    for keys in (((0, 0), (0, 1)), ((3, 0), (1, 0)), ((3, 1), (1, 1)), ((2, 0), (2, 1))):
-        for tables, values in ((mine, halves), (theirs, partner)):
-            out = place([(tables[r][8 * h : 8 * h + 8], values[r, h]) for r, h in keys], out)
+    for keys in (((0, 0), (0, 1)), ((3, 0), (1, 0), (3, 1), (1, 1)), ((2, 0),), ((2, 1),)):
+        pairs = [(mine[r] + 8 * h, halves[r, h]) for r, h in keys]
+        pairs += [(theirs[r] + 8 * h, partner[r, h]) for r, h in keys]
+        out = place(places, pairs, out)
     return (master_new, m_new, v_new, out.reshape(count * width))
 
 

time: 139 us -> 135 us (0.971)
  Pallas kernels: 32.8 us -> 28.1 us
  waiting for transfers between devices: 45.2 us -> 48.6 us
  starting transfers between devices: 56.5 us -> 54.5 us
    pallas_call x25 -> x21, Pallas kernels: 32.8 us -> 28.1 us  [call(): pl.pallas_call(body, grid_spec=pltpu.PrefetchScalarGridSpec(num_scalar_pr...]
    ppermute x37, waiting for transfers between devices: 38.3 us -> 41.6 us  [send(): return lax.ppermute(value, DP, perm(axis, s))]
    ppermute x37, starting transfers between devices: 46.9 us -> 44.9 us  [send(): return lax.ppermute(value, DP, perm(axis, s))]
  transfers between devices with their start and end apart: 40 -> 40, of which waited for: 15 -> 18; matrix products, arithmetic and copies ran while one was open for 2% -> 2% of each run, Pallas kernels for 19% -> 16%
where the time goes in v4:
time: 135 us; the launch traced here: 134 us
  starting transfers between devices  54.5 us (40%)
  waiting for transfers between devices  48.6 us (36%)
  Pallas kernels  28.1 us (21%)
  other arithmetic  1.57 us (1%)
    ppermute x37, starting transfers between devices, send(): return lax.ppermute(value, DP, perm(axis, s))  44.9 us
    ppermute x37, waiting for transfers between devices, send(): return lax.ppermute(value, DP, perm(axis, s))  41.6 us
    pallas_call x21, Pallas kernels, call(): pl.pallas_call(body, grid_spec=pltpu.PrefetchScalarGridSpec(num_scalar_pr...  28.1 us
    all_to_all x1, starting transfers between devices, step(): squares = lax.all_to_all(squares, ('y', 'x', 'core'), 0, 0, tiled=True)  6.41 us
    ppermute x1, waiting for transfers between devices, step(): passed = lax.ppermute(after, DP, [(d, d - 2) for d in range(3, 128, 2)])  3.97 us
    all_to_all x1, waiting for transfers between devices, step(): squares = lax.all_to_all(squares, ('y', 'x', 'core'), 0, 0, tiled=True)  2.91 us
  transfers between devices with their start and end apart: 40, of which 18 were waited for; matrix products, arithmetic and copies ran while one was open for 2% of the time, Pallas kernels for 16%

profile of v4, /device:TPU:1, one launch (start us, length us, event | category | flops | bytes accessed | tf_op | source)
XLA Modules:
  0.0 134.5 jit_solution(5411981299123727674)
XLA Ops:
  0.7 2.3 %shard_map.89 = bf16[16,256,128]{2,1,0:T(8,128)(2,1)S(1)} custom-call(s32[128]{0:T(128)S(1)} %compare_select_fusion.16.t_ref, f32[128,256,128]{2,1,0:T(8,128)} %bitcast.30), custom_call_target="tpu_custom_call" | custom-call | flops 524288 | bytes 3145728 | tf_op jit(solution)/shard_map/pallas_call | solution.py:61
  3.0 1.5 %collective-permute-start.5 = (bf16[16,256,128]{2,1,0:T(8,128)(2,1)S(1)}, bf16[16,256,128]{2,1,0:T(8,128)(2,1)S(1)}, u32[]{:S(2)}, u32[]{:S(2)}) collective-permute-start(bf16[16,256,128]{2,1,0:T(8,128)(2,1)S(1)} %shard_map.89), channel_id=1, source_target_pairs={{0,1},{1,0},{2,3},{3,2},{4,5},{5,4},{6,7},{7,6},{8,9},{9,8},{10,11... | collective-permute-start | bytes 3145736 | tf_op jit(solution)/shard_map/ppermute | solution.py:39
  4.5 3.8 %shard_map.88 = (f32[16,256,128]{2,1,0:T(8,128)S(1)}, bf16[16,256,128]{2,1,0:T(8,128)(2,1)S(1)}, bf16[16,256,128]{2,1,0:T(8,128)(2,1)S(1)}) custom-call(s32[128]{0:T(128)S(1)} %compare_select_fusion.16.t_ref, f32[128,256,128]{2,1,0:T(8,128)} %bitcast.31), custom_call_target="tpu_custom_call" | custom-call | flops 1572864 | bytes 9437184 | tf_op jit(solution)/shard_map/pallas_call | solution.py:61
  8.9 3.1 %shard_map.86 = (bf16[16,256,128]{2,1,0:T(8,128)(2,1)S(1)}, f32[16,256,128]{2,1,0:T(8,128)S(1)}) custom-call(s32[128]{0:T(128)S(1)} %compare_select_fusion.16.t_ref, f32[128,256,128]{2,1,0:T(8,128)} %bitcast.32), custom_call_target="tpu_custom_call" | custom-call | flops 1048576 | bytes 6291456 | tf_op jit(solution)/shard_map/pallas_call | solution.py:61
  12.2 2.9 %collective-permute-start.11 = (bf16[8,256,128]{2,1,0:T(8,128)(2,1)S(1)}, bf16[8,256,128]{2,1,0:T(8,128)(2,1)S(1)}, u32[]{:S(2)}, u32[]{:S(2)}) collective-permute-start(bf16[8,256,128]{2,1,0:T(8,128)(2,1)S(1)} %get-tuple-element.37), channel_id=1, source_target_pairs={{0,6},{1,25},{2,0},{3,27},{4,2},{5,29},{6,4},{7,31},{8,14},{9,1},{... | collective-permute-start | bytes 1572872 | tf_op jit(solution)/shard_map/ppermute | solution.py:39
  15.3 1.3 collective-permute-start.6
  16.6 3.1 %shard_map.87 = (f32[16,256,128]{2,1,0:T(8,128)S(1)}, f32[16,256,128]{2,1,0:T(8,128)S(1)}) custom-call(s32[128]{0:T(128)S(1)} %compare_select_fusion.16.t_ref, f32[128,256,128]{2,1,0:T(8,128)} %bitcast.33), custom_call_target="tpu_custom_call" | custom-call | flops 1048576 | bytes 6291456 | tf_op jit(solution)/shard_map/pallas_call | solution.py:61
  19.8 1.5 %collective-permute-start.10 = (bf16[8,256,128]{2,1,0:T(8,128)(2,1)S(1)}, bf16[8,256,128]{2,1,0:T(8,128)(2,1)S(1)}, u32[]{:S(2)}, u32[]{:S(2)}) collective-permute-start(bf16[8,256,128]{2,1,0:T(8,128)(2,1)S(1)} %shard_map.93), channel_id=1, source_target_pairs={{0,6},{1,25},{2,0},{3,27},{4,2},{5,29},{6,4},{7,31},{8,14},{9,1},{... | collective-permute-start | bytes 1572872 | tf_op jit(solution)/shard_map/ppermute | solution.py:39
  21.8 3.2 %collective-permute-start.12 = (bf16[8,256,128]{2,1,0:T(8,128)(2,1)S(1)}, bf16[8,256,128]{2,1,0:T(8,128)(2,1)S(1)}, u32[]{:S(2)}, u32[]{:S(2)}) collective-permute-start(bf16[8,256,128]{2,1,0:T(8,128)(2,1)S(1)} %shard_map.94), channel_id=1, source_target_pairs={{0,6},{1,25},{2,0},{3,27},{4,2},{5,29},{6,4},{7,31},{8,14},{9,1},{... | collective-permute-start | bytes 1572872 | tf_op jit(solution)/shard_map/ppermute | solution.py:39
  25.3 2.9 %collective-permute-done.10.refs_4_ = bf16[8,256,128]{2,1,0:T(8,128)(2,1)S(1)} collective-permute-done((bf16[8,256,128]{2,1,0:T(8,128)(2,1)S(1)}, bf16[8,256,128]{2,1,0:T(8,128)(2,1)S(1)}, u32[]{:S(2)}, u32[]{:S(2)}) %collective-permute-start.10) | collective-permute-done | bytes 524320 | tf_op jit(solution)/shard_map/ppermute | solution.py:39
  28.2 2.9 %collective-permute-done.8.refs_3_ = bf16[8,256,128]{2,1,0:T(8,128)(2,1)S(1)} collective-permute-done((bf16[8,256,128]{2,1,0:T(8,128)(2,1)S(1)}, bf16[8,256,128]{2,1,0:T(8,128)(2,1)S(1)}, u32[]{:S(2)}, u32[]{:S(2)}) %collective-permute-start.8) | collective-permute-done | bytes 524320 | tf_op jit(solution)/shard_map/ppermute | solution.py:39
  31.1 2.7 %collective-permute-done.12.refs_5_ = bf16[8,256,128]{2,1,0:T(8,128)(2,1)S(1)} collective-permute-done((bf16[8,256,128]{2,1,0:T(8,128)(2,1)S(1)}, bf16[8,256,128]{2,1,0:T(8,128)(2,1)S(1)}, u32[]{:S(2)}, u32[]{:S(2)}) %collective-permute-start.12) | collective-permute-done | bytes 524320 | tf_op jit(solution)/shard_map/ppermute | solution.py:39
  33.8 2.9 %collective-permute-done.7.refs_2_ = bf16[8,256,128]{2,1,0:T(8,128)(2,1)S(1)} collective-permute-done((bf16[8,256,128]{2,1,0:T(8,128)(2,1)S(1)}, bf16[8,256,128]{2,1,0:T(8,128)(2,1)S(1)}, u32[]{:S(2)}, u32[]{:S(2)}) %collective-permute-start.7) | collective-permute-done | bytes 524320 | tf_op jit(solution)/shard_map/ppermute | solution.py:39
  38.1 2.5 %collective-permute-start.14 = (bf16[4,256,128]{2,1,0:T(8,128)(2,1)S(1)}, bf16[4,256,128]{2,1,0:T(8,128)(2,1)S(1)}, u32[]{:S(2)}, u32[]{:S(2)}) collective-permute-start(bf16[4,256,128]{2,1,0:T(8,128)(2,1)S(1)} %get-tuple-element.40), channel_id=1, source_target_pairs={{0,16},{1,5},{2,18},{3,7},{4,20},{5,1},{6,22},{7,3},{8,24},{9,13},... | collective-permute-start | bytes 786440 | tf_op jit(solution)/shard_map/ppermute | solution.py:39
  40.5 1.2 collective-permute-start.15
  41.7 2.4 %collective-permute-done.13.refs_1_ = bf16[4,256,128]{2,1,0:T(8,128)(2,1)S(1)} collective-permute-done((bf16[4,256,128]{2,1,0:T(8,128)(2,1)S(1)}, bf16[4,256,128]{2,1,0:T(8,128)(2,1)S(1)}, u32[]{:S(2)}, u32[]{:S(2)}) %collective-permute-start.13) | collective-permute-done | bytes 262176 | tf_op jit(solution)/shard_map/ppermute | solution.py:39
  44.1 3.3 %collective-permute-done.14.refs_2_ = bf16[4,256,128]{2,1,0:T(8,128)(2,1)S(1)} collective-permute-done((bf16[4,256,128]{2,1,0:T(8,128)(2,1)S(1)}, bf16[4,256,128]{2,1,0:T(8,128)(2,1)S(1)}, u32[]{:S(2)}, u32[]{:S(2)}) %collective-permute-start.14) | collective-permute-done | bytes 262176 | tf_op jit(solution)/shard_map/ppermute | solution.py:39
  47.6 1.7 %collective-permute-start.16 = (bf16[4,256,128]{2,1,0:T(8,128)(2,1)S(1)}, bf16[4,256,128]{2,1,0:T(8,128)(2,1)S(1)}, u32[]{:S(2)}, u32[]{:S(2)}) collective-permute-start(bf16[4,256,128]{2,1,0:T(8,128)(2,1)S(1)} %shard_map.96.w), channel_id=1, source_target_pairs={{0,32},{1,33},{2,34},{3,35},{4,36},{5,37},{6,38},{7,39},{8,40},{9,... | collective-permute-start | bytes 786440 | tf_op jit(solution)/shard_map/ppermute | solution.py:39
  50.0 3.2 %collective-permute-start.1 = (bf16[2,128,128]{2,1,0:T(8,128)(2,1)S(1)}, bf16[2,128,128]{2,1,0:T(8,128)(2,1)S(1)}, u32[]{:S(2)}, u32[]{:S(2)}) collective-permute-start(bf16[2,128,128]{2,1,0:T(8,128)(2,1)S(1)} %get-tuple-element.27), channel_id=1, source_target_pairs={{0,1},{1,0},{2,3},{3,2},{4,5},{5,4},{6,7},{7,6},{8,9},{9,8},{10,11... | collective-permute-start | bytes 196616 | tf_op jit(solution)/shard_map/ppermute | solution.py:39
  53.2 3.3 %collective-permute-start.17 = (bf16[4,256,128]{2,1,0:T(8,128)(2,1)S(1)}, bf16[4,256,128]{2,1,0:T(8,128)(2,1)S(1)}, u32[]{:S(2)}, u32[]{:S(2)}) collective-permute-start(bf16[4,256,128]{2,1,0:T(8,128)(2,1)S(1)} %shard_map.96.w), channel_id=1, source_target_pairs={{0,64},{1,65},{2,66},{3,67},{4,68},{5,69},{6,70},{7,71},{8,72},{9,... | collective-permute-start | bytes 786440 | tf_op jit(solution)/shard_map/ppermute | solution.py:39
  57.2 1.9 %collective-permute-start = (bf16[2,136,128]{2,1,0:T(8,128)(2,1)S(1)}, bf16[2,136,128]{2,1,0:T(8,128)(2,1)S(1)}, u32[]{:S(2)}, u32[]{:S(2)}) collective-permute-start(bf16[2,136,128]{2,1,0:T(8,128)(2,1)S(1)} %get-tuple-element.26), channel_id=1, source_target_pairs={{0,1},{1,2},{2,3},{3,4},{4,5},{5,6},{6,7},{7,8},{8,9},{9,10},{10,1... | collective-permute-start | bytes 208904 | tf_op jit(solution)/shard_map/ppermute | solution.py:377
  59.2 1.3 collective-permute-start.2
  60.5 4.0 %collective-permute-done.2.p = bf16[2,128,128]{2,1,0:T(8,128)(2,1)S(1)} collective-permute-done((bf16[2,128,128]{2,1,0:T(8,128)(2,1)S(1)}, bf16[2,128,128]{2,1,0:T(8,128)(2,1)S(1)}, u32[]{:S(2)}, u32[]{:S(2)}) %collective-permute-start.2) | collective-permute-done | bytes 65568 | tf_op jit(solution)/shard_map/ppermute | solution.py:379
  64.5 2.0 %shard_map.85 = (f32[256,128]{1,0:T(8,128)S(1)}, f32[256,128]{1,0:T(8,128)S(1)}, bf16[4,256,128]{2,1,0:T(8,128)(2,1)S(1)}) custom-call(s32[130]{0:T(256)S(1)} %pad_add_fusion.t_ref, f32[512,128]{1,0:T(8,128)S(1)} %bitcast.26, f32[512,128]{1,0:T(8,128)S(1)} %bitcast.28, bf16[2,136,128]{2,1,0:T(8,128)(2,1)S(1)} %collective-permute-done.b, ...), custom_call_target="tpu_custom_call" | custom-call | flops 1310720 | bytes 1310720 | tf_op jit(solution)/shard_map/pallas_call | solution.py:61
  66.5 3.9 %collective-permute-start.19 = (bf16[4,256,128]{2,1,0:T(8,128)(2,1)S(1)}, bf16[4,256,128]{2,1,0:T(8,128)(2,1)S(1)}, u32[]{:S(2)}, u32[]{:S(2)}) collective-permute-start(bf16[4,256,128]{2,1,0:T(8,128)(2,1)S(1)} %get-tuple-element.43.refs_0_), channel_id=1, source_target_pairs={{0,96},{1,97},{2,98},{3,99},{4,100},{5,101},{6,102},{7,103},{8,104... | collective-permute-start | bytes 786440 | tf_op jit(solution)/shard_map/ppermute | solution.py:39
  70.4 2.8 %collective-permute-start.20 = (bf16[4,256,128]{2,1,0:T(8,128)(2,1)S(1)}, bf16[4,256,128]{2,1,0:T(8,128)(2,1)S(1)}, u32[]{:S(2)}, u32[]{:S(2)}) collective-permute-start(bf16[4,256,128]{2,1,0:T(8,128)(2,1)S(1)} %get-tuple-element.43.refs_0_), channel_id=1, source_target_pairs={{0,64},{1,65},{2,66},{3,67},{4,68},{5,69},{6,70},{7,71},{8,72},{9,... | collective-permute-start | bytes 786440 | tf_op jit(solution)/shard_map/ppermute | solution.py:39
  73.2 1.4 %shard_map.97 = (f32[4,256,128]{2,1,0:T(8,128)S(1)}, f32[32,8,128]{2,1,0:T(8,128)}) custom-call(s32[1]{0:T(128)} %constant.166.clone.1.t_ref, bf16[4,256,128]{2,1,0:T(8,128)(2,1)S(1)} %shard_map.96.w, bf16[4,256,128]{2,1,0:T(8,128)(2,1)S(1)} %collective-permute-done.16.x1, bf16[4,256,128]{2,1,0:T(8,128)(2,1)S(1)} %collective-permute-done.17.x2, ...), custom_call_target="tpu_custom_call" | custom-call | flops 786432 | bytes 1572864 | tf_op jit(solution)/shard_map/pallas_call | solution.py:61
  74.6 6.4 %all-to-all-start = ((f32[32,8,128]{2,1,0:T(8,128)}), f32[32,8,128]{2,1,0:T(8,128)S(1)}, u32[]{:S(2)}, u32[]{:S(2)}) async-start(f32[32,8,128]{2,1,0:T(8,128)} %get-tuple-element.44), calls=%async_computation | async-start | bytes 262144 | tf_op jit(solution)/shard_map/all_to_all | solution.py:399
  81.1 4.7 %collective-permute-done.21.refs_3_ = bf16[4,256,128]{2,1,0:T(8,128)(2,1)S(1)} collective-permute-done((bf16[4,256,128]{2,1,0:T(8,128)(2,1)S(1)}, bf16[4,256,128]{2,1,0:T(8,128)(2,1)S(1)}, u32[]{:S(2)}, u32[]{:S(2)}) %collective-permute-start.21) | collective-permute-done | bytes 262176 | tf_op jit(solution)/shard_map/ppermute | solution.py:39
  85.7 2.9 %all-to-all-done.refs_4_ = f32[32,8,128]{2,1,0:T(8,128)S(1)} async-done(((f32[32,8,128]{2,1,0:T(8,128)}), f32[32,8,128]{2,1,0:T(8,128)S(1)}, u32[]{:S(2)}, u32[]{:S(2)}) %all-to-all-start) | async-done | bytes 131104 | tf_op jit(solution)/shard_map/all_to_all | solution.py:399
  88.6 1.8 %shard_map.98 = (bf16[4,256,128]{2,1,0:T(8,128)(2,1)S(1)}, f32[8,128]{1,0:T(8,128)S(1)}) custom-call(s32[1]{0:T(128)} %constant.166.clone.1.t_ref, f32[4,256,128]{2,1,0:T(8,128)S(1)} %get-tuple-element.42.g, bf16[4,256,128]{2,1,0:T(8,128)(2,1)S(1)} %get-tuple-element.43.refs_0_, bf16[4,256,128]{2,1,0:T(8,128)(2,1)S(1)} %collective-permute-done.19.refs_1_, ...), custom_call_target="tpu_custom_call" | custom-call | flops 2621440 | bytes 1835008 | tf_op jit(solution)/shard_map/pallas_call | solution.py:61
  90.4 1.1 collective-permute-start.27
  91.5 1.2 collective-permute-start.22
  92.7 3.3 %collective-permute-done.27.b = bf16[4,256,128]{2,1,0:T(8,128)(2,1)S(1)} collective-permute-done((bf16[4,256,128]{2,1,0:T(8,128)(2,1)S(1)}, bf16[4,256,128]{2,1,0:T(8,128)(2,1)S(1)}, u32[]{:S(2)}, u32[]{:S(2)}) %collective-permute-start.27) | collective-permute-done | bytes 262176 | tf_op jit(solution)/shard_map/ppermute | solution.py:39
  96.0 1.3 collective-permute-start.37
  98.5 2.8 %collective-permute-done.23.b = bf16[4,256,128]{2,1,0:T(8,128)(2,1)S(1)} collective-permute-done((bf16[4,256,128]{2,1,0:T(8,128)(2,1)S(1)}, bf16[4,256,128]{2,1,0:T(8,128)(2,1)S(1)}, u32[]{:S(2)}, u32[]{:S(2)}) %collective-permute-start.23) | collective-permute-done | bytes 262176 | tf_op jit(solution)/shard_map/ppermute | solution.py:39
  101.4 2.5 %collective-permute-start.38 = (bf16[8,256,128]{2,1,0:T(8,128)(2,1)S(1)}, bf16[8,256,128]{2,1,0:T(8,128)(2,1)S(1)}, u32[]{:S(2)}, u32[]{:S(2)}) collective-permute-start(bf16[8,256,128]{2,1,0:T(8,128)(2,1)S(1)} %shard_map.99.refs_1_), channel_id=1, source_target_pairs={{0,1},{1,0},{2,3},{3,2},{4,5},{5,4},{6,7},{7,6},{8,9},{9,8},{10,11... | collective-permute-start | bytes 1572872 | tf_op jit(solution)/shard_map/ppermute | solution.py:39
  103.8 3.0 %collective-permute-start.31 = (bf16[8,256,128]{2,1,0:T(8,128)(2,1)S(1)}, bf16[8,256,128]{2,1,0:T(8,128)(2,1)S(1)}, u32[]{:S(2)}, u32[]{:S(2)}) collective-permute-start(bf16[8,256,128]{2,1,0:T(8,128)(2,1)S(1)} %shard_map.100.refs_0_), channel_id=1, source_target_pairs={{0,6},{1,25},{2,0},{3,27},{4,2},{5,29},{6,4},{7,31},{8,14},{9,1},{... | collective-permute-start | bytes 1572872 | tf_op jit(solution)/shard_map/ppermute | solution.py:39
  108.2 4.0 %collective-permute-done.24.refs_3_ = bf16[8,256,128]{2,1,0:T(8,128)(2,1)S(1)} collective-permute-done((bf16[8,256,128]{2,1,0:T(8,128)(2,1)S(1)}, bf16[8,256,128]{2,1,0:T(8,128)(2,1)S(1)}, u32[]{:S(2)}, u32[]{:S(2)}) %collective-permute-start.24) | collective-permute-done | bytes 524320 | tf_op jit(solution)/shard_map/ppermute | solution.py:39
  112.1 1.2 collective-permute-start.25
  113.9 3.9 %collective-permute-done.31.refs_1_ = bf16[8,256,128]{2,1,0:T(8,128)(2,1)S(1)} collective-permute-done((bf16[8,256,128]{2,1,0:T(8,128)(2,1)S(1)}, bf16[8,256,128]{2,1,0:T(8,128)(2,1)S(1)}, u32[]{:S(2)}, u32[]{:S(2)}) %collective-permute-start.31) | collective-permute-done | bytes 524320 | tf_op jit(solution)/shard_map/ppermute | solution.py:39
  119.2 2.5 %collective-permute-done.29.refs_0_ = bf16[8,256,128]{2,1,0:T(8,128)(2,1)S(1)} collective-permute-done((bf16[8,256,128]{2,1,0:T(8,128)(2,1)S(1)}, bf16[8,256,128]{2,1,0:T(8,128)(2,1)S(1)}, u32[]{:S(2)}, u32[]{:S(2)}) %collective-permute-start.29) | collective-permute-done | bytes 524320 | tf_op jit(solution)/shard_map/ppermute | solution.py:39
  121.7 1.7 %collective-permute-done.25.refs_0_ = bf16[8,256,128]{2,1,0:T(8,128)(2,1)S(1)} collective-permute-done((bf16[8,256,128]{2,1,0:T(8,128)(2,1)S(1)}, bf16[8,256,128]{2,1,0:T(8,128)(2,1)S(1)}, u32[]{:S(2)}, u32[]{:S(2)}) %collective-permute-start.25) | collective-permute-done | bytes 524320 | tf_op jit(solution)/shard_map/ppermute | solution.py:39
  124.3 1.5 %fusion.1 = (f32[32768]{0:T(1024)}, f32[32768]{0:T(1024)}, f32[32768]{0:T(1024)}) fusion(f32[4,256,128]{2,1,0:T(8,128)S(1)} %get-tuple-element.42.g, f32[]{:T(128)} %bitcast.5, f32[256,128]{1,0:T(8,128)S(1)} %get-tuple-element.46, f32[256,128]{1,0:T(8,128)S(1)} %get-tuple-element.28, f32[32768]{0:T(1024)S(1)} %copy-done.2), kind=kLoop, calls=%fused_computation.6 | loop fusion | flops 491520 | bytes 917508 | tf_op jit(solution)/shard_map/reshape | solution.py:402
  125.8 2.1 %shard_map.101.refs_8_ = bf16[128,256,128]{2,1,0:T(8,128)(2,1)} custom-call(s32[128]{0:T(128)S(1)} %compare_select_fusion.16.t_ref, bf16[8,256,128]{2,1,0:T(8,128)(2,1)S(1)} %shard_map.100.refs_0_, bf16[8,256,128]{2,1,0:T(8,128)(2,1)S(1)} %shard_map.99.refs_1_, bf16[8,256,128]{2,1,0:T(8,128)(2,1)S(1)} %collective-permute-done.37.refs_2_, ...), custom_call_target="tpu_custom_call" | custom-call | flops 4194304 | bytes 4194304 | tf_op jit(solution)/shard_map/pallas_call | solution.py:61
  127.9 3.1 %shard_map.102.refs_2_ = bf16[128,256,128]{2,1,0:T(8,128)(2,1)} custom-call(s32[128]{0:T(128)S(1)} %compare_select_fusion.16.t_ref, bf16[8,256,128]{2,1,0:T(8,128)(2,1)S(1)} %collective-permute-done.28.refs_0_, bf16[8,256,128]{2,1,0:T(8,128)(2,1)S(1)} %collective-permute-done.31.refs_1_, ...), custom_call_target="tpu_custom_call", output_to_operand_aliasing={{}: (9, {})} | custom-call | flops 8388608 | bytes 8388608 | tf_op jit(solution)/shard_map/pallas_call | solution.py:61
  131.0 1.6 %shard_map.103.refs_2_ = bf16[128,256,128]{2,1,0:T(8,128)(2,1)} custom-call(s32[128]{0:T(128)S(1)} %compare_select_fusion.16.t_ref, bf16[8,256,128]{2,1,0:T(8,128)(2,1)S(1)} %collective-permute-done.29.refs_0_, bf16[8,256,128]{2,1,0:T(8,128)(2,1)S(1)} %collective-permute-done.30.refs_1_, ...), custom_call_target="tpu_custom_call", output_to_operand_aliasing={{}: (3, {})} | custom-call | flops 2097152 | bytes 2097152 | tf_op jit(solution)/shard_map/pallas_call | solution.py:61
  132.7 1.6 %shard_map.104 = bf16[128,256,128]{2,1,0:T(8,128)(2,1)} custom-call(s32[128]{0:T(128)S(1)} %compare_select_fusion.16.t_ref, bf16[8,256,128]{2,1,0:T(8,128)(2,1)S(1)} %collective-permute-done.25.refs_0_, bf16[8,256,128]{2,1,0:T(8,128)(2,1)S(1)} %collective-permute-done.26.refs_1_, ...), custom_call_target="tpu_custom_call", output_to_operand_aliasing={{}: (3, {})} | custom-call | flops 2097152 | bytes 2097152 | tf_op jit(solution)/shard_map/pallas_call | solution.py:61
  (65 shorter events, 10.3 us)
Async XLA Ops:
  3.0 9.0 %collective-permute-start.5 = (bf16[16,256,128]{2,1,0:T(8,128)(2,1)S(1)}, bf16[16,256,128]{2,1,0:T(8,128)(2,1)S(1)}, u32[]{:S(2)}, u32[]{:S(2)}) collective-permute-start(bf16[16,256,128]{2,1,0:T(8,128)(2,1)S(1)} %shard_map.89), channel_id=1, source_target_pairs={{0,1},{1,0},{2,3},{3,2},{4,5},{5,4},{6,7},{7,6},{8,9},{9,8},{10,11... | collective-permute-start | bytes 3145736 | tf_op jit(solution)/shard_map/ppermute | solution.py:39
  8.3 11.3 %collective-permute-start.9 = (bf16[16,256,128]{2,1,0:T(8,128)(2,1)S(1)}, bf16[16,256,128]{2,1,0:T(8,128)(2,1)S(1)}, u32[]{:S(2)}, u32[]{:S(2)}) collective-permute-start(bf16[16,256,128]{2,1,0:T(8,128)(2,1)S(1)} %get-tuple-element.36), channel_id=1, source_target_pairs={{0,1},{1,0},{2,3},{3,2},{4,5},{5,4},{6,7},{7,6},{8,9},{9,8},{10,11... | collective-permute-start | bytes 3145736 | tf_op jit(solution)/shard_map/ppermute | solution.py:39
  8.4 12.9 %collective-permute-start.4 = (bf16[16,256,128]{2,1,0:T(8,128)(2,1)S(1)}, bf16[16,256,128]{2,1,0:T(8,128)(2,1)S(1)}, u32[]{:S(2)}, u32[]{:S(2)}) collective-permute-start(bf16[16,256,128]{2,1,0:T(8,128)(2,1)S(1)} %get-tuple-element.32), channel_id=1, source_target_pairs={{0,1},{1,0},{2,3},{3,2},{4,5},{5,4},{6,7},{7,6},{8,9},{9,8},{10,11... | collective-permute-start | bytes 3145736 | tf_op jit(solution)/shard_map/ppermute | solution.py:39
  12.2 9.3 %collective-permute-start.11 = (bf16[8,256,128]{2,1,0:T(8,128)(2,1)S(1)}, bf16[8,256,128]{2,1,0:T(8,128)(2,1)S(1)}, u32[]{:S(2)}, u32[]{:S(2)}) collective-permute-start(bf16[8,256,128]{2,1,0:T(8,128)(2,1)S(1)} %get-tuple-element.37), channel_id=1, source_target_pairs={{0,6},{1,25},{2,0},{3,27},{4,2},{5,29},{6,4},{7,31},{8,14},{9,1},{... | collective-permute-start | bytes 1572872 | tf_op jit(solution)/shard_map/ppermute | solution.py:39
  15.2 10.1 %collective-permute-start.3 = (bf16[16,256,128]{2,1,0:T(8,128)(2,1)S(1)}, bf16[16,256,128]{2,1,0:T(8,128)(2,1)S(1)}, u32[]{:S(2)}, u32[]{:S(2)}) collective-permute-start(bf16[16,256,128]{2,1,0:T(8,128)(2,1)S(1)} %get-tuple-element.30), channel_id=1, source_target_pairs={{0,1},{1,0},{2,3},{3,2},{4,5},{5,4},{6,7},{7,6},{8,9},{9,8},{10,11... | collective-permute-start | bytes 3145736 | tf_op jit(solution)/shard_map/ppermute | solution.py:39
  15.3 9.7 %collective-permute-start.6 = (bf16[8,256,128]{2,1,0:T(8,128)(2,1)S(1)}, bf16[8,256,128]{2,1,0:T(8,128)(2,1)S(1)}, u32[]{:S(2)}, u32[]{:S(2)}) collective-permute-start(bf16[8,256,128]{2,1,0:T(8,128)(2,1)S(1)} %get-tuple-element.34), channel_id=1, source_target_pairs={{0,2},{1,9},{2,4},{3,11},{4,6},{5,13},{6,0},{7,15},{8,10},{9,17},{... | collective-permute-start | bytes 1572872 | tf_op jit(solution)/shard_map/ppermute | solution.py:39
  19.8 8.4 %collective-permute-start.10 = (bf16[8,256,128]{2,1,0:T(8,128)(2,1)S(1)}, bf16[8,256,128]{2,1,0:T(8,128)(2,1)S(1)}, u32[]{:S(2)}, u32[]{:S(2)}) collective-permute-start(bf16[8,256,128]{2,1,0:T(8,128)(2,1)S(1)} %shard_map.93), channel_id=1, source_target_pairs={{0,6},{1,25},{2,0},{3,27},{4,2},{5,29},{6,4},{7,31},{8,14},{9,1},{... | collective-permute-start | bytes 1572872 | tf_op jit(solution)/shard_map/ppermute | solution.py:39
  21.4 27.9 %copy-start.3 = (s32[129]{0:T(256)S(1)}, s32[129]{0:T(256)}, u32[]{:S(2)}) copy-start(s32[129]{0:T(256)} %param.9) | copy-start | bytes 1552
  21.4 28.0 %copy-start = (f32[1,65536]{1,0:T(1,128)S(1)}, f32[1,65536]{1,0:T(1,128)}, u32[]{:S(2)}) copy-start(f32[1,65536]{1,0:T(1,128)} %param.7) | copy-start | bytes 786436
  21.4 28.0 %copy-start.1 = (f32[1,65536]{1,0:T(1,128)S(1)}, f32[1,65536]{1,0:T(1,128)}, u32[]{:S(2)}) copy-start(f32[1,65536]{1,0:T(1,128)} %param.8) | copy-start | bytes 786436
  21.5 43.0 %copy-start.2 = (f32[32768]{0:T(1024)S(1)}, f32[32768]{0:T(1024)}, u32[]{:S(2)}) copy-start(f32[32768]{0:T(1024)} %param.6) | copy-start | bytes 393220
  21.5 9.6 %collective-permute-start.8 = (bf16[8,256,128]{2,1,0:T(8,128)(2,1)S(1)}, bf16[8,256,128]{2,1,0:T(8,128)(2,1)S(1)}, u32[]{:S(2)}, u32[]{:S(2)}) collective-permute-start(bf16[8,256,128]{2,1,0:T(8,128)(2,1)S(1)} %shard_map.92), channel_id=1, source_target_pairs={{0,2},{1,9},{2,4},{3,11},{4,6},{5,13},{6,0},{7,15},{8,10},{9,17},{... | collective-permute-start | bytes 1572872 | tf_op jit(solution)/shard_map/ppermute | solution.py:39
  21.8 12.0 %collective-permute-start.12 = (bf16[8,256,128]{2,1,0:T(8,128)(2,1)S(1)}, bf16[8,256,128]{2,1,0:T(8,128)(2,1)S(1)}, u32[]{:S(2)}, u32[]{:S(2)}) collective-permute-start(bf16[8,256,128]{2,1,0:T(8,128)(2,1)S(1)} %shard_map.94), channel_id=1, source_target_pairs={{0,6},{1,25},{2,0},{3,27},{4,2},{5,29},{6,4},{7,31},{8,14},{9,1},{... | collective-permute-start | bytes 1572872 | tf_op jit(solution)/shard_map/ppermute | solution.py:39
  25.2 11.5 %collective-permute-start.7 = (bf16[8,256,128]{2,1,0:T(8,128)(2,1)S(1)}, bf16[8,256,128]{2,1,0:T(8,128)(2,1)S(1)}, u32[]{:S(2)}, u32[]{:S(2)}) collective-permute-start(bf16[8,256,128]{2,1,0:T(8,128)(2,1)S(1)} %shard_map.91), channel_id=1, source_target_pairs={{0,2},{1,9},{2,4},{3,11},{4,6},{5,13},{6,0},{7,15},{8,10},{9,17},{... | collective-permute-start | bytes 1572872 | tf_op jit(solution)/shard_map/ppermute | solution.py:39
  37.3 6.8 %collective-permute-start.13 = (bf16[4,256,128]{2,1,0:T(8,128)(2,1)S(1)}, bf16[4,256,128]{2,1,0:T(8,128)(2,1)S(1)}, u32[]{:S(2)}, u32[]{:S(2)}) collective-permute-start(bf16[4,256,128]{2,1,0:T(8,128)(2,1)S(1)} %get-tuple-element.39), channel_id=1, source_target_pairs={{0,8},{1,3},{2,10},{3,5},{4,12},{5,7},{6,14},{7,1},{8,16},{9,11},{... | collective-permute-start | bytes 786440 | tf_op jit(solution)/shard_map/ppermute | solution.py:39
  38.1 9.3 %collective-permute-start.14 = (bf16[4,256,128]{2,1,0:T(8,128)(2,1)S(1)}, bf16[4,256,128]{2,1,0:T(8,128)(2,1)S(1)}, u32[]{:S(2)}, u32[]{:S(2)}) collective-permute-start(bf16[4,256,128]{2,1,0:T(8,128)(2,1)S(1)} %get-tuple-element.40), channel_id=1, source_target_pairs={{0,16},{1,5},{2,18},{3,7},{4,20},{5,1},{6,22},{7,3},{8,24},{9,13},... | collective-permute-start | bytes 786440 | tf_op jit(solution)/shard_map/ppermute | solution.py:39
  40.5 6.9 %collective-permute-start.15 = (bf16[4,256,128]{2,1,0:T(8,128)(2,1)S(1)}, bf16[4,256,128]{2,1,0:T(8,128)(2,1)S(1)}, u32[]{:S(2)}, u32[]{:S(2)}) collective-permute-start(bf16[4,256,128]{2,1,0:T(8,128)(2,1)S(1)} %get-tuple-element.41), channel_id=1, source_target_pairs={{0,24},{1,7},{2,26},{3,1},{4,28},{5,3},{6,30},{7,5},{8,0},{9,15},{... | collective-permute-start | bytes 786440 | tf_op jit(solution)/shard_map/ppermute | solution.py:39
  47.6 25.6 %collective-permute-start.16 = (bf16[4,256,128]{2,1,0:T(8,128)(2,1)S(1)}, bf16[4,256,128]{2,1,0:T(8,128)(2,1)S(1)}, u32[]{:S(2)}, u32[]{:S(2)}) collective-permute-start(bf16[4,256,128]{2,1,0:T(8,128)(2,1)S(1)} %shard_map.96.w), channel_id=1, source_target_pairs={{0,32},{1,33},{2,34},{3,35},{4,36},{5,37},{6,38},{7,39},{8,40},{9,... | collective-permute-start | bytes 786440 | tf_op jit(solution)/shard_map/ppermute | solution.py:39
  50.0 9.2 %collective-permute-start.1 = (bf16[2,128,128]{2,1,0:T(8,128)(2,1)S(1)}, bf16[2,128,128]{2,1,0:T(8,128)(2,1)S(1)}, u32[]{:S(2)}, u32[]{:S(2)}) collective-permute-start(bf16[2,128,128]{2,1,0:T(8,128)(2,1)S(1)} %get-tuple-element.27), channel_id=1, source_target_pairs={{0,1},{1,0},{2,3},{3,2},{4,5},{5,4},{6,7},{7,6},{8,9},{9,8},{10,11... | collective-permute-start | bytes 196616 | tf_op jit(solution)/shard_map/ppermute | solution.py:39
  53.2 20.0 %collective-permute-start.17 = (bf16[4,256,128]{2,1,0:T(8,128)(2,1)S(1)}, bf16[4,256,128]{2,1,0:T(8,128)(2,1)S(1)}, u32[]{:S(2)}, u32[]{:S(2)}) collective-permute-start(bf16[4,256,128]{2,1,0:T(8,128)(2,1)S(1)} %shard_map.96.w), channel_id=1, source_target_pairs={{0,64},{1,65},{2,66},{3,67},{4,68},{5,69},{6,70},{7,71},{8,72},{9,... | collective-permute-start | bytes 786440 | tf_op jit(solution)/shard_map/ppermute | solution.py:39
  56.5 16.7 %collective-permute-start.18 = (bf16[4,256,128]{2,1,0:T(8,128)(2,1)S(1)}, bf16[4,256,128]{2,1,0:T(8,128)(2,1)S(1)}, u32[]{:S(2)}, u32[]{:S(2)}) collective-permute-start(bf16[4,256,128]{2,1,0:T(8,128)(2,1)S(1)} %shard_map.96.w), channel_id=1, source_target_pairs={{0,96},{1,97},{2,98},{3,99},{4,100},{5,101},{6,102},{7,103},{8,104... | collective-permute-start | bytes 786440 | tf_op jit(solution)/shard_map/ppermute | solution.py:39
  57.2 3.3 %collective-permute-start = (bf16[2,136,128]{2,1,0:T(8,128)(2,1)S(1)}, bf16[2,136,128]{2,1,0:T(8,128)(2,1)S(1)}, u32[]{:S(2)}, u32[]{:S(2)}) collective-permute-start(bf16[2,136,128]{2,1,0:T(8,128)(2,1)S(1)} %get-tuple-element.26), channel_id=1, source_target_pairs={{0,1},{1,2},{2,3},{3,4},{4,5},{5,6},{6,7},{7,8},{8,9},{9,10},{10,1... | collective-permute-start | bytes 208904 | tf_op jit(solution)/shard_map/ppermute | solution.py:377
  59.2 5.3 %collective-permute-start.2 = (bf16[2,128,128]{2,1,0:T(8,128)(2,1)S(1)}, bf16[2,128,128]{2,1,0:T(8,128)(2,1)S(1)}, u32[]{:S(2)}, u32[]{:S(2)}) collective-permute-start(bf16[2,128,128]{2,1,0:T(8,128)(2,1)S(1)} %collective-permute-done.1.a), channel_id=1, source_target_pairs={{3,1},{5,3},{7,5},{9,7},{11,9},{13,11},{15,13},{17,15},{19,17},{21... | collective-permute-start | bytes 196616 | tf_op jit(solution)/shard_map/ppermute | solution.py:379
  66.5 14.5 %collective-permute-start.19 = (bf16[4,256,128]{2,1,0:T(8,128)(2,1)S(1)}, bf16[4,256,128]{2,1,0:T(8,128)(2,1)S(1)}, u32[]{:S(2)}, u32[]{:S(2)}) collective-permute-start(bf16[4,256,128]{2,1,0:T(8,128)(2,1)S(1)} %get-tuple-element.43.refs_0_), channel_id=1, source_target_pairs={{0,96},{1,97},{2,98},{3,99},{4,100},{5,101},{6,102},{7,103},{8,104... | collective-permute-start | bytes 786440 | tf_op jit(solution)/shard_map/ppermute | solution.py:39
  70.4 10.6 %collective-permute-start.20 = (bf16[4,256,128]{2,1,0:T(8,128)(2,1)S(1)}, bf16[4,256,128]{2,1,0:T(8,128)(2,1)S(1)}, u32[]{:S(2)}, u32[]{:S(2)}) collective-permute-start(bf16[4,256,128]{2,1,0:T(8,128)(2,1)S(1)} %get-tuple-element.43.refs_0_), channel_id=1, source_target_pairs={{0,64},{1,65},{2,66},{3,67},{4,68},{5,69},{6,70},{7,71},{8,72},{9,... | collective-permute-start | bytes 786440 | tf_op jit(solution)/shard_map/ppermute | solution.py:39
  73.2 12.5 %collective-permute-start.21 = (bf16[4,256,128]{2,1,0:T(8,128)(2,1)S(1)}, bf16[4,256,128]{2,1,0:T(8,128)(2,1)S(1)}, u32[]{:S(2)}, u32[]{:S(2)}) collective-permute-start(bf16[4,256,128]{2,1,0:T(8,128)(2,1)S(1)} %get-tuple-element.43.refs_0_), channel_id=1, source_target_pairs={{0,32},{1,33},{2,34},{3,35},{4,36},{5,37},{6,38},{7,39},{8,40},{9,... | collective-permute-start | bytes 786440 | tf_op jit(solution)/shard_map/ppermute | solution.py:39
  74.6 14.0 %all-to-all-start = ((f32[32,8,128]{2,1,0:T(8,128)}), f32[32,8,128]{2,1,0:T(8,128)S(1)}, u32[]{:S(2)}, u32[]{:S(2)}) async-start(f32[32,8,128]{2,1,0:T(8,128)} %get-tuple-element.44), calls=%async_computation | async-start | bytes 262144 | tf_op jit(solution)/shard_map/all_to_all | solution.py:399
  90.4 5.6 %collective-permute-start.27 = (bf16[4,256,128]{2,1,0:T(8,128)(2,1)S(1)}, bf16[4,256,128]{2,1,0:T(8,128)(2,1)S(1)}, u32[]{:S(2)}, u32[]{:S(2)}) collective-permute-start(bf16[4,256,128]{2,1,0:T(8,128)(2,1)S(1)} %get-tuple-element.47.a), channel_id=1, source_target_pairs={{0,24},{1,7},{2,26},{3,1},{4,28},{5,3},{6,30},{7,5},{8,0},{9,15},{... | collective-permute-start | bytes 786440 | tf_op jit(solution)/shard_map/ppermute | solution.py:39
  91.5 7.1 %collective-permute-start.22 = (bf16[4,256,128]{2,1,0:T(8,128)(2,1)S(1)}, bf16[4,256,128]{2,1,0:T(8,128)(2,1)S(1)}, u32[]{:S(2)}, u32[]{:S(2)}) collective-permute-start(bf16[4,256,128]{2,1,0:T(8,128)(2,1)S(1)} %get-tuple-element.47.a), channel_id=1, source_target_pairs={{0,16},{1,5},{2,18},{3,7},{4,20},{5,1},{6,22},{7,3},{8,24},{9,13},... | collective-permute-start | bytes 786440 | tf_op jit(solution)/shard_map/ppermute | solution.py:39
  92.6 8.7 %collective-permute-start.23 = (bf16[4,256,128]{2,1,0:T(8,128)(2,1)S(1)}, bf16[4,256,128]{2,1,0:T(8,128)(2,1)S(1)}, u32[]{:S(2)}, u32[]{:S(2)}) collective-permute-start(bf16[4,256,128]{2,1,0:T(8,128)(2,1)S(1)} %get-tuple-element.47.a), channel_id=1, source_target_pairs={{0,8},{1,3},{2,10},{3,5},{4,12},{5,7},{6,14},{7,1},{8,16},{9,11},{... | collective-permute-start | bytes 786440 | tf_op jit(solution)/shard_map/ppermute | solution.py:39
  96.0 10.8 %collective-permute-start.37 = (bf16[8,256,128]{2,1,0:T(8,128)(2,1)S(1)}, bf16[8,256,128]{2,1,0:T(8,128)(2,1)S(1)}, u32[]{:S(2)}, u32[]{:S(2)}) collective-permute-start(bf16[8,256,128]{2,1,0:T(8,128)(2,1)S(1)} %shard_map.100.refs_0_), channel_id=1, source_target_pairs={{0,1},{1,0},{2,3},{3,2},{4,5},{5,4},{6,7},{7,6},{8,9},{9,8},{10,11... | collective-permute-start | bytes 1572872 | tf_op jit(solution)/shard_map/ppermute | solution.py:39
  97.4 10.2 %collective-permute-start.28 = (bf16[8,256,128]{2,1,0:T(8,128)(2,1)S(1)}, bf16[8,256,128]{2,1,0:T(8,128)(2,1)S(1)}, u32[]{:S(2)}, u32[]{:S(2)}) collective-permute-start(bf16[8,256,128]{2,1,0:T(8,128)(2,1)S(1)} %shard_map.100.refs_0_), channel_id=1, source_target_pairs={{0,2},{1,9},{2,4},{3,11},{4,6},{5,13},{6,0},{7,15},{8,10},{9,17},{... | collective-permute-start | bytes 1572872 | tf_op jit(solution)/shard_map/ppermute | solution.py:39
  101.4 6.5 %collective-permute-start.38 = (bf16[8,256,128]{2,1,0:T(8,128)(2,1)S(1)}, bf16[8,256,128]{2,1,0:T(8,128)(2,1)S(1)}, u32[]{:S(2)}, u32[]{:S(2)}) collective-permute-start(bf16[8,256,128]{2,1,0:T(8,128)(2,1)S(1)} %shard_map.99.refs_1_), channel_id=1, source_target_pairs={{0,1},{1,0},{2,3},{3,2},{4,5},{5,4},{6,7},{7,6},{8,9},{9,8},{10,11... | collective-permute-start | bytes 1572872 | tf_op jit(solution)/shard_map/ppermute | solution.py:39
  103.8 8.3 %collective-permute-start.24 = (bf16[8,256,128]{2,1,0:T(8,128)(2,1)S(1)}, bf16[8,256,128]{2,1,0:T(8,128)(2,1)S(1)}, u32[]{:S(2)}, u32[]{:S(2)}) collective-permute-start(bf16[8,256,128]{2,1,0:T(8,128)(2,1)S(1)} %shard_map.99.refs_1_), channel_id=1, source_target_pairs={{0,6},{1,25},{2,0},{3,27},{4,2},{5,29},{6,4},{7,31},{8,14},{9,1},{... | collective-permute-start | bytes 1572872 | tf_op jit(solution)/shard_map/ppermute | solution.py:39
  103.8 13.9 %collective-permute-start.31 = (bf16[8,256,128]{2,1,0:T(8,128)(2,1)S(1)}, bf16[8,256,128]{2,1,0:T(8,128)(2,1)S(1)}, u32[]{:S(2)}, u32[]{:S(2)}) collective-permute-start(bf16[8,256,128]{2,1,0:T(8,128)(2,1)S(1)} %shard_map.100.refs_0_), channel_id=1, source_target_pairs={{0,6},{1,25},{2,0},{3,27},{4,2},{5,29},{6,4},{7,31},{8,14},{9,1},{... | collective-permute-start | bytes 1572872 | tf_op jit(solution)/shard_map/ppermute | solution.py:39
  106.9 11.8 %collective-permute-start.32 = (bf16[8,256,128]{2,1,0:T(8,128)(2,1)S(1)}, bf16[8,256,128]{2,1,0:T(8,128)(2,1)S(1)}, u32[]{:S(2)}, u32[]{:S(2)}) collective-permute-start(bf16[8,256,128]{2,1,0:T(8,128)(2,1)S(1)} %shard_map.99.refs_1_), channel_id=1, source_target_pairs={{0,2},{1,9},{2,4},{3,11},{4,6},{5,13},{6,0},{7,15},{8,10},{9,17},{... | collective-permute-start | bytes 1572872 | tf_op jit(solution)/shard_map/ppermute | solution.py:39
  107.6 11.1 %collective-permute-start.33 = (bf16[8,256,128]{2,1,0:T(8,128)(2,1)S(1)}, bf16[8,256,128]{2,1,0:T(8,128)(2,1)S(1)}, u32[]{:S(2)}, u32[]{:S(2)}) collective-permute-start(bf16[8,256,128]{2,1,0:T(8,128)(2,1)S(1)} %collective-permute-done.28.refs_0_), channel_id=1, source_target_pairs={{0,1},{1,0},{2,3},{3,2},{4,5},{5,4},{6,7},{7,6},{8,9},{9,8},{10,11... | collective-permute-start | bytes 1572872 | tf_op jit(solution)/shard_map/ppermute | solution.py:39
  107.9 13.9 %collective-permute-start.29 = (bf16[8,256,128]{2,1,0:T(8,128)(2,1)S(1)}, bf16[8,256,128]{2,1,0:T(8,128)(2,1)S(1)}, u32[]{:S(2)}, u32[]{:S(2)}) collective-permute-start(bf16[8,256,128]{2,1,0:T(8,128)(2,1)S(1)} %collective-permute-done.28.refs_0_), channel_id=1, source_target_pairs={{0,2},{1,9},{2,4},{3,11},{4,6},{5,13},{6,0},{7,15},{8,10},{9,17},{... | collective-permute-start | bytes 1572872 | tf_op jit(solution)/shard_map/ppermute | solution.py:39
  112.1 11.2 %collective-permute-start.25 = (bf16[8,256,128]{2,1,0:T(8,128)(2,1)S(1)}, bf16[8,256,128]{2,1,0:T(8,128)(2,1)S(1)}, u32[]{:S(2)}, u32[]{:S(2)}) collective-permute-start(bf16[8,256,128]{2,1,0:T(8,128)(2,1)S(1)} %collective-permute-done.24.refs_3_), channel_id=1, source_target_pairs={{0,6},{1,25},{2,0},{3,27},{4,2},{5,29},{6,4},{7,31},{8,14},{9,1},{... | collective-permute-start | bytes 1572872 | tf_op jit(solution)/shard_map/ppermute | solution.py:39
  117.8 10.2 %collective-permute-start.36 = (bf16[8,256,128]{2,1,0:T(8,128)(2,1)S(1)}, bf16[8,256,128]{2,1,0:T(8,128)(2,1)S(1)}, u32[]{:S(2)}, u32[]{:S(2)}) collective-permute-start(bf16[8,256,128]{2,1,0:T(8,128)(2,1)S(1)} %collective-permute-done.24.refs_3_), channel_id=1, source_target_pairs={{0,1},{1,0},{2,3},{3,2},{4,5},{5,4},{6,7},{7,6},{8,9},{9,8},{10,11... | collective-permute-start | bytes 1572872 | tf_op jit(solution)/shard_map/ppermute | solution.py:39
  118.7 9.2 %collective-permute-start.34 = (bf16[8,256,128]{2,1,0:T(8,128)(2,1)S(1)}, bf16[8,256,128]{2,1,0:T(8,128)(2,1)S(1)}, u32[]{:S(2)}, u32[]{:S(2)}) collective-permute-start(bf16[8,256,128]{2,1,0:T(8,128)(2,1)S(1)} %collective-permute-done.31.refs_1_), channel_id=1, source_target_pairs={{0,1},{1,0},{2,3},{3,2},{4,5},{5,4},{6,7},{7,6},{8,9},{9,8},{10,11... | collective-permute-start | bytes 1572872 | tf_op jit(solution)/shard_map/ppermute | solution.py:39
  118.7 9.2 %collective-permute-start.35 = (bf16[8,256,128]{2,1,0:T(8,128)(2,1)S(1)}, bf16[8,256,128]{2,1,0:T(8,128)(2,1)S(1)}, u32[]{:S(2)}, u32[]{:S(2)}) collective-permute-start(bf16[8,256,128]{2,1,0:T(8,128)(2,1)S(1)} %collective-permute-done.32.refs_2_), channel_id=1, source_target_pairs={{0,1},{1,0},{2,3},{3,2},{4,5},{5,4},{6,7},{7,6},{8,9},{9,8},{10,11... | collective-permute-start | bytes 1572872 | tf_op jit(solution)/shard_map/ppermute | solution.py:39
  121.7 9.3 %collective-permute-start.30 = (bf16[8,256,128]{2,1,0:T(8,128)(2,1)S(1)}, bf16[8,256,128]{2,1,0:T(8,128)(2,1)S(1)}, u32[]{:S(2)}, u32[]{:S(2)}) collective-permute-start(bf16[8,256,128]{2,1,0:T(8,128)(2,1)S(1)} %collective-permute-done.29.refs_0_), channel_id=1, source_target_pairs={{0,1},{1,0},{2,3},{3,2},{4,5},{5,4},{6,7},{7,6},{8,9},{9,8},{10,11... | collective-permute-start | bytes 1572872 | tf_op jit(solution)/shard_map/ppermute | solution.py:39
  123.4 9.3 %collective-permute-start.26 = (bf16[8,256,128]{2,1,0:T(8,128)(2,1)S(1)}, bf16[8,256,128]{2,1,0:T(8,128)(2,1)S(1)}, u32[]{:S(2)}, u32[]{:S(2)}) collective-permute-start(bf16[8,256,128]{2,1,0:T(8,128)(2,1)S(1)} %collective-permute-done.25.refs_0_), channel_id=1, source_target_pairs={{0,1},{1,0},{2,3},{3,2},{4,5},{5,4},{6,7},{7,6},{8,9},{9,8},{10,11... | collective-permute-start | bytes 1572872 | tf_op jit(solution)/shard_map/ppermute | solution.py:39

commit v5 on v4

--- a/solution.py
+++ b/solution.py
@@ -349,10 +349,10 @@
     given, kept, swapped = {}, {}, {}
     (given[2],) = fetch(places, g, (theirs[2], BF))
     swapped[2] = send(given[2], "core")
-    kept[2], given[1], given[3] = fetch(places, g, (mine[2], F32), (theirs[1], BF), (theirs[3], BF))
+    kept[2], given[1] = fetch(places, g, (mine[2], F32), (theirs[1], BF))
     swapped[1] = send(given[1], "core")
+    given[3], kept[1], kept[3] = fetch(places, g, (theirs[3], BF), (mine[1], F32), (mine[3], F32))
     swapped[3] = send(given[3], "core")
-    kept[1], kept[3] = fetch(places, g, (mine[1], F32), (mine[3], F32))
     given[0], kept[0] = fetch(places, g, (theirs[0], BF), (mine[0], F32))
     swapped[0] = send(given[0], "core")
     low, high = (0, 8), (8, 8)
@@ -394,8 +394,10 @@
     for s in (2, 1, 3):
         quarters[s] = send(quarters[s], "b", s)
     (partial,) = sum_piece([[(v, 0, 4)] for v in (own, quarters[1], quarters[2], quarters[3])], [(4, BF)])
-    w2, w1, w3 = send(partial, "z", 2), send(partial, "z", 1), send(partial, "z", 3)
-    gradient, squares = total_piece(partial, w1, w2, w3, 32)
+    parts = {}
+    for s in (2, 1, 3):
+        parts[s] = send(partial, "z", s)
+    gradient, squares = total_piece(partial, parts[1], parts[2], parts[3], 32)
     squares = lax.all_to_all(squares, ("y", "x", "core"), 0, 0, tiled=True)
     piece, clip = updated_piece(gradient, states, squares, count * width)
     new = adam(master_tiles, m_prev, v_prev, gradient[0], clip[0, 0])
@@ -416,7 +418,7 @@
     for r, h in halves:
         partner[r, h] = send(halves[r, h], "core")
     out = None
-    for keys in (((0, 0), (0, 1)), ((3, 0), (1, 0), (3, 1), (1, 1)), ((2, 0),), ((2, 1),)):
+    for keys in (((0, 0), (0, 1)), ((3, 0), (1, 0), (3, 1), (1, 1), (2, 0)), ((2, 1),)):
         pairs = [(mine[r] + 8 * h, halves[r, h]) for r, h in keys]
         pairs += [(theirs[r] + 8 * h, partner[r, h]) for r, h in keys]
         out = place(places, pairs, out)

time: 135 us -> 136 us (level)
    pallas_call x21 -> x20, Pallas kernels: 28.1 us -> 26.9 us  [call(): pl.pallas_call(body, grid_spec=pltpu.PrefetchScalarGridSpec(num_scalar_pr...]
  transfers between devices with their start and end apart: 40 -> 40, of which waited for: 18 -> 18; matrix products, arithmetic and copies ran while one was open for 2% -> 2% of each run, Pallas kernels for 16% -> 15%
where the time goes in v5:
time: 136 us; the launch traced here: 135 us
  starting transfers between devices  55.5 us (41%)
  waiting for transfers between devices  49.6 us (36%)
  Pallas kernels  26.9 us (20%)
  other arithmetic  1.57 us (1%)
    ppermute x37, starting transfers between devices, send(): return lax.ppermute(value, DP, perm(axis, s))  45.3 us
    ppermute x37, waiting for transfers between devices, send(): return lax.ppermute(value, DP, perm(axis, s))  42.7 us
    pallas_call x20, Pallas kernels, call(): pl.pallas_call(body, grid_spec=pltpu.PrefetchScalarGridSpec(num_scalar_pr...  26.9 us
    all_to_all x1, starting transfers between devices, step(): squares = lax.all_to_all(squares, ('y', 'x', 'core'), 0, 0, tiled=True)  6.41 us
    ppermute x1, waiting for transfers between devices, step(): passed = lax.ppermute(after, DP, [(d, d - 2) for d in range(3, 128, 2)])  3.97 us
    all_to_all x1, waiting for transfers between devices, step(): squares = lax.all_to_all(squares, ('y', 'x', 'core'), 0, 0, tiled=True)  2.91 us
  transfers between devices with their start and end apart: 40, of which 18 were waited for; matrix products, arithmetic and copies ran while one was open for 2% of the time, Pallas kernels for 15%

profile of v5, /device:TPU:1, one launch (start us, length us, event | category | flops | bytes accessed | tf_op | source)
XLA Modules:
  0.0 135.3 jit_solution(10216591485411592194)
XLA Ops:
  0.7 2.3 %shard_map.89 = bf16[16,256,128]{2,1,0:T(8,128)(2,1)S(1)} custom-call(s32[128]{0:T(128)S(1)} %compare_select_fusion.16.t_ref, f32[128,256,128]{2,1,0:T(8,128)} %bitcast.30), custom_call_target="tpu_custom_call" | custom-call | flops 524288 | bytes 3145728 | tf_op jit(solution)/shard_map/pallas_call | solution.py:61
  3.0 1.5 %collective-permute-start.5 = (bf16[16,256,128]{2,1,0:T(8,128)(2,1)S(1)}, bf16[16,256,128]{2,1,0:T(8,128)(2,1)S(1)}, u32[]{:S(2)}, u32[]{:S(2)}) collective-permute-start(bf16[16,256,128]{2,1,0:T(8,128)(2,1)S(1)} %shard_map.89), channel_id=1, source_target_pairs={{0,1},{1,0},{2,3},{3,2},{4,5},{5,4},{6,7},{7,6},{8,9},{9,8},{10,11... | collective-permute-start | bytes 3145736 | tf_op jit(solution)/shard_map/ppermute | solution.py:39
  4.5 3.8 %shard_map.87 = (bf16[16,256,128]{2,1,0:T(8,128)(2,1)S(1)}, f32[16,256,128]{2,1,0:T(8,128)S(1)}, f32[16,256,128]{2,1,0:T(8,128)S(1)}) custom-call(s32[128]{0:T(128)S(1)} %compare_select_fusion.16.t_ref, f32[128,256,128]{2,1,0:T(8,128)} %bitcast.31), custom_call_target="tpu_custom_call" | custom-call | flops 1572864 | bytes 9437184 | tf_op jit(solution)/shard_map/pallas_call | solution.py:61
  8.4 3.1 %shard_map.88 = (f32[16,256,128]{2,1,0:T(8,128)S(1)}, bf16[16,256,128]{2,1,0:T(8,128)(2,1)S(1)}) custom-call(s32[128]{0:T(128)S(1)} %compare_select_fusion.16.t_ref, f32[128,256,128]{2,1,0:T(8,128)} %bitcast.32), custom_call_target="tpu_custom_call" | custom-call | flops 1048576 | bytes 6291456 | tf_op jit(solution)/shard_map/pallas_call | solution.py:61
  12.1 3.1 %shard_map.86 = (bf16[16,256,128]{2,1,0:T(8,128)(2,1)S(1)}, f32[16,256,128]{2,1,0:T(8,128)S(1)}) custom-call(s32[128]{0:T(128)S(1)} %compare_select_fusion.16.t_ref, f32[128,256,128]{2,1,0:T(8,128)} %bitcast.33), custom_call_target="tpu_custom_call" | custom-call | flops 1048576 | bytes 6291456 | tf_op jit(solution)/shard_map/pallas_call | solution.py:61
  15.4 2.9 %collective-permute-start.11 = (bf16[8,256,128]{2,1,0:T(8,128)(2,1)S(1)}, bf16[8,256,128]{2,1,0:T(8,128)(2,1)S(1)}, u32[]{:S(2)}, u32[]{:S(2)}) collective-permute-start(bf16[8,256,128]{2,1,0:T(8,128)(2,1)S(1)} %get-tuple-element.37), channel_id=1, source_target_pairs={{0,6},{1,25},{2,0},{3,27},{4,2},{5,29},{6,4},{7,31},{8,14},{9,1},{... | collective-permute-start | bytes 1572872 | tf_op jit(solution)/shard_map/ppermute | solution.py:39
  18.3 1.3 collective-permute-start.6
  19.8 1.5 %collective-permute-start.10 = (bf16[8,256,128]{2,1,0:T(8,128)(2,1)S(1)}, bf16[8,256,128]{2,1,0:T(8,128)(2,1)S(1)}, u32[]{:S(2)}, u32[]{:S(2)}) collective-permute-start(bf16[8,256,128]{2,1,0:T(8,128)(2,1)S(1)} %shard_map.93), channel_id=1, source_target_pairs={{0,6},{1,25},{2,0},{3,27},{4,2},{5,29},{6,4},{7,31},{8,14},{9,1},{... | collective-permute-start | bytes 1572872 | tf_op jit(solution)/shard_map/ppermute | solution.py:39
  21.5 2.9 %collective-permute-done.11.refs_2_ = bf16[8,256,128]{2,1,0:T(8,128)(2,1)S(1)} collective-permute-done((bf16[8,256,128]{2,1,0:T(8,128)(2,1)S(1)}, bf16[8,256,128]{2,1,0:T(8,128)(2,1)S(1)}, u32[]{:S(2)}, u32[]{:S(2)}) %collective-permute-start.11) | collective-permute-done | bytes 524320 | tf_op jit(solution)/shard_map/ppermute | solution.py:39
  24.6 3.5 %collective-permute-start.12 = (bf16[8,256,128]{2,1,0:T(8,128)(2,1)S(1)}, bf16[8,256,128]{2,1,0:T(8,128)(2,1)S(1)}, u32[]{:S(2)}, u32[]{:S(2)}) collective-permute-start(bf16[8,256,128]{2,1,0:T(8,128)(2,1)S(1)} %shard_map.94), channel_id=1, source_target_pairs={{0,6},{1,25},{2,0},{3,27},{4,2},{5,29},{6,4},{7,31},{8,14},{9,1},{... | collective-permute-start | bytes 1572872 | tf_op jit(solution)/shard_map/ppermute | solution.py:39
  28.4 1.6 %collective-permute-done.10.refs_4_ = bf16[8,256,128]{2,1,0:T(8,128)(2,1)S(1)} collective-permute-done((bf16[8,256,128]{2,1,0:T(8,128)(2,1)S(1)}, bf16[8,256,128]{2,1,0:T(8,128)(2,1)S(1)}, u32[]{:S(2)}, u32[]{:S(2)}) %collective-permute-start.10) | collective-permute-done | bytes 524320 | tf_op jit(solution)/shard_map/ppermute | solution.py:39
  30.0 3.5 %collective-permute-done.8.refs_3_ = bf16[8,256,128]{2,1,0:T(8,128)(2,1)S(1)} collective-permute-done((bf16[8,256,128]{2,1,0:T(8,128)(2,1)S(1)}, bf16[8,256,128]{2,1,0:T(8,128)(2,1)S(1)}, u32[]{:S(2)}, u32[]{:S(2)}) %collective-permute-start.8) | collective-permute-done | bytes 524320 | tf_op jit(solution)/shard_map/ppermute | solution.py:39
  33.6 2.1 %collective-permute-done.12.refs_5_ = bf16[8,256,128]{2,1,0:T(8,128)(2,1)S(1)} collective-permute-done((bf16[8,256,128]{2,1,0:T(8,128)(2,1)S(1)}, bf16[8,256,128]{2,1,0:T(8,128)(2,1)S(1)}, u32[]{:S(2)}, u32[]{:S(2)}) %collective-permute-start.12) | collective-permute-done | bytes 524320 | tf_op jit(solution)/shard_map/ppermute | solution.py:39
  35.7 3.5 %collective-permute-done.7.refs_2_ = bf16[8,256,128]{2,1,0:T(8,128)(2,1)S(1)} collective-permute-done((bf16[8,256,128]{2,1,0:T(8,128)(2,1)S(1)}, bf16[8,256,128]{2,1,0:T(8,128)(2,1)S(1)}, u32[]{:S(2)}, u32[]{:S(2)}) %collective-permute-start.7) | collective-permute-done | bytes 524320 | tf_op jit(solution)/shard_map/ppermute | solution.py:39
  40.7 2.5 %collective-permute-start.14 = (bf16[4,256,128]{2,1,0:T(8,128)(2,1)S(1)}, bf16[4,256,128]{2,1,0:T(8,128)(2,1)S(1)}, u32[]{:S(2)}, u32[]{:S(2)}) collective-permute-start(bf16[4,256,128]{2,1,0:T(8,128)(2,1)S(1)} %get-tuple-element.40), channel_id=1, source_target_pairs={{0,16},{1,5},{2,18},{3,7},{4,20},{5,1},{6,22},{7,3},{8,24},{9,13},... | collective-permute-start | bytes 786440 | tf_op jit(solution)/shard_map/ppermute | solution.py:39
  43.1 1.2 collective-permute-start.15
  44.3 2.3 %collective-permute-done.13.refs_1_ = bf16[4,256,128]{2,1,0:T(8,128)(2,1)S(1)} collective-permute-done((bf16[4,256,128]{2,1,0:T(8,128)(2,1)S(1)}, bf16[4,256,128]{2,1,0:T(8,128)(2,1)S(1)}, u32[]{:S(2)}, u32[]{:S(2)}) %collective-permute-start.13) | collective-permute-done | bytes 262176 | tf_op jit(solution)/shard_map/ppermute | solution.py:39
  46.6 3.4 %collective-permute-done.14.refs_2_ = bf16[4,256,128]{2,1,0:T(8,128)(2,1)S(1)} collective-permute-done((bf16[4,256,128]{2,1,0:T(8,128)(2,1)S(1)}, bf16[4,256,128]{2,1,0:T(8,128)(2,1)S(1)}, u32[]{:S(2)}, u32[]{:S(2)}) %collective-permute-start.14) | collective-permute-done | bytes 262176 | tf_op jit(solution)/shard_map/ppermute | solution.py:39
  50.1 1.7 %collective-permute-start.16 = (bf16[4,256,128]{2,1,0:T(8,128)(2,1)S(1)}, bf16[4,256,128]{2,1,0:T(8,128)(2,1)S(1)}, u32[]{:S(2)}, u32[]{:S(2)}) collective-permute-start(bf16[4,256,128]{2,1,0:T(8,128)(2,1)S(1)} %shard_map.96.w), channel_id=1, source_target_pairs={{0,32},{1,33},{2,34},{3,35},{4,36},{5,37},{6,38},{7,39},{8,40},{9,... | collective-permute-start | bytes 786440 | tf_op jit(solution)/shard_map/ppermute | solution.py:39
  52.5 2.7 %collective-permute-start.1 = (bf16[2,128,128]{2,1,0:T(8,128)(2,1)S(1)}, bf16[2,128,128]{2,1,0:T(8,128)(2,1)S(1)}, u32[]{:S(2)}, u32[]{:S(2)}) collective-permute-start(bf16[2,128,128]{2,1,0:T(8,128)(2,1)S(1)} %get-tuple-element.27), channel_id=1, source_target_pairs={{0,1},{1,0},{2,3},{3,2},{4,5},{5,4},{6,7},{7,6},{8,9},{9,8},{10,11... | collective-permute-start | bytes 196616 | tf_op jit(solution)/shard_map/ppermute | solution.py:39
  55.2 3.3 %collective-permute-start.17 = (bf16[4,256,128]{2,1,0:T(8,128)(2,1)S(1)}, bf16[4,256,128]{2,1,0:T(8,128)(2,1)S(1)}, u32[]{:S(2)}, u32[]{:S(2)}) collective-permute-start(bf16[4,256,128]{2,1,0:T(8,128)(2,1)S(1)} %shard_map.96.w), channel_id=1, source_target_pairs={{0,64},{1,65},{2,66},{3,67},{4,68},{5,69},{6,70},{7,71},{8,72},{9,... | collective-permute-start | bytes 786440 | tf_op jit(solution)/shard_map/ppermute | solution.py:39
  59.3 2.5 %collective-permute-start = (bf16[2,136,128]{2,1,0:T(8,128)(2,1)S(1)}, bf16[2,136,128]{2,1,0:T(8,128)(2,1)S(1)}, u32[]{:S(2)}, u32[]{:S(2)}) collective-permute-start(bf16[2,136,128]{2,1,0:T(8,128)(2,1)S(1)} %get-tuple-element.26), channel_id=1, source_target_pairs={{0,1},{1,2},{2,3},{3,4},{4,5},{5,6},{6,7},{7,8},{8,9},{9,10},{10,1... | collective-permute-start | bytes 208904 | tf_op jit(solution)/shard_map/ppermute | solution.py:377
  61.7 1.3 collective-permute-start.2
  63.1 4.0 %collective-permute-done.2.p = bf16[2,128,128]{2,1,0:T(8,128)(2,1)S(1)} collective-permute-done((bf16[2,128,128]{2,1,0:T(8,128)(2,1)S(1)}, bf16[2,128,128]{2,1,0:T(8,128)(2,1)S(1)}, u32[]{:S(2)}, u32[]{:S(2)}) %collective-permute-start.2) | collective-permute-done | bytes 65568 | tf_op jit(solution)/shard_map/ppermute | solution.py:379
  67.1 2.0 %shard_map.85 = (f32[256,128]{1,0:T(8,128)S(1)}, f32[256,128]{1,0:T(8,128)S(1)}, bf16[4,256,128]{2,1,0:T(8,128)(2,1)S(1)}) custom-call(s32[130]{0:T(256)S(1)} %pad_add_fusion.t_ref, f32[512,128]{1,0:T(8,128)S(1)} %bitcast.26, f32[512,128]{1,0:T(8,128)S(1)} %bitcast.28, bf16[2,136,128]{2,1,0:T(8,128)(2,1)S(1)} %collective-permute-done.b, ...), custom_call_target="tpu_custom_call" | custom-call | flops 1310720 | bytes 1310720 | tf_op jit(solution)/shard_map/pallas_call | solution.py:61
  69.1 3.4 %collective-permute-start.19 = (bf16[4,256,128]{2,1,0:T(8,128)(2,1)S(1)}, bf16[4,256,128]{2,1,0:T(8,128)(2,1)S(1)}, u32[]{:S(2)}, u32[]{:S(2)}) collective-permute-start(bf16[4,256,128]{2,1,0:T(8,128)(2,1)S(1)} %get-tuple-element.43.refs_0_), channel_id=1, source_target_pairs={{0,96},{1,97},{2,98},{3,99},{4,100},{5,101},{6,102},{7,103},{8,104... | collective-permute-start | bytes 786440 | tf_op jit(solution)/shard_map/ppermute | solution.py:39
  72.4 2.8 %collective-permute-start.20 = (bf16[4,256,128]{2,1,0:T(8,128)(2,1)S(1)}, bf16[4,256,128]{2,1,0:T(8,128)(2,1)S(1)}, u32[]{:S(2)}, u32[]{:S(2)}) collective-permute-start(bf16[4,256,128]{2,1,0:T(8,128)(2,1)S(1)} %get-tuple-element.43.refs_0_), channel_id=1, source_target_pairs={{0,64},{1,65},{2,66},{3,67},{4,68},{5,69},{6,70},{7,71},{8,72},{9,... | collective-permute-start | bytes 786440 | tf_op jit(solution)/shard_map/ppermute | solution.py:39
  75.2 1.4 %shard_map.97 = (f32[4,256,128]{2,1,0:T(8,128)S(1)}, f32[32,8,128]{2,1,0:T(8,128)}) custom-call(s32[1]{0:T(128)} %constant.166.clone.1.t_ref, bf16[4,256,128]{2,1,0:T(8,128)(2,1)S(1)} %shard_map.96.w, bf16[4,256,128]{2,1,0:T(8,128)(2,1)S(1)} %collective-permute-done.16.x1, bf16[4,256,128]{2,1,0:T(8,128)(2,1)S(1)} %collective-permute-done.17.x2, ...), custom_call_target="tpu_custom_call" | custom-call | flops 786432 | bytes 1572864 | tf_op jit(solution)/shard_map/pallas_call | solution.py:61
  76.6 6.4 %all-to-all-start = ((f32[32,8,128]{2,1,0:T(8,128)}), f32[32,8,128]{2,1,0:T(8,128)S(1)}, u32[]{:S(2)}, u32[]{:S(2)}) async-start(f32[32,8,128]{2,1,0:T(8,128)} %get-tuple-element.44), calls=%async_computation | async-start | bytes 262144 | tf_op jit(solution)/shard_map/all_to_all | solution.py:401
  83.1 4.7 %collective-permute-done.21.refs_3_ = bf16[4,256,128]{2,1,0:T(8,128)(2,1)S(1)} collective-permute-done((bf16[4,256,128]{2,1,0:T(8,128)(2,1)S(1)}, bf16[4,256,128]{2,1,0:T(8,128)(2,1)S(1)}, u32[]{:S(2)}, u32[]{:S(2)}) %collective-permute-start.21) | collective-permute-done | bytes 262176 | tf_op jit(solution)/shard_map/ppermute | solution.py:39
  87.7 2.9 %all-to-all-done.refs_4_ = f32[32,8,128]{2,1,0:T(8,128)S(1)} async-done(((f32[32,8,128]{2,1,0:T(8,128)}), f32[32,8,128]{2,1,0:T(8,128)S(1)}, u32[]{:S(2)}, u32[]{:S(2)}) %all-to-all-start) | async-done | bytes 131104 | tf_op jit(solution)/shard_map/all_to_all | solution.py:401
  90.6 1.8 %shard_map.98 = (bf16[4,256,128]{2,1,0:T(8,128)(2,1)S(1)}, f32[8,128]{1,0:T(8,128)S(1)}) custom-call(s32[1]{0:T(128)} %constant.166.clone.1.t_ref, f32[4,256,128]{2,1,0:T(8,128)S(1)} %get-tuple-element.42.g, bf16[4,256,128]{2,1,0:T(8,128)(2,1)S(1)} %get-tuple-element.43.refs_0_, bf16[4,256,128]{2,1,0:T(8,128)(2,1)S(1)} %collective-permute-done.19.refs_1_, ...), custom_call_target="tpu_custom_call" | custom-call | flops 2621440 | bytes 1835008 | tf_op jit(solution)/shard_map/pallas_call | solution.py:61
  93.5 1.2 collective-permute-start.22
  94.7 3.3 %collective-permute-done.27.b = bf16[4,256,128]{2,1,0:T(8,128)(2,1)S(1)} collective-permute-done((bf16[4,256,128]{2,1,0:T(8,128)(2,1)S(1)}, bf16[4,256,128]{2,1,0:T(8,128)(2,1)S(1)}, u32[]{:S(2)}, u32[]{:S(2)}) %collective-permute-start.27) | collective-permute-done | bytes 262176 | tf_op jit(solution)/shard_map/ppermute | solution.py:39
  98.0 1.3 collective-permute-start.37
  100.6 2.8 %collective-permute-done.23.b = bf16[4,256,128]{2,1,0:T(8,128)(2,1)S(1)} collective-permute-done((bf16[4,256,128]{2,1,0:T(8,128)(2,1)S(1)}, bf16[4,256,128]{2,1,0:T(8,128)(2,1)S(1)}, u32[]{:S(2)}, u32[]{:S(2)}) %collective-permute-start.23) | collective-permute-done | bytes 262176 | tf_op jit(solution)/shard_map/ppermute | solution.py:39
  103.4 2.5 %collective-permute-start.38 = (bf16[8,256,128]{2,1,0:T(8,128)(2,1)S(1)}, bf16[8,256,128]{2,1,0:T(8,128)(2,1)S(1)}, u32[]{:S(2)}, u32[]{:S(2)}) collective-permute-start(bf16[8,256,128]{2,1,0:T(8,128)(2,1)S(1)} %shard_map.99.refs_1_), channel_id=1, source_target_pairs={{0,1},{1,0},{2,3},{3,2},{4,5},{5,4},{6,7},{7,6},{8,9},{9,8},{10,11... | collective-permute-start | bytes 1572872 | tf_op jit(solution)/shard_map/ppermute | solution.py:39
  105.8 3.0 %collective-permute-start.29 = (bf16[8,256,128]{2,1,0:T(8,128)(2,1)S(1)}, bf16[8,256,128]{2,1,0:T(8,128)(2,1)S(1)}, u32[]{:S(2)}, u32[]{:S(2)}) collective-permute-start(bf16[8,256,128]{2,1,0:T(8,128)(2,1)S(1)} %shard_map.100.refs_0_), channel_id=1, source_target_pairs={{0,6},{1,25},{2,0},{3,27},{4,2},{5,29},{6,4},{7,31},{8,14},{9,1},{... | collective-permute-start | bytes 1572872 | tf_op jit(solution)/shard_map/ppermute | solution.py:39
  109.7 1.6 %collective-permute-start.32 = (bf16[8,256,128]{2,1,0:T(8,128)(2,1)S(1)}, bf16[8,256,128]{2,1,0:T(8,128)(2,1)S(1)}, u32[]{:S(2)}, u32[]{:S(2)}) collective-permute-start(bf16[8,256,128]{2,1,0:T(8,128)(2,1)S(1)} %collective-permute-done.28.refs_0_), channel_id=1, source_target_pairs={{0,1},{1,0},{2,3},{3,2},{4,5},{5,4},{6,7},{7,6},{8,9},{9,8},{10,11... | collective-permute-start | bytes 1572872 | tf_op jit(solution)/shard_map/ppermute | solution.py:39
  111.3 2.9 %collective-permute-done.24.refs_3_ = bf16[8,256,128]{2,1,0:T(8,128)(2,1)S(1)} collective-permute-done((bf16[8,256,128]{2,1,0:T(8,128)(2,1)S(1)}, bf16[8,256,128]{2,1,0:T(8,128)(2,1)S(1)}, u32[]{:S(2)}, u32[]{:S(2)}) %collective-permute-start.24) | collective-permute-done | bytes 524320 | tf_op jit(solution)/shard_map/ppermute | solution.py:39
  114.1 1.2 collective-permute-start.25
  115.9 3.9 %collective-permute-done.29.refs_1_ = bf16[8,256,128]{2,1,0:T(8,128)(2,1)S(1)} collective-permute-done((bf16[8,256,128]{2,1,0:T(8,128)(2,1)S(1)}, bf16[8,256,128]{2,1,0:T(8,128)(2,1)S(1)}, u32[]{:S(2)}, u32[]{:S(2)}) %collective-permute-start.29) | collective-permute-done | bytes 524320 | tf_op jit(solution)/shard_map/ppermute | solution.py:39
  120.7 3.0 %collective-permute-done.31.refs_4_ = bf16[8,256,128]{2,1,0:T(8,128)(2,1)S(1)} collective-permute-done((bf16[8,256,128]{2,1,0:T(8,128)(2,1)S(1)}, bf16[8,256,128]{2,1,0:T(8,128)(2,1)S(1)}, u32[]{:S(2)}, u32[]{:S(2)}) %collective-permute-start.31) | collective-permute-done | bytes 524320 | tf_op jit(solution)/shard_map/ppermute | solution.py:39
  124.2 1.1 collective-permute-done.25.refs_0_
  126.3 1.5 %fusion.1 = (f32[32768]{0:T(1024)}, f32[32768]{0:T(1024)}, f32[32768]{0:T(1024)}) fusion(f32[4,256,128]{2,1,0:T(8,128)S(1)} %get-tuple-element.42.g, f32[]{:T(128)} %bitcast.5, f32[256,128]{1,0:T(8,128)S(1)} %get-tuple-element.46, f32[256,128]{1,0:T(8,128)S(1)} %get-tuple-element.28, f32[32768]{0:T(1024)S(1)} %copy-done.2), kind=kLoop, calls=%fused_computation.6 | loop fusion | flops 491520 | bytes 917508 | tf_op jit(solution)/shard_map/reshape | solution.py:404
  127.8 2.1 %shard_map.101.refs_10_ = bf16[128,256,128]{2,1,0:T(8,128)(2,1)} custom-call(s32[128]{0:T(128)S(1)} %compare_select_fusion.16.t_ref, bf16[8,256,128]{2,1,0:T(8,128)(2,1)S(1)} %shard_map.100.refs_0_, bf16[8,256,128]{2,1,0:T(8,128)(2,1)S(1)} %shard_map.99.refs_1_, bf16[8,256,128]{2,1,0:T(8,128)(2,1)S(1)} %collective-permute-done.37.refs_2_, ...), custom_call_target="tpu_custom_call" | custom-call | flops 4194304 | bytes 4194304 | tf_op jit(solution)/shard_map/pallas_call | solution.py:61
  130.0 3.5 %shard_map.102.refs_2_ = bf16[128,256,128]{2,1,0:T(8,128)(2,1)} custom-call(s32[128]{0:T(128)S(1)} %compare_select_fusion.16.t_ref, bf16[8,256,128]{2,1,0:T(8,128)(2,1)S(1)} %collective-permute-done.28.refs_0_, bf16[8,256,128]{2,1,0:T(8,128)(2,1)S(1)} %collective-permute-done.29.refs_1_, ...), custom_call_target="tpu_custom_call", output_to_operand_aliasing={{}: (11, {})} | custom-call | flops 10485760 | bytes 10485760 | tf_op jit(solution)/shard_map/pallas_call | solution.py:61
  133.5 1.6 %shard_map.103 = bf16[128,256,128]{2,1,0:T(8,128)(2,1)} custom-call(s32[128]{0:T(128)S(1)} %compare_select_fusion.16.t_ref, bf16[8,256,128]{2,1,0:T(8,128)(2,1)S(1)} %collective-permute-done.25.refs_0_, bf16[8,256,128]{2,1,0:T(8,128)(2,1)S(1)} %collective-permute-done.26.refs_1_, ...), custom_call_target="tpu_custom_call", output_to_operand_aliasing={{}: (3, {})} | custom-call | flops 2097152 | bytes 2097152 | tf_op jit(solution)/shard_map/pallas_call | solution.py:61
  (64 shorter events, 11.0 us)
Async XLA Ops:
  3.0 12.1 %collective-permute-start.5 = (bf16[16,256,128]{2,1,0:T(8,128)(2,1)S(1)}, bf16[16,256,128]{2,1,0:T(8,128)(2,1)S(1)}, u32[]{:S(2)}, u32[]{:S(2)}) collective-permute-start(bf16[16,256,128]{2,1,0:T(8,128)(2,1)S(1)} %shard_map.89), channel_id=1, source_target_pairs={{0,1},{1,0},{2,3},{3,2},{4,5},{5,4},{6,7},{7,6},{8,9},{9,8},{10,11... | collective-permute-start | bytes 3145736 | tf_op jit(solution)/shard_map/ppermute | solution.py:39
  8.3 11.3 %collective-permute-start.9 = (bf16[16,256,128]{2,1,0:T(8,128)(2,1)S(1)}, bf16[16,256,128]{2,1,0:T(8,128)(2,1)S(1)}, u32[]{:S(2)}, u32[]{:S(2)}) collective-permute-start(bf16[16,256,128]{2,1,0:T(8,128)(2,1)S(1)} %get-tuple-element.36), channel_id=1, source_target_pairs={{0,1},{1,0},{2,3},{3,2},{4,5},{5,4},{6,7},{7,6},{8,9},{9,8},{10,11... | collective-permute-start | bytes 3145736 | tf_op jit(solution)/shard_map/ppermute | solution.py:39
  11.5 9.8 %collective-permute-start.4 = (bf16[16,256,128]{2,1,0:T(8,128)(2,1)S(1)}, bf16[16,256,128]{2,1,0:T(8,128)(2,1)S(1)}, u32[]{:S(2)}, u32[]{:S(2)}) collective-permute-start(bf16[16,256,128]{2,1,0:T(8,128)(2,1)S(1)} %get-tuple-element.32), channel_id=1, source_target_pairs={{0,1},{1,0},{2,3},{3,2},{4,5},{5,4},{6,7},{7,6},{8,9},{9,8},{10,11... | collective-permute-start | bytes 3145736 | tf_op jit(solution)/shard_map/ppermute | solution.py:39
  15.4 9.0 %collective-permute-start.11 = (bf16[8,256,128]{2,1,0:T(8,128)(2,1)S(1)}, bf16[8,256,128]{2,1,0:T(8,128)(2,1)S(1)}, u32[]{:S(2)}, u32[]{:S(2)}) collective-permute-start(bf16[8,256,128]{2,1,0:T(8,128)(2,1)S(1)} %get-tuple-element.37), channel_id=1, source_target_pairs={{0,6},{1,25},{2,0},{3,27},{4,2},{5,29},{6,4},{7,31},{8,14},{9,1},{... | collective-permute-start | bytes 1572872 | tf_op jit(solution)/shard_map/ppermute | solution.py:39
  18.3 10.1 %collective-permute-start.3 = (bf16[16,256,128]{2,1,0:T(8,128)(2,1)S(1)}, bf16[16,256,128]{2,1,0:T(8,128)(2,1)S(1)}, u32[]{:S(2)}, u32[]{:S(2)}) collective-permute-start(bf16[16,256,128]{2,1,0:T(8,128)(2,1)S(1)} %get-tuple-element.30), channel_id=1, source_target_pairs={{0,1},{1,0},{2,3},{3,2},{4,5},{5,4},{6,7},{7,6},{8,9},{9,8},{10,11... | collective-permute-start | bytes 3145736 | tf_op jit(solution)/shard_map/ppermute | solution.py:39
  18.3 9.8 %collective-permute-start.6 = (bf16[8,256,128]{2,1,0:T(8,128)(2,1)S(1)}, bf16[8,256,128]{2,1,0:T(8,128)(2,1)S(1)}, u32[]{:S(2)}, u32[]{:S(2)}) collective-permute-start(bf16[8,256,128]{2,1,0:T(8,128)(2,1)S(1)} %get-tuple-element.34), channel_id=1, source_target_pairs={{0,2},{1,9},{2,4},{3,11},{4,6},{5,13},{6,0},{7,15},{8,10},{9,17},{... | collective-permute-start | bytes 1572872 | tf_op jit(solution)/shard_map/ppermute | solution.py:39
  19.8 10.3 %collective-permute-start.10 = (bf16[8,256,128]{2,1,0:T(8,128)(2,1)S(1)}, bf16[8,256,128]{2,1,0:T(8,128)(2,1)S(1)}, u32[]{:S(2)}, u32[]{:S(2)}) collective-permute-start(bf16[8,256,128]{2,1,0:T(8,128)(2,1)S(1)} %shard_map.93), channel_id=1, source_target_pairs={{0,6},{1,25},{2,0},{3,27},{4,2},{5,29},{6,4},{7,31},{8,14},{9,1},{... | collective-permute-start | bytes 1572872 | tf_op jit(solution)/shard_map/ppermute | solution.py:39
  21.4 30.4 %copy-start.3 = (s32[129]{0:T(256)S(1)}, s32[129]{0:T(256)}, u32[]{:S(2)}) copy-start(s32[129]{0:T(256)} %param.9) | copy-start | bytes 1552
  21.4 30.5 %copy-start = (f32[1,65536]{1,0:T(1,128)S(1)}, f32[1,65536]{1,0:T(1,128)}, u32[]{:S(2)}) copy-start(f32[1,65536]{1,0:T(1,128)} %param.7) | copy-start | bytes 786436
  21.4 30.5 %copy-start.1 = (f32[1,65536]{1,0:T(1,128)S(1)}, f32[1,65536]{1,0:T(1,128)}, u32[]{:S(2)}) copy-start(f32[1,65536]{1,0:T(1,128)} %param.8) | copy-start | bytes 786436
  21.4 45.6 %copy-start.2 = (f32[32768]{0:T(1024)S(1)}, f32[32768]{0:T(1024)}, u32[]{:S(2)}) copy-start(f32[32768]{0:T(1024)} %param.6) | copy-start | bytes 393220
  21.5 12.1 %collective-permute-start.8 = (bf16[8,256,128]{2,1,0:T(8,128)(2,1)S(1)}, bf16[8,256,128]{2,1,0:T(8,128)(2,1)S(1)}, u32[]{:S(2)}, u32[]{:S(2)}) collective-permute-start(bf16[8,256,128]{2,1,0:T(8,128)(2,1)S(1)} %shard_map.92), channel_id=1, source_target_pairs={{0,2},{1,9},{2,4},{3,11},{4,6},{5,13},{6,0},{7,15},{8,10},{9,17},{... | collective-permute-start | bytes 1572872 | tf_op jit(solution)/shard_map/ppermute | solution.py:39
  24.6 11.0 %collective-permute-start.12 = (bf16[8,256,128]{2,1,0:T(8,128)(2,1)S(1)}, bf16[8,256,128]{2,1,0:T(8,128)(2,1)S(1)}, u32[]{:S(2)}, u32[]{:S(2)}) collective-permute-start(bf16[8,256,128]{2,1,0:T(8,128)(2,1)S(1)} %shard_map.94), channel_id=1, source_target_pairs={{0,6},{1,25},{2,0},{3,27},{4,2},{5,29},{6,4},{7,31},{8,14},{9,1},{... | collective-permute-start | bytes 1572872 | tf_op jit(solution)/shard_map/ppermute | solution.py:39
  28.3 10.8 %collective-permute-start.7 = (bf16[8,256,128]{2,1,0:T(8,128)(2,1)S(1)}, bf16[8,256,128]{2,1,0:T(8,128)(2,1)S(1)}, u32[]{:S(2)}, u32[]{:S(2)}) collective-permute-start(bf16[8,256,128]{2,1,0:T(8,128)(2,1)S(1)} %shard_map.91), channel_id=1, source_target_pairs={{0,2},{1,9},{2,4},{3,11},{4,6},{5,13},{6,0},{7,15},{8,10},{9,17},{... | collective-permute-start | bytes 1572872 | tf_op jit(solution)/shard_map/ppermute | solution.py:39
  39.8 6.8 %collective-permute-start.13 = (bf16[4,256,128]{2,1,0:T(8,128)(2,1)S(1)}, bf16[4,256,128]{2,1,0:T(8,128)(2,1)S(1)}, u32[]{:S(2)}, u32[]{:S(2)}) collective-permute-start(bf16[4,256,128]{2,1,0:T(8,128)(2,1)S(1)} %get-tuple-element.39), channel_id=1, source_target_pairs={{0,8},{1,3},{2,10},{3,5},{4,12},{5,7},{6,14},{7,1},{8,16},{9,11},{... | collective-permute-start | bytes 786440 | tf_op jit(solution)/shard_map/ppermute | solution.py:39
  40.7 9.3 %collective-permute-start.14 = (bf16[4,256,128]{2,1,0:T(8,128)(2,1)S(1)}, bf16[4,256,128]{2,1,0:T(8,128)(2,1)S(1)}, u32[]{:S(2)}, u32[]{:S(2)}) collective-permute-start(bf16[4,256,128]{2,1,0:T(8,128)(2,1)S(1)} %get-tuple-element.40), channel_id=1, source_target_pairs={{0,16},{1,5},{2,18},{3,7},{4,20},{5,1},{6,22},{7,3},{8,24},{9,13},... | collective-permute-start | bytes 786440 | tf_op jit(solution)/shard_map/ppermute | solution.py:39
  43.1 6.9 %collective-permute-start.15 = (bf16[4,256,128]{2,1,0:T(8,128)(2,1)S(1)}, bf16[4,256,128]{2,1,0:T(8,128)(2,1)S(1)}, u32[]{:S(2)}, u32[]{:S(2)}) collective-permute-start(bf16[4,256,128]{2,1,0:T(8,128)(2,1)S(1)} %get-tuple-element.41), channel_id=1, source_target_pairs={{0,24},{1,7},{2,26},{3,1},{4,28},{5,3},{6,30},{7,5},{8,0},{9,15},{... | collective-permute-start | bytes 786440 | tf_op jit(solution)/shard_map/ppermute | solution.py:39
  50.1 25.1 %collective-permute-start.16 = (bf16[4,256,128]{2,1,0:T(8,128)(2,1)S(1)}, bf16[4,256,128]{2,1,0:T(8,128)(2,1)S(1)}, u32[]{:S(2)}, u32[]{:S(2)}) collective-permute-start(bf16[4,256,128]{2,1,0:T(8,128)(2,1)S(1)} %shard_map.96.w), channel_id=1, source_target_pairs={{0,32},{1,33},{2,34},{3,35},{4,36},{5,37},{6,38},{7,39},{8,40},{9,... | collective-permute-start | bytes 786440 | tf_op jit(solution)/shard_map/ppermute | solution.py:39
  52.5 9.3 %collective-permute-start.1 = (bf16[2,128,128]{2,1,0:T(8,128)(2,1)S(1)}, bf16[2,128,128]{2,1,0:T(8,128)(2,1)S(1)}, u32[]{:S(2)}, u32[]{:S(2)}) collective-permute-start(bf16[2,128,128]{2,1,0:T(8,128)(2,1)S(1)} %get-tuple-element.27), channel_id=1, source_target_pairs={{0,1},{1,0},{2,3},{3,2},{4,5},{5,4},{6,7},{7,6},{8,9},{9,8},{10,11... | collective-permute-start | bytes 196616 | tf_op jit(solution)/shard_map/ppermute | solution.py:39
  55.2 20.0 %collective-permute-start.17 = (bf16[4,256,128]{2,1,0:T(8,128)(2,1)S(1)}, bf16[4,256,128]{2,1,0:T(8,128)(2,1)S(1)}, u32[]{:S(2)}, u32[]{:S(2)}) collective-permute-start(bf16[4,256,128]{2,1,0:T(8,128)(2,1)S(1)} %shard_map.96.w), channel_id=1, source_target_pairs={{0,64},{1,65},{2,66},{3,67},{4,68},{5,69},{6,70},{7,71},{8,72},{9,... | collective-permute-start | bytes 786440 | tf_op jit(solution)/shard_map/ppermute | solution.py:39
  58.5 16.7 %collective-permute-start.18 = (bf16[4,256,128]{2,1,0:T(8,128)(2,1)S(1)}, bf16[4,256,128]{2,1,0:T(8,128)(2,1)S(1)}, u32[]{:S(2)}, u32[]{:S(2)}) collective-permute-start(bf16[4,256,128]{2,1,0:T(8,128)(2,1)S(1)} %shard_map.96.w), channel_id=1, source_target_pairs={{0,96},{1,97},{2,98},{3,99},{4,100},{5,101},{6,102},{7,103},{8,104... | collective-permute-start | bytes 786440 | tf_op jit(solution)/shard_map/ppermute | solution.py:39
  59.3 3.8 %collective-permute-start = (bf16[2,136,128]{2,1,0:T(8,128)(2,1)S(1)}, bf16[2,136,128]{2,1,0:T(8,128)(2,1)S(1)}, u32[]{:S(2)}, u32[]{:S(2)}) collective-permute-start(bf16[2,136,128]{2,1,0:T(8,128)(2,1)S(1)} %get-tuple-element.26), channel_id=1, source_target_pairs={{0,1},{1,2},{2,3},{3,4},{4,5},{5,6},{6,7},{7,8},{8,9},{9,10},{10,1... | collective-permute-start | bytes 208904 | tf_op jit(solution)/shard_map/ppermute | solution.py:377
  61.7 5.3 %collective-permute-start.2 = (bf16[2,128,128]{2,1,0:T(8,128)(2,1)S(1)}, bf16[2,128,128]{2,1,0:T(8,128)(2,1)S(1)}, u32[]{:S(2)}, u32[]{:S(2)}) collective-permute-start(bf16[2,128,128]{2,1,0:T(8,128)(2,1)S(1)} %collective-permute-done.1.a), channel_id=1, source_target_pairs={{3,1},{5,3},{7,5},{9,7},{11,9},{13,11},{15,13},{17,15},{19,17},{21... | collective-permute-start | bytes 196616 | tf_op jit(solution)/shard_map/ppermute | solution.py:379
  69.1 14.0 %collective-permute-start.19 = (bf16[4,256,128]{2,1,0:T(8,128)(2,1)S(1)}, bf16[4,256,128]{2,1,0:T(8,128)(2,1)S(1)}, u32[]{:S(2)}, u32[]{:S(2)}) collective-permute-start(bf16[4,256,128]{2,1,0:T(8,128)(2,1)S(1)} %get-tuple-element.43.refs_0_), channel_id=1, source_target_pairs={{0,96},{1,97},{2,98},{3,99},{4,100},{5,101},{6,102},{7,103},{8,104... | collective-permute-start | bytes 786440 | tf_op jit(solution)/shard_map/ppermute | solution.py:39
  72.4 10.6 %collective-permute-start.20 = (bf16[4,256,128]{2,1,0:T(8,128)(2,1)S(1)}, bf16[4,256,128]{2,1,0:T(8,128)(2,1)S(1)}, u32[]{:S(2)}, u32[]{:S(2)}) collective-permute-start(bf16[4,256,128]{2,1,0:T(8,128)(2,1)S(1)} %get-tuple-element.43.refs_0_), channel_id=1, source_target_pairs={{0,64},{1,65},{2,66},{3,67},{4,68},{5,69},{6,70},{7,71},{8,72},{9,... | collective-permute-start | bytes 786440 | tf_op jit(solution)/shard_map/ppermute | solution.py:39
  75.2 12.5 %collective-permute-start.21 = (bf16[4,256,128]{2,1,0:T(8,128)(2,1)S(1)}, bf16[4,256,128]{2,1,0:T(8,128)(2,1)S(1)}, u32[]{:S(2)}, u32[]{:S(2)}) collective-permute-start(bf16[4,256,128]{2,1,0:T(8,128)(2,1)S(1)} %get-tuple-element.43.refs_0_), channel_id=1, source_target_pairs={{0,32},{1,33},{2,34},{3,35},{4,36},{5,37},{6,38},{7,39},{8,40},{9,... | collective-permute-start | bytes 786440 | tf_op jit(solution)/shard_map/ppermute | solution.py:39
  76.6 14.0 %all-to-all-start = ((f32[32,8,128]{2,1,0:T(8,128)}), f32[32,8,128]{2,1,0:T(8,128)S(1)}, u32[]{:S(2)}, u32[]{:S(2)}) async-start(f32[32,8,128]{2,1,0:T(8,128)} %get-tuple-element.44), calls=%async_computation | async-start | bytes 262144 | tf_op jit(solution)/shard_map/all_to_all | solution.py:401
  92.4 5.6 %collective-permute-start.27 = (bf16[4,256,128]{2,1,0:T(8,128)(2,1)S(1)}, bf16[4,256,128]{2,1,0:T(8,128)(2,1)S(1)}, u32[]{:S(2)}, u32[]{:S(2)}) collective-permute-start(bf16[4,256,128]{2,1,0:T(8,128)(2,1)S(1)} %get-tuple-element.47.a), channel_id=1, source_target_pairs={{0,24},{1,7},{2,26},{3,1},{4,28},{5,3},{6,30},{7,5},{8,0},{9,15},{... | collective-permute-start | bytes 786440 | tf_op jit(solution)/shard_map/ppermute | solution.py:39
  93.5 7.1 %collective-permute-start.22 = (bf16[4,256,128]{2,1,0:T(8,128)(2,1)S(1)}, bf16[4,256,128]{2,1,0:T(8,128)(2,1)S(1)}, u32[]{:S(2)}, u32[]{:S(2)}) collective-permute-start(bf16[4,256,128]{2,1,0:T(8,128)(2,1)S(1)} %get-tuple-element.47.a), channel_id=1, source_target_pairs={{0,16},{1,5},{2,18},{3,7},{4,20},{5,1},{6,22},{7,3},{8,24},{9,13},... | collective-permute-start | bytes 786440 | tf_op jit(solution)/shard_map/ppermute | solution.py:39
  94.7 8.7 %collective-permute-start.23 = (bf16[4,256,128]{2,1,0:T(8,128)(2,1)S(1)}, bf16[4,256,128]{2,1,0:T(8,128)(2,1)S(1)}, u32[]{:S(2)}, u32[]{:S(2)}) collective-permute-start(bf16[4,256,128]{2,1,0:T(8,128)(2,1)S(1)} %get-tuple-element.47.a), channel_id=1, source_target_pairs={{0,8},{1,3},{2,10},{3,5},{4,12},{5,7},{6,14},{7,1},{8,16},{9,11},{... | collective-permute-start | bytes 786440 | tf_op jit(solution)/shard_map/ppermute | solution.py:39
  98.0 10.8 %collective-permute-start.37 = (bf16[8,256,128]{2,1,0:T(8,128)(2,1)S(1)}, bf16[8,256,128]{2,1,0:T(8,128)(2,1)S(1)}, u32[]{:S(2)}, u32[]{:S(2)}) collective-permute-start(bf16[8,256,128]{2,1,0:T(8,128)(2,1)S(1)} %shard_map.100.refs_0_), channel_id=1, source_target_pairs={{0,1},{1,0},{2,3},{3,2},{4,5},{5,4},{6,7},{7,6},{8,9},{9,8},{10,11... | collective-permute-start | bytes 1572872 | tf_op jit(solution)/shard_map/ppermute | solution.py:39
  99.4 10.2 %collective-permute-start.28 = (bf16[8,256,128]{2,1,0:T(8,128)(2,1)S(1)}, bf16[8,256,128]{2,1,0:T(8,128)(2,1)S(1)}, u32[]{:S(2)}, u32[]{:S(2)}) collective-permute-start(bf16[8,256,128]{2,1,0:T(8,128)(2,1)S(1)} %shard_map.100.refs_0_), channel_id=1, source_target_pairs={{0,2},{1,9},{2,4},{3,11},{4,6},{5,13},{6,0},{7,15},{8,10},{9,17},{... | collective-permute-start | bytes 1572872 | tf_op jit(solution)/shard_map/ppermute | solution.py:39
  103.4 6.4 %collective-permute-start.38 = (bf16[8,256,128]{2,1,0:T(8,128)(2,1)S(1)}, bf16[8,256,128]{2,1,0:T(8,128)(2,1)S(1)}, u32[]{:S(2)}, u32[]{:S(2)}) collective-permute-start(bf16[8,256,128]{2,1,0:T(8,128)(2,1)S(1)} %shard_map.99.refs_1_), channel_id=1, source_target_pairs={{0,1},{1,0},{2,3},{3,2},{4,5},{5,4},{6,7},{7,6},{8,9},{9,8},{10,11... | collective-permute-start | bytes 1572872 | tf_op jit(solution)/shard_map/ppermute | solution.py:39
  105.8 8.3 %collective-permute-start.24 = (bf16[8,256,128]{2,1,0:T(8,128)(2,1)S(1)}, bf16[8,256,128]{2,1,0:T(8,128)(2,1)S(1)}, u32[]{:S(2)}, u32[]{:S(2)}) collective-permute-start(bf16[8,256,128]{2,1,0:T(8,128)(2,1)S(1)} %shard_map.99.refs_1_), channel_id=1, source_target_pairs={{0,6},{1,25},{2,0},{3,27},{4,2},{5,29},{6,4},{7,31},{8,14},{9,1},{... | collective-permute-start | bytes 1572872 | tf_op jit(solution)/shard_map/ppermute | solution.py:39
  105.8 13.9 %collective-permute-start.29 = (bf16[8,256,128]{2,1,0:T(8,128)(2,1)S(1)}, bf16[8,256,128]{2,1,0:T(8,128)(2,1)S(1)}, u32[]{:S(2)}, u32[]{:S(2)}) collective-permute-start(bf16[8,256,128]{2,1,0:T(8,128)(2,1)S(1)} %shard_map.100.refs_0_), channel_id=1, source_target_pairs={{0,6},{1,25},{2,0},{3,27},{4,2},{5,29},{6,4},{7,31},{8,14},{9,1},{... | collective-permute-start | bytes 1572872 | tf_op jit(solution)/shard_map/ppermute | solution.py:39
  108.9 11.8 %collective-permute-start.30 = (bf16[8,256,128]{2,1,0:T(8,128)(2,1)S(1)}, bf16[8,256,128]{2,1,0:T(8,128)(2,1)S(1)}, u32[]{:S(2)}, u32[]{:S(2)}) collective-permute-start(bf16[8,256,128]{2,1,0:T(8,128)(2,1)S(1)} %shard_map.99.refs_1_), channel_id=1, source_target_pairs={{0,2},{1,9},{2,4},{3,11},{4,6},{5,13},{6,0},{7,15},{8,10},{9,17},{... | collective-permute-start | bytes 1572872 | tf_op jit(solution)/shard_map/ppermute | solution.py:39
  109.6 14.1 %collective-permute-start.31 = (bf16[8,256,128]{2,1,0:T(8,128)(2,1)S(1)}, bf16[8,256,128]{2,1,0:T(8,128)(2,1)S(1)}, u32[]{:S(2)}, u32[]{:S(2)}) collective-permute-start(bf16[8,256,128]{2,1,0:T(8,128)(2,1)S(1)} %collective-permute-done.28.refs_0_), channel_id=1, source_target_pairs={{0,2},{1,9},{2,4},{3,11},{4,6},{5,13},{6,0},{7,15},{8,10},{9,17},{... | collective-permute-start | bytes 1572872 | tf_op jit(solution)/shard_map/ppermute | solution.py:39
  109.7 14.0 %collective-permute-start.32 = (bf16[8,256,128]{2,1,0:T(8,128)(2,1)S(1)}, bf16[8,256,128]{2,1,0:T(8,128)(2,1)S(1)}, u32[]{:S(2)}, u32[]{:S(2)}) collective-permute-start(bf16[8,256,128]{2,1,0:T(8,128)(2,1)S(1)} %collective-permute-done.28.refs_0_), channel_id=1, source_target_pairs={{0,1},{1,0},{2,3},{3,2},{4,5},{5,4},{6,7},{7,6},{8,9},{9,8},{10,11... | collective-permute-start | bytes 1572872 | tf_op jit(solution)/shard_map/ppermute | solution.py:39
  114.1 11.2 %collective-permute-start.25 = (bf16[8,256,128]{2,1,0:T(8,128)(2,1)S(1)}, bf16[8,256,128]{2,1,0:T(8,128)(2,1)S(1)}, u32[]{:S(2)}, u32[]{:S(2)}) collective-permute-start(bf16[8,256,128]{2,1,0:T(8,128)(2,1)S(1)} %collective-permute-done.24.refs_3_), channel_id=1, source_target_pairs={{0,6},{1,25},{2,0},{3,27},{4,2},{5,29},{6,4},{7,31},{8,14},{9,1},{... | collective-permute-start | bytes 1572872 | tf_op jit(solution)/shard_map/ppermute | solution.py:39
  119.8 10.2 %collective-permute-start.35 = (bf16[8,256,128]{2,1,0:T(8,128)(2,1)S(1)}, bf16[8,256,128]{2,1,0:T(8,128)(2,1)S(1)}, u32[]{:S(2)}, u32[]{:S(2)}) collective-permute-start(bf16[8,256,128]{2,1,0:T(8,128)(2,1)S(1)} %collective-permute-done.24.refs_3_), channel_id=1, source_target_pairs={{0,1},{1,0},{2,3},{3,2},{4,5},{5,4},{6,7},{7,6},{8,9},{9,8},{10,11... | collective-permute-start | bytes 1572872 | tf_op jit(solution)/shard_map/ppermute | solution.py:39
  120.7 9.2 %collective-permute-start.33 = (bf16[8,256,128]{2,1,0:T(8,128)(2,1)S(1)}, bf16[8,256,128]{2,1,0:T(8,128)(2,1)S(1)}, u32[]{:S(2)}, u32[]{:S(2)}) collective-permute-start(bf16[8,256,128]{2,1,0:T(8,128)(2,1)S(1)} %collective-permute-done.29.refs_1_), channel_id=1, source_target_pairs={{0,1},{1,0},{2,3},{3,2},{4,5},{5,4},{6,7},{7,6},{8,9},{9,8},{10,11... | collective-permute-start | bytes 1572872 | tf_op jit(solution)/shard_map/ppermute | solution.py:39
  123.7 6.2 %collective-permute-start.34 = (bf16[8,256,128]{2,1,0:T(8,128)(2,1)S(1)}, bf16[8,256,128]{2,1,0:T(8,128)(2,1)S(1)}, u32[]{:S(2)}, u32[]{:S(2)}) collective-permute-start(bf16[8,256,128]{2,1,0:T(8,128)(2,1)S(1)} %collective-permute-done.30.refs_2_), channel_id=1, source_target_pairs={{0,1},{1,0},{2,3},{3,2},{4,5},{5,4},{6,7},{7,6},{8,9},{9,8},{10,11... | collective-permute-start | bytes 1572872 | tf_op jit(solution)/shard_map/ppermute | solution.py:39
  123.7 6.2 %collective-permute-start.36 = (bf16[8,256,128]{2,1,0:T(8,128)(2,1)S(1)}, bf16[8,256,128]{2,1,0:T(8,128)(2,1)S(1)}, u32[]{:S(2)}, u32[]{:S(2)}) collective-permute-start(bf16[8,256,128]{2,1,0:T(8,128)(2,1)S(1)} %collective-permute-done.31.refs_4_), channel_id=1, source_target_pairs={{0,1},{1,0},{2,3},{3,2},{4,5},{5,4},{6,7},{7,6},{8,9},{9,8},{10,11... | collective-permute-start | bytes 1572872 | tf_op jit(solution)/shard_map/ppermute | solution.py:39
  125.4 8.1 %collective-permute-start.26 = (bf16[8,256,128]{2,1,0:T(8,128)(2,1)S(1)}, bf16[8,256,128]{2,1,0:T(8,128)(2,1)S(1)}, u32[]{:S(2)}, u32[]{:S(2)}) collective-permute-start(bf16[8,256,128]{2,1,0:T(8,128)(2,1)S(1)} %collective-permute-done.25.refs_0_), channel_id=1, source_target_pairs={{0,1},{1,0},{2,3},{3,2},{4,5},{5,4},{6,7},{7,6},{8,9},{9,8},{10,11... | collective-permute-start | bytes 1572872 | tf_op jit(solution)/shard_map/ppermute | solution.py:39

commit v6 on v5

--- a/solution.py
+++ b/solution.py
@@ -347,14 +347,14 @@
     g = grads[0].reshape(128, rows, 128)
 
     given, kept, swapped = {}, {}, {}
-    (given[2],) = fetch(places, g, (theirs[2], BF))
-    swapped[2] = send(given[2], "core")
-    kept[2], given[1] = fetch(places, g, (mine[2], F32), (theirs[1], BF))
-    swapped[1] = send(given[1], "core")
-    given[3], kept[1], kept[3] = fetch(places, g, (theirs[3], BF), (mine[1], F32), (mine[3], F32))
-    swapped[3] = send(given[3], "core")
-    given[0], kept[0] = fetch(places, g, (theirs[0], BF), (mine[0], F32))
+    given[2], given[1], given[3] = fetch(places, g, *((theirs[k], BF) for k in (2, 1, 3)))
+    for k in (2, 1, 3):
+        swapped[k] = send(given[k], "core")
+    kept[2], kept[1], kept[3], given[0], kept[0] = fetch(
+        places, g, (mine[2], F32), (mine[1], F32), (mine[3], F32), (theirs[0], BF), (mine[0], F32)
+    )
     swapped[0] = send(given[0], "core")
+
     low, high = (0, 8), (8, 8)
 
     def local_sum(s, half, *more):
@@ -418,7 +418,7 @@
     for r, h in halves:
         partner[r, h] = send(halves[r, h], "core")
     out = None
-    for keys in (((0, 0), (0, 1)), ((3, 0), (1, 0), (3, 1), (1, 1), (2, 0)), ((2, 1),)):
+    for keys in (((0, 0), (0, 1)), ((3, 0), (1, 0), (3, 1), (1, 1)), ((2, 0), (2, 1))):
         pairs = [(mine[r] + 8 * h, halves[r, h]) for r, h in keys]
         pairs += [(theirs[r] + 8 * h, partner[r, h]) for r, h in keys]
         out = place(places, pairs, out)

time: 136 us -> 136 us (level)
  Pallas kernels: 26.9 us -> 23.8 us
  starting transfers between devices: 55.5 us -> 58.2 us
    pallas_call x20 -> x18, Pallas kernels: 26.9 us -> 23.8 us  [call(): pl.pallas_call(body, grid_spec=pltpu.PrefetchScalarGridSpec(num_scalar_pr...]
    ppermute x37, starting transfers between devices: 45.3 us -> 48 us  [send(): return lax.ppermute(value, DP, perm(axis, s))]
  transfers between devices with their start and end apart: 40 -> 40, of which waited for: 18 -> 17; matrix products, arithmetic and copies ran while one was open for 2% -> 2% of each run, Pallas kernels for 15% -> 11%
where the time goes in v6:
time: 136 us
  starting transfers between devices  58.2 us (43%)
  waiting for transfers between devices  50.6 us (37%)
  Pallas kernels  23.8 us (18%)
  other arithmetic  1.57 us (1%)
    ppermute x37, starting transfers between devices, send(): return lax.ppermute(value, DP, perm(axis, s))  48 us
    ppermute x37, waiting for transfers between devices, send(): return lax.ppermute(value, DP, perm(axis, s))  43.7 us
    pallas_call x18, Pallas kernels, call(): pl.pallas_call(body, grid_spec=pltpu.PrefetchScalarGridSpec(num_scalar_pr...  23.8 us
    all_to_all x1, starting transfers between devices, step(): squares = lax.all_to_all(squares, ('y', 'x', 'core'), 0, 0, tiled=True)  6.41 us
    ppermute x1, waiting for transfers between devices, step(): passed = lax.ppermute(after, DP, [(d, d - 2) for d in range(3, 128, 2)])  3.97 us
    all_to_all x1, waiting for transfers between devices, step(): squares = lax.all_to_all(squares, ('y', 'x', 'core'), 0, 0, tiled=True)  2.91 us
  transfers between devices with their start and end apart: 40, of which 17 were waited for; matrix products, arithmetic and copies ran while one was open for 2% of the time, Pallas kernels for 11%

profile of v6, /device:TPU:1, one launch (start us, length us, event | category | flops | bytes accessed | tf_op | source)
XLA Modules:
  0.0 135.9 jit_solution(453815126428833222)
XLA Ops:
  0.7 3.8 %shard_map.87 = (bf16[16,256,128]{2,1,0:T(8,128)(2,1)S(1)}, bf16[16,256,128]{2,1,0:T(8,128)(2,1)S(1)}, bf16[16,256,128]{2,1,0:T(8,128)(2,1)S(1)}) custom-call(s32[128]{0:T(128)S(1)} %compare_select_fusion.16.t_ref, f32[128,256,128]{2,1,0:T(8,128)} %bitcast.31), custom_call_target="tpu_custom_call" | custom-call | flops 1572864 | bytes 9437184 | tf_op jit(solution)/shard_map/pallas_call | solution.py:61
  4.6 1.5 %collective-permute-start.5 = (bf16[16,256,128]{2,1,0:T(8,128)(2,1)S(1)}, bf16[16,256,128]{2,1,0:T(8,128)(2,1)S(1)}, u32[]{:S(2)}, u32[]{:S(2)}) collective-permute-start(bf16[16,256,128]{2,1,0:T(8,128)(2,1)S(1)} %get-tuple-element.35), channel_id=1, source_target_pairs={{0,1},{1,0},{2,3},{3,2},{4,5},{5,4},{6,7},{7,6},{8,9},{9,8},{10,11... | collective-permute-start | bytes 3145736 | tf_op jit(solution)/shard_map/ppermute | solution.py:39
  6.5 5.3 %shard_map.86 = (f32[16,256,128]{2,1,0:T(8,128)S(1)}, f32[16,256,128]{2,1,0:T(8,128)S(1)}, f32[16,256,128]{2,1,0:T(8,128)S(1)}, bf16[16,256,128]{2,1,0:T(8,128)(2,1)S(1)}, f32[16,256,128]{2,1,0:T(8,128)S(1)}) custom-call(s32[128]{0:T(128)S(1)} %compare_select_fusion.16.t_ref, f32[128,256,128]{2,1,0:T(8,128)} %bitcast.32), custom_call_target="tpu_custom_call" | custom-call | flops 2621440 | bytes 15728640 | tf_op jit(solution)/shard_map/pallas_call | solution.py:61
  12.1 2.9 %collective-permute-start.11 = (bf16[8,256,128]{2,1,0:T(8,128)(2,1)S(1)}, bf16[8,256,128]{2,1,0:T(8,128)(2,1)S(1)}, u32[]{:S(2)}, u32[]{:S(2)}) collective-permute-start(bf16[8,256,128]{2,1,0:T(8,128)(2,1)S(1)} %get-tuple-element.39), channel_id=1, source_target_pairs={{0,6},{1,25},{2,0},{3,27},{4,2},{5,29},{6,4},{7,31},{8,14},{9,1},{... | collective-permute-start | bytes 1572872 | tf_op jit(solution)/shard_map/ppermute | solution.py:39
  15.2 1.3 collective-permute-start.6
  16.6 1.5 %collective-permute-start.10 = (bf16[8,256,128]{2,1,0:T(8,128)(2,1)S(1)}, bf16[8,256,128]{2,1,0:T(8,128)(2,1)S(1)}, u32[]{:S(2)}, u32[]{:S(2)}) collective-permute-start(bf16[8,256,128]{2,1,0:T(8,128)(2,1)S(1)} %shard_map.91), channel_id=1, source_target_pairs={{0,6},{1,25},{2,0},{3,27},{4,2},{5,29},{6,4},{7,31},{8,14},{9,1},{... | collective-permute-start | bytes 1572872 | tf_op jit(solution)/shard_map/ppermute | solution.py:39
  18.4 2.8 %collective-permute-done.11.refs_2_ = bf16[8,256,128]{2,1,0:T(8,128)(2,1)S(1)} collective-permute-done((bf16[8,256,128]{2,1,0:T(8,128)(2,1)S(1)}, bf16[8,256,128]{2,1,0:T(8,128)(2,1)S(1)}, u32[]{:S(2)}, u32[]{:S(2)}) %collective-permute-start.11) | collective-permute-done | bytes 524320 | tf_op jit(solution)/shard_map/ppermute | solution.py:39
  21.4 3.5 %collective-permute-start.12 = (bf16[8,256,128]{2,1,0:T(8,128)(2,1)S(1)}, bf16[8,256,128]{2,1,0:T(8,128)(2,1)S(1)}, u32[]{:S(2)}, u32[]{:S(2)}) collective-permute-start(bf16[8,256,128]{2,1,0:T(8,128)(2,1)S(1)} %shard_map.92), channel_id=1, source_target_pairs={{0,6},{1,25},{2,0},{3,27},{4,2},{5,29},{6,4},{7,31},{8,14},{9,1},{... | collective-permute-start | bytes 1572872 | tf_op jit(solution)/shard_map/ppermute | solution.py:39
  25.2 1.6 %collective-permute-done.10.refs_4_ = bf16[8,256,128]{2,1,0:T(8,128)(2,1)S(1)} collective-permute-done((bf16[8,256,128]{2,1,0:T(8,128)(2,1)S(1)}, bf16[8,256,128]{2,1,0:T(8,128)(2,1)S(1)}, u32[]{:S(2)}, u32[]{:S(2)}) %collective-permute-start.10) | collective-permute-done | bytes 524320 | tf_op jit(solution)/shard_map/ppermute | solution.py:39
  26.8 3.6 %collective-permute-done.8.refs_3_ = bf16[8,256,128]{2,1,0:T(8,128)(2,1)S(1)} collective-permute-done((bf16[8,256,128]{2,1,0:T(8,128)(2,1)S(1)}, bf16[8,256,128]{2,1,0:T(8,128)(2,1)S(1)}, u32[]{:S(2)}, u32[]{:S(2)}) %collective-permute-start.8) | collective-permute-done | bytes 524320 | tf_op jit(solution)/shard_map/ppermute | solution.py:39
  30.4 2.0 %collective-permute-done.12.refs_5_ = bf16[8,256,128]{2,1,0:T(8,128)(2,1)S(1)} collective-permute-done((bf16[8,256,128]{2,1,0:T(8,128)(2,1)S(1)}, bf16[8,256,128]{2,1,0:T(8,128)(2,1)S(1)}, u32[]{:S(2)}, u32[]{:S(2)}) %collective-permute-start.12) | collective-permute-done | bytes 524320 | tf_op jit(solution)/shard_map/ppermute | solution.py:39
  32.4 3.6 %collective-permute-done.7.refs_2_ = bf16[8,256,128]{2,1,0:T(8,128)(2,1)S(1)} collective-permute-done((bf16[8,256,128]{2,1,0:T(8,128)(2,1)S(1)}, bf16[8,256,128]{2,1,0:T(8,128)(2,1)S(1)}, u32[]{:S(2)}, u32[]{:S(2)}) %collective-permute-start.7) | collective-permute-done | bytes 524320 | tf_op jit(solution)/shard_map/ppermute | solution.py:39
  37.4 2.5 %collective-permute-start.14 = (bf16[4,256,128]{2,1,0:T(8,128)(2,1)S(1)}, bf16[4,256,128]{2,1,0:T(8,128)(2,1)S(1)}, u32[]{:S(2)}, u32[]{:S(2)}) collective-permute-start(bf16[4,256,128]{2,1,0:T(8,128)(2,1)S(1)} %get-tuple-element.42), channel_id=1, source_target_pairs={{0,16},{1,5},{2,18},{3,7},{4,20},{5,1},{6,22},{7,3},{8,24},{9,13},... | collective-permute-start | bytes 786440 | tf_op jit(solution)/shard_map/ppermute | solution.py:39
  39.8 1.2 collective-permute-start.15
  41.0 2.4 %collective-permute-done.13.refs_1_ = bf16[4,256,128]{2,1,0:T(8,128)(2,1)S(1)} collective-permute-done((bf16[4,256,128]{2,1,0:T(8,128)(2,1)S(1)}, bf16[4,256,128]{2,1,0:T(8,128)(2,1)S(1)}, u32[]{:S(2)}, u32[]{:S(2)}) %collective-permute-start.13) | collective-permute-done | bytes 262176 | tf_op jit(solution)/shard_map/ppermute | solution.py:39
  43.4 3.3 %collective-permute-done.14.refs_2_ = bf16[4,256,128]{2,1,0:T(8,128)(2,1)S(1)} collective-permute-done((bf16[4,256,128]{2,1,0:T(8,128)(2,1)S(1)}, bf16[4,256,128]{2,1,0:T(8,128)(2,1)S(1)}, u32[]{:S(2)}, u32[]{:S(2)}) %collective-permute-start.14) | collective-permute-done | bytes 262176 | tf_op jit(solution)/shard_map/ppermute | solution.py:39
  46.9 1.7 %collective-permute-start.16 = (bf16[4,256,128]{2,1,0:T(8,128)(2,1)S(1)}, bf16[4,256,128]{2,1,0:T(8,128)(2,1)S(1)}, u32[]{:S(2)}, u32[]{:S(2)}) collective-permute-start(bf16[4,256,128]{2,1,0:T(8,128)(2,1)S(1)} %shard_map.94.w), channel_id=1, source_target_pairs={{0,32},{1,33},{2,34},{3,35},{4,36},{5,37},{6,38},{7,39},{8,40},{9,... | collective-permute-start | bytes 786440 | tf_op jit(solution)/shard_map/ppermute | solution.py:39
  49.3 2.7 %collective-permute-start.1 = (bf16[2,128,128]{2,1,0:T(8,128)(2,1)S(1)}, bf16[2,128,128]{2,1,0:T(8,128)(2,1)S(1)}, u32[]{:S(2)}, u32[]{:S(2)}) collective-permute-start(bf16[2,128,128]{2,1,0:T(8,128)(2,1)S(1)} %get-tuple-element.28), channel_id=1, source_target_pairs={{0,1},{1,0},{2,3},{3,2},{4,5},{5,4},{6,7},{7,6},{8,9},{9,8},{10,11... | collective-permute-start | bytes 196616 | tf_op jit(solution)/shard_map/ppermute | solution.py:39
  52.0 3.3 %collective-permute-start.17 = (bf16[4,256,128]{2,1,0:T(8,128)(2,1)S(1)}, bf16[4,256,128]{2,1,0:T(8,128)(2,1)S(1)}, u32[]{:S(2)}, u32[]{:S(2)}) collective-permute-start(bf16[4,256,128]{2,1,0:T(8,128)(2,1)S(1)} %shard_map.94.w), channel_id=1, source_target_pairs={{0,64},{1,65},{2,66},{3,67},{4,68},{5,69},{6,70},{7,71},{8,72},{9,... | collective-permute-start | bytes 786440 | tf_op jit(solution)/shard_map/ppermute | solution.py:39
  56.0 2.5 %collective-permute-start = (bf16[2,136,128]{2,1,0:T(8,128)(2,1)S(1)}, bf16[2,136,128]{2,1,0:T(8,128)(2,1)S(1)}, u32[]{:S(2)}, u32[]{:S(2)}) collective-permute-start(bf16[2,136,128]{2,1,0:T(8,128)(2,1)S(1)} %get-tuple-element.27), channel_id=1, source_target_pairs={{0,1},{1,2},{2,3},{3,4},{4,5},{5,6},{6,7},{7,8},{8,9},{9,10},{10,1... | collective-permute-start | bytes 208904 | tf_op jit(solution)/shard_map/ppermute | solution.py:377
  58.5 1.3 collective-permute-start.2
  59.8 4.0 %collective-permute-done.2.p = bf16[2,128,128]{2,1,0:T(8,128)(2,1)S(1)} collective-permute-done((bf16[2,128,128]{2,1,0:T(8,128)(2,1)S(1)}, bf16[2,128,128]{2,1,0:T(8,128)(2,1)S(1)}, u32[]{:S(2)}, u32[]{:S(2)}) %collective-permute-start.2) | collective-permute-done | bytes 65568 | tf_op jit(solution)/shard_map/ppermute | solution.py:379
  63.8 2.0 %shard_map.85 = (f32[256,128]{1,0:T(8,128)S(1)}, f32[256,128]{1,0:T(8,128)S(1)}, bf16[4,256,128]{2,1,0:T(8,128)(2,1)S(1)}) custom-call(s32[130]{0:T(256)S(1)} %pad_add_fusion.t_ref, f32[512,128]{1,0:T(8,128)S(1)} %bitcast.26, f32[512,128]{1,0:T(8,128)S(1)} %bitcast.28, bf16[2,136,128]{2,1,0:T(8,128)(2,1)S(1)} %collective-permute-done.b, ...), custom_call_target="tpu_custom_call" | custom-call | flops 1310720 | bytes 1310720 | tf_op jit(solution)/shard_map/pallas_call | solution.py:61
  65.8 3.4 %collective-permute-start.19 = (bf16[4,256,128]{2,1,0:T(8,128)(2,1)S(1)}, bf16[4,256,128]{2,1,0:T(8,128)(2,1)S(1)}, u32[]{:S(2)}, u32[]{:S(2)}) collective-permute-start(bf16[4,256,128]{2,1,0:T(8,128)(2,1)S(1)} %get-tuple-element.45.refs_0_), channel_id=1, source_target_pairs={{0,96},{1,97},{2,98},{3,99},{4,100},{5,101},{6,102},{7,103},{8,104... | collective-permute-start | bytes 786440 | tf_op jit(solution)/shard_map/ppermute | solution.py:39
  69.2 2.8 %collective-permute-start.20 = (bf16[4,256,128]{2,1,0:T(8,128)(2,1)S(1)}, bf16[4,256,128]{2,1,0:T(8,128)(2,1)S(1)}, u32[]{:S(2)}, u32[]{:S(2)}) collective-permute-start(bf16[4,256,128]{2,1,0:T(8,128)(2,1)S(1)} %get-tuple-element.45.refs_0_), channel_id=1, source_target_pairs={{0,64},{1,65},{2,66},{3,67},{4,68},{5,69},{6,70},{7,71},{8,72},{9,... | collective-permute-start | bytes 786440 | tf_op jit(solution)/shard_map/ppermute | solution.py:39
  72.0 1.4 %shard_map.95 = (f32[4,256,128]{2,1,0:T(8,128)S(1)}, f32[32,8,128]{2,1,0:T(8,128)}) custom-call(s32[1]{0:T(128)} %constant.166.clone.1.t_ref, bf16[4,256,128]{2,1,0:T(8,128)(2,1)S(1)} %shard_map.94.w, bf16[4,256,128]{2,1,0:T(8,128)(2,1)S(1)} %collective-permute-done.16.x1, bf16[4,256,128]{2,1,0:T(8,128)(2,1)S(1)} %collective-permute-done.17.x2, ...), custom_call_target="tpu_custom_call" | custom-call | flops 786432 | bytes 1572864 | tf_op jit(solution)/shard_map/pallas_call | solution.py:61
  73.4 6.4 %all-to-all-start = ((f32[32,8,128]{2,1,0:T(8,128)}), f32[32,8,128]{2,1,0:T(8,128)S(1)}, u32[]{:S(2)}, u32[]{:S(2)}) async-start(f32[32,8,128]{2,1,0:T(8,128)} %get-tuple-element.46), calls=%async_computation | async-start | bytes 262144 | tf_op jit(solution)/shard_map/all_to_all | solution.py:401
  79.8 4.7 %collective-permute-done.21.refs_3_ = bf16[4,256,128]{2,1,0:T(8,128)(2,1)S(1)} collective-permute-done((bf16[4,256,128]{2,1,0:T(8,128)(2,1)S(1)}, bf16[4,256,128]{2,1,0:T(8,128)(2,1)S(1)}, u32[]{:S(2)}, u32[]{:S(2)}) %collective-permute-start.21) | collective-permute-done | bytes 262176 | tf_op jit(solution)/shard_map/ppermute | solution.py:39
  84.5 2.9 %all-to-all-done.refs_4_ = f32[32,8,128]{2,1,0:T(8,128)S(1)} async-done(((f32[32,8,128]{2,1,0:T(8,128)}), f32[32,8,128]{2,1,0:T(8,128)S(1)}, u32[]{:S(2)}, u32[]{:S(2)}) %all-to-all-start) | async-done | bytes 131104 | tf_op jit(solution)/shard_map/all_to_all | solution.py:401
  87.4 1.8 %shard_map.96 = (bf16[4,256,128]{2,1,0:T(8,128)(2,1)S(1)}, f32[8,128]{1,0:T(8,128)S(1)}) custom-call(s32[1]{0:T(128)} %constant.166.clone.1.t_ref, f32[4,256,128]{2,1,0:T(8,128)S(1)} %get-tuple-element.44.g, bf16[4,256,128]{2,1,0:T(8,128)(2,1)S(1)} %get-tuple-element.45.refs_0_, bf16[4,256,128]{2,1,0:T(8,128)(2,1)S(1)} %collective-permute-done.19.refs_1_, ...), custom_call_target="tpu_custom_call" | custom-call | flops 2621440 | bytes 1835008 | tf_op jit(solution)/shard_map/pallas_call | solution.py:61
  90.8 1.9 %collective-permute-start.22 = (bf16[4,256,128]{2,1,0:T(8,128)(2,1)S(1)}, bf16[4,256,128]{2,1,0:T(8,128)(2,1)S(1)}, u32[]{:S(2)}, u32[]{:S(2)}) collective-permute-start(bf16[4,256,128]{2,1,0:T(8,128)(2,1)S(1)} %get-tuple-element.49.a), channel_id=1, source_target_pairs={{0,24},{1,7},{2,26},{3,1},{4,28},{5,3},{6,30},{7,5},{8,0},{9,15},{... | collective-permute-start | bytes 786440 | tf_op jit(solution)/shard_map/ppermute | solution.py:39
  92.7 3.6 %collective-permute-done.25.a = bf16[4,256,128]{2,1,0:T(8,128)(2,1)S(1)} collective-permute-done((bf16[4,256,128]{2,1,0:T(8,128)(2,1)S(1)}, bf16[4,256,128]{2,1,0:T(8,128)(2,1)S(1)}, u32[]{:S(2)}, u32[]{:S(2)}) %collective-permute-start.25) | collective-permute-done | bytes 262176 | tf_op jit(solution)/shard_map/ppermute | solution.py:39
  96.3 2.8 %collective-permute-done.26.b = bf16[4,256,128]{2,1,0:T(8,128)(2,1)S(1)} collective-permute-done((bf16[4,256,128]{2,1,0:T(8,128)(2,1)S(1)}, bf16[4,256,128]{2,1,0:T(8,128)(2,1)S(1)}, u32[]{:S(2)}, u32[]{:S(2)}) %collective-permute-start.26) | collective-permute-done | bytes 262176 | tf_op jit(solution)/shard_map/ppermute | solution.py:39
  99.1 1.3 collective-permute-start.38
  100.4 2.7 %collective-permute-start.27 = (bf16[8,256,128]{2,1,0:T(8,128)(2,1)S(1)}, bf16[8,256,128]{2,1,0:T(8,128)(2,1)S(1)}, u32[]{:S(2)}, u32[]{:S(2)}) collective-permute-start(bf16[8,256,128]{2,1,0:T(8,128)(2,1)S(1)} %shard_map.98.refs_1_), channel_id=1, source_target_pairs={{0,6},{1,25},{2,0},{3,27},{4,2},{5,29},{6,4},{7,31},{8,14},{9,1},{... | collective-permute-start | bytes 1572872 | tf_op jit(solution)/shard_map/ppermute | solution.py:39
  104.1 1.9 %collective-permute-start.31 = (bf16[8,256,128]{2,1,0:T(8,128)(2,1)S(1)}, bf16[8,256,128]{2,1,0:T(8,128)(2,1)S(1)}, u32[]{:S(2)}, u32[]{:S(2)}) collective-permute-start(bf16[8,256,128]{2,1,0:T(8,128)(2,1)S(1)} %shard_map.97.refs_0_), channel_id=1, source_target_pairs={{0,6},{1,25},{2,0},{3,27},{4,2},{5,29},{6,4},{7,31},{8,14},{9,1},{... | collective-permute-start | bytes 1572872 | tf_op jit(solution)/shard_map/ppermute | solution.py:39
  106.1 3.9 %collective-permute-done.32.refs_2_ = bf16[8,256,128]{2,1,0:T(8,128)(2,1)S(1)} collective-permute-done((bf16[8,256,128]{2,1,0:T(8,128)(2,1)S(1)}, bf16[8,256,128]{2,1,0:T(8,128)(2,1)S(1)}, u32[]{:S(2)}, u32[]{:S(2)}) %collective-permute-start.32) | collective-permute-done | bytes 524320 | tf_op jit(solution)/shard_map/ppermute | solution.py:39
  110.9 1.7 %collective-permute-start.28 = (bf16[8,256,128]{2,1,0:T(8,128)(2,1)S(1)}, bf16[8,256,128]{2,1,0:T(8,128)(2,1)S(1)}, u32[]{:S(2)}, u32[]{:S(2)}) collective-permute-start(bf16[8,256,128]{2,1,0:T(8,128)(2,1)S(1)} %collective-permute-done.27.refs_3_), channel_id=1, source_target_pairs={{0,6},{1,25},{2,0},{3,27},{4,2},{5,29},{6,4},{7,31},{8,14},{9,1},{... | collective-permute-start | bytes 1572872 | tf_op jit(solution)/shard_map/ppermute | solution.py:39
  112.6 2.9 %collective-permute-done.23.refs_0_ = bf16[8,256,128]{2,1,0:T(8,128)(2,1)S(1)} collective-permute-done((bf16[8,256,128]{2,1,0:T(8,128)(2,1)S(1)}, bf16[8,256,128]{2,1,0:T(8,128)(2,1)S(1)}, u32[]{:S(2)}, u32[]{:S(2)}) %collective-permute-start.23) | collective-permute-done | bytes 524320 | tf_op jit(solution)/shard_map/ppermute | solution.py:39
  116.1 0.9 collective-permute-start.36
  117.6 2.9 %collective-permute-done.28.refs_1_ = bf16[8,256,128]{2,1,0:T(8,128)(2,1)S(1)} collective-permute-done((bf16[8,256,128]{2,1,0:T(8,128)(2,1)S(1)}, bf16[8,256,128]{2,1,0:T(8,128)(2,1)S(1)}, u32[]{:S(2)}, u32[]{:S(2)}) %collective-permute-start.28) | collective-permute-done | bytes 524320 | tf_op jit(solution)/shard_map/ppermute | solution.py:39
  120.5 1.2 collective-permute-start.30
  121.7 3.4 %collective-permute-done.24.refs_0_ = bf16[8,256,128]{2,1,0:T(8,128)(2,1)S(1)} collective-permute-done((bf16[8,256,128]{2,1,0:T(8,128)(2,1)S(1)}, bf16[8,256,128]{2,1,0:T(8,128)(2,1)S(1)}, u32[]{:S(2)}, u32[]{:S(2)}) %collective-permute-start.24) | collective-permute-done | bytes 524320 | tf_op jit(solution)/shard_map/ppermute | solution.py:39
  125.1 1.8 %collective-permute-start.29 = (bf16[8,256,128]{2,1,0:T(8,128)(2,1)S(1)}, bf16[8,256,128]{2,1,0:T(8,128)(2,1)S(1)}, u32[]{:S(2)}, u32[]{:S(2)}) collective-permute-start(bf16[8,256,128]{2,1,0:T(8,128)(2,1)S(1)} %collective-permute-done.24.refs_0_), channel_id=1, source_target_pairs={{0,1},{1,0},{2,3},{3,2},{4,5},{5,4},{6,7},{7,6},{8,9},{9,8},{10,11... | collective-permute-start | bytes 1572872 | tf_op jit(solution)/shard_map/ppermute | solution.py:39
  126.9 1.5 %fusion.1 = (f32[32768]{0:T(1024)}, f32[32768]{0:T(1024)}, f32[32768]{0:T(1024)}) fusion(f32[4,256,128]{2,1,0:T(8,128)S(1)} %get-tuple-element.44.g, f32[]{:T(128)} %bitcast.5, f32[256,128]{1,0:T(8,128)S(1)} %get-tuple-element.48, f32[256,128]{1,0:T(8,128)S(1)} %get-tuple-element.29, f32[32768]{0:T(1024)S(1)} %copy-done.2), kind=kLoop, calls=%fused_computation.6 | loop fusion | flops 491520 | bytes 917508 | tf_op jit(solution)/shard_map/reshape | solution.py:404
  128.4 2.1 %shard_map.99.refs_8_ = bf16[128,256,128]{2,1,0:T(8,128)(2,1)} custom-call(s32[128]{0:T(128)S(1)} %compare_select_fusion.16.t_ref, bf16[8,256,128]{2,1,0:T(8,128)(2,1)S(1)} %shard_map.97.refs_0_, bf16[8,256,128]{2,1,0:T(8,128)(2,1)S(1)} %shard_map.98.refs_1_, bf16[8,256,128]{2,1,0:T(8,128)(2,1)S(1)} %collective-permute-done.37.refs_2_, ...), custom_call_target="tpu_custom_call" | custom-call | flops 4194304 | bytes 4194304 | tf_op jit(solution)/shard_map/pallas_call | solution.py:61
  130.5 3.1 %shard_map.100.refs_4_ = bf16[128,256,128]{2,1,0:T(8,128)(2,1)} custom-call(s32[128]{0:T(128)S(1)} %compare_select_fusion.16.t_ref, bf16[8,256,128]{2,1,0:T(8,128)(2,1)S(1)} %collective-permute-done.23.refs_0_, bf16[8,256,128]{2,1,0:T(8,128)(2,1)S(1)} %collective-permute-done.31.refs_1_, ...), custom_call_target="tpu_custom_call", output_to_operand_aliasing={{}: (9, {})} | custom-call | flops 8388608 | bytes 8388608 | tf_op jit(solution)/shard_map/pallas_call | solution.py:61
  133.6 2.1 %shard_map.101 = bf16[128,256,128]{2,1,0:T(8,128)(2,1)} custom-call(s32[128]{0:T(128)S(1)} %compare_select_fusion.16.t_ref, bf16[8,256,128]{2,1,0:T(8,128)(2,1)S(1)} %collective-permute-done.24.refs_0_, bf16[8,256,128]{2,1,0:T(8,128)(2,1)S(1)} %collective-permute-done.28.refs_1_, ...), custom_call_target="tpu_custom_call", output_to_operand_aliasing={{}: (5, {})} | custom-call | flops 4194304 | bytes 4194304 | tf_op jit(solution)/shard_map/pallas_call | solution.py:61
  (62 shorter events, 9.5 us)
Async XLA Ops:
  4.6 7.3 %collective-permute-start.5 = (bf16[16,256,128]{2,1,0:T(8,128)(2,1)S(1)}, bf16[16,256,128]{2,1,0:T(8,128)(2,1)S(1)}, u32[]{:S(2)}, u32[]{:S(2)}) collective-permute-start(bf16[16,256,128]{2,1,0:T(8,128)(2,1)S(1)} %get-tuple-element.35), channel_id=1, source_target_pairs={{0,1},{1,0},{2,3},{3,2},{4,5},{5,4},{6,7},{7,6},{8,9},{9,8},{10,11... | collective-permute-start | bytes 3145736 | tf_op jit(solution)/shard_map/ppermute | solution.py:39
  6.0 10.4 %collective-permute-start.9 = (bf16[16,256,128]{2,1,0:T(8,128)(2,1)S(1)}, bf16[16,256,128]{2,1,0:T(8,128)(2,1)S(1)}, u32[]{:S(2)}, u32[]{:S(2)}) collective-permute-start(bf16[16,256,128]{2,1,0:T(8,128)(2,1)S(1)} %get-tuple-element.38), channel_id=1, source_target_pairs={{0,1},{1,0},{2,3},{3,2},{4,5},{5,4},{6,7},{7,6},{8,9},{9,8},{10,11... | collective-permute-start | bytes 3145736 | tf_op jit(solution)/shard_map/ppermute | solution.py:39
  6.1 12.0 %collective-permute-start.4 = (bf16[16,256,128]{2,1,0:T(8,128)(2,1)S(1)}, bf16[16,256,128]{2,1,0:T(8,128)(2,1)S(1)}, u32[]{:S(2)}, u32[]{:S(2)}) collective-permute-start(bf16[16,256,128]{2,1,0:T(8,128)(2,1)S(1)} %get-tuple-element.33), channel_id=1, source_target_pairs={{0,1},{1,0},{2,3},{3,2},{4,5},{5,4},{6,7},{7,6},{8,9},{9,8},{10,11... | collective-permute-start | bytes 3145736 | tf_op jit(solution)/shard_map/ppermute | solution.py:39
  12.1 9.0 %collective-permute-start.11 = (bf16[8,256,128]{2,1,0:T(8,128)(2,1)S(1)}, bf16[8,256,128]{2,1,0:T(8,128)(2,1)S(1)}, u32[]{:S(2)}, u32[]{:S(2)}) collective-permute-start(bf16[8,256,128]{2,1,0:T(8,128)(2,1)S(1)} %get-tuple-element.39), channel_id=1, source_target_pairs={{0,6},{1,25},{2,0},{3,27},{4,2},{5,29},{6,4},{7,31},{8,14},{9,1},{... | collective-permute-start | bytes 1572872 | tf_op jit(solution)/shard_map/ppermute | solution.py:39
  15.0 10.1 %collective-permute-start.3 = (bf16[16,256,128]{2,1,0:T(8,128)(2,1)S(1)}, bf16[16,256,128]{2,1,0:T(8,128)(2,1)S(1)}, u32[]{:S(2)}, u32[]{:S(2)}) collective-permute-start(bf16[16,256,128]{2,1,0:T(8,128)(2,1)S(1)} %get-tuple-element.31), channel_id=1, source_target_pairs={{0,1},{1,0},{2,3},{3,2},{4,5},{5,4},{6,7},{7,6},{8,9},{9,8},{10,11... | collective-permute-start | bytes 3145736 | tf_op jit(solution)/shard_map/ppermute | solution.py:39
  15.2 9.7 %collective-permute-start.6 = (bf16[8,256,128]{2,1,0:T(8,128)(2,1)S(1)}, bf16[8,256,128]{2,1,0:T(8,128)(2,1)S(1)}, u32[]{:S(2)}, u32[]{:S(2)}) collective-permute-start(bf16[8,256,128]{2,1,0:T(8,128)(2,1)S(1)} %get-tuple-element.36), channel_id=1, source_target_pairs={{0,2},{1,9},{2,4},{3,11},{4,6},{5,13},{6,0},{7,15},{8,10},{9,17},{... | collective-permute-start | bytes 1572872 | tf_op jit(solution)/shard_map/ppermute | solution.py:39
  16.6 10.2 %collective-permute-start.10 = (bf16[8,256,128]{2,1,0:T(8,128)(2,1)S(1)}, bf16[8,256,128]{2,1,0:T(8,128)(2,1)S(1)}, u32[]{:S(2)}, u32[]{:S(2)}) collective-permute-start(bf16[8,256,128]{2,1,0:T(8,128)(2,1)S(1)} %shard_map.91), channel_id=1, source_target_pairs={{0,6},{1,25},{2,0},{3,27},{4,2},{5,29},{6,4},{7,31},{8,14},{9,1},{... | collective-permute-start | bytes 1572872 | tf_op jit(solution)/shard_map/ppermute | solution.py:39
  18.2 30.4 %copy-start.3 = (s32[129]{0:T(256)S(1)}, s32[129]{0:T(256)}, u32[]{:S(2)}) copy-start(s32[129]{0:T(256)} %param.9) | copy-start | bytes 1552
  18.2 30.5 %copy-start = (f32[1,65536]{1,0:T(1,128)S(1)}, f32[1,65536]{1,0:T(1,128)}, u32[]{:S(2)}) copy-start(f32[1,65536]{1,0:T(1,128)} %param.7) | copy-start | bytes 786436
  18.2 30.4 %copy-start.1 = (f32[1,65536]{1,0:T(1,128)S(1)}, f32[1,65536]{1,0:T(1,128)}, u32[]{:S(2)}) copy-start(f32[1,65536]{1,0:T(1,128)} %param.8) | copy-start | bytes 786436
  18.3 45.5 %copy-start.2 = (f32[32768]{0:T(1024)S(1)}, f32[32768]{0:T(1024)}, u32[]{:S(2)}) copy-start(f32[32768]{0:T(1024)} %param.6) | copy-start | bytes 393220
  18.3 12.1 %collective-permute-start.8 = (bf16[8,256,128]{2,1,0:T(8,128)(2,1)S(1)}, bf16[8,256,128]{2,1,0:T(8,128)(2,1)S(1)}, u32[]{:S(2)}, u32[]{:S(2)}) collective-permute-start(bf16[8,256,128]{2,1,0:T(8,128)(2,1)S(1)} %shard_map.90), channel_id=1, source_target_pairs={{0,2},{1,9},{2,4},{3,11},{4,6},{5,13},{6,0},{7,15},{8,10},{9,17},{... | collective-permute-start | bytes 1572872 | tf_op jit(solution)/shard_map/ppermute | solution.py:39
  21.4 11.0 %collective-permute-start.12 = (bf16[8,256,128]{2,1,0:T(8,128)(2,1)S(1)}, bf16[8,256,128]{2,1,0:T(8,128)(2,1)S(1)}, u32[]{:S(2)}, u32[]{:S(2)}) collective-permute-start(bf16[8,256,128]{2,1,0:T(8,128)(2,1)S(1)} %shard_map.92), channel_id=1, source_target_pairs={{0,6},{1,25},{2,0},{3,27},{4,2},{5,29},{6,4},{7,31},{8,14},{9,1},{... | collective-permute-start | bytes 1572872 | tf_op jit(solution)/shard_map/ppermute | solution.py:39
  25.1 10.9 %collective-permute-start.7 = (bf16[8,256,128]{2,1,0:T(8,128)(2,1)S(1)}, bf16[8,256,128]{2,1,0:T(8,128)(2,1)S(1)}, u32[]{:S(2)}, u32[]{:S(2)}) collective-permute-start(bf16[8,256,128]{2,1,0:T(8,128)(2,1)S(1)} %shard_map.89), channel_id=1, source_target_pairs={{0,2},{1,9},{2,4},{3,11},{4,6},{5,13},{6,0},{7,15},{8,10},{9,17},{... | collective-permute-start | bytes 1572872 | tf_op jit(solution)/shard_map/ppermute | solution.py:39
  36.6 6.8 %collective-permute-start.13 = (bf16[4,256,128]{2,1,0:T(8,128)(2,1)S(1)}, bf16[4,256,128]{2,1,0:T(8,128)(2,1)S(1)}, u32[]{:S(2)}, u32[]{:S(2)}) collective-permute-start(bf16[4,256,128]{2,1,0:T(8,128)(2,1)S(1)} %get-tuple-element.41), channel_id=1, source_target_pairs={{0,8},{1,3},{2,10},{3,5},{4,12},{5,7},{6,14},{7,1},{8,16},{9,11},{... | collective-permute-start | bytes 786440 | tf_op jit(solution)/shard_map/ppermute | solution.py:39
  37.4 9.3 %collective-permute-start.14 = (bf16[4,256,128]{2,1,0:T(8,128)(2,1)S(1)}, bf16[4,256,128]{2,1,0:T(8,128)(2,1)S(1)}, u32[]{:S(2)}, u32[]{:S(2)}) collective-permute-start(bf16[4,256,128]{2,1,0:T(8,128)(2,1)S(1)} %get-tuple-element.42), channel_id=1, source_target_pairs={{0,16},{1,5},{2,18},{3,7},{4,20},{5,1},{6,22},{7,3},{8,24},{9,13},... | collective-permute-start | bytes 786440 | tf_op jit(solution)/shard_map/ppermute | solution.py:39
  39.8 6.9 %collective-permute-start.15 = (bf16[4,256,128]{2,1,0:T(8,128)(2,1)S(1)}, bf16[4,256,128]{2,1,0:T(8,128)(2,1)S(1)}, u32[]{:S(2)}, u32[]{:S(2)}) collective-permute-start(bf16[4,256,128]{2,1,0:T(8,128)(2,1)S(1)} %get-tuple-element.43), channel_id=1, source_target_pairs={{0,24},{1,7},{2,26},{3,1},{4,28},{5,3},{6,30},{7,5},{8,0},{9,15},{... | collective-permute-start | bytes 786440 | tf_op jit(solution)/shard_map/ppermute | solution.py:39
  46.9 25.1 %collective-permute-start.16 = (bf16[4,256,128]{2,1,0:T(8,128)(2,1)S(1)}, bf16[4,256,128]{2,1,0:T(8,128)(2,1)S(1)}, u32[]{:S(2)}, u32[]{:S(2)}) collective-permute-start(bf16[4,256,128]{2,1,0:T(8,128)(2,1)S(1)} %shard_map.94.w), channel_id=1, source_target_pairs={{0,32},{1,33},{2,34},{3,35},{4,36},{5,37},{6,38},{7,39},{8,40},{9,... | collective-permute-start | bytes 786440 | tf_op jit(solution)/shard_map/ppermute | solution.py:39
  49.3 9.2 %collective-permute-start.1 = (bf16[2,128,128]{2,1,0:T(8,128)(2,1)S(1)}, bf16[2,128,128]{2,1,0:T(8,128)(2,1)S(1)}, u32[]{:S(2)}, u32[]{:S(2)}) collective-permute-start(bf16[2,128,128]{2,1,0:T(8,128)(2,1)S(1)} %get-tuple-element.28), channel_id=1, source_target_pairs={{0,1},{1,0},{2,3},{3,2},{4,5},{5,4},{6,7},{7,6},{8,9},{9,8},{10,11... | collective-permute-start | bytes 196616 | tf_op jit(solution)/shard_map/ppermute | solution.py:39
  52.0 20.0 %collective-permute-start.17 = (bf16[4,256,128]{2,1,0:T(8,128)(2,1)S(1)}, bf16[4,256,128]{2,1,0:T(8,128)(2,1)S(1)}, u32[]{:S(2)}, u32[]{:S(2)}) collective-permute-start(bf16[4,256,128]{2,1,0:T(8,128)(2,1)S(1)} %shard_map.94.w), channel_id=1, source_target_pairs={{0,64},{1,65},{2,66},{3,67},{4,68},{5,69},{6,70},{7,71},{8,72},{9,... | collective-permute-start | bytes 786440 | tf_op jit(solution)/shard_map/ppermute | solution.py:39
  55.3 16.7 %collective-permute-start.18 = (bf16[4,256,128]{2,1,0:T(8,128)(2,1)S(1)}, bf16[4,256,128]{2,1,0:T(8,128)(2,1)S(1)}, u32[]{:S(2)}, u32[]{:S(2)}) collective-permute-start(bf16[4,256,128]{2,1,0:T(8,128)(2,1)S(1)} %shard_map.94.w), channel_id=1, source_target_pairs={{0,96},{1,97},{2,98},{3,99},{4,100},{5,101},{6,102},{7,103},{8,104... | collective-permute-start | bytes 786440 | tf_op jit(solution)/shard_map/ppermute | solution.py:39
  56.0 3.8 %collective-permute-start = (bf16[2,136,128]{2,1,0:T(8,128)(2,1)S(1)}, bf16[2,136,128]{2,1,0:T(8,128)(2,1)S(1)}, u32[]{:S(2)}, u32[]{:S(2)}) collective-permute-start(bf16[2,136,128]{2,1,0:T(8,128)(2,1)S(1)} %get-tuple-element.27), channel_id=1, source_target_pairs={{0,1},{1,2},{2,3},{3,4},{4,5},{5,6},{6,7},{7,8},{8,9},{9,10},{10,1... | collective-permute-start | bytes 208904 | tf_op jit(solution)/shard_map/ppermute | solution.py:377
  58.5 5.3 %collective-permute-start.2 = (bf16[2,128,128]{2,1,0:T(8,128)(2,1)S(1)}, bf16[2,128,128]{2,1,0:T(8,128)(2,1)S(1)}, u32[]{:S(2)}, u32[]{:S(2)}) collective-permute-start(bf16[2,128,128]{2,1,0:T(8,128)(2,1)S(1)} %collective-permute-done.1.a), channel_id=1, source_target_pairs={{3,1},{5,3},{7,5},{9,7},{11,9},{13,11},{15,13},{17,15},{19,17},{21... | collective-permute-start | bytes 196616 | tf_op jit(solution)/shard_map/ppermute | solution.py:379
  65.8 14.0 %collective-permute-start.19 = (bf16[4,256,128]{2,1,0:T(8,128)(2,1)S(1)}, bf16[4,256,128]{2,1,0:T(8,128)(2,1)S(1)}, u32[]{:S(2)}, u32[]{:S(2)}) collective-permute-start(bf16[4,256,128]{2,1,0:T(8,128)(2,1)S(1)} %get-tuple-element.45.refs_0_), channel_id=1, source_target_pairs={{0,96},{1,97},{2,98},{3,99},{4,100},{5,101},{6,102},{7,103},{8,104... | collective-permute-start | bytes 786440 | tf_op jit(solution)/shard_map/ppermute | solution.py:39
  69.2 10.6 %collective-permute-start.20 = (bf16[4,256,128]{2,1,0:T(8,128)(2,1)S(1)}, bf16[4,256,128]{2,1,0:T(8,128)(2,1)S(1)}, u32[]{:S(2)}, u32[]{:S(2)}) collective-permute-start(bf16[4,256,128]{2,1,0:T(8,128)(2,1)S(1)} %get-tuple-element.45.refs_0_), channel_id=1, source_target_pairs={{0,64},{1,65},{2,66},{3,67},{4,68},{5,69},{6,70},{7,71},{8,72},{9,... | collective-permute-start | bytes 786440 | tf_op jit(solution)/shard_map/ppermute | solution.py:39
  72.0 12.5 %collective-permute-start.21 = (bf16[4,256,128]{2,1,0:T(8,128)(2,1)S(1)}, bf16[4,256,128]{2,1,0:T(8,128)(2,1)S(1)}, u32[]{:S(2)}, u32[]{:S(2)}) collective-permute-start(bf16[4,256,128]{2,1,0:T(8,128)(2,1)S(1)} %get-tuple-element.45.refs_0_), channel_id=1, source_target_pairs={{0,32},{1,33},{2,34},{3,35},{4,36},{5,37},{6,38},{7,39},{8,40},{9,... | collective-permute-start | bytes 786440 | tf_op jit(solution)/shard_map/ppermute | solution.py:39
  73.4 14.0 %all-to-all-start = ((f32[32,8,128]{2,1,0:T(8,128)}), f32[32,8,128]{2,1,0:T(8,128)S(1)}, u32[]{:S(2)}, u32[]{:S(2)}) async-start(f32[32,8,128]{2,1,0:T(8,128)} %get-tuple-element.46), calls=%async_computation | async-start | bytes 262144 | tf_op jit(solution)/shard_map/all_to_all | solution.py:401
  89.1 7.1 %collective-permute-start.25 = (bf16[4,256,128]{2,1,0:T(8,128)(2,1)S(1)}, bf16[4,256,128]{2,1,0:T(8,128)(2,1)S(1)}, u32[]{:S(2)}, u32[]{:S(2)}) collective-permute-start(bf16[4,256,128]{2,1,0:T(8,128)(2,1)S(1)} %get-tuple-element.49.a), channel_id=1, source_target_pairs={{0,16},{1,5},{2,18},{3,7},{4,20},{5,1},{6,22},{7,3},{8,24},{9,13},... | collective-permute-start | bytes 786440 | tf_op jit(solution)/shard_map/ppermute | solution.py:39
  90.0 9.1 %collective-permute-start.26 = (bf16[4,256,128]{2,1,0:T(8,128)(2,1)S(1)}, bf16[4,256,128]{2,1,0:T(8,128)(2,1)S(1)}, u32[]{:S(2)}, u32[]{:S(2)}) collective-permute-start(bf16[4,256,128]{2,1,0:T(8,128)(2,1)S(1)} %get-tuple-element.49.a), channel_id=1, source_target_pairs={{0,8},{1,3},{2,10},{3,5},{4,12},{5,7},{6,14},{7,1},{8,16},{9,11},{... | collective-permute-start | bytes 786440 | tf_op jit(solution)/shard_map/ppermute | solution.py:39
  90.8 12.3 %collective-permute-start.22 = (bf16[4,256,128]{2,1,0:T(8,128)(2,1)S(1)}, bf16[4,256,128]{2,1,0:T(8,128)(2,1)S(1)}, u32[]{:S(2)}, u32[]{:S(2)}) collective-permute-start(bf16[4,256,128]{2,1,0:T(8,128)(2,1)S(1)} %get-tuple-element.49.a), channel_id=1, source_target_pairs={{0,24},{1,7},{2,26},{3,1},{4,28},{5,3},{6,30},{7,5},{8,0},{9,15},{... | collective-permute-start | bytes 786440 | tf_op jit(solution)/shard_map/ppermute | solution.py:39
  99.1 5.0 %collective-permute-start.38 = (bf16[8,256,128]{2,1,0:T(8,128)(2,1)S(1)}, bf16[8,256,128]{2,1,0:T(8,128)(2,1)S(1)}, u32[]{:S(2)}, u32[]{:S(2)}) collective-permute-start(bf16[8,256,128]{2,1,0:T(8,128)(2,1)S(1)} %shard_map.98.refs_1_), channel_id=1, source_target_pairs={{0,1},{1,0},{2,3},{3,2},{4,5},{5,4},{6,7},{7,6},{8,9},{9,8},{10,11... | collective-permute-start | bytes 1572872 | tf_op jit(solution)/shard_map/ppermute | solution.py:39
  100.4 9.5 %collective-permute-start.32 = (bf16[8,256,128]{2,1,0:T(8,128)(2,1)S(1)}, bf16[8,256,128]{2,1,0:T(8,128)(2,1)S(1)}, u32[]{:S(2)}, u32[]{:S(2)}) collective-permute-start(bf16[8,256,128]{2,1,0:T(8,128)(2,1)S(1)} %shard_map.98.refs_1_), channel_id=1, source_target_pairs={{0,2},{1,9},{2,4},{3,11},{4,6},{5,13},{6,0},{7,15},{8,10},{9,17},{... | collective-permute-start | bytes 1572872 | tf_op jit(solution)/shard_map/ppermute | solution.py:39
  100.4 10.5 %collective-permute-start.27 = (bf16[8,256,128]{2,1,0:T(8,128)(2,1)S(1)}, bf16[8,256,128]{2,1,0:T(8,128)(2,1)S(1)}, u32[]{:S(2)}, u32[]{:S(2)}) collective-permute-start(bf16[8,256,128]{2,1,0:T(8,128)(2,1)S(1)} %shard_map.98.refs_1_), channel_id=1, source_target_pairs={{0,6},{1,25},{2,0},{3,27},{4,2},{5,29},{6,4},{7,31},{8,14},{9,1},{... | collective-permute-start | bytes 1572872 | tf_op jit(solution)/shard_map/ppermute | solution.py:39
  103.2 12.4 %collective-permute-start.23 = (bf16[8,256,128]{2,1,0:T(8,128)(2,1)S(1)}, bf16[8,256,128]{2,1,0:T(8,128)(2,1)S(1)}, u32[]{:S(2)}, u32[]{:S(2)}) collective-permute-start(bf16[8,256,128]{2,1,0:T(8,128)(2,1)S(1)} %shard_map.97.refs_0_), channel_id=1, source_target_pairs={{0,2},{1,9},{2,4},{3,11},{4,6},{5,13},{6,0},{7,15},{8,10},{9,17},{... | collective-permute-start | bytes 1572872 | tf_op jit(solution)/shard_map/ppermute | solution.py:39
  103.4 12.7 %collective-permute-start.37 = (bf16[8,256,128]{2,1,0:T(8,128)(2,1)S(1)}, bf16[8,256,128]{2,1,0:T(8,128)(2,1)S(1)}, u32[]{:S(2)}, u32[]{:S(2)}) collective-permute-start(bf16[8,256,128]{2,1,0:T(8,128)(2,1)S(1)} %shard_map.97.refs_0_), channel_id=1, source_target_pairs={{0,1},{1,0},{2,3},{3,2},{4,5},{5,4},{6,7},{7,6},{8,9},{9,8},{10,11... | collective-permute-start | bytes 1572872 | tf_op jit(solution)/shard_map/ppermute | solution.py:39
  104.1 12.9 %collective-permute-start.31 = (bf16[8,256,128]{2,1,0:T(8,128)(2,1)S(1)}, bf16[8,256,128]{2,1,0:T(8,128)(2,1)S(1)}, u32[]{:S(2)}, u32[]{:S(2)}) collective-permute-start(bf16[8,256,128]{2,1,0:T(8,128)(2,1)S(1)} %shard_map.97.refs_0_), channel_id=1, source_target_pairs={{0,6},{1,25},{2,0},{3,27},{4,2},{5,29},{6,4},{7,31},{8,14},{9,1},{... | collective-permute-start | bytes 1572872 | tf_op jit(solution)/shard_map/ppermute | solution.py:39
  110.0 7.2 %collective-permute-start.35 = (bf16[8,256,128]{2,1,0:T(8,128)(2,1)S(1)}, bf16[8,256,128]{2,1,0:T(8,128)(2,1)S(1)}, u32[]{:S(2)}, u32[]{:S(2)}) collective-permute-start(bf16[8,256,128]{2,1,0:T(8,128)(2,1)S(1)} %collective-permute-done.32.refs_2_), channel_id=1, source_target_pairs={{0,1},{1,0},{2,3},{3,2},{4,5},{5,4},{6,7},{7,6},{8,9},{9,8},{10,11... | collective-permute-start | bytes 1572872 | tf_op jit(solution)/shard_map/ppermute | solution.py:39
  110.9 9.6 %collective-permute-start.28 = (bf16[8,256,128]{2,1,0:T(8,128)(2,1)S(1)}, bf16[8,256,128]{2,1,0:T(8,128)(2,1)S(1)}, u32[]{:S(2)}, u32[]{:S(2)}) collective-permute-start(bf16[8,256,128]{2,1,0:T(8,128)(2,1)S(1)} %collective-permute-done.27.refs_3_), channel_id=1, source_target_pairs={{0,6},{1,25},{2,0},{3,27},{4,2},{5,29},{6,4},{7,31},{8,14},{9,1},{... | collective-permute-start | bytes 1572872 | tf_op jit(solution)/shard_map/ppermute | solution.py:39
  115.6 9.5 %collective-permute-start.24 = (bf16[8,256,128]{2,1,0:T(8,128)(2,1)S(1)}, bf16[8,256,128]{2,1,0:T(8,128)(2,1)S(1)}, u32[]{:S(2)}, u32[]{:S(2)}) collective-permute-start(bf16[8,256,128]{2,1,0:T(8,128)(2,1)S(1)} %collective-permute-done.23.refs_0_), channel_id=1, source_target_pairs={{0,2},{1,9},{2,4},{3,11},{4,6},{5,13},{6,0},{7,15},{8,10},{9,17},{... | collective-permute-start | bytes 1572872 | tf_op jit(solution)/shard_map/ppermute | solution.py:39
  116.1 14.4 %collective-permute-start.36 = (bf16[8,256,128]{2,1,0:T(8,128)(2,1)S(1)}, bf16[8,256,128]{2,1,0:T(8,128)(2,1)S(1)}, u32[]{:S(2)}, u32[]{:S(2)}) collective-permute-start(bf16[8,256,128]{2,1,0:T(8,128)(2,1)S(1)} %collective-permute-done.27.refs_3_), channel_id=1, source_target_pairs={{0,1},{1,0},{2,3},{3,2},{4,5},{5,4},{6,7},{7,6},{8,9},{9,8},{10,11... | collective-permute-start | bytes 1572872 | tf_op jit(solution)/shard_map/ppermute | solution.py:39
  117.0 13.5 %collective-permute-start.33 = (bf16[8,256,128]{2,1,0:T(8,128)(2,1)S(1)}, bf16[8,256,128]{2,1,0:T(8,128)(2,1)S(1)}, u32[]{:S(2)}, u32[]{:S(2)}) collective-permute-start(bf16[8,256,128]{2,1,0:T(8,128)(2,1)S(1)} %collective-permute-done.23.refs_0_), channel_id=1, source_target_pairs={{0,1},{1,0},{2,3},{3,2},{4,5},{5,4},{6,7},{7,6},{8,9},{9,8},{10,11... | collective-permute-start | bytes 1572872 | tf_op jit(solution)/shard_map/ppermute | solution.py:39
  117.1 13.4 %collective-permute-start.34 = (bf16[8,256,128]{2,1,0:T(8,128)(2,1)S(1)}, bf16[8,256,128]{2,1,0:T(8,128)(2,1)S(1)}, u32[]{:S(2)}, u32[]{:S(2)}) collective-permute-start(bf16[8,256,128]{2,1,0:T(8,128)(2,1)S(1)} %collective-permute-done.31.refs_1_), channel_id=1, source_target_pairs={{0,1},{1,0},{2,3},{3,2},{4,5},{5,4},{6,7},{7,6},{8,9},{9,8},{10,11... | collective-permute-start | bytes 1572872 | tf_op jit(solution)/shard_map/ppermute | solution.py:39
  120.5 13.2 %collective-permute-start.30 = (bf16[8,256,128]{2,1,0:T(8,128)(2,1)S(1)}, bf16[8,256,128]{2,1,0:T(8,128)(2,1)S(1)}, u32[]{:S(2)}, u32[]{:S(2)}) collective-permute-start(bf16[8,256,128]{2,1,0:T(8,128)(2,1)S(1)} %collective-permute-done.28.refs_1_), channel_id=1, source_target_pairs={{0,1},{1,0},{2,3},{3,2},{4,5},{5,4},{6,7},{7,6},{8,9},{9,8},{10,11... | collective-permute-start | bytes 1572872 | tf_op jit(solution)/shard_map/ppermute | solution.py:39
  125.1 8.5 %collective-permute-start.29 = (bf16[8,256,128]{2,1,0:T(8,128)(2,1)S(1)}, bf16[8,256,128]{2,1,0:T(8,128)(2,1)S(1)}, u32[]{:S(2)}, u32[]{:S(2)}) collective-permute-start(bf16[8,256,128]{2,1,0:T(8,128)(2,1)S(1)} %collective-permute-done.24.refs_0_), channel_id=1, source_target_pairs={{0,1},{1,0},{2,3},{3,2},{4,5},{5,4},{6,7},{7,6},{8,9},{9,8},{10,11... | collective-permute-start | bytes 1572872 | tf_op jit(solution)/shard_map/ppermute | solution.py:39

commit v7 on v6

--- a/solution.py
+++ b/solution.py
@@ -394,10 +394,10 @@
     for s in (2, 1, 3):
         quarters[s] = send(quarters[s], "b", s)
     (partial,) = sum_piece([[(v, 0, 4)] for v in (own, quarters[1], quarters[2], quarters[3])], [(4, BF)])
-    parts = {}
+    last = {}
     for s in (2, 1, 3):
-        parts[s] = send(partial, "z", s)
-    gradient, squares = total_piece(partial, parts[1], parts[2], parts[3], 32)
+        last[s] = send(partial, "z", s)
+    gradient, squares = total_piece(partial, last[1], last[2], last[3], 32)
     squares = lax.all_to_all(squares, ("y", "x", "core"), 0, 0, tiled=True)
     piece, clip = updated_piece(gradient, states, squares, count * width)
     new = adam(master_tiles, m_prev, v_prev, gradient[0], clip[0, 0])
@@ -406,21 +406,23 @@
     got = {}
     for s in (3, 2, 1):
         got[s] = send(piece, "b", s)
-    halves = {}
-    halves[0, 0] = joined(piece, got[3])
-    halves[0, 1] = joined(got[2], got[1])
-    for h in range(2):
-        halves[3, h] = send(halves[0, h], "a", 1)
-        halves[1, h] = send(halves[0, h], "a", 3)
-    halves[2, 0] = send(halves[3, 0], "a", 1)
-    halves[2, 1] = send(halves[1, 1], "a", 3)
+    parts = {}
+    parts[0, 0] = joined(piece, got[3])
+    parts[0, 1], parts[0, 2] = got[2], got[1]
+    for p in range(3):
+        parts[1, p] = send(parts[0, p], "a", 3)
+        parts[3, p] = send(parts[0, p], "a", 1)
+    parts[2, 0] = send(parts[3, 0], "a", 1)
+    for p in (1, 2):
+        parts[2, p] = send(parts[1, p], "a", 3)
     partner = {}
-    for r, h in halves:
-        partner[r, h] = send(halves[r, h], "core")
+    for r, p in parts:
+        partner[r, p] = send(parts[r, p], "core")
     out = None
-    for keys in (((0, 0), (0, 1)), ((3, 0), (1, 0), (3, 1), (1, 1)), ((2, 0), (2, 1))):
-        pairs = [(mine[r] + 8 * h, halves[r, h]) for r, h in keys]
-        pairs += [(theirs[r] + 8 * h, partner[r, h]) for r, h in keys]
+    for near in ((0, 3, 1), (2,)):
+        keys = [(r, p) for r in near for p in range(3)]
+        pairs = [(mine[r] + (0, 8, 12)[p], parts[r, p]) for r, p in keys]
+        pairs += [(theirs[r] + (0, 8, 12)[p], partner[r, p]) for r, p in keys]
         out = place(places, pairs, out)
     return (master_new, m_new, v_new, out.reshape(count * width))
 

time: 136 us -> 140 us (1.029)
  waiting for transfers between devices: 50.6 us -> 55.4 us
    all_to_all x1, waiting for transfers between devices: 2.91 us -> 5.82 us  [step(): squares = lax.all_to_all(squares, ('y', 'x', 'core'), 0, 0, tiled=True)]
    ppermute x37 -> x44, waiting for transfers between devices: 43.7 us -> 45.6 us  [send(): return lax.ppermute(value, DP, perm(axis, s))]
    ppermute x37 -> x44, starting transfers between devices: 48 us -> 46.4 us  [send(): return lax.ppermute(value, DP, perm(axis, s))]
    pallas_call x18 -> x16, Pallas kernels: 23.8 us -> 22.6 us  [call(): pl.pallas_call(body, grid_spec=pltpu.PrefetchScalarGridSpec(num_scalar_pr...]
  transfers between devices with their start and end apart: 40 -> 47, of which waited for: 17 -> 18; matrix products, arithmetic and copies ran while one was open for 2% -> 1% of each run, Pallas kernels for 11% -> 10%
where the time goes in v7:
time: 140 us; the launch traced here: 139 us
  starting transfers between devices  58.1 us (42%)
  waiting for transfers between devices  55.4 us (40%)
  Pallas kernels  22.6 us (16%)
  other arithmetic  1.57 us (1%)
    ppermute x44, starting transfers between devices, send(): return lax.ppermute(value, DP, perm(axis, s))  46.4 us
    ppermute x44, waiting for transfers between devices, send(): return lax.ppermute(value, DP, perm(axis, s))  45.6 us
    pallas_call x16, Pallas kernels, call(): pl.pallas_call(body, grid_spec=pltpu.PrefetchScalarGridSpec(num_scalar_pr...  22.6 us
    all_to_all x1, starting transfers between devices, step(): squares = lax.all_to_all(squares, ('y', 'x', 'core'), 0, 0, tiled=True)  6.84 us
    all_to_all x1, waiting for transfers between devices, step(): squares = lax.all_to_all(squares, ('y', 'x', 'core'), 0, 0, tiled=True)  5.82 us
    ppermute x1, waiting for transfers between devices, step(): passed = lax.ppermute(after, DP, [(d, d - 2) for d in range(3, 128, 2)])  3.97 us
    ppermute x1, starting transfers between devices, step(): before = lax.ppermute(up, DP, [(d, d + 1) for d in range(127)])  3.53 us
  transfers between devices with their start and end apart: 47, of which 18 were waited for; matrix products, arithmetic and copies ran while one was open for 1% of the time, Pallas kernels for 10%

profile of v7, /device:TPU:1, one launch (start us, length us, event | category | flops | bytes accessed | tf_op | source)
XLA Modules:
  0.0 139.3 jit_solution(876288895136841892)
XLA Ops:
  0.7 3.8 %shard_map.87 = (bf16[16,256,128]{2,1,0:T(8,128)(2,1)S(1)}, bf16[16,256,128]{2,1,0:T(8,128)(2,1)S(1)}, bf16[16,256,128]{2,1,0:T(8,128)(2,1)S(1)}) custom-call(s32[128]{0:T(128)S(1)} %compare_select_fusion.16.t_ref, f32[128,256,128]{2,1,0:T(8,128)} %bitcast.30), custom_call_target="tpu_custom_call" | custom-call | flops 1572864 | bytes 9437184 | tf_op jit(solution)/shard_map/pallas_call | solution.py:61
  4.6 1.5 %collective-permute-start.5 = (bf16[16,256,128]{2,1,0:T(8,128)(2,1)S(1)}, bf16[16,256,128]{2,1,0:T(8,128)(2,1)S(1)}, u32[]{:S(2)}, u32[]{:S(2)}) collective-permute-start(bf16[16,256,128]{2,1,0:T(8,128)(2,1)S(1)} %get-tuple-element.35), channel_id=1, source_target_pairs={{0,1},{1,0},{2,3},{3,2},{4,5},{5,4},{6,7},{7,6},{8,9},{9,8},{10,11... | collective-permute-start | bytes 3145736 | tf_op jit(solution)/shard_map/ppermute | solution.py:39
  6.5 5.3 %shard_map.86 = (f32[16,256,128]{2,1,0:T(8,128)S(1)}, f32[16,256,128]{2,1,0:T(8,128)S(1)}, f32[16,256,128]{2,1,0:T(8,128)S(1)}, bf16[16,256,128]{2,1,0:T(8,128)(2,1)S(1)}, f32[16,256,128]{2,1,0:T(8,128)S(1)}) custom-call(s32[128]{0:T(128)S(1)} %compare_select_fusion.16.t_ref, f32[128,256,128]{2,1,0:T(8,128)} %bitcast.31), custom_call_target="tpu_custom_call" | custom-call | flops 2621440 | bytes 15728640 | tf_op jit(solution)/shard_map/pallas_call | solution.py:61
  12.1 1.5 %collective-permute-start.6 = (bf16[8,256,128]{2,1,0:T(8,128)(2,1)S(1)}, bf16[8,256,128]{2,1,0:T(8,128)(2,1)S(1)}, u32[]{:S(2)}, u32[]{:S(2)}) collective-permute-start(bf16[8,256,128]{2,1,0:T(8,128)(2,1)S(1)} %get-tuple-element.36), channel_id=1, source_target_pairs={{0,2},{1,9},{2,4},{3,11},{4,6},{5,13},{6,0},{7,15},{8,10},{9,17},{... | collective-permute-start | bytes 1572872 | tf_op jit(solution)/shard_map/ppermute | solution.py:39
  13.9 2.7 %collective-permute-start.11 = (bf16[8,256,128]{2,1,0:T(8,128)(2,1)S(1)}, bf16[8,256,128]{2,1,0:T(8,128)(2,1)S(1)}, u32[]{:S(2)}, u32[]{:S(2)}) collective-permute-start(bf16[8,256,128]{2,1,0:T(8,128)(2,1)S(1)} %get-tuple-element.39), channel_id=1, source_target_pairs={{0,6},{1,25},{2,0},{3,27},{4,2},{5,29},{6,4},{7,31},{8,14},{9,1},{... | collective-permute-start | bytes 1572872 | tf_op jit(solution)/shard_map/ppermute | solution.py:39
  17.4 1.1 collective-permute-start.8
  18.5 3.4 %collective-permute-done.6.refs_2_ = bf16[8,256,128]{2,1,0:T(8,128)(2,1)S(1)} collective-permute-done((bf16[8,256,128]{2,1,0:T(8,128)(2,1)S(1)}, bf16[8,256,128]{2,1,0:T(8,128)(2,1)S(1)}, u32[]{:S(2)}, u32[]{:S(2)}) %collective-permute-start.6) | collective-permute-done | bytes 524320 | tf_op jit(solution)/shard_map/ppermute | solution.py:39
  23.0 3.5 %collective-permute-start.12 = (bf16[8,256,128]{2,1,0:T(8,128)(2,1)S(1)}, bf16[8,256,128]{2,1,0:T(8,128)(2,1)S(1)}, u32[]{:S(2)}, u32[]{:S(2)}) collective-permute-start(bf16[8,256,128]{2,1,0:T(8,128)(2,1)S(1)} %shard_map.92), channel_id=1, source_target_pairs={{0,6},{1,25},{2,0},{3,27},{4,2},{5,29},{6,4},{7,31},{8,14},{9,1},{... | collective-permute-start | bytes 1572872 | tf_op jit(solution)/shard_map/ppermute | solution.py:39
  26.4 1.9 %collective-permute-done.10.refs_4_ = bf16[8,256,128]{2,1,0:T(8,128)(2,1)S(1)} collective-permute-done((bf16[8,256,128]{2,1,0:T(8,128)(2,1)S(1)}, bf16[8,256,128]{2,1,0:T(8,128)(2,1)S(1)}, u32[]{:S(2)}, u32[]{:S(2)}) %collective-permute-start.10) | collective-permute-done | bytes 524320 | tf_op jit(solution)/shard_map/ppermute | solution.py:39
  28.4 4.8 %collective-permute-done.7.refs_2_ = bf16[8,256,128]{2,1,0:T(8,128)(2,1)S(1)} collective-permute-done((bf16[8,256,128]{2,1,0:T(8,128)(2,1)S(1)}, bf16[8,256,128]{2,1,0:T(8,128)(2,1)S(1)}, u32[]{:S(2)}, u32[]{:S(2)}) %collective-permute-start.7) | collective-permute-done | bytes 524320 | tf_op jit(solution)/shard_map/ppermute | solution.py:39
  33.1 0.8 collective-permute-done.12.refs_5_
  34.6 1.3 collective-permute-start.13
  35.9 1.6 %collective-permute-start.14 = (bf16[4,256,128]{2,1,0:T(8,128)(2,1)S(1)}, bf16[4,256,128]{2,1,0:T(8,128)(2,1)S(1)}, u32[]{:S(2)}, u32[]{:S(2)}) collective-permute-start(bf16[4,256,128]{2,1,0:T(8,128)(2,1)S(1)} %get-tuple-element.42), channel_id=1, source_target_pairs={{0,16},{1,5},{2,18},{3,7},{4,20},{5,1},{6,22},{7,3},{8,24},{9,13},... | collective-permute-start | bytes 786440 | tf_op jit(solution)/shard_map/ppermute | solution.py:39
  37.5 1.7 %collective-permute-start.15 = (bf16[4,256,128]{2,1,0:T(8,128)(2,1)S(1)}, bf16[4,256,128]{2,1,0:T(8,128)(2,1)S(1)}, u32[]{:S(2)}, u32[]{:S(2)}) collective-permute-start(bf16[4,256,128]{2,1,0:T(8,128)(2,1)S(1)} %get-tuple-element.43), channel_id=1, source_target_pairs={{0,24},{1,7},{2,26},{3,1},{4,28},{5,3},{6,30},{7,5},{8,0},{9,15},{... | collective-permute-start | bytes 786440 | tf_op jit(solution)/shard_map/ppermute | solution.py:39
  39.2 2.2 %collective-permute-done.13.refs_1_ = bf16[4,256,128]{2,1,0:T(8,128)(2,1)S(1)} collective-permute-done((bf16[4,256,128]{2,1,0:T(8,128)(2,1)S(1)}, bf16[4,256,128]{2,1,0:T(8,128)(2,1)S(1)}, u32[]{:S(2)}, u32[]{:S(2)}) %collective-permute-start.13) | collective-permute-done | bytes 262176 | tf_op jit(solution)/shard_map/ppermute | solution.py:39
  41.4 3.0 %collective-permute-done.14.refs_2_ = bf16[4,256,128]{2,1,0:T(8,128)(2,1)S(1)} collective-permute-done((bf16[4,256,128]{2,1,0:T(8,128)(2,1)S(1)}, bf16[4,256,128]{2,1,0:T(8,128)(2,1)S(1)}, u32[]{:S(2)}, u32[]{:S(2)}) %collective-permute-start.14) | collective-permute-done | bytes 262176 | tf_op jit(solution)/shard_map/ppermute | solution.py:39
  44.9 3.8 %collective-permute-start.18 = (bf16[4,256,128]{2,1,0:T(8,128)(2,1)S(1)}, bf16[4,256,128]{2,1,0:T(8,128)(2,1)S(1)}, u32[]{:S(2)}, u32[]{:S(2)}) collective-permute-start(bf16[4,256,128]{2,1,0:T(8,128)(2,1)S(1)} %shard_map.94.w), channel_id=1, source_target_pairs={{0,96},{1,97},{2,98},{3,99},{4,100},{5,101},{6,102},{7,103},{8,104... | collective-permute-start | bytes 786440 | tf_op jit(solution)/shard_map/ppermute | solution.py:39
  49.4 2.3 %collective-permute-start.1 = (bf16[2,128,128]{2,1,0:T(8,128)(2,1)S(1)}, bf16[2,128,128]{2,1,0:T(8,128)(2,1)S(1)}, u32[]{:S(2)}, u32[]{:S(2)}) collective-permute-start(bf16[2,128,128]{2,1,0:T(8,128)(2,1)S(1)} %get-tuple-element.28), channel_id=1, source_target_pairs={{0,1},{1,0},{2,3},{3,2},{4,5},{5,4},{6,7},{7,6},{8,9},{9,8},{10,11... | collective-permute-start | bytes 196616 | tf_op jit(solution)/shard_map/ppermute | solution.py:39
  51.7 0.7 collective-permute-start.16
  52.4 3.5 %collective-permute-start = (bf16[2,136,128]{2,1,0:T(8,128)(2,1)S(1)}, bf16[2,136,128]{2,1,0:T(8,128)(2,1)S(1)}, u32[]{:S(2)}, u32[]{:S(2)}) collective-permute-start(bf16[2,136,128]{2,1,0:T(8,128)(2,1)S(1)} %get-tuple-element.27), channel_id=1, source_target_pairs={{0,1},{1,2},{2,3},{3,4},{4,5},{5,6},{6,7},{7,8},{8,9},{9,10},{10,1... | collective-permute-start | bytes 208904 | tf_op jit(solution)/shard_map/ppermute | solution.py:377
  56.0 1.3 collective-permute-start.2
  57.3 4.0 %collective-permute-done.2.p = bf16[2,128,128]{2,1,0:T(8,128)(2,1)S(1)} collective-permute-done((bf16[2,128,128]{2,1,0:T(8,128)(2,1)S(1)}, bf16[2,128,128]{2,1,0:T(8,128)(2,1)S(1)}, u32[]{:S(2)}, u32[]{:S(2)}) %collective-permute-start.2) | collective-permute-done | bytes 65568 | tf_op jit(solution)/shard_map/ppermute | solution.py:379
  61.3 2.0 %shard_map.85 = (f32[256,128]{1,0:T(8,128)S(1)}, f32[256,128]{1,0:T(8,128)S(1)}, bf16[4,256,128]{2,1,0:T(8,128)(2,1)S(1)}) custom-call(s32[130]{0:T(256)S(1)} %pad_add_fusion.t_ref, f32[512,128]{1,0:T(8,128)S(1)} %bitcast.26, f32[512,128]{1,0:T(8,128)S(1)} %bitcast.28, bf16[2,136,128]{2,1,0:T(8,128)(2,1)S(1)} %collective-permute-done.b, ...), custom_call_target="tpu_custom_call" | custom-call | flops 1310720 | bytes 1310720 | tf_op jit(solution)/shard_map/pallas_call | solution.py:61
  63.3 4.5 %collective-permute-start.21 = (bf16[4,256,128]{2,1,0:T(8,128)(2,1)S(1)}, bf16[4,256,128]{2,1,0:T(8,128)(2,1)S(1)}, u32[]{:S(2)}, u32[]{:S(2)}) collective-permute-start(bf16[4,256,128]{2,1,0:T(8,128)(2,1)S(1)} %get-tuple-element.45.refs_0_), channel_id=1, source_target_pairs={{0,32},{1,33},{2,34},{3,35},{4,36},{5,37},{6,38},{7,39},{8,40},{9,... | collective-permute-start | bytes 786440 | tf_op jit(solution)/shard_map/ppermute | solution.py:39
  67.8 1.0 collective-permute-start.20
  68.8 1.9 %collective-permute-start.19 = (bf16[4,256,128]{2,1,0:T(8,128)(2,1)S(1)}, bf16[4,256,128]{2,1,0:T(8,128)(2,1)S(1)}, u32[]{:S(2)}, u32[]{:S(2)}) collective-permute-start(bf16[4,256,128]{2,1,0:T(8,128)(2,1)S(1)} %get-tuple-element.45.refs_0_), channel_id=1, source_target_pairs={{0,96},{1,97},{2,98},{3,99},{4,100},{5,101},{6,102},{7,103},{8,104... | collective-permute-start | bytes 786440 | tf_op jit(solution)/shard_map/ppermute | solution.py:39
  70.7 1.4 shard_map.95
  72.1 6.8 %all-to-all-start = ((f32[32,8,128]{2,1,0:T(8,128)}), f32[32,8,128]{2,1,0:T(8,128)S(1)}, u32[]{:S(2)}, u32[]{:S(2)}) async-start(f32[32,8,128]{2,1,0:T(8,128)} %get-tuple-element.46), calls=%async_computation | async-start | bytes 262144 | tf_op jit(solution)/shard_map/all_to_all | solution.py:401
  78.9 1.8 %collective-permute-done.20.refs_2_ = bf16[4,256,128]{2,1,0:T(8,128)(2,1)S(1)} collective-permute-done((bf16[4,256,128]{2,1,0:T(8,128)(2,1)S(1)}, bf16[4,256,128]{2,1,0:T(8,128)(2,1)S(1)}, u32[]{:S(2)}, u32[]{:S(2)}) %collective-permute-start.20) | collective-permute-done | bytes 262176 | tf_op jit(solution)/shard_map/ppermute | solution.py:39
  80.7 5.8 %all-to-all-done.refs_4_ = f32[32,8,128]{2,1,0:T(8,128)S(1)} async-done(((f32[32,8,128]{2,1,0:T(8,128)}), f32[32,8,128]{2,1,0:T(8,128)S(1)}, u32[]{:S(2)}, u32[]{:S(2)}) %all-to-all-start) | async-done | bytes 131104 | tf_op jit(solution)/shard_map/all_to_all | solution.py:401
  86.5 1.8 %shard_map.96 = (bf16[4,256,128]{2,1,0:T(8,128)(2,1)S(1)}, f32[8,128]{1,0:T(8,128)S(1)}) custom-call(s32[1]{0:T(128)} %constant.166.clone.1.t_ref, f32[4,256,128]{2,1,0:T(8,128)S(1)} %get-tuple-element.44.g, bf16[4,256,128]{2,1,0:T(8,128)(2,1)S(1)} %get-tuple-element.45.refs_0_, bf16[4,256,128]{2,1,0:T(8,128)(2,1)S(1)} %collective-permute-done.19.refs_1_, ...), custom_call_target="tpu_custom_call" | custom-call | flops 2621440 | bytes 1835008 | tf_op jit(solution)/shard_map/pallas_call | solution.py:61
  88.7 1.8 %collective-permute-start.25 = (bf16[4,256,128]{2,1,0:T(8,128)(2,1)S(1)}, bf16[4,256,128]{2,1,0:T(8,128)(2,1)S(1)}, u32[]{:S(2)}, u32[]{:S(2)}) collective-permute-start(bf16[4,256,128]{2,1,0:T(8,128)(2,1)S(1)} %get-tuple-element.49.a), channel_id=1, source_target_pairs={{0,16},{1,5},{2,18},{3,7},{4,20},{5,1},{6,22},{7,3},{8,24},{9,13},... | collective-permute-start | bytes 786440 | tf_op jit(solution)/shard_map/ppermute | solution.py:39
  90.5 0.7 collective-permute-start.22
  91.2 6.7 %collective-permute-done.28.refs_2_ = bf16[4,256,128]{2,1,0:T(8,128)(2,1)S(1)} collective-permute-done((bf16[4,256,128]{2,1,0:T(8,128)(2,1)S(1)}, bf16[4,256,128]{2,1,0:T(8,128)(2,1)S(1)}, u32[]{:S(2)}, u32[]{:S(2)}) %collective-permute-start.28) | collective-permute-done | bytes 262176 | tf_op jit(solution)/shard_map/ppermute | solution.py:39
  97.9 1.3 collective-permute-start.39
  99.2 2.7 %collective-permute-start.29 = (bf16[4,256,128]{2,1,0:T(8,128)(2,1)S(1)}, bf16[4,256,128]{2,1,0:T(8,128)(2,1)S(1)}, u32[]{:S(2)}, u32[]{:S(2)}) collective-permute-start(bf16[4,256,128]{2,1,0:T(8,128)(2,1)S(1)} %collective-permute-done.28.refs_2_), channel_id=1, source_target_pairs={{0,6},{1,25},{2,0},{3,27},{4,2},{5,29},{6,4},{7,31},{8,14},{9,1},{... | collective-permute-start | bytes 786440 | tf_op jit(solution)/shard_map/ppermute | solution.py:39
  102.8 3.1 %collective-permute-done.35.refs_5_ = bf16[4,256,128]{2,1,0:T(8,128)(2,1)S(1)} collective-permute-done((bf16[4,256,128]{2,1,0:T(8,128)(2,1)S(1)}, bf16[4,256,128]{2,1,0:T(8,128)(2,1)S(1)}, u32[]{:S(2)}, u32[]{:S(2)}) %collective-permute-start.35) | collective-permute-done | bytes 262176 | tf_op jit(solution)/shard_map/ppermute | solution.py:39
  105.9 0.9 collective-permute-start.42
  106.9 8.1 %collective-permute-done.34.refs_4_ = bf16[4,256,128]{2,1,0:T(8,128)(2,1)S(1)} collective-permute-done((bf16[4,256,128]{2,1,0:T(8,128)(2,1)S(1)}, bf16[4,256,128]{2,1,0:T(8,128)(2,1)S(1)}, u32[]{:S(2)}, u32[]{:S(2)}) %collective-permute-start.34) | collective-permute-done | bytes 262176 | tf_op jit(solution)/shard_map/ppermute | solution.py:39
  115.0 0.9 collective-permute-start.41
  116.1 1.4 collective-permute-start.24
  117.5 3.1 %collective-permute-done.30.refs_2_ = bf16[4,256,128]{2,1,0:T(8,128)(2,1)S(1)} collective-permute-done((bf16[4,256,128]{2,1,0:T(8,128)(2,1)S(1)}, bf16[4,256,128]{2,1,0:T(8,128)(2,1)S(1)}, u32[]{:S(2)}, u32[]{:S(2)}) %collective-permute-start.30) | collective-permute-done | bytes 262176 | tf_op jit(solution)/shard_map/ppermute | solution.py:39
  120.6 1.7 %collective-permute-start.44 = (bf16[4,256,128]{2,1,0:T(8,128)(2,1)S(1)}, bf16[4,256,128]{2,1,0:T(8,128)(2,1)S(1)}, u32[]{:S(2)}, u32[]{:S(2)}) collective-permute-start(bf16[4,256,128]{2,1,0:T(8,128)(2,1)S(1)} %collective-permute-done.26.refs_7_), channel_id=1, source_target_pairs={{0,1},{1,0},{2,3},{3,2},{4,5},{5,4},{6,7},{7,6},{8,9},{9,8},{10,11... | collective-permute-start | bytes 786440 | tf_op jit(solution)/shard_map/ppermute | solution.py:39
  124.0 5.0 %collective-permute-done.27.refs_1_ = bf16[4,256,128]{2,1,0:T(8,128)(2,1)S(1)} collective-permute-done((bf16[4,256,128]{2,1,0:T(8,128)(2,1)S(1)}, bf16[4,256,128]{2,1,0:T(8,128)(2,1)S(1)}, u32[]{:S(2)}, u32[]{:S(2)}) %collective-permute-start.27) | collective-permute-done | bytes 262176 | tf_op jit(solution)/shard_map/ppermute | solution.py:39
  129.0 1.7 %collective-permute-start.33 = (bf16[4,256,128]{2,1,0:T(8,128)(2,1)S(1)}, bf16[4,256,128]{2,1,0:T(8,128)(2,1)S(1)}, u32[]{:S(2)}, u32[]{:S(2)}) collective-permute-start(bf16[4,256,128]{2,1,0:T(8,128)(2,1)S(1)} %collective-permute-done.30.refs_2_), channel_id=1, source_target_pairs={{0,1},{1,0},{2,3},{3,2},{4,5},{5,4},{6,7},{7,6},{8,9},{9,8},{10,11... | collective-permute-start | bytes 786440 | tf_op jit(solution)/shard_map/ppermute | solution.py:39
  131.3 1.5 %fusion.1 = (f32[32768]{0:T(1024)}, f32[32768]{0:T(1024)}, f32[32768]{0:T(1024)}) fusion(f32[4,256,128]{2,1,0:T(8,128)S(1)} %get-tuple-element.44.g, f32[]{:T(128)} %bitcast.5, f32[256,128]{1,0:T(8,128)S(1)} %get-tuple-element.48, f32[256,128]{1,0:T(8,128)S(1)} %get-tuple-element.29, f32[32768]{0:T(1024)S(1)} %copy-done.2), kind=kLoop, calls=%fused_computation.6 | loop fusion | flops 491520 | bytes 917508 | tf_op jit(solution)/shard_map/reshape | solution.py:404
  133.0 4.0 %shard_map.98.refs_6_ = bf16[128,256,128]{2,1,0:T(8,128)(2,1)} custom-call(s32[128]{0:T(128)S(1)} %compare_select_fusion.16.t_ref, bf16[8,256,128]{2,1,0:T(8,128)(2,1)S(1)} %shard_map.97.refs_0_, bf16[4,256,128]{2,1,0:T(8,128)(2,1)S(1)} %collective-permute-done.25.refs_1_, bf16[4,256,128]{2,1,0:T(8,128)(2,1)S(1)} %collective-permute-done.28.refs_2_, ...), custom_call_target="tpu_custom_call" | custom-call | flops 12582912 | bytes 12582912 | tf_op jit(solution)/shard_map/pallas_call | solution.py:61
  137.0 2.1 %shard_map.99 = bf16[128,256,128]{2,1,0:T(8,128)(2,1)} custom-call(s32[128]{0:T(128)S(1)} %compare_select_fusion.16.t_ref, bf16[8,256,128]{2,1,0:T(8,128)(2,1)S(1)} %collective-permute-done.24.refs_0_, bf16[4,256,128]{2,1,0:T(8,128)(2,1)S(1)} %collective-permute-done.27.refs_1_, ...), custom_call_target="tpu_custom_call", output_to_operand_aliasing={{}: (7, {})} | custom-call | flops 4194304 | bytes 4194304 | tf_op jit(solution)/shard_map/pallas_call | solution.py:61
  (74 shorter events, 9.0 us)
Async XLA Ops:
  4.6 7.3 %collective-permute-start.5 = (bf16[16,256,128]{2,1,0:T(8,128)(2,1)S(1)}, bf16[16,256,128]{2,1,0:T(8,128)(2,1)S(1)}, u32[]{:S(2)}, u32[]{:S(2)}) collective-permute-start(bf16[16,256,128]{2,1,0:T(8,128)(2,1)S(1)} %get-tuple-element.35), channel_id=1, source_target_pairs={{0,1},{1,0},{2,3},{3,2},{4,5},{5,4},{6,7},{7,6},{8,9},{9,8},{10,11... | collective-permute-start | bytes 3145736 | tf_op jit(solution)/shard_map/ppermute | solution.py:39
  6.0 10.6 %collective-permute-start.9 = (bf16[16,256,128]{2,1,0:T(8,128)(2,1)S(1)}, bf16[16,256,128]{2,1,0:T(8,128)(2,1)S(1)}, u32[]{:S(2)}, u32[]{:S(2)}) collective-permute-start(bf16[16,256,128]{2,1,0:T(8,128)(2,1)S(1)} %get-tuple-element.38), channel_id=1, source_target_pairs={{0,1},{1,0},{2,3},{3,2},{4,5},{5,4},{6,7},{7,6},{8,9},{9,8},{10,11... | collective-permute-start | bytes 3145736 | tf_op jit(solution)/shard_map/ppermute | solution.py:39
  6.1 11.2 %collective-permute-start.4 = (bf16[16,256,128]{2,1,0:T(8,128)(2,1)S(1)}, bf16[16,256,128]{2,1,0:T(8,128)(2,1)S(1)}, u32[]{:S(2)}, u32[]{:S(2)}) collective-permute-start(bf16[16,256,128]{2,1,0:T(8,128)(2,1)S(1)} %get-tuple-element.33), channel_id=1, source_target_pairs={{0,1},{1,0},{2,3},{3,2},{4,5},{5,4},{6,7},{7,6},{8,9},{9,8},{10,11... | collective-permute-start | bytes 3145736 | tf_op jit(solution)/shard_map/ppermute | solution.py:39
  12.1 9.8 %collective-permute-start.6 = (bf16[8,256,128]{2,1,0:T(8,128)(2,1)S(1)}, bf16[8,256,128]{2,1,0:T(8,128)(2,1)S(1)}, u32[]{:S(2)}, u32[]{:S(2)}) collective-permute-start(bf16[8,256,128]{2,1,0:T(8,128)(2,1)S(1)} %get-tuple-element.36), channel_id=1, source_target_pairs={{0,2},{1,9},{2,4},{3,11},{4,6},{5,13},{6,0},{7,15},{8,10},{9,17},{... | collective-permute-start | bytes 1572872 | tf_op jit(solution)/shard_map/ppermute | solution.py:39
  13.6 12.8 %collective-permute-start.3 = (bf16[16,256,128]{2,1,0:T(8,128)(2,1)S(1)}, bf16[16,256,128]{2,1,0:T(8,128)(2,1)S(1)}, u32[]{:S(2)}, u32[]{:S(2)}) collective-permute-start(bf16[16,256,128]{2,1,0:T(8,128)(2,1)S(1)} %get-tuple-element.31), channel_id=1, source_target_pairs={{0,1},{1,0},{2,3},{3,2},{4,5},{5,4},{6,7},{7,6},{8,9},{9,8},{10,11... | collective-permute-start | bytes 3145736 | tf_op jit(solution)/shard_map/ppermute | solution.py:39
  13.9 8.9 %collective-permute-start.11 = (bf16[8,256,128]{2,1,0:T(8,128)(2,1)S(1)}, bf16[8,256,128]{2,1,0:T(8,128)(2,1)S(1)}, u32[]{:S(2)}, u32[]{:S(2)}) collective-permute-start(bf16[8,256,128]{2,1,0:T(8,128)(2,1)S(1)} %get-tuple-element.39), channel_id=1, source_target_pairs={{0,6},{1,25},{2,0},{3,27},{4,2},{5,29},{6,4},{7,31},{8,14},{9,1},{... | collective-permute-start | bytes 1572872 | tf_op jit(solution)/shard_map/ppermute | solution.py:39
  16.7 11.6 %collective-permute-start.10 = (bf16[8,256,128]{2,1,0:T(8,128)(2,1)S(1)}, bf16[8,256,128]{2,1,0:T(8,128)(2,1)S(1)}, u32[]{:S(2)}, u32[]{:S(2)}) collective-permute-start(bf16[8,256,128]{2,1,0:T(8,128)(2,1)S(1)} %shard_map.91), channel_id=1, source_target_pairs={{0,6},{1,25},{2,0},{3,27},{4,2},{5,29},{6,4},{7,31},{8,14},{9,1},{... | collective-permute-start | bytes 1572872 | tf_op jit(solution)/shard_map/ppermute | solution.py:39
  17.4 11.0 %collective-permute-start.8 = (bf16[8,256,128]{2,1,0:T(8,128)(2,1)S(1)}, bf16[8,256,128]{2,1,0:T(8,128)(2,1)S(1)}, u32[]{:S(2)}, u32[]{:S(2)}) collective-permute-start(bf16[8,256,128]{2,1,0:T(8,128)(2,1)S(1)} %shard_map.90), channel_id=1, source_target_pairs={{0,2},{1,9},{2,4},{3,11},{4,6},{5,13},{6,0},{7,15},{8,10},{9,17},{... | collective-permute-start | bytes 1572872 | tf_op jit(solution)/shard_map/ppermute | solution.py:39
  22.1 11.0 %collective-permute-start.7 = (bf16[8,256,128]{2,1,0:T(8,128)(2,1)S(1)}, bf16[8,256,128]{2,1,0:T(8,128)(2,1)S(1)}, u32[]{:S(2)}, u32[]{:S(2)}) collective-permute-start(bf16[8,256,128]{2,1,0:T(8,128)(2,1)S(1)} %shard_map.89), channel_id=1, source_target_pairs={{0,2},{1,9},{2,4},{3,11},{4,6},{5,13},{6,0},{7,15},{8,10},{9,17},{... | collective-permute-start | bytes 1572872 | tf_op jit(solution)/shard_map/ppermute | solution.py:39
  23.0 11.0 %collective-permute-start.12 = (bf16[8,256,128]{2,1,0:T(8,128)(2,1)S(1)}, bf16[8,256,128]{2,1,0:T(8,128)(2,1)S(1)}, u32[]{:S(2)}, u32[]{:S(2)}) collective-permute-start(bf16[8,256,128]{2,1,0:T(8,128)(2,1)S(1)} %shard_map.92), channel_id=1, source_target_pairs={{0,6},{1,25},{2,0},{3,27},{4,2},{5,29},{6,4},{7,31},{8,14},{9,1},{... | collective-permute-start | bytes 1572872 | tf_op jit(solution)/shard_map/ppermute | solution.py:39
  34.6 26.7 %copy-start.2 = (f32[32768]{0:T(1024)S(1)}, f32[32768]{0:T(1024)}, u32[]{:S(2)}) copy-start(f32[32768]{0:T(1024)} %param.6) | copy-start | bytes 393220
  34.6 6.8 %collective-permute-start.13 = (bf16[4,256,128]{2,1,0:T(8,128)(2,1)S(1)}, bf16[4,256,128]{2,1,0:T(8,128)(2,1)S(1)}, u32[]{:S(2)}, u32[]{:S(2)}) collective-permute-start(bf16[4,256,128]{2,1,0:T(8,128)(2,1)S(1)} %get-tuple-element.41), channel_id=1, source_target_pairs={{0,8},{1,3},{2,10},{3,5},{4,12},{5,7},{6,14},{7,1},{8,16},{9,11},{... | collective-permute-start | bytes 786440 | tf_op jit(solution)/shard_map/ppermute | solution.py:39
  35.9 8.5 %collective-permute-start.14 = (bf16[4,256,128]{2,1,0:T(8,128)(2,1)S(1)}, bf16[4,256,128]{2,1,0:T(8,128)(2,1)S(1)}, u32[]{:S(2)}, u32[]{:S(2)}) collective-permute-start(bf16[4,256,128]{2,1,0:T(8,128)(2,1)S(1)} %get-tuple-element.42), channel_id=1, source_target_pairs={{0,16},{1,5},{2,18},{3,7},{4,20},{5,1},{6,22},{7,3},{8,24},{9,13},... | collective-permute-start | bytes 786440 | tf_op jit(solution)/shard_map/ppermute | solution.py:39
  37.5 7.3 %collective-permute-start.15 = (bf16[4,256,128]{2,1,0:T(8,128)(2,1)S(1)}, bf16[4,256,128]{2,1,0:T(8,128)(2,1)S(1)}, u32[]{:S(2)}, u32[]{:S(2)}) collective-permute-start(bf16[4,256,128]{2,1,0:T(8,128)(2,1)S(1)} %get-tuple-element.43), channel_id=1, source_target_pairs={{0,24},{1,7},{2,26},{3,1},{4,28},{5,3},{6,30},{7,5},{8,0},{9,15},{... | collective-permute-start | bytes 786440 | tf_op jit(solution)/shard_map/ppermute | solution.py:39
  44.9 23.9 %collective-permute-start.18 = (bf16[4,256,128]{2,1,0:T(8,128)(2,1)S(1)}, bf16[4,256,128]{2,1,0:T(8,128)(2,1)S(1)}, u32[]{:S(2)}, u32[]{:S(2)}) collective-permute-start(bf16[4,256,128]{2,1,0:T(8,128)(2,1)S(1)} %shard_map.94.w), channel_id=1, source_target_pairs={{0,96},{1,97},{2,98},{3,99},{4,100},{5,101},{6,102},{7,103},{8,104... | collective-permute-start | bytes 786440 | tf_op jit(solution)/shard_map/ppermute | solution.py:39
  49.4 6.6 %collective-permute-start.1 = (bf16[2,128,128]{2,1,0:T(8,128)(2,1)S(1)}, bf16[2,128,128]{2,1,0:T(8,128)(2,1)S(1)}, u32[]{:S(2)}, u32[]{:S(2)}) collective-permute-start(bf16[2,128,128]{2,1,0:T(8,128)(2,1)S(1)} %get-tuple-element.28), channel_id=1, source_target_pairs={{0,1},{1,0},{2,3},{3,2},{4,5},{5,4},{6,7},{7,6},{8,9},{9,8},{10,11... | collective-permute-start | bytes 196616 | tf_op jit(solution)/shard_map/ppermute | solution.py:39
  51.7 19.0 %collective-permute-start.17 = (bf16[4,256,128]{2,1,0:T(8,128)(2,1)S(1)}, bf16[4,256,128]{2,1,0:T(8,128)(2,1)S(1)}, u32[]{:S(2)}, u32[]{:S(2)}) collective-permute-start(bf16[4,256,128]{2,1,0:T(8,128)(2,1)S(1)} %shard_map.94.w), channel_id=1, source_target_pairs={{0,64},{1,65},{2,66},{3,67},{4,68},{5,69},{6,70},{7,71},{8,72},{9,... | collective-permute-start | bytes 786440 | tf_op jit(solution)/shard_map/ppermute | solution.py:39
  51.7 19.0 %collective-permute-start.16 = (bf16[4,256,128]{2,1,0:T(8,128)(2,1)S(1)}, bf16[4,256,128]{2,1,0:T(8,128)(2,1)S(1)}, u32[]{:S(2)}, u32[]{:S(2)}) collective-permute-start(bf16[4,256,128]{2,1,0:T(8,128)(2,1)S(1)} %shard_map.94.w), channel_id=1, source_target_pairs={{0,32},{1,33},{2,34},{3,35},{4,36},{5,37},{6,38},{7,39},{8,40},{9,... | collective-permute-start | bytes 786440 | tf_op jit(solution)/shard_map/ppermute | solution.py:39
  52.4 4.9 %collective-permute-start = (bf16[2,136,128]{2,1,0:T(8,128)(2,1)S(1)}, bf16[2,136,128]{2,1,0:T(8,128)(2,1)S(1)}, u32[]{:S(2)}, u32[]{:S(2)}) collective-permute-start(bf16[2,136,128]{2,1,0:T(8,128)(2,1)S(1)} %get-tuple-element.27), channel_id=1, source_target_pairs={{0,1},{1,2},{2,3},{3,4},{4,5},{5,6},{6,7},{7,8},{8,9},{9,10},{10,1... | collective-permute-start | bytes 208904 | tf_op jit(solution)/shard_map/ppermute | solution.py:377
  56.0 5.3 %collective-permute-start.2 = (bf16[2,128,128]{2,1,0:T(8,128)(2,1)S(1)}, bf16[2,128,128]{2,1,0:T(8,128)(2,1)S(1)}, u32[]{:S(2)}, u32[]{:S(2)}) collective-permute-start(bf16[2,128,128]{2,1,0:T(8,128)(2,1)S(1)} %collective-permute-done.1.a), channel_id=1, source_target_pairs={{3,1},{5,3},{7,5},{9,7},{11,9},{13,11},{15,13},{17,15},{19,17},{21... | collective-permute-start | bytes 196616 | tf_op jit(solution)/shard_map/ppermute | solution.py:379
  63.3 15.6 %collective-permute-start.21 = (bf16[4,256,128]{2,1,0:T(8,128)(2,1)S(1)}, bf16[4,256,128]{2,1,0:T(8,128)(2,1)S(1)}, u32[]{:S(2)}, u32[]{:S(2)}) collective-permute-start(bf16[4,256,128]{2,1,0:T(8,128)(2,1)S(1)} %get-tuple-element.45.refs_0_), channel_id=1, source_target_pairs={{0,32},{1,33},{2,34},{3,35},{4,36},{5,37},{6,38},{7,39},{8,40},{9,... | collective-permute-start | bytes 786440 | tf_op jit(solution)/shard_map/ppermute | solution.py:39
  67.8 12.9 %collective-permute-start.20 = (bf16[4,256,128]{2,1,0:T(8,128)(2,1)S(1)}, bf16[4,256,128]{2,1,0:T(8,128)(2,1)S(1)}, u32[]{:S(2)}, u32[]{:S(2)}) collective-permute-start(bf16[4,256,128]{2,1,0:T(8,128)(2,1)S(1)} %get-tuple-element.45.refs_0_), channel_id=1, source_target_pairs={{0,64},{1,65},{2,66},{3,67},{4,68},{5,69},{6,70},{7,71},{8,72},{9,... | collective-permute-start | bytes 786440 | tf_op jit(solution)/shard_map/ppermute | solution.py:39
  68.8 11.9 %collective-permute-start.19 = (bf16[4,256,128]{2,1,0:T(8,128)(2,1)S(1)}, bf16[4,256,128]{2,1,0:T(8,128)(2,1)S(1)}, u32[]{:S(2)}, u32[]{:S(2)}) collective-permute-start(bf16[4,256,128]{2,1,0:T(8,128)(2,1)S(1)} %get-tuple-element.45.refs_0_), channel_id=1, source_target_pairs={{0,96},{1,97},{2,98},{3,99},{4,100},{5,101},{6,102},{7,103},{8,104... | collective-permute-start | bytes 786440 | tf_op jit(solution)/shard_map/ppermute | solution.py:39
  72.1 14.5 %all-to-all-start = ((f32[32,8,128]{2,1,0:T(8,128)}), f32[32,8,128]{2,1,0:T(8,128)S(1)}, u32[]{:S(2)}, u32[]{:S(2)}) async-start(f32[32,8,128]{2,1,0:T(8,128)} %get-tuple-element.46), calls=%async_computation | async-start | bytes 262144 | tf_op jit(solution)/shard_map/all_to_all | solution.py:401
  88.3 9.6 %collective-permute-start.28 = (bf16[4,256,128]{2,1,0:T(8,128)(2,1)S(1)}, bf16[4,256,128]{2,1,0:T(8,128)(2,1)S(1)}, u32[]{:S(2)}, u32[]{:S(2)}) collective-permute-start(bf16[4,256,128]{2,1,0:T(8,128)(2,1)S(1)} %get-tuple-element.49.a), channel_id=1, source_target_pairs={{0,8},{1,3},{2,10},{3,5},{4,12},{5,7},{6,14},{7,1},{8,16},{9,11},{... | collective-permute-start | bytes 786440 | tf_op jit(solution)/shard_map/ppermute | solution.py:39
  88.7 13.1 %collective-permute-start.25 = (bf16[4,256,128]{2,1,0:T(8,128)(2,1)S(1)}, bf16[4,256,128]{2,1,0:T(8,128)(2,1)S(1)}, u32[]{:S(2)}, u32[]{:S(2)}) collective-permute-start(bf16[4,256,128]{2,1,0:T(8,128)(2,1)S(1)} %get-tuple-element.49.a), channel_id=1, source_target_pairs={{0,16},{1,5},{2,18},{3,7},{4,20},{5,1},{6,22},{7,3},{8,24},{9,13},... | collective-permute-start | bytes 786440 | tf_op jit(solution)/shard_map/ppermute | solution.py:39
  90.5 11.9 %collective-permute-start.22 = (bf16[4,256,128]{2,1,0:T(8,128)(2,1)S(1)}, bf16[4,256,128]{2,1,0:T(8,128)(2,1)S(1)}, u32[]{:S(2)}, u32[]{:S(2)}) collective-permute-start(bf16[4,256,128]{2,1,0:T(8,128)(2,1)S(1)} %get-tuple-element.49.a), channel_id=1, source_target_pairs={{0,24},{1,7},{2,26},{3,1},{4,28},{5,3},{6,30},{7,5},{8,0},{9,15},{... | collective-permute-start | bytes 786440 | tf_op jit(solution)/shard_map/ppermute | solution.py:39
  97.9 4.8 %collective-permute-start.39 = (bf16[4,256,128]{2,1,0:T(8,128)(2,1)S(1)}, bf16[4,256,128]{2,1,0:T(8,128)(2,1)S(1)}, u32[]{:S(2)}, u32[]{:S(2)}) collective-permute-start(bf16[4,256,128]{2,1,0:T(8,128)(2,1)S(1)} %collective-permute-done.28.refs_2_), channel_id=1, source_target_pairs={{0,1},{1,0},{2,3},{3,2},{4,5},{5,4},{6,7},{7,6},{8,9},{9,8},{10,11... | collective-permute-start | bytes 786440 | tf_op jit(solution)/shard_map/ppermute | solution.py:39
  99.2 6.7 %collective-permute-start.35 = (bf16[4,256,128]{2,1,0:T(8,128)(2,1)S(1)}, bf16[4,256,128]{2,1,0:T(8,128)(2,1)S(1)}, u32[]{:S(2)}, u32[]{:S(2)}) collective-permute-start(bf16[4,256,128]{2,1,0:T(8,128)(2,1)S(1)} %collective-permute-done.28.refs_2_), channel_id=1, source_target_pairs={{0,2},{1,9},{2,4},{3,11},{4,6},{5,13},{6,0},{7,15},{8,10},{9,17},{... | collective-permute-start | bytes 786440 | tf_op jit(solution)/shard_map/ppermute | solution.py:39
  99.2 6.7 %collective-permute-start.29 = (bf16[4,256,128]{2,1,0:T(8,128)(2,1)S(1)}, bf16[4,256,128]{2,1,0:T(8,128)(2,1)S(1)}, u32[]{:S(2)}, u32[]{:S(2)}) collective-permute-start(bf16[4,256,128]{2,1,0:T(8,128)(2,1)S(1)} %collective-permute-done.28.refs_2_), channel_id=1, source_target_pairs={{0,6},{1,25},{2,0},{3,27},{4,2},{5,29},{6,4},{7,31},{8,14},{9,1},{... | collective-permute-start | bytes 786440 | tf_op jit(solution)/shard_map/ppermute | solution.py:39
  101.8 5.0 %collective-permute-start.38 = (bf16[4,256,128]{2,1,0:T(8,128)(2,1)S(1)}, bf16[4,256,128]{2,1,0:T(8,128)(2,1)S(1)}, u32[]{:S(2)}, u32[]{:S(2)}) collective-permute-start(bf16[4,256,128]{2,1,0:T(8,128)(2,1)S(1)} %collective-permute-done.25.refs_1_), channel_id=1, source_target_pairs={{0,1},{1,0},{2,3},{3,2},{4,5},{5,4},{6,7},{7,6},{8,9},{9,8},{10,11... | collective-permute-start | bytes 786440 | tf_op jit(solution)/shard_map/ppermute | solution.py:39
  102.4 13.7 %collective-permute-start.23 = (bf16[8,256,128]{2,1,0:T(8,128)(2,1)S(1)}, bf16[8,256,128]{2,1,0:T(8,128)(2,1)S(1)}, u32[]{:S(2)}, u32[]{:S(2)}) collective-permute-start(bf16[8,256,128]{2,1,0:T(8,128)(2,1)S(1)} %shard_map.97.refs_0_), channel_id=1, source_target_pairs={{0,2},{1,9},{2,4},{3,11},{4,6},{5,13},{6,0},{7,15},{8,10},{9,17},{... | collective-permute-start | bytes 1572872 | tf_op jit(solution)/shard_map/ppermute | solution.py:39
  102.7 12.3 %collective-permute-start.34 = (bf16[4,256,128]{2,1,0:T(8,128)(2,1)S(1)}, bf16[4,256,128]{2,1,0:T(8,128)(2,1)S(1)}, u32[]{:S(2)}, u32[]{:S(2)}) collective-permute-start(bf16[4,256,128]{2,1,0:T(8,128)(2,1)S(1)} %collective-permute-done.25.refs_1_), channel_id=1, source_target_pairs={{0,2},{1,9},{2,4},{3,11},{4,6},{5,13},{6,0},{7,15},{8,10},{9,17},{... | collective-permute-start | bytes 786440 | tf_op jit(solution)/shard_map/ppermute | solution.py:39
  105.9 9.2 %collective-permute-start.26 = (bf16[4,256,128]{2,1,0:T(8,128)(2,1)S(1)}, bf16[4,256,128]{2,1,0:T(8,128)(2,1)S(1)}, u32[]{:S(2)}, u32[]{:S(2)}) collective-permute-start(bf16[4,256,128]{2,1,0:T(8,128)(2,1)S(1)} %collective-permute-done.25.refs_1_), channel_id=1, source_target_pairs={{0,6},{1,25},{2,0},{3,27},{4,2},{5,29},{6,4},{7,31},{8,14},{9,1},{... | collective-permute-start | bytes 786440 | tf_op jit(solution)/shard_map/ppermute | solution.py:39
  105.9 10.0 %collective-permute-start.42 = (bf16[4,256,128]{2,1,0:T(8,128)(2,1)S(1)}, bf16[4,256,128]{2,1,0:T(8,128)(2,1)S(1)}, u32[]{:S(2)}, u32[]{:S(2)}) collective-permute-start(bf16[4,256,128]{2,1,0:T(8,128)(2,1)S(1)} %collective-permute-done.35.refs_5_), channel_id=1, source_target_pairs={{0,1},{1,0},{2,3},{3,2},{4,5},{5,4},{6,7},{7,6},{8,9},{9,8},{10,11... | collective-permute-start | bytes 786440 | tf_op jit(solution)/shard_map/ppermute | solution.py:39
  106.8 9.2 %collective-permute-start.45 = (bf16[4,256,128]{2,1,0:T(8,128)(2,1)S(1)}, bf16[4,256,128]{2,1,0:T(8,128)(2,1)S(1)}, u32[]{:S(2)}, u32[]{:S(2)}) collective-permute-start(bf16[4,256,128]{2,1,0:T(8,128)(2,1)S(1)} %collective-permute-done.29.refs_8_), channel_id=1, source_target_pairs={{0,1},{1,0},{2,3},{3,2},{4,5},{5,4},{6,7},{7,6},{8,9},{9,8},{10,11... | collective-permute-start | bytes 786440 | tf_op jit(solution)/shard_map/ppermute | solution.py:39
  115.0 5.5 %collective-permute-start.30 = (bf16[4,256,128]{2,1,0:T(8,128)(2,1)S(1)}, bf16[4,256,128]{2,1,0:T(8,128)(2,1)S(1)}, u32[]{:S(2)}, u32[]{:S(2)}) collective-permute-start(bf16[4,256,128]{2,1,0:T(8,128)(2,1)S(1)} %collective-permute-done.29.refs_8_), channel_id=1, source_target_pairs={{0,6},{1,25},{2,0},{3,27},{4,2},{5,29},{6,4},{7,31},{8,14},{9,1},{... | collective-permute-start | bytes 786440 | tf_op jit(solution)/shard_map/ppermute | solution.py:39
  115.0 7.2 %collective-permute-start.41 = (bf16[4,256,128]{2,1,0:T(8,128)(2,1)S(1)}, bf16[4,256,128]{2,1,0:T(8,128)(2,1)S(1)}, u32[]{:S(2)}, u32[]{:S(2)}) collective-permute-start(bf16[4,256,128]{2,1,0:T(8,128)(2,1)S(1)} %collective-permute-done.34.refs_4_), channel_id=1, source_target_pairs={{0,1},{1,0},{2,3},{3,2},{4,5},{5,4},{6,7},{7,6},{8,9},{9,8},{10,11... | collective-permute-start | bytes 786440 | tf_op jit(solution)/shard_map/ppermute | solution.py:39
  115.9 14.8 %collective-permute-start.37 = (bf16[8,256,128]{2,1,0:T(8,128)(2,1)S(1)}, bf16[8,256,128]{2,1,0:T(8,128)(2,1)S(1)}, u32[]{:S(2)}, u32[]{:S(2)}) collective-permute-start(bf16[8,256,128]{2,1,0:T(8,128)(2,1)S(1)} %shard_map.97.refs_0_), channel_id=1, source_target_pairs={{0,1},{1,0},{2,3},{3,2},{4,5},{5,4},{6,7},{7,6},{8,9},{9,8},{10,11... | collective-permute-start | bytes 1572872 | tf_op jit(solution)/shard_map/ppermute | solution.py:39
  116.0 14.7 %collective-permute-start.36 = (bf16[8,256,128]{2,1,0:T(8,128)(2,1)S(1)}, bf16[8,256,128]{2,1,0:T(8,128)(2,1)S(1)}, u32[]{:S(2)}, u32[]{:S(2)}) collective-permute-start(bf16[8,256,128]{2,1,0:T(8,128)(2,1)S(1)} %shard_map.97.refs_0_), channel_id=1, source_target_pairs={{0,6},{1,25},{2,0},{3,27},{4,2},{5,29},{6,4},{7,31},{8,14},{9,1},{... | collective-permute-start | bytes 1572872 | tf_op jit(solution)/shard_map/ppermute | solution.py:39
  116.1 15.1 %collective-permute-start.24 = (bf16[8,256,128]{2,1,0:T(8,128)(2,1)S(1)}, bf16[8,256,128]{2,1,0:T(8,128)(2,1)S(1)}, u32[]{:S(2)}, u32[]{:S(2)}) collective-permute-start(bf16[8,256,128]{2,1,0:T(8,128)(2,1)S(1)} %collective-permute-done.23.refs_3_), channel_id=1, source_target_pairs={{0,2},{1,9},{2,4},{3,11},{4,6},{5,13},{6,0},{7,15},{8,10},{9,17},{... | collective-permute-start | bytes 1572872 | tf_op jit(solution)/shard_map/ppermute | solution.py:39
  120.6 2.9 %collective-permute-start.44 = (bf16[4,256,128]{2,1,0:T(8,128)(2,1)S(1)}, bf16[4,256,128]{2,1,0:T(8,128)(2,1)S(1)}, u32[]{:S(2)}, u32[]{:S(2)}) collective-permute-start(bf16[4,256,128]{2,1,0:T(8,128)(2,1)S(1)} %collective-permute-done.26.refs_7_), channel_id=1, source_target_pairs={{0,1},{1,0},{2,3},{3,2},{4,5},{5,4},{6,7},{7,6},{8,9},{9,8},{10,11... | collective-permute-start | bytes 786440 | tf_op jit(solution)/shard_map/ppermute | solution.py:39
  122.3 6.7 %collective-permute-start.27 = (bf16[4,256,128]{2,1,0:T(8,128)(2,1)S(1)}, bf16[4,256,128]{2,1,0:T(8,128)(2,1)S(1)}, u32[]{:S(2)}, u32[]{:S(2)}) collective-permute-start(bf16[4,256,128]{2,1,0:T(8,128)(2,1)S(1)} %collective-permute-done.26.refs_7_), channel_id=1, source_target_pairs={{0,6},{1,25},{2,0},{3,27},{4,2},{5,29},{6,4},{7,31},{8,14},{9,1},{... | collective-permute-start | bytes 786440 | tf_op jit(solution)/shard_map/ppermute | solution.py:39
  123.4 9.6 %collective-permute-start.40 = (bf16[8,256,128]{2,1,0:T(8,128)(2,1)S(1)}, bf16[8,256,128]{2,1,0:T(8,128)(2,1)S(1)}, u32[]{:S(2)}, u32[]{:S(2)}) collective-permute-start(bf16[8,256,128]{2,1,0:T(8,128)(2,1)S(1)} %collective-permute-done.23.refs_3_), channel_id=1, source_target_pairs={{0,1},{1,0},{2,3},{3,2},{4,5},{5,4},{6,7},{7,6},{8,9},{9,8},{10,11... | collective-permute-start | bytes 1572872 | tf_op jit(solution)/shard_map/ppermute | solution.py:39
  129.0 8.0 %collective-permute-start.33 = (bf16[4,256,128]{2,1,0:T(8,128)(2,1)S(1)}, bf16[4,256,128]{2,1,0:T(8,128)(2,1)S(1)}, u32[]{:S(2)}, u32[]{:S(2)}) collective-permute-start(bf16[4,256,128]{2,1,0:T(8,128)(2,1)S(1)} %collective-permute-done.30.refs_2_), channel_id=1, source_target_pairs={{0,1},{1,0},{2,3},{3,2},{4,5},{5,4},{6,7},{7,6},{8,9},{9,8},{10,11... | collective-permute-start | bytes 786440 | tf_op jit(solution)/shard_map/ppermute | solution.py:39
  130.7 6.3 %collective-permute-start.32 = (bf16[4,256,128]{2,1,0:T(8,128)(2,1)S(1)}, bf16[4,256,128]{2,1,0:T(8,128)(2,1)S(1)}, u32[]{:S(2)}, u32[]{:S(2)}) collective-permute-start(bf16[4,256,128]{2,1,0:T(8,128)(2,1)S(1)} %collective-permute-done.27.refs_1_), channel_id=1, source_target_pairs={{0,1},{1,0},{2,3},{3,2},{4,5},{5,4},{6,7},{7,6},{8,9},{9,8},{10,11... | collective-permute-start | bytes 786440 | tf_op jit(solution)/shard_map/ppermute | solution.py:39
  130.7 2.3 %collective-permute-start.43 = (bf16[8,256,128]{2,1,0:T(8,128)(2,1)S(1)}, bf16[8,256,128]{2,1,0:T(8,128)(2,1)S(1)}, u32[]{:S(2)}, u32[]{:S(2)}) collective-permute-start(bf16[8,256,128]{2,1,0:T(8,128)(2,1)S(1)} %collective-permute-done.36.refs_6_), channel_id=1, source_target_pairs={{0,1},{1,0},{2,3},{3,2},{4,5},{5,4},{6,7},{7,6},{8,9},{9,8},{10,11... | collective-permute-start | bytes 1572872 | tf_op jit(solution)/shard_map/ppermute | solution.py:39
  131.2 5.8 %collective-permute-start.31 = (bf16[8,256,128]{2,1,0:T(8,128)(2,1)S(1)}, bf16[8,256,128]{2,1,0:T(8,128)(2,1)S(1)}, u32[]{:S(2)}, u32[]{:S(2)}) collective-permute-start(bf16[8,256,128]{2,1,0:T(8,128)(2,1)S(1)} %collective-permute-done.24.refs_0_), channel_id=1, source_target_pairs={{0,1},{1,0},{2,3},{3,2},{4,5},{5,4},{6,7},{7,6},{8,9},{9,8},{10,11... | collective-permute-start | bytes 1572872 | tf_op jit(solution)/shard_map/ppermute | solution.py:39
  (3 other events, 44.4 us)

commit v8 on v7

--- a/solution.py
+++ b/solution.py
@@ -209,7 +209,7 @@
         squares[...] = jnp.broadcast_to(jnp.sum(acc), squares.shape)
 
     size = n * rows * lanes
-    outs = [pltpu.VMEM((n, rows, lanes), F32), pltpu.VMEM((copies, 8, lanes), F32)]
+    outs = [pltpu.VMEM((n, rows, lanes), F32), pltpu.VMEM((copies, 1, lanes), F32)]
     return call(body, jnp.zeros((1,), jnp.int32), (own, from1, from2, from3), outs, [], 6 * size, 12 * size)
 
 
@@ -230,8 +230,8 @@
         for i in range(1, part.shape[0]):
             total = total + part[i]
         clip = jnp.minimum(1.0, jnp.sqrt(jnp.float32(flat)) / (jnp.sqrt(total) + 1e-06))
-        clip_ref[...] = clip
-        clip = jnp.concatenate([clip, clip])
+        clip_ref[...] = jnp.broadcast_to(clip, clip_ref.shape)
+        clip = jnp.broadcast_to(clip, (16, lanes))
         for r in range(n):
 
             @pl.loop(0, rows // 16)
@@ -347,11 +347,13 @@
     g = grads[0].reshape(128, rows, 128)
 
     given, kept, swapped = {}, {}, {}
-    given[2], given[1], given[3] = fetch(places, g, *((theirs[k], BF) for k in (2, 1, 3)))
-    for k in (2, 1, 3):
+    (given[2],) = fetch(places, g, (theirs[2], BF))
+    swapped[2] = send(given[2], "core")
+    kept[2], given[1], given[3] = fetch(places, g, (mine[2], F32), (theirs[1], BF), (theirs[3], BF))
+    for k in (1, 3):
         swapped[k] = send(given[k], "core")
-    kept[2], kept[1], kept[3], given[0], kept[0] = fetch(
-        places, g, (mine[2], F32), (mine[1], F32), (mine[3], F32), (theirs[0], BF), (mine[0], F32)
+    kept[1], kept[3], given[0], kept[0] = fetch(
+        places, g, (mine[1], F32), (mine[3], F32), (theirs[0], BF), (mine[0], F32)
     )
     swapped[0] = send(given[0], "core")
 

time: 140 us -> 142 us (1.014)
  waiting for transfers between devices: 55.4 us -> 57.1 us
  Pallas kernels: 22.6 us -> 24.1 us
    ppermute x44, waiting for transfers between devices: 45.6 us -> 55.6 us  [send(): return lax.ppermute(value, DP, perm(axis, s))]
    all_to_all x1, waiting for transfers between devices: 5.82 us -> 1.52 us  [step(): squares = lax.all_to_all(squares, ('y', 'x', 'core'), 0, 0, tiled=True)]
    ppermute x1, waiting for transfers between devices: 3.97 us -> 0.01 us  [step(): passed = lax.ppermute(after, DP, [(d, d - 2) for d in range(3, 128, 2)])]
    ppermute x44, starting transfers between devices: 46.4 us -> 49.5 us  [send(): return lax.ppermute(value, DP, perm(axis, s))]
    all_to_all x1, starting transfers between devices: 6.84 us -> 4.2 us  [step(): squares = lax.all_to_all(squares, ('y', 'x', 'core'), 0, 0, tiled=True)]
    ppermute x1, starting transfers between devices: 3.53 us -> 1.91 us  [step(): before = lax.ppermute(up, DP, [(d, d + 1) for d in range(127)])]
    pallas_call x16 -> x17, Pallas kernels: 22.6 us -> 24.1 us  [call(): pl.pallas_call(body, grid_spec=pltpu.PrefetchScalarGridSpec(num_scalar_pr...]
  transfers between devices with their start and end apart: 47 -> 47, of which waited for: 18 -> 18; matrix products, arithmetic and copies ran while one was open for 1% -> 1% of each run, Pallas kernels for 10% -> 12%
where the time goes in v8:
time: 142 us; the launch traced here: 141 us
  waiting for transfers between devices  57.1 us (40%)
  starting transfers between devices  56.9 us (40%)
  Pallas kernels  24.1 us (17%)
  other arithmetic  1.57 us (1%)
    ppermute x44, waiting for transfers between devices, send(): return lax.ppermute(value, DP, perm(axis, s))  55.6 us
    ppermute x44, starting transfers between devices, send(): return lax.ppermute(value, DP, perm(axis, s))  49.5 us
    pallas_call x17, Pallas kernels, call(): pl.pallas_call(body, grid_spec=pltpu.PrefetchScalarGridSpec(num_scalar_pr...  24.1 us
    all_to_all x1, starting transfers between devices, step(): squares = lax.all_to_all(squares, ('y', 'x', 'core'), 0, 0, tiled=True)  4.2 us
  transfers between devices with their start and end apart: 47, of which 18 were waited for; matrix products, arithmetic and copies ran while one was open for 1% of the time, Pallas kernels for 12%

profile of v8, /device:TPU:1, one launch (start us, length us, event | category | flops | bytes accessed | tf_op | source)
XLA Modules:
  0.0 141.3 jit_solution(13723173512545437958)
XLA Ops:
  0.7 2.3 %shard_map.88 = bf16[16,256,128]{2,1,0:T(8,128)(2,1)S(1)} custom-call(s32[128]{0:T(128)S(1)} %compare_select_fusion.16.t_ref, f32[128,256,128]{2,1,0:T(8,128)} %bitcast.30), custom_call_target="tpu_custom_call" | custom-call | flops 524288 | bytes 3145728 | tf_op jit(solution)/shard_map/pallas_call | solution.py:61
  3.0 1.5 %collective-permute-start.5 = (bf16[16,256,128]{2,1,0:T(8,128)(2,1)S(1)}, bf16[16,256,128]{2,1,0:T(8,128)(2,1)S(1)}, u32[]{:S(2)}, u32[]{:S(2)}) collective-permute-start(bf16[16,256,128]{2,1,0:T(8,128)(2,1)S(1)} %shard_map.88), channel_id=1, source_target_pairs={{0,1},{1,0},{2,3},{3,2},{4,5},{5,4},{6,7},{7,6},{8,9},{9,8},{10,11... | collective-permute-start | bytes 3145736 | tf_op jit(solution)/shard_map/ppermute | solution.py:39
  4.5 3.8 %shard_map.87 = (f32[16,256,128]{2,1,0:T(8,128)S(1)}, bf16[16,256,128]{2,1,0:T(8,128)(2,1)S(1)}, bf16[16,256,128]{2,1,0:T(8,128)(2,1)S(1)}) custom-call(s32[128]{0:T(128)S(1)} %compare_select_fusion.16.t_ref, f32[128,256,128]{2,1,0:T(8,128)} %bitcast.31), custom_call_target="tpu_custom_call" | custom-call | flops 1572864 | bytes 9437184 | tf_op jit(solution)/shard_map/pallas_call | solution.py:61
  8.9 4.6 %shard_map.86 = (f32[16,256,128]{2,1,0:T(8,128)S(1)}, f32[16,256,128]{2,1,0:T(8,128)S(1)}, bf16[16,256,128]{2,1,0:T(8,128)(2,1)S(1)}, f32[16,256,128]{2,1,0:T(8,128)S(1)}) custom-call(s32[128]{0:T(128)S(1)} %compare_select_fusion.16.t_ref, f32[128,256,128]{2,1,0:T(8,128)} %bitcast.32), custom_call_target="tpu_custom_call" | custom-call | flops 2097152 | bytes 12582912 | tf_op jit(solution)/shard_map/pallas_call | solution.py:61
  13.8 2.9 %collective-permute-start.11 = (bf16[8,256,128]{2,1,0:T(8,128)(2,1)S(1)}, bf16[8,256,128]{2,1,0:T(8,128)(2,1)S(1)}, u32[]{:S(2)}, u32[]{:S(2)}) collective-permute-start(bf16[8,256,128]{2,1,0:T(8,128)(2,1)S(1)} %get-tuple-element.37), channel_id=1, source_target_pairs={{0,6},{1,25},{2,0},{3,27},{4,2},{5,29},{6,4},{7,31},{8,14},{9,1},{... | collective-permute-start | bytes 1572872 | tf_op jit(solution)/shard_map/ppermute | solution.py:39
  16.8 1.3 collective-permute-start.6
  18.2 1.5 %collective-permute-start.10 = (bf16[8,256,128]{2,1,0:T(8,128)(2,1)S(1)}, bf16[8,256,128]{2,1,0:T(8,128)(2,1)S(1)}, u32[]{:S(2)}, u32[]{:S(2)}) collective-permute-start(bf16[8,256,128]{2,1,0:T(8,128)(2,1)S(1)} %shard_map.92), channel_id=1, source_target_pairs={{0,6},{1,25},{2,0},{3,27},{4,2},{5,29},{6,4},{7,31},{8,14},{9,1},{... | collective-permute-start | bytes 1572872 | tf_op jit(solution)/shard_map/ppermute | solution.py:39
  19.9 2.8 %collective-permute-done.11.refs_2_ = bf16[8,256,128]{2,1,0:T(8,128)(2,1)S(1)} collective-permute-done((bf16[8,256,128]{2,1,0:T(8,128)(2,1)S(1)}, bf16[8,256,128]{2,1,0:T(8,128)(2,1)S(1)}, u32[]{:S(2)}, u32[]{:S(2)}) %collective-permute-start.11) | collective-permute-done | bytes 524320 | tf_op jit(solution)/shard_map/ppermute | solution.py:39
  23.0 3.5 %collective-permute-start.12 = (bf16[8,256,128]{2,1,0:T(8,128)(2,1)S(1)}, bf16[8,256,128]{2,1,0:T(8,128)(2,1)S(1)}, u32[]{:S(2)}, u32[]{:S(2)}) collective-permute-start(bf16[8,256,128]{2,1,0:T(8,128)(2,1)S(1)} %shard_map.93), channel_id=1, source_target_pairs={{0,6},{1,25},{2,0},{3,27},{4,2},{5,29},{6,4},{7,31},{8,14},{9,1},{... | collective-permute-start | bytes 1572872 | tf_op jit(solution)/shard_map/ppermute | solution.py:39
  26.8 1.6 %collective-permute-done.10.refs_4_ = bf16[8,256,128]{2,1,0:T(8,128)(2,1)S(1)} collective-permute-done((bf16[8,256,128]{2,1,0:T(8,128)(2,1)S(1)}, bf16[8,256,128]{2,1,0:T(8,128)(2,1)S(1)}, u32[]{:S(2)}, u32[]{:S(2)}) %collective-permute-start.10) | collective-permute-done | bytes 524320 | tf_op jit(solution)/shard_map/ppermute | solution.py:39
  28.4 3.6 %collective-permute-done.8.refs_3_ = bf16[8,256,128]{2,1,0:T(8,128)(2,1)S(1)} collective-permute-done((bf16[8,256,128]{2,1,0:T(8,128)(2,1)S(1)}, bf16[8,256,128]{2,1,0:T(8,128)(2,1)S(1)}, u32[]{:S(2)}, u32[]{:S(2)}) %collective-permute-start.8) | collective-permute-done | bytes 524320 | tf_op jit(solution)/shard_map/ppermute | solution.py:39
  32.0 2.0 %collective-permute-done.12.refs_5_ = bf16[8,256,128]{2,1,0:T(8,128)(2,1)S(1)} collective-permute-done((bf16[8,256,128]{2,1,0:T(8,128)(2,1)S(1)}, bf16[8,256,128]{2,1,0:T(8,128)(2,1)S(1)}, u32[]{:S(2)}, u32[]{:S(2)}) %collective-permute-start.12) | collective-permute-done | bytes 524320 | tf_op jit(solution)/shard_map/ppermute | solution.py:39
  34.0 3.6 %collective-permute-done.7.refs_2_ = bf16[8,256,128]{2,1,0:T(8,128)(2,1)S(1)} collective-permute-done((bf16[8,256,128]{2,1,0:T(8,128)(2,1)S(1)}, bf16[8,256,128]{2,1,0:T(8,128)(2,1)S(1)}, u32[]{:S(2)}, u32[]{:S(2)}) %collective-permute-start.7) | collective-permute-done | bytes 524320 | tf_op jit(solution)/shard_map/ppermute | solution.py:39
  39.0 2.5 %collective-permute-start.14 = (bf16[4,256,128]{2,1,0:T(8,128)(2,1)S(1)}, bf16[4,256,128]{2,1,0:T(8,128)(2,1)S(1)}, u32[]{:S(2)}, u32[]{:S(2)}) collective-permute-start(bf16[4,256,128]{2,1,0:T(8,128)(2,1)S(1)} %get-tuple-element.40), channel_id=1, source_target_pairs={{0,16},{1,5},{2,18},{3,7},{4,20},{5,1},{6,22},{7,3},{8,24},{9,13},... | collective-permute-start | bytes 786440 | tf_op jit(solution)/shard_map/ppermute | solution.py:39
  41.5 1.2 collective-permute-start.15
  42.6 2.4 %collective-permute-done.13.refs_1_ = bf16[4,256,128]{2,1,0:T(8,128)(2,1)S(1)} collective-permute-done((bf16[4,256,128]{2,1,0:T(8,128)(2,1)S(1)}, bf16[4,256,128]{2,1,0:T(8,128)(2,1)S(1)}, u32[]{:S(2)}, u32[]{:S(2)}) %collective-permute-start.13) | collective-permute-done | bytes 262176 | tf_op jit(solution)/shard_map/ppermute | solution.py:39
  45.0 3.3 %collective-permute-done.14.refs_2_ = bf16[4,256,128]{2,1,0:T(8,128)(2,1)S(1)} collective-permute-done((bf16[4,256,128]{2,1,0:T(8,128)(2,1)S(1)}, bf16[4,256,128]{2,1,0:T(8,128)(2,1)S(1)}, u32[]{:S(2)}, u32[]{:S(2)}) %collective-permute-start.14) | collective-permute-done | bytes 262176 | tf_op jit(solution)/shard_map/ppermute | solution.py:39
  48.6 3.8 %collective-permute-start.18 = (bf16[4,256,128]{2,1,0:T(8,128)(2,1)S(1)}, bf16[4,256,128]{2,1,0:T(8,128)(2,1)S(1)}, u32[]{:S(2)}, u32[]{:S(2)}) collective-permute-start(bf16[4,256,128]{2,1,0:T(8,128)(2,1)S(1)} %shard_map.95.w), channel_id=1, source_target_pairs={{0,96},{1,97},{2,98},{3,99},{4,100},{5,101},{6,102},{7,103},{8,104... | collective-permute-start | bytes 786440 | tf_op jit(solution)/shard_map/ppermute | solution.py:39
  53.0 2.7 %collective-permute-start.1 = (bf16[2,128,128]{2,1,0:T(8,128)(2,1)S(1)}, bf16[2,128,128]{2,1,0:T(8,128)(2,1)S(1)}, u32[]{:S(2)}, u32[]{:S(2)}) collective-permute-start(bf16[2,128,128]{2,1,0:T(8,128)(2,1)S(1)} %get-tuple-element.27), channel_id=1, source_target_pairs={{0,1},{1,0},{2,3},{3,2},{4,5},{5,4},{6,7},{7,6},{8,9},{9,8},{10,11... | collective-permute-start | bytes 196616 | tf_op jit(solution)/shard_map/ppermute | solution.py:39
  55.7 1.9 %collective-permute-start = (bf16[2,136,128]{2,1,0:T(8,128)(2,1)S(1)}, bf16[2,136,128]{2,1,0:T(8,128)(2,1)S(1)}, u32[]{:S(2)}, u32[]{:S(2)}) collective-permute-start(bf16[2,136,128]{2,1,0:T(8,128)(2,1)S(1)} %get-tuple-element.26), channel_id=1, source_target_pairs={{0,1},{1,2},{2,3},{3,4},{4,5},{5,6},{6,7},{7,8},{8,9},{9,10},{10,1... | collective-permute-start | bytes 208904 | tf_op jit(solution)/shard_map/ppermute | solution.py:379
  57.6 1.3 collective-permute-start.2
  58.9 5.9 %collective-permute-start.17 = (bf16[4,256,128]{2,1,0:T(8,128)(2,1)S(1)}, bf16[4,256,128]{2,1,0:T(8,128)(2,1)S(1)}, u32[]{:S(2)}, u32[]{:S(2)}) collective-permute-start(bf16[4,256,128]{2,1,0:T(8,128)(2,1)S(1)} %shard_map.95.w), channel_id=1, source_target_pairs={{0,64},{1,65},{2,66},{3,67},{4,68},{5,69},{6,70},{7,71},{8,72},{9,... | collective-permute-start | bytes 786440 | tf_op jit(solution)/shard_map/ppermute | solution.py:39
  64.9 1.0 collective-permute-start.16
  65.9 2.0 %shard_map.85 = (f32[256,128]{1,0:T(8,128)S(1)}, f32[256,128]{1,0:T(8,128)S(1)}, bf16[4,256,128]{2,1,0:T(8,128)(2,1)S(1)}) custom-call(s32[130]{0:T(256)S(1)} %pad_add_fusion.t_ref, f32[512,128]{1,0:T(8,128)S(1)} %bitcast.26, f32[512,128]{1,0:T(8,128)S(1)} %bitcast.28, bf16[2,136,128]{2,1,0:T(8,128)(2,1)S(1)} %collective-permute-done.b, ...), custom_call_target="tpu_custom_call" | custom-call | flops 1310720 | bytes 1310720 | tf_op jit(solution)/shard_map/pallas_call | solution.py:61
  68.0 2.8 %collective-permute-start.20 = (bf16[4,256,128]{2,1,0:T(8,128)(2,1)S(1)}, bf16[4,256,128]{2,1,0:T(8,128)(2,1)S(1)}, u32[]{:S(2)}, u32[]{:S(2)}) collective-permute-start(bf16[4,256,128]{2,1,0:T(8,128)(2,1)S(1)} %get-tuple-element.43.refs_0_), channel_id=1, source_target_pairs={{0,64},{1,65},{2,66},{3,67},{4,68},{5,69},{6,70},{7,71},{8,72},{9,... | collective-permute-start | bytes 786440 | tf_op jit(solution)/shard_map/ppermute | solution.py:39
  70.9 1.1 collective-permute-start.19
  72.0 3.9 %collective-permute-done.16.x1 = bf16[4,256,128]{2,1,0:T(8,128)(2,1)S(1)} collective-permute-done((bf16[4,256,128]{2,1,0:T(8,128)(2,1)S(1)}, bf16[4,256,128]{2,1,0:T(8,128)(2,1)S(1)}, u32[]{:S(2)}, u32[]{:S(2)}) %collective-permute-start.16) | collective-permute-done | bytes 262176 | tf_op jit(solution)/shard_map/ppermute | solution.py:39
  75.9 1.3 shard_map.96
  77.2 4.2 %all-to-all-start = ((f32[32,1,128]{2,1,0:T(1,128)}), f32[32,1,128]{2,1,0:T(1,128)S(1)}, u32[]{:S(2)}, u32[]{:S(2)}) async-start(f32[32,1,128]{2,1,0:T(1,128)} %get-tuple-element.44), calls=%async_computation | async-start | bytes 32768 | tf_op jit(solution)/shard_map/all_to_all | solution.py:403
  81.4 5.4 %collective-permute-done.20.refs_2_ = bf16[4,256,128]{2,1,0:T(8,128)(2,1)S(1)} collective-permute-done((bf16[4,256,128]{2,1,0:T(8,128)(2,1)S(1)}, bf16[4,256,128]{2,1,0:T(8,128)(2,1)S(1)}, u32[]{:S(2)}, u32[]{:S(2)}) %collective-permute-start.20) | collective-permute-done | bytes 262176 | tf_op jit(solution)/shard_map/ppermute | solution.py:39
  86.8 1.5 %all-to-all-done.refs_4_ = f32[32,1,128]{2,1,0:T(1,128)S(1)} async-done(((f32[32,1,128]{2,1,0:T(1,128)}), f32[32,1,128]{2,1,0:T(1,128)S(1)}, u32[]{:S(2)}, u32[]{:S(2)}) %all-to-all-start) | async-done | bytes 16416 | tf_op jit(solution)/shard_map/all_to_all | solution.py:403
  88.3 1.8 %shard_map.97 = (bf16[4,256,128]{2,1,0:T(8,128)(2,1)S(1)}, f32[8,128]{1,0:T(8,128)S(1)}) custom-call(s32[1]{0:T(128)} %constant.166.clone.1.t_ref, f32[4,256,128]{2,1,0:T(8,128)S(1)} %get-tuple-element.42.g, bf16[4,256,128]{2,1,0:T(8,128)(2,1)S(1)} %get-tuple-element.43.refs_0_, bf16[4,256,128]{2,1,0:T(8,128)(2,1)S(1)} %collective-permute-done.19.refs_1_, ...), custom_call_target="tpu_custom_call" | custom-call | flops 2621440 | bytes 1835008 | tf_op jit(solution)/shard_map/pallas_call | solution.py:61
  90.5 1.8 %collective-permute-start.25 = (bf16[4,256,128]{2,1,0:T(8,128)(2,1)S(1)}, bf16[4,256,128]{2,1,0:T(8,128)(2,1)S(1)}, u32[]{:S(2)}, u32[]{:S(2)}) collective-permute-start(bf16[4,256,128]{2,1,0:T(8,128)(2,1)S(1)} %get-tuple-element.47.a), channel_id=1, source_target_pairs={{0,16},{1,5},{2,18},{3,7},{4,20},{5,1},{6,22},{7,3},{8,24},{9,13},... | collective-permute-start | bytes 786440 | tf_op jit(solution)/shard_map/ppermute | solution.py:39
  92.2 0.9 collective-permute-start.22
  93.1 6.6 %collective-permute-done.28.refs_2_ = bf16[4,256,128]{2,1,0:T(8,128)(2,1)S(1)} collective-permute-done((bf16[4,256,128]{2,1,0:T(8,128)(2,1)S(1)}, bf16[4,256,128]{2,1,0:T(8,128)(2,1)S(1)}, u32[]{:S(2)}, u32[]{:S(2)}) %collective-permute-start.28) | collective-permute-done | bytes 262176 | tf_op jit(solution)/shard_map/ppermute | solution.py:39
  99.7 1.5 %collective-permute-start.39 = (bf16[4,256,128]{2,1,0:T(8,128)(2,1)S(1)}, bf16[4,256,128]{2,1,0:T(8,128)(2,1)S(1)}, u32[]{:S(2)}, u32[]{:S(2)}) collective-permute-start(bf16[4,256,128]{2,1,0:T(8,128)(2,1)S(1)} %collective-permute-done.28.refs_2_), channel_id=1, source_target_pairs={{0,1},{1,0},{2,3},{3,2},{4,5},{5,4},{6,7},{7,6},{8,9},{9,8},{10,11... | collective-permute-start | bytes 786440 | tf_op jit(solution)/shard_map/ppermute | solution.py:39
  101.2 2.7 %collective-permute-start.29 = (bf16[4,256,128]{2,1,0:T(8,128)(2,1)S(1)}, bf16[4,256,128]{2,1,0:T(8,128)(2,1)S(1)}, u32[]{:S(2)}, u32[]{:S(2)}) collective-permute-start(bf16[4,256,128]{2,1,0:T(8,128)(2,1)S(1)} %collective-permute-done.28.refs_2_), channel_id=1, source_target_pairs={{0,6},{1,25},{2,0},{3,27},{4,2},{5,29},{6,4},{7,31},{8,14},{9,1},{... | collective-permute-start | bytes 786440 | tf_op jit(solution)/shard_map/ppermute | solution.py:39
  104.8 3.1 %collective-permute-done.35.refs_5_ = bf16[4,256,128]{2,1,0:T(8,128)(2,1)S(1)} collective-permute-done((bf16[4,256,128]{2,1,0:T(8,128)(2,1)S(1)}, bf16[4,256,128]{2,1,0:T(8,128)(2,1)S(1)}, u32[]{:S(2)}, u32[]{:S(2)}) %collective-permute-start.35) | collective-permute-done | bytes 262176 | tf_op jit(solution)/shard_map/ppermute | solution.py:39
  108.9 8.2 %collective-permute-done.34.refs_4_ = bf16[4,256,128]{2,1,0:T(8,128)(2,1)S(1)} collective-permute-done((bf16[4,256,128]{2,1,0:T(8,128)(2,1)S(1)}, bf16[4,256,128]{2,1,0:T(8,128)(2,1)S(1)}, u32[]{:S(2)}, u32[]{:S(2)}) %collective-permute-start.34) | collective-permute-done | bytes 262176 | tf_op jit(solution)/shard_map/ppermute | solution.py:39
  117.1 0.9 collective-permute-start.41
  118.1 1.5 %collective-permute-start.24 = (bf16[8,256,128]{2,1,0:T(8,128)(2,1)S(1)}, bf16[8,256,128]{2,1,0:T(8,128)(2,1)S(1)}, u32[]{:S(2)}, u32[]{:S(2)}) collective-permute-start(bf16[8,256,128]{2,1,0:T(8,128)(2,1)S(1)} %collective-permute-done.23.refs_3_), channel_id=1, source_target_pairs={{0,2},{1,9},{2,4},{3,11},{4,6},{5,13},{6,0},{7,15},{8,10},{9,17},{... | collective-permute-start | bytes 1572872 | tf_op jit(solution)/shard_map/ppermute | solution.py:39
  119.5 3.1 %collective-permute-done.30.refs_2_ = bf16[4,256,128]{2,1,0:T(8,128)(2,1)S(1)} collective-permute-done((bf16[4,256,128]{2,1,0:T(8,128)(2,1)S(1)}, bf16[4,256,128]{2,1,0:T(8,128)(2,1)S(1)}, u32[]{:S(2)}, u32[]{:S(2)}) %collective-permute-start.30) | collective-permute-done | bytes 262176 | tf_op jit(solution)/shard_map/ppermute | solution.py:39
  122.6 1.7 %collective-permute-start.44 = (bf16[4,256,128]{2,1,0:T(8,128)(2,1)S(1)}, bf16[4,256,128]{2,1,0:T(8,128)(2,1)S(1)}, u32[]{:S(2)}, u32[]{:S(2)}) collective-permute-start(bf16[4,256,128]{2,1,0:T(8,128)(2,1)S(1)} %collective-permute-done.26.refs_7_), channel_id=1, source_target_pairs={{0,1},{1,0},{2,3},{3,2},{4,5},{5,4},{6,7},{7,6},{8,9},{9,8},{10,11... | collective-permute-start | bytes 786440 | tf_op jit(solution)/shard_map/ppermute | solution.py:39
  126.1 5.0 %collective-permute-done.27.refs_1_ = bf16[4,256,128]{2,1,0:T(8,128)(2,1)S(1)} collective-permute-done((bf16[4,256,128]{2,1,0:T(8,128)(2,1)S(1)}, bf16[4,256,128]{2,1,0:T(8,128)(2,1)S(1)}, u32[]{:S(2)}, u32[]{:S(2)}) %collective-permute-start.27) | collective-permute-done | bytes 262176 | tf_op jit(solution)/shard_map/ppermute | solution.py:39
  131.0 1.7 %collective-permute-start.33 = (bf16[4,256,128]{2,1,0:T(8,128)(2,1)S(1)}, bf16[4,256,128]{2,1,0:T(8,128)(2,1)S(1)}, u32[]{:S(2)}, u32[]{:S(2)}) collective-permute-start(bf16[4,256,128]{2,1,0:T(8,128)(2,1)S(1)} %collective-permute-done.30.refs_2_), channel_id=1, source_target_pairs={{0,1},{1,0},{2,3},{3,2},{4,5},{5,4},{6,7},{7,6},{8,9},{9,8},{10,11... | collective-permute-start | bytes 786440 | tf_op jit(solution)/shard_map/ppermute | solution.py:39
  133.4 1.5 %fusion.1 = (f32[32768]{0:T(1024)}, f32[32768]{0:T(1024)}, f32[32768]{0:T(1024)}) fusion(f32[4,256,128]{2,1,0:T(8,128)S(1)} %get-tuple-element.42.g, f32[]{:T(128)} %bitcast.5, f32[256,128]{1,0:T(8,128)S(1)} %get-tuple-element.46, f32[256,128]{1,0:T(8,128)S(1)} %get-tuple-element.28, f32[32768]{0:T(1024)S(1)} %copy-done.2), kind=kLoop, calls=%fused_computation.6 | loop fusion | flops 491520 | bytes 917508 | tf_op jit(solution)/shard_map/reshape | solution.py:406
  135.0 4.0 %shard_map.99.refs_6_ = bf16[128,256,128]{2,1,0:T(8,128)(2,1)} custom-call(s32[128]{0:T(128)S(1)} %compare_select_fusion.16.t_ref, bf16[8,256,128]{2,1,0:T(8,128)(2,1)S(1)} %shard_map.98.refs_0_, bf16[4,256,128]{2,1,0:T(8,128)(2,1)S(1)} %collective-permute-done.25.refs_1_, bf16[4,256,128]{2,1,0:T(8,128)(2,1)S(1)} %collective-permute-done.28.refs_2_, ...), custom_call_target="tpu_custom_call" | custom-call | flops 12582912 | bytes 12582912 | tf_op jit(solution)/shard_map/pallas_call | solution.py:61
  139.1 2.1 %shard_map.100 = bf16[128,256,128]{2,1,0:T(8,128)(2,1)} custom-call(s32[128]{0:T(128)S(1)} %compare_select_fusion.16.t_ref, bf16[8,256,128]{2,1,0:T(8,128)(2,1)S(1)} %collective-permute-done.24.refs_0_, bf16[4,256,128]{2,1,0:T(8,128)(2,1)S(1)} %collective-permute-done.27.refs_1_, ...), custom_call_target="tpu_custom_call", output_to_operand_aliasing={{}: (7, {})} | custom-call | flops 4194304 | bytes 4194304 | tf_op jit(solution)/shard_map/pallas_call | solution.py:61
  (75 shorter events, 9.1 us)
Async XLA Ops:
  3.0 10.5 %collective-permute-start.5 = (bf16[16,256,128]{2,1,0:T(8,128)(2,1)S(1)}, bf16[16,256,128]{2,1,0:T(8,128)(2,1)S(1)}, u32[]{:S(2)}, u32[]{:S(2)}) collective-permute-start(bf16[16,256,128]{2,1,0:T(8,128)(2,1)S(1)} %shard_map.88), channel_id=1, source_target_pairs={{0,1},{1,0},{2,3},{3,2},{4,5},{5,4},{6,7},{7,6},{8,9},{9,8},{10,11... | collective-permute-start | bytes 3145736 | tf_op jit(solution)/shard_map/ppermute | solution.py:39
  8.3 9.8 %collective-permute-start.9 = (bf16[16,256,128]{2,1,0:T(8,128)(2,1)S(1)}, bf16[16,256,128]{2,1,0:T(8,128)(2,1)S(1)}, u32[]{:S(2)}, u32[]{:S(2)}) collective-permute-start(bf16[16,256,128]{2,1,0:T(8,128)(2,1)S(1)} %get-tuple-element.36), channel_id=1, source_target_pairs={{0,1},{1,0},{2,3},{3,2},{4,5},{5,4},{6,7},{7,6},{8,9},{9,8},{10,11... | collective-permute-start | bytes 3145736 | tf_op jit(solution)/shard_map/ppermute | solution.py:39
  8.4 11.3 %collective-permute-start.4 = (bf16[16,256,128]{2,1,0:T(8,128)(2,1)S(1)}, bf16[16,256,128]{2,1,0:T(8,128)(2,1)S(1)}, u32[]{:S(2)}, u32[]{:S(2)}) collective-permute-start(bf16[16,256,128]{2,1,0:T(8,128)(2,1)S(1)} %get-tuple-element.32), channel_id=1, source_target_pairs={{0,1},{1,0},{2,3},{3,2},{4,5},{5,4},{6,7},{7,6},{8,9},{9,8},{10,11... | collective-permute-start | bytes 3145736 | tf_op jit(solution)/shard_map/ppermute | solution.py:39
  13.8 9.0 %collective-permute-start.11 = (bf16[8,256,128]{2,1,0:T(8,128)(2,1)S(1)}, bf16[8,256,128]{2,1,0:T(8,128)(2,1)S(1)}, u32[]{:S(2)}, u32[]{:S(2)}) collective-permute-start(bf16[8,256,128]{2,1,0:T(8,128)(2,1)S(1)} %get-tuple-element.37), channel_id=1, source_target_pairs={{0,6},{1,25},{2,0},{3,27},{4,2},{5,29},{6,4},{7,31},{8,14},{9,1},{... | collective-permute-start | bytes 1572872 | tf_op jit(solution)/shard_map/ppermute | solution.py:39
  16.7 10.1 %collective-permute-start.3 = (bf16[16,256,128]{2,1,0:T(8,128)(2,1)S(1)}, bf16[16,256,128]{2,1,0:T(8,128)(2,1)S(1)}, u32[]{:S(2)}, u32[]{:S(2)}) collective-permute-start(bf16[16,256,128]{2,1,0:T(8,128)(2,1)S(1)} %get-tuple-element.30), channel_id=1, source_target_pairs={{0,1},{1,0},{2,3},{3,2},{4,5},{5,4},{6,7},{7,6},{8,9},{9,8},{10,11... | collective-permute-start | bytes 3145736 | tf_op jit(solution)/shard_map/ppermute | solution.py:39
  16.8 9.7 %collective-permute-start.6 = (bf16[8,256,128]{2,1,0:T(8,128)(2,1)S(1)}, bf16[8,256,128]{2,1,0:T(8,128)(2,1)S(1)}, u32[]{:S(2)}, u32[]{:S(2)}) collective-permute-start(bf16[8,256,128]{2,1,0:T(8,128)(2,1)S(1)} %get-tuple-element.34), channel_id=1, source_target_pairs={{0,2},{1,9},{2,4},{3,11},{4,6},{5,13},{6,0},{7,15},{8,10},{9,17},{... | collective-permute-start | bytes 1572872 | tf_op jit(solution)/shard_map/ppermute | solution.py:39
  18.2 10.2 %collective-permute-start.10 = (bf16[8,256,128]{2,1,0:T(8,128)(2,1)S(1)}, bf16[8,256,128]{2,1,0:T(8,128)(2,1)S(1)}, u32[]{:S(2)}, u32[]{:S(2)}) collective-permute-start(bf16[8,256,128]{2,1,0:T(8,128)(2,1)S(1)} %shard_map.92), channel_id=1, source_target_pairs={{0,6},{1,25},{2,0},{3,27},{4,2},{5,29},{6,4},{7,31},{8,14},{9,1},{... | collective-permute-start | bytes 1572872 | tf_op jit(solution)/shard_map/ppermute | solution.py:39
  19.9 12.1 %collective-permute-start.8 = (bf16[8,256,128]{2,1,0:T(8,128)(2,1)S(1)}, bf16[8,256,128]{2,1,0:T(8,128)(2,1)S(1)}, u32[]{:S(2)}, u32[]{:S(2)}) collective-permute-start(bf16[8,256,128]{2,1,0:T(8,128)(2,1)S(1)} %shard_map.91), channel_id=1, source_target_pairs={{0,2},{1,9},{2,4},{3,11},{4,6},{5,13},{6,0},{7,15},{8,10},{9,17},{... | collective-permute-start | bytes 1572872 | tf_op jit(solution)/shard_map/ppermute | solution.py:39
  23.0 11.0 %collective-permute-start.12 = (bf16[8,256,128]{2,1,0:T(8,128)(2,1)S(1)}, bf16[8,256,128]{2,1,0:T(8,128)(2,1)S(1)}, u32[]{:S(2)}, u32[]{:S(2)}) collective-permute-start(bf16[8,256,128]{2,1,0:T(8,128)(2,1)S(1)} %shard_map.93), channel_id=1, source_target_pairs={{0,6},{1,25},{2,0},{3,27},{4,2},{5,29},{6,4},{7,31},{8,14},{9,1},{... | collective-permute-start | bytes 1572872 | tf_op jit(solution)/shard_map/ppermute | solution.py:39
  26.7 10.9 %collective-permute-start.7 = (bf16[8,256,128]{2,1,0:T(8,128)(2,1)S(1)}, bf16[8,256,128]{2,1,0:T(8,128)(2,1)S(1)}, u32[]{:S(2)}, u32[]{:S(2)}) collective-permute-start(bf16[8,256,128]{2,1,0:T(8,128)(2,1)S(1)} %shard_map.90), channel_id=1, source_target_pairs={{0,2},{1,9},{2,4},{3,11},{4,6},{5,13},{6,0},{7,15},{8,10},{9,17},{... | collective-permute-start | bytes 1572872 | tf_op jit(solution)/shard_map/ppermute | solution.py:39
  38.2 27.7 %copy-start.2 = (f32[32768]{0:T(1024)S(1)}, f32[32768]{0:T(1024)}, u32[]{:S(2)}) copy-start(f32[32768]{0:T(1024)} %param.6) | copy-start | bytes 393220
  38.2 6.8 %collective-permute-start.13 = (bf16[4,256,128]{2,1,0:T(8,128)(2,1)S(1)}, bf16[4,256,128]{2,1,0:T(8,128)(2,1)S(1)}, u32[]{:S(2)}, u32[]{:S(2)}) collective-permute-start(bf16[4,256,128]{2,1,0:T(8,128)(2,1)S(1)} %get-tuple-element.39), channel_id=1, source_target_pairs={{0,8},{1,3},{2,10},{3,5},{4,12},{5,7},{6,14},{7,1},{8,16},{9,11},{... | collective-permute-start | bytes 786440 | tf_op jit(solution)/shard_map/ppermute | solution.py:39
  39.0 9.3 %collective-permute-start.14 = (bf16[4,256,128]{2,1,0:T(8,128)(2,1)S(1)}, bf16[4,256,128]{2,1,0:T(8,128)(2,1)S(1)}, u32[]{:S(2)}, u32[]{:S(2)}) collective-permute-start(bf16[4,256,128]{2,1,0:T(8,128)(2,1)S(1)} %get-tuple-element.40), channel_id=1, source_target_pairs={{0,16},{1,5},{2,18},{3,7},{4,20},{5,1},{6,22},{7,3},{8,24},{9,13},... | collective-permute-start | bytes 786440 | tf_op jit(solution)/shard_map/ppermute | solution.py:39
  41.5 6.9 %collective-permute-start.15 = (bf16[4,256,128]{2,1,0:T(8,128)(2,1)S(1)}, bf16[4,256,128]{2,1,0:T(8,128)(2,1)S(1)}, u32[]{:S(2)}, u32[]{:S(2)}) collective-permute-start(bf16[4,256,128]{2,1,0:T(8,128)(2,1)S(1)} %get-tuple-element.41), channel_id=1, source_target_pairs={{0,24},{1,7},{2,26},{3,1},{4,28},{5,3},{6,30},{7,5},{8,0},{9,15},{... | collective-permute-start | bytes 786440 | tf_op jit(solution)/shard_map/ppermute | solution.py:39
  48.6 22.3 %collective-permute-start.18 = (bf16[4,256,128]{2,1,0:T(8,128)(2,1)S(1)}, bf16[4,256,128]{2,1,0:T(8,128)(2,1)S(1)}, u32[]{:S(2)}, u32[]{:S(2)}) collective-permute-start(bf16[4,256,128]{2,1,0:T(8,128)(2,1)S(1)} %shard_map.95.w), channel_id=1, source_target_pairs={{0,96},{1,97},{2,98},{3,99},{4,100},{5,101},{6,102},{7,103},{8,104... | collective-permute-start | bytes 786440 | tf_op jit(solution)/shard_map/ppermute | solution.py:39
  53.0 4.6 %collective-permute-start.1 = (bf16[2,128,128]{2,1,0:T(8,128)(2,1)S(1)}, bf16[2,128,128]{2,1,0:T(8,128)(2,1)S(1)}, u32[]{:S(2)}, u32[]{:S(2)}) collective-permute-start(bf16[2,128,128]{2,1,0:T(8,128)(2,1)S(1)} %get-tuple-element.27), channel_id=1, source_target_pairs={{0,1},{1,0},{2,3},{3,2},{4,5},{5,4},{6,7},{7,6},{8,9},{9,8},{10,11... | collective-permute-start | bytes 196616 | tf_op jit(solution)/shard_map/ppermute | solution.py:39
  55.7 10.2 %collective-permute-start = (bf16[2,136,128]{2,1,0:T(8,128)(2,1)S(1)}, bf16[2,136,128]{2,1,0:T(8,128)(2,1)S(1)}, u32[]{:S(2)}, u32[]{:S(2)}) collective-permute-start(bf16[2,136,128]{2,1,0:T(8,128)(2,1)S(1)} %get-tuple-element.26), channel_id=1, source_target_pairs={{0,1},{1,2},{2,3},{3,4},{4,5},{5,6},{6,7},{7,8},{8,9},{9,10},{10,1... | collective-permute-start | bytes 208904 | tf_op jit(solution)/shard_map/ppermute | solution.py:379
  57.6 8.3 %collective-permute-start.2 = (bf16[2,128,128]{2,1,0:T(8,128)(2,1)S(1)}, bf16[2,128,128]{2,1,0:T(8,128)(2,1)S(1)}, u32[]{:S(2)}, u32[]{:S(2)}) collective-permute-start(bf16[2,128,128]{2,1,0:T(8,128)(2,1)S(1)} %collective-permute-done.1.a), channel_id=1, source_target_pairs={{3,1},{5,3},{7,5},{9,7},{11,9},{13,11},{15,13},{17,15},{19,17},{21... | collective-permute-start | bytes 196616 | tf_op jit(solution)/shard_map/ppermute | solution.py:381
  58.9 13.0 %collective-permute-start.17 = (bf16[4,256,128]{2,1,0:T(8,128)(2,1)S(1)}, bf16[4,256,128]{2,1,0:T(8,128)(2,1)S(1)}, u32[]{:S(2)}, u32[]{:S(2)}) collective-permute-start(bf16[4,256,128]{2,1,0:T(8,128)(2,1)S(1)} %shard_map.95.w), channel_id=1, source_target_pairs={{0,64},{1,65},{2,66},{3,67},{4,68},{5,69},{6,70},{7,71},{8,72},{9,... | collective-permute-start | bytes 786440 | tf_op jit(solution)/shard_map/ppermute | solution.py:39
  64.9 11.0 %collective-permute-start.16 = (bf16[4,256,128]{2,1,0:T(8,128)(2,1)S(1)}, bf16[4,256,128]{2,1,0:T(8,128)(2,1)S(1)}, u32[]{:S(2)}, u32[]{:S(2)}) collective-permute-start(bf16[4,256,128]{2,1,0:T(8,128)(2,1)S(1)} %shard_map.95.w), channel_id=1, source_target_pairs={{0,32},{1,33},{2,34},{3,35},{4,36},{5,37},{6,38},{7,39},{8,40},{9,... | collective-permute-start | bytes 786440 | tf_op jit(solution)/shard_map/ppermute | solution.py:39
  68.0 13.5 %collective-permute-start.21 = (bf16[4,256,128]{2,1,0:T(8,128)(2,1)S(1)}, bf16[4,256,128]{2,1,0:T(8,128)(2,1)S(1)}, u32[]{:S(2)}, u32[]{:S(2)}) collective-permute-start(bf16[4,256,128]{2,1,0:T(8,128)(2,1)S(1)} %get-tuple-element.43.refs_0_), channel_id=1, source_target_pairs={{0,32},{1,33},{2,34},{3,35},{4,36},{5,37},{6,38},{7,39},{8,40},{9,... | collective-permute-start | bytes 786440 | tf_op jit(solution)/shard_map/ppermute | solution.py:39
  68.0 18.7 %collective-permute-start.20 = (bf16[4,256,128]{2,1,0:T(8,128)(2,1)S(1)}, bf16[4,256,128]{2,1,0:T(8,128)(2,1)S(1)}, u32[]{:S(2)}, u32[]{:S(2)}) collective-permute-start(bf16[4,256,128]{2,1,0:T(8,128)(2,1)S(1)} %get-tuple-element.43.refs_0_), channel_id=1, source_target_pairs={{0,64},{1,65},{2,66},{3,67},{4,68},{5,69},{6,70},{7,71},{8,72},{9,... | collective-permute-start | bytes 786440 | tf_op jit(solution)/shard_map/ppermute | solution.py:39
  70.9 15.9 %collective-permute-start.19 = (bf16[4,256,128]{2,1,0:T(8,128)(2,1)S(1)}, bf16[4,256,128]{2,1,0:T(8,128)(2,1)S(1)}, u32[]{:S(2)}, u32[]{:S(2)}) collective-permute-start(bf16[4,256,128]{2,1,0:T(8,128)(2,1)S(1)} %get-tuple-element.43.refs_0_), channel_id=1, source_target_pairs={{0,96},{1,97},{2,98},{3,99},{4,100},{5,101},{6,102},{7,103},{8,104... | collective-permute-start | bytes 786440 | tf_op jit(solution)/shard_map/ppermute | solution.py:39
  77.2 11.1 %all-to-all-start = ((f32[32,1,128]{2,1,0:T(1,128)}), f32[32,1,128]{2,1,0:T(1,128)S(1)}, u32[]{:S(2)}, u32[]{:S(2)}) async-start(f32[32,1,128]{2,1,0:T(1,128)} %get-tuple-element.44), calls=%async_computation | async-start | bytes 32768 | tf_op jit(solution)/shard_map/all_to_all | solution.py:403
  90.1 9.6 %collective-permute-start.28 = (bf16[4,256,128]{2,1,0:T(8,128)(2,1)S(1)}, bf16[4,256,128]{2,1,0:T(8,128)(2,1)S(1)}, u32[]{:S(2)}, u32[]{:S(2)}) collective-permute-start(bf16[4,256,128]{2,1,0:T(8,128)(2,1)S(1)} %get-tuple-element.47.a), channel_id=1, source_target_pairs={{0,8},{1,3},{2,10},{3,5},{4,12},{5,7},{6,14},{7,1},{8,16},{9,11},{... | collective-permute-start | bytes 786440 | tf_op jit(solution)/shard_map/ppermute | solution.py:39
  90.5 13.4 %collective-permute-start.25 = (bf16[4,256,128]{2,1,0:T(8,128)(2,1)S(1)}, bf16[4,256,128]{2,1,0:T(8,128)(2,1)S(1)}, u32[]{:S(2)}, u32[]{:S(2)}) collective-permute-start(bf16[4,256,128]{2,1,0:T(8,128)(2,1)S(1)} %get-tuple-element.47.a), channel_id=1, source_target_pairs={{0,16},{1,5},{2,18},{3,7},{4,20},{5,1},{6,22},{7,3},{8,24},{9,13},... | collective-permute-start | bytes 786440 | tf_op jit(solution)/shard_map/ppermute | solution.py:39
  92.2 12.2 %collective-permute-start.22 = (bf16[4,256,128]{2,1,0:T(8,128)(2,1)S(1)}, bf16[4,256,128]{2,1,0:T(8,128)(2,1)S(1)}, u32[]{:S(2)}, u32[]{:S(2)}) collective-permute-start(bf16[4,256,128]{2,1,0:T(8,128)(2,1)S(1)} %get-tuple-element.47.a), channel_id=1, source_target_pairs={{0,24},{1,7},{2,26},{3,1},{4,28},{5,3},{6,30},{7,5},{8,0},{9,15},{... | collective-permute-start | bytes 786440 | tf_op jit(solution)/shard_map/ppermute | solution.py:39
  99.7 5.1 %collective-permute-start.39 = (bf16[4,256,128]{2,1,0:T(8,128)(2,1)S(1)}, bf16[4,256,128]{2,1,0:T(8,128)(2,1)S(1)}, u32[]{:S(2)}, u32[]{:S(2)}) collective-permute-start(bf16[4,256,128]{2,1,0:T(8,128)(2,1)S(1)} %collective-permute-done.28.refs_2_), channel_id=1, source_target_pairs={{0,1},{1,0},{2,3},{3,2},{4,5},{5,4},{6,7},{7,6},{8,9},{9,8},{10,11... | collective-permute-start | bytes 786440 | tf_op jit(solution)/shard_map/ppermute | solution.py:39
  101.2 6.7 %collective-permute-start.35 = (bf16[4,256,128]{2,1,0:T(8,128)(2,1)S(1)}, bf16[4,256,128]{2,1,0:T(8,128)(2,1)S(1)}, u32[]{:S(2)}, u32[]{:S(2)}) collective-permute-start(bf16[4,256,128]{2,1,0:T(8,128)(2,1)S(1)} %collective-permute-done.28.refs_2_), channel_id=1, source_target_pairs={{0,2},{1,9},{2,4},{3,11},{4,6},{5,13},{6,0},{7,15},{8,10},{9,17},{... | collective-permute-start | bytes 786440 | tf_op jit(solution)/shard_map/ppermute | solution.py:39
  101.2 6.7 %collective-permute-start.29 = (bf16[4,256,128]{2,1,0:T(8,128)(2,1)S(1)}, bf16[4,256,128]{2,1,0:T(8,128)(2,1)S(1)}, u32[]{:S(2)}, u32[]{:S(2)}) collective-permute-start(bf16[4,256,128]{2,1,0:T(8,128)(2,1)S(1)} %collective-permute-done.28.refs_2_), channel_id=1, source_target_pairs={{0,6},{1,25},{2,0},{3,27},{4,2},{5,29},{6,4},{7,31},{8,14},{9,1},{... | collective-permute-start | bytes 786440 | tf_op jit(solution)/shard_map/ppermute | solution.py:39
  103.9 4.9 %collective-permute-start.38 = (bf16[4,256,128]{2,1,0:T(8,128)(2,1)S(1)}, bf16[4,256,128]{2,1,0:T(8,128)(2,1)S(1)}, u32[]{:S(2)}, u32[]{:S(2)}) collective-permute-start(bf16[4,256,128]{2,1,0:T(8,128)(2,1)S(1)} %collective-permute-done.25.refs_1_), channel_id=1, source_target_pairs={{0,1},{1,0},{2,3},{3,2},{4,5},{5,4},{6,7},{7,6},{8,9},{9,8},{10,11... | collective-permute-start | bytes 786440 | tf_op jit(solution)/shard_map/ppermute | solution.py:39
  104.5 13.6 %collective-permute-start.23 = (bf16[8,256,128]{2,1,0:T(8,128)(2,1)S(1)}, bf16[8,256,128]{2,1,0:T(8,128)(2,1)S(1)}, u32[]{:S(2)}, u32[]{:S(2)}) collective-permute-start(bf16[8,256,128]{2,1,0:T(8,128)(2,1)S(1)} %shard_map.98.refs_0_), channel_id=1, source_target_pairs={{0,2},{1,9},{2,4},{3,11},{4,6},{5,13},{6,0},{7,15},{8,10},{9,17},{... | collective-permute-start | bytes 1572872 | tf_op jit(solution)/shard_map/ppermute | solution.py:39
  104.8 12.3 %collective-permute-start.34 = (bf16[4,256,128]{2,1,0:T(8,128)(2,1)S(1)}, bf16[4,256,128]{2,1,0:T(8,128)(2,1)S(1)}, u32[]{:S(2)}, u32[]{:S(2)}) collective-permute-start(bf16[4,256,128]{2,1,0:T(8,128)(2,1)S(1)} %collective-permute-done.25.refs_1_), channel_id=1, source_target_pairs={{0,2},{1,9},{2,4},{3,11},{4,6},{5,13},{6,0},{7,15},{8,10},{9,17},{... | collective-permute-start | bytes 786440 | tf_op jit(solution)/shard_map/ppermute | solution.py:39
  107.9 9.2 %collective-permute-start.26 = (bf16[4,256,128]{2,1,0:T(8,128)(2,1)S(1)}, bf16[4,256,128]{2,1,0:T(8,128)(2,1)S(1)}, u32[]{:S(2)}, u32[]{:S(2)}) collective-permute-start(bf16[4,256,128]{2,1,0:T(8,128)(2,1)S(1)} %collective-permute-done.25.refs_1_), channel_id=1, source_target_pairs={{0,6},{1,25},{2,0},{3,27},{4,2},{5,29},{6,4},{7,31},{8,14},{9,1},{... | collective-permute-start | bytes 786440 | tf_op jit(solution)/shard_map/ppermute | solution.py:39
  107.9 10.0 %collective-permute-start.42 = (bf16[4,256,128]{2,1,0:T(8,128)(2,1)S(1)}, bf16[4,256,128]{2,1,0:T(8,128)(2,1)S(1)}, u32[]{:S(2)}, u32[]{:S(2)}) collective-permute-start(bf16[4,256,128]{2,1,0:T(8,128)(2,1)S(1)} %collective-permute-done.35.refs_5_), channel_id=1, source_target_pairs={{0,1},{1,0},{2,3},{3,2},{4,5},{5,4},{6,7},{7,6},{8,9},{9,8},{10,11... | collective-permute-start | bytes 786440 | tf_op jit(solution)/shard_map/ppermute | solution.py:39
  108.8 9.3 %collective-permute-start.45 = (bf16[4,256,128]{2,1,0:T(8,128)(2,1)S(1)}, bf16[4,256,128]{2,1,0:T(8,128)(2,1)S(1)}, u32[]{:S(2)}, u32[]{:S(2)}) collective-permute-start(bf16[4,256,128]{2,1,0:T(8,128)(2,1)S(1)} %collective-permute-done.29.refs_8_), channel_id=1, source_target_pairs={{0,1},{1,0},{2,3},{3,2},{4,5},{5,4},{6,7},{7,6},{8,9},{9,8},{10,11... | collective-permute-start | bytes 786440 | tf_op jit(solution)/shard_map/ppermute | solution.py:39
  117.1 5.5 %collective-permute-start.30 = (bf16[4,256,128]{2,1,0:T(8,128)(2,1)S(1)}, bf16[4,256,128]{2,1,0:T(8,128)(2,1)S(1)}, u32[]{:S(2)}, u32[]{:S(2)}) collective-permute-start(bf16[4,256,128]{2,1,0:T(8,128)(2,1)S(1)} %collective-permute-done.29.refs_8_), channel_id=1, source_target_pairs={{0,6},{1,25},{2,0},{3,27},{4,2},{5,29},{6,4},{7,31},{8,14},{9,1},{... | collective-permute-start | bytes 786440 | tf_op jit(solution)/shard_map/ppermute | solution.py:39
  117.1 7.2 %collective-permute-start.41 = (bf16[4,256,128]{2,1,0:T(8,128)(2,1)S(1)}, bf16[4,256,128]{2,1,0:T(8,128)(2,1)S(1)}, u32[]{:S(2)}, u32[]{:S(2)}) collective-permute-start(bf16[4,256,128]{2,1,0:T(8,128)(2,1)S(1)} %collective-permute-done.34.refs_4_), channel_id=1, source_target_pairs={{0,1},{1,0},{2,3},{3,2},{4,5},{5,4},{6,7},{7,6},{8,9},{9,8},{10,11... | collective-permute-start | bytes 786440 | tf_op jit(solution)/shard_map/ppermute | solution.py:39
  118.0 14.8 %collective-permute-start.37 = (bf16[8,256,128]{2,1,0:T(8,128)(2,1)S(1)}, bf16[8,256,128]{2,1,0:T(8,128)(2,1)S(1)}, u32[]{:S(2)}, u32[]{:S(2)}) collective-permute-start(bf16[8,256,128]{2,1,0:T(8,128)(2,1)S(1)} %shard_map.98.refs_0_), channel_id=1, source_target_pairs={{0,1},{1,0},{2,3},{3,2},{4,5},{5,4},{6,7},{7,6},{8,9},{9,8},{10,11... | collective-permute-start | bytes 1572872 | tf_op jit(solution)/shard_map/ppermute | solution.py:39
  118.1 14.7 %collective-permute-start.36 = (bf16[8,256,128]{2,1,0:T(8,128)(2,1)S(1)}, bf16[8,256,128]{2,1,0:T(8,128)(2,1)S(1)}, u32[]{:S(2)}, u32[]{:S(2)}) collective-permute-start(bf16[8,256,128]{2,1,0:T(8,128)(2,1)S(1)} %shard_map.98.refs_0_), channel_id=1, source_target_pairs={{0,6},{1,25},{2,0},{3,27},{4,2},{5,29},{6,4},{7,31},{8,14},{9,1},{... | collective-permute-start | bytes 1572872 | tf_op jit(solution)/shard_map/ppermute | solution.py:39
  118.1 15.2 %collective-permute-start.24 = (bf16[8,256,128]{2,1,0:T(8,128)(2,1)S(1)}, bf16[8,256,128]{2,1,0:T(8,128)(2,1)S(1)}, u32[]{:S(2)}, u32[]{:S(2)}) collective-permute-start(bf16[8,256,128]{2,1,0:T(8,128)(2,1)S(1)} %collective-permute-done.23.refs_3_), channel_id=1, source_target_pairs={{0,2},{1,9},{2,4},{3,11},{4,6},{5,13},{6,0},{7,15},{8,10},{9,17},{... | collective-permute-start | bytes 1572872 | tf_op jit(solution)/shard_map/ppermute | solution.py:39
  122.6 2.9 %collective-permute-start.44 = (bf16[4,256,128]{2,1,0:T(8,128)(2,1)S(1)}, bf16[4,256,128]{2,1,0:T(8,128)(2,1)S(1)}, u32[]{:S(2)}, u32[]{:S(2)}) collective-permute-start(bf16[4,256,128]{2,1,0:T(8,128)(2,1)S(1)} %collective-permute-done.26.refs_7_), channel_id=1, source_target_pairs={{0,1},{1,0},{2,3},{3,2},{4,5},{5,4},{6,7},{7,6},{8,9},{9,8},{10,11... | collective-permute-start | bytes 786440 | tf_op jit(solution)/shard_map/ppermute | solution.py:39
  124.3 6.7 %collective-permute-start.27 = (bf16[4,256,128]{2,1,0:T(8,128)(2,1)S(1)}, bf16[4,256,128]{2,1,0:T(8,128)(2,1)S(1)}, u32[]{:S(2)}, u32[]{:S(2)}) collective-permute-start(bf16[4,256,128]{2,1,0:T(8,128)(2,1)S(1)} %collective-permute-done.26.refs_7_), channel_id=1, source_target_pairs={{0,6},{1,25},{2,0},{3,27},{4,2},{5,29},{6,4},{7,31},{8,14},{9,1},{... | collective-permute-start | bytes 786440 | tf_op jit(solution)/shard_map/ppermute | solution.py:39
  125.5 9.6 %collective-permute-start.40 = (bf16[8,256,128]{2,1,0:T(8,128)(2,1)S(1)}, bf16[8,256,128]{2,1,0:T(8,128)(2,1)S(1)}, u32[]{:S(2)}, u32[]{:S(2)}) collective-permute-start(bf16[8,256,128]{2,1,0:T(8,128)(2,1)S(1)} %collective-permute-done.23.refs_3_), channel_id=1, source_target_pairs={{0,1},{1,0},{2,3},{3,2},{4,5},{5,4},{6,7},{7,6},{8,9},{9,8},{10,11... | collective-permute-start | bytes 1572872 | tf_op jit(solution)/shard_map/ppermute | solution.py:39
  131.0 8.0 %collective-permute-start.33 = (bf16[4,256,128]{2,1,0:T(8,128)(2,1)S(1)}, bf16[4,256,128]{2,1,0:T(8,128)(2,1)S(1)}, u32[]{:S(2)}, u32[]{:S(2)}) collective-permute-start(bf16[4,256,128]{2,1,0:T(8,128)(2,1)S(1)} %collective-permute-done.30.refs_2_), channel_id=1, source_target_pairs={{0,1},{1,0},{2,3},{3,2},{4,5},{5,4},{6,7},{7,6},{8,9},{9,8},{10,11... | collective-permute-start | bytes 786440 | tf_op jit(solution)/shard_map/ppermute | solution.py:39
  132.7 6.3 %collective-permute-start.32 = (bf16[4,256,128]{2,1,0:T(8,128)(2,1)S(1)}, bf16[4,256,128]{2,1,0:T(8,128)(2,1)S(1)}, u32[]{:S(2)}, u32[]{:S(2)}) collective-permute-start(bf16[4,256,128]{2,1,0:T(8,128)(2,1)S(1)} %collective-permute-done.27.refs_1_), channel_id=1, source_target_pairs={{0,1},{1,0},{2,3},{3,2},{4,5},{5,4},{6,7},{7,6},{8,9},{9,8},{10,11... | collective-permute-start | bytes 786440 | tf_op jit(solution)/shard_map/ppermute | solution.py:39
  132.8 2.3 %collective-permute-start.43 = (bf16[8,256,128]{2,1,0:T(8,128)(2,1)S(1)}, bf16[8,256,128]{2,1,0:T(8,128)(2,1)S(1)}, u32[]{:S(2)}, u32[]{:S(2)}) collective-permute-start(bf16[8,256,128]{2,1,0:T(8,128)(2,1)S(1)} %collective-permute-done.36.refs_6_), channel_id=1, source_target_pairs={{0,1},{1,0},{2,3},{3,2},{4,5},{5,4},{6,7},{7,6},{8,9},{9,8},{10,11... | collective-permute-start | bytes 1572872 | tf_op jit(solution)/shard_map/ppermute | solution.py:39
  133.3 5.8 %collective-permute-start.31 = (bf16[8,256,128]{2,1,0:T(8,128)(2,1)S(1)}, bf16[8,256,128]{2,1,0:T(8,128)(2,1)S(1)}, u32[]{:S(2)}, u32[]{:S(2)}) collective-permute-start(bf16[8,256,128]{2,1,0:T(8,128)(2,1)S(1)} %collective-permute-done.24.refs_0_), channel_id=1, source_target_pairs={{0,1},{1,0},{2,3},{3,2},{4,5},{5,4},{6,7},{7,6},{8,9},{9,8},{10,11... | collective-permute-start | bytes 1572872 | tf_op jit(solution)/shard_map/ppermute | solution.py:39
  (3 other events, 44.4 us)

commit v9 on v6

--- a/solution.py
+++ b/solution.py
@@ -209,7 +209,7 @@
         squares[...] = jnp.broadcast_to(jnp.sum(acc), squares.shape)
 
     size = n * rows * lanes
-    outs = [pltpu.VMEM((n, rows, lanes), F32), pltpu.VMEM((copies, 8, lanes), F32)]
+    outs = [pltpu.VMEM((n, rows, lanes), F32), pltpu.VMEM((copies, 1, lanes), F32)]
     return call(body, jnp.zeros((1,), jnp.int32), (own, from1, from2, from3), outs, [], 6 * size, 12 * size)
 
 
@@ -230,8 +230,8 @@
         for i in range(1, part.shape[0]):
             total = total + part[i]
         clip = jnp.minimum(1.0, jnp.sqrt(jnp.float32(flat)) / (jnp.sqrt(total) + 1e-06))
-        clip_ref[...] = clip
-        clip = jnp.concatenate([clip, clip])
+        clip_ref[...] = jnp.broadcast_to(clip, clip_ref.shape)
+        clip = jnp.broadcast_to(clip, (16, lanes))
         for r in range(n):
 
             @pl.loop(0, rows // 16)

time: 136 us -> 136 us (level)
    ppermute x1, waiting for transfers between devices: 3.97 us -> 0.01 us  [step(): passed = lax.ppermute(after, DP, [(d, d - 2) for d in range(3, 128, 2)])]
    ppermute x37, starting transfers between devices: 48 us -> 51.1 us  [send(): return lax.ppermute(value, DP, perm(axis, s))]
    all_to_all x1, starting transfers between devices: 6.41 us -> 4.22 us  [step(): squares = lax.all_to_all(squares, ('y', 'x', 'core'), 0, 0, tiled=True)]
    all_to_all x1, waiting for transfers between devices: 2.91 us -> 4.91 us  [step(): squares = lax.all_to_all(squares, ('y', 'x', 'core'), 0, 0, tiled=True)]
    ppermute x37, waiting for transfers between devices: 43.7 us -> 45.1 us  [send(): return lax.ppermute(value, DP, perm(axis, s))]
where the time goes in v9:
time: 136 us
  starting transfers between devices  58.5 us (43%)
  waiting for transfers between devices  50.1 us (37%)
  Pallas kernels  23.8 us (18%)
  other arithmetic  1.57 us (1%)
    ppermute x37, starting transfers between devices, send(): return lax.ppermute(value, DP, perm(axis, s))  51.1 us
    ppermute x37, waiting for transfers between devices, send(): return lax.ppermute(value, DP, perm(axis, s))  45.1 us
    pallas_call x18, Pallas kernels, call(): pl.pallas_call(body, grid_spec=pltpu.PrefetchScalarGridSpec(num_scalar_pr...  23.8 us
    all_to_all x1, waiting for transfers between devices, step(): squares = lax.all_to_all(squares, ('y', 'x', 'core'), 0, 0, tiled=True)  4.91 us
    all_to_all x1, starting transfers between devices, step(): squares = lax.all_to_all(squares, ('y', 'x', 'core'), 0, 0, tiled=True)  4.22 us
  transfers between devices with their start and end apart: 40, of which 17 were waited for; matrix products, arithmetic and copies ran while one was open for 2% of the time, Pallas kernels for 11%

profile of v9, /device:TPU:1, one launch (start us, length us, event | category | flops | bytes accessed | tf_op | source)
XLA Modules:
  0.0 135.7 jit_solution(6719942649077430869)
XLA Ops:
  0.7 3.8 %shard_map.87 = (bf16[16,256,128]{2,1,0:T(8,128)(2,1)S(1)}, bf16[16,256,128]{2,1,0:T(8,128)(2,1)S(1)}, bf16[16,256,128]{2,1,0:T(8,128)(2,1)S(1)}) custom-call(s32[128]{0:T(128)S(1)} %compare_select_fusion.16.t_ref, f32[128,256,128]{2,1,0:T(8,128)} %bitcast.31), custom_call_target="tpu_custom_call" | custom-call | flops 1572864 | bytes 9437184 | tf_op jit(solution)/shard_map/pallas_call | solution.py:61
  4.6 1.5 %collective-permute-start.5 = (bf16[16,256,128]{2,1,0:T(8,128)(2,1)S(1)}, bf16[16,256,128]{2,1,0:T(8,128)(2,1)S(1)}, u32[]{:S(2)}, u32[]{:S(2)}) collective-permute-start(bf16[16,256,128]{2,1,0:T(8,128)(2,1)S(1)} %get-tuple-element.35), channel_id=1, source_target_pairs={{0,1},{1,0},{2,3},{3,2},{4,5},{5,4},{6,7},{7,6},{8,9},{9,8},{10,11... | collective-permute-start | bytes 3145736 | tf_op jit(solution)/shard_map/ppermute | solution.py:39
  6.5 5.3 %shard_map.86 = (f32[16,256,128]{2,1,0:T(8,128)S(1)}, f32[16,256,128]{2,1,0:T(8,128)S(1)}, f32[16,256,128]{2,1,0:T(8,128)S(1)}, bf16[16,256,128]{2,1,0:T(8,128)(2,1)S(1)}, f32[16,256,128]{2,1,0:T(8,128)S(1)}) custom-call(s32[128]{0:T(128)S(1)} %compare_select_fusion.16.t_ref, f32[128,256,128]{2,1,0:T(8,128)} %bitcast.32), custom_call_target="tpu_custom_call" | custom-call | flops 2621440 | bytes 15728640 | tf_op jit(solution)/shard_map/pallas_call | solution.py:61
  12.1 2.9 %collective-permute-start.11 = (bf16[8,256,128]{2,1,0:T(8,128)(2,1)S(1)}, bf16[8,256,128]{2,1,0:T(8,128)(2,1)S(1)}, u32[]{:S(2)}, u32[]{:S(2)}) collective-permute-start(bf16[8,256,128]{2,1,0:T(8,128)(2,1)S(1)} %get-tuple-element.39), channel_id=1, source_target_pairs={{0,6},{1,25},{2,0},{3,27},{4,2},{5,29},{6,4},{7,31},{8,14},{9,1},{... | collective-permute-start | bytes 1572872 | tf_op jit(solution)/shard_map/ppermute | solution.py:39
  15.2 1.3 collective-permute-start.6
  16.6 1.5 %collective-permute-start.10 = (bf16[8,256,128]{2,1,0:T(8,128)(2,1)S(1)}, bf16[8,256,128]{2,1,0:T(8,128)(2,1)S(1)}, u32[]{:S(2)}, u32[]{:S(2)}) collective-permute-start(bf16[8,256,128]{2,1,0:T(8,128)(2,1)S(1)} %shard_map.91), channel_id=1, source_target_pairs={{0,6},{1,25},{2,0},{3,27},{4,2},{5,29},{6,4},{7,31},{8,14},{9,1},{... | collective-permute-start | bytes 1572872 | tf_op jit(solution)/shard_map/ppermute | solution.py:39
  18.4 2.8 %collective-permute-done.11.refs_2_ = bf16[8,256,128]{2,1,0:T(8,128)(2,1)S(1)} collective-permute-done((bf16[8,256,128]{2,1,0:T(8,128)(2,1)S(1)}, bf16[8,256,128]{2,1,0:T(8,128)(2,1)S(1)}, u32[]{:S(2)}, u32[]{:S(2)}) %collective-permute-start.11) | collective-permute-done | bytes 524320 | tf_op jit(solution)/shard_map/ppermute | solution.py:39
  21.4 3.5 %collective-permute-start.12 = (bf16[8,256,128]{2,1,0:T(8,128)(2,1)S(1)}, bf16[8,256,128]{2,1,0:T(8,128)(2,1)S(1)}, u32[]{:S(2)}, u32[]{:S(2)}) collective-permute-start(bf16[8,256,128]{2,1,0:T(8,128)(2,1)S(1)} %shard_map.92), channel_id=1, source_target_pairs={{0,6},{1,25},{2,0},{3,27},{4,2},{5,29},{6,4},{7,31},{8,14},{9,1},{... | collective-permute-start | bytes 1572872 | tf_op jit(solution)/shard_map/ppermute | solution.py:39
  25.2 1.6 %collective-permute-done.10.refs_4_ = bf16[8,256,128]{2,1,0:T(8,128)(2,1)S(1)} collective-permute-done((bf16[8,256,128]{2,1,0:T(8,128)(2,1)S(1)}, bf16[8,256,128]{2,1,0:T(8,128)(2,1)S(1)}, u32[]{:S(2)}, u32[]{:S(2)}) %collective-permute-start.10) | collective-permute-done | bytes 524320 | tf_op jit(solution)/shard_map/ppermute | solution.py:39
  26.8 3.6 %collective-permute-done.8.refs_3_ = bf16[8,256,128]{2,1,0:T(8,128)(2,1)S(1)} collective-permute-done((bf16[8,256,128]{2,1,0:T(8,128)(2,1)S(1)}, bf16[8,256,128]{2,1,0:T(8,128)(2,1)S(1)}, u32[]{:S(2)}, u32[]{:S(2)}) %collective-permute-start.8) | collective-permute-done | bytes 524320 | tf_op jit(solution)/shard_map/ppermute | solution.py:39
  30.4 2.0 %collective-permute-done.12.refs_5_ = bf16[8,256,128]{2,1,0:T(8,128)(2,1)S(1)} collective-permute-done((bf16[8,256,128]{2,1,0:T(8,128)(2,1)S(1)}, bf16[8,256,128]{2,1,0:T(8,128)(2,1)S(1)}, u32[]{:S(2)}, u32[]{:S(2)}) %collective-permute-start.12) | collective-permute-done | bytes 524320 | tf_op jit(solution)/shard_map/ppermute | solution.py:39
  32.4 3.6 %collective-permute-done.7.refs_2_ = bf16[8,256,128]{2,1,0:T(8,128)(2,1)S(1)} collective-permute-done((bf16[8,256,128]{2,1,0:T(8,128)(2,1)S(1)}, bf16[8,256,128]{2,1,0:T(8,128)(2,1)S(1)}, u32[]{:S(2)}, u32[]{:S(2)}) %collective-permute-start.7) | collective-permute-done | bytes 524320 | tf_op jit(solution)/shard_map/ppermute | solution.py:39
  37.4 2.5 %collective-permute-start.14 = (bf16[4,256,128]{2,1,0:T(8,128)(2,1)S(1)}, bf16[4,256,128]{2,1,0:T(8,128)(2,1)S(1)}, u32[]{:S(2)}, u32[]{:S(2)}) collective-permute-start(bf16[4,256,128]{2,1,0:T(8,128)(2,1)S(1)} %get-tuple-element.42), channel_id=1, source_target_pairs={{0,16},{1,5},{2,18},{3,7},{4,20},{5,1},{6,22},{7,3},{8,24},{9,13},... | collective-permute-start | bytes 786440 | tf_op jit(solution)/shard_map/ppermute | solution.py:39
  39.8 1.2 collective-permute-start.15
  41.0 2.4 %collective-permute-done.13.refs_1_ = bf16[4,256,128]{2,1,0:T(8,128)(2,1)S(1)} collective-permute-done((bf16[4,256,128]{2,1,0:T(8,128)(2,1)S(1)}, bf16[4,256,128]{2,1,0:T(8,128)(2,1)S(1)}, u32[]{:S(2)}, u32[]{:S(2)}) %collective-permute-start.13) | collective-permute-done | bytes 262176 | tf_op jit(solution)/shard_map/ppermute | solution.py:39
  43.4 3.3 %collective-permute-done.14.refs_2_ = bf16[4,256,128]{2,1,0:T(8,128)(2,1)S(1)} collective-permute-done((bf16[4,256,128]{2,1,0:T(8,128)(2,1)S(1)}, bf16[4,256,128]{2,1,0:T(8,128)(2,1)S(1)}, u32[]{:S(2)}, u32[]{:S(2)}) %collective-permute-start.14) | collective-permute-done | bytes 262176 | tf_op jit(solution)/shard_map/ppermute | solution.py:39
  46.9 1.7 %collective-permute-start.16 = (bf16[4,256,128]{2,1,0:T(8,128)(2,1)S(1)}, bf16[4,256,128]{2,1,0:T(8,128)(2,1)S(1)}, u32[]{:S(2)}, u32[]{:S(2)}) collective-permute-start(bf16[4,256,128]{2,1,0:T(8,128)(2,1)S(1)} %shard_map.94.w), channel_id=1, source_target_pairs={{0,32},{1,33},{2,34},{3,35},{4,36},{5,37},{6,38},{7,39},{8,40},{9,... | collective-permute-start | bytes 786440 | tf_op jit(solution)/shard_map/ppermute | solution.py:39
  49.3 2.7 %collective-permute-start.1 = (bf16[2,128,128]{2,1,0:T(8,128)(2,1)S(1)}, bf16[2,128,128]{2,1,0:T(8,128)(2,1)S(1)}, u32[]{:S(2)}, u32[]{:S(2)}) collective-permute-start(bf16[2,128,128]{2,1,0:T(8,128)(2,1)S(1)} %get-tuple-element.28), channel_id=1, source_target_pairs={{0,1},{1,0},{2,3},{3,2},{4,5},{5,4},{6,7},{7,6},{8,9},{9,8},{10,11... | collective-permute-start | bytes 196616 | tf_op jit(solution)/shard_map/ppermute | solution.py:39
  52.0 1.9 %collective-permute-start = (bf16[2,136,128]{2,1,0:T(8,128)(2,1)S(1)}, bf16[2,136,128]{2,1,0:T(8,128)(2,1)S(1)}, u32[]{:S(2)}, u32[]{:S(2)}) collective-permute-start(bf16[2,136,128]{2,1,0:T(8,128)(2,1)S(1)} %get-tuple-element.27), channel_id=1, source_target_pairs={{0,1},{1,2},{2,3},{3,4},{4,5},{5,6},{6,7},{7,8},{8,9},{9,10},{10,1... | collective-permute-start | bytes 208904 | tf_op jit(solution)/shard_map/ppermute | solution.py:377
  53.9 1.3 collective-permute-start.2
  55.2 9.6 %collective-permute-start.17 = (bf16[4,256,128]{2,1,0:T(8,128)(2,1)S(1)}, bf16[4,256,128]{2,1,0:T(8,128)(2,1)S(1)}, u32[]{:S(2)}, u32[]{:S(2)}) collective-permute-start(bf16[4,256,128]{2,1,0:T(8,128)(2,1)S(1)} %shard_map.94.w), channel_id=1, source_target_pairs={{0,64},{1,65},{2,66},{3,67},{4,68},{5,69},{6,70},{7,71},{8,72},{9,... | collective-permute-start | bytes 786440 | tf_op jit(solution)/shard_map/ppermute | solution.py:39
  65.5 2.0 %shard_map.85 = (f32[256,128]{1,0:T(8,128)S(1)}, f32[256,128]{1,0:T(8,128)S(1)}, bf16[4,256,128]{2,1,0:T(8,128)(2,1)S(1)}) custom-call(s32[130]{0:T(256)S(1)} %pad_add_fusion.t_ref, f32[512,128]{1,0:T(8,128)S(1)} %bitcast.26, f32[512,128]{1,0:T(8,128)S(1)} %bitcast.28, bf16[2,136,128]{2,1,0:T(8,128)(2,1)S(1)} %collective-permute-done.b, ...), custom_call_target="tpu_custom_call" | custom-call | flops 1310720 | bytes 1310720 | tf_op jit(solution)/shard_map/pallas_call | solution.py:61
  67.6 2.5 %collective-permute-start.20 = (bf16[4,256,128]{2,1,0:T(8,128)(2,1)S(1)}, bf16[4,256,128]{2,1,0:T(8,128)(2,1)S(1)}, u32[]{:S(2)}, u32[]{:S(2)}) collective-permute-start(bf16[4,256,128]{2,1,0:T(8,128)(2,1)S(1)} %get-tuple-element.45.refs_0_), channel_id=1, source_target_pairs={{0,64},{1,65},{2,66},{3,67},{4,68},{5,69},{6,70},{7,71},{8,72},{9,... | collective-permute-start | bytes 786440 | tf_op jit(solution)/shard_map/ppermute | solution.py:39
  70.1 4.3 %collective-permute-done.18.x3 = bf16[4,256,128]{2,1,0:T(8,128)(2,1)S(1)} collective-permute-done((bf16[4,256,128]{2,1,0:T(8,128)(2,1)S(1)}, bf16[4,256,128]{2,1,0:T(8,128)(2,1)S(1)}, u32[]{:S(2)}, u32[]{:S(2)}) %collective-permute-start.18) | collective-permute-done | bytes 262176 | tf_op jit(solution)/shard_map/ppermute | solution.py:39
  74.4 1.3 shard_map.95
  75.8 4.2 %all-to-all-start = ((f32[32,1,128]{2,1,0:T(1,128)}), f32[32,1,128]{2,1,0:T(1,128)S(1)}, u32[]{:S(2)}, u32[]{:S(2)}) async-start(f32[32,1,128]{2,1,0:T(1,128)} %get-tuple-element.46), calls=%async_computation | async-start | bytes 32768 | tf_op jit(solution)/shard_map/all_to_all | solution.py:401
  80.0 2.0 %collective-permute-done.21.refs_3_ = bf16[4,256,128]{2,1,0:T(8,128)(2,1)S(1)} collective-permute-done((bf16[4,256,128]{2,1,0:T(8,128)(2,1)S(1)}, bf16[4,256,128]{2,1,0:T(8,128)(2,1)S(1)}, u32[]{:S(2)}, u32[]{:S(2)}) %collective-permute-start.21) | collective-permute-done | bytes 262176 | tf_op jit(solution)/shard_map/ppermute | solution.py:39
  82.0 4.9 %all-to-all-done.refs_4_ = f32[32,1,128]{2,1,0:T(1,128)S(1)} async-done(((f32[32,1,128]{2,1,0:T(1,128)}), f32[32,1,128]{2,1,0:T(1,128)S(1)}, u32[]{:S(2)}, u32[]{:S(2)}) %all-to-all-start) | async-done | bytes 16416 | tf_op jit(solution)/shard_map/all_to_all | solution.py:401
  86.9 1.8 %shard_map.96 = (bf16[4,256,128]{2,1,0:T(8,128)(2,1)S(1)}, f32[8,128]{1,0:T(8,128)S(1)}) custom-call(s32[1]{0:T(128)} %constant.166.clone.1.t_ref, f32[4,256,128]{2,1,0:T(8,128)S(1)} %get-tuple-element.44.g, bf16[4,256,128]{2,1,0:T(8,128)(2,1)S(1)} %get-tuple-element.45.refs_0_, bf16[4,256,128]{2,1,0:T(8,128)(2,1)S(1)} %collective-permute-done.19.refs_1_, ...), custom_call_target="tpu_custom_call" | custom-call | flops 2621440 | bytes 1835008 | tf_op jit(solution)/shard_map/pallas_call | solution.py:61
  88.6 1.0 collective-permute-start.25
  90.2 2.1 %collective-permute-start.22 = (bf16[4,256,128]{2,1,0:T(8,128)(2,1)S(1)}, bf16[4,256,128]{2,1,0:T(8,128)(2,1)S(1)}, u32[]{:S(2)}, u32[]{:S(2)}) collective-permute-start(bf16[4,256,128]{2,1,0:T(8,128)(2,1)S(1)} %get-tuple-element.49.a), channel_id=1, source_target_pairs={{0,24},{1,7},{2,26},{3,1},{4,28},{5,3},{6,30},{7,5},{8,0},{9,15},{... | collective-permute-start | bytes 786440 | tf_op jit(solution)/shard_map/ppermute | solution.py:39
  92.3 3.5 %collective-permute-done.25.a = bf16[4,256,128]{2,1,0:T(8,128)(2,1)S(1)} collective-permute-done((bf16[4,256,128]{2,1,0:T(8,128)(2,1)S(1)}, bf16[4,256,128]{2,1,0:T(8,128)(2,1)S(1)}, u32[]{:S(2)}, u32[]{:S(2)}) %collective-permute-start.25) | collective-permute-done | bytes 262176 | tf_op jit(solution)/shard_map/ppermute | solution.py:39
  95.8 2.8 %collective-permute-done.26.b = bf16[4,256,128]{2,1,0:T(8,128)(2,1)S(1)} collective-permute-done((bf16[4,256,128]{2,1,0:T(8,128)(2,1)S(1)}, bf16[4,256,128]{2,1,0:T(8,128)(2,1)S(1)}, u32[]{:S(2)}, u32[]{:S(2)}) %collective-permute-start.26) | collective-permute-done | bytes 262176 | tf_op jit(solution)/shard_map/ppermute | solution.py:39
  98.6 1.6 %collective-permute-start.38 = (bf16[8,256,128]{2,1,0:T(8,128)(2,1)S(1)}, bf16[8,256,128]{2,1,0:T(8,128)(2,1)S(1)}, u32[]{:S(2)}, u32[]{:S(2)}) collective-permute-start(bf16[8,256,128]{2,1,0:T(8,128)(2,1)S(1)} %shard_map.98.refs_1_), channel_id=1, source_target_pairs={{0,1},{1,0},{2,3},{3,2},{4,5},{5,4},{6,7},{7,6},{8,9},{9,8},{10,11... | collective-permute-start | bytes 1572872 | tf_op jit(solution)/shard_map/ppermute | solution.py:39
  100.2 2.7 %collective-permute-start.27 = (bf16[8,256,128]{2,1,0:T(8,128)(2,1)S(1)}, bf16[8,256,128]{2,1,0:T(8,128)(2,1)S(1)}, u32[]{:S(2)}, u32[]{:S(2)}) collective-permute-start(bf16[8,256,128]{2,1,0:T(8,128)(2,1)S(1)} %shard_map.98.refs_1_), channel_id=1, source_target_pairs={{0,6},{1,25},{2,0},{3,27},{4,2},{5,29},{6,4},{7,31},{8,14},{9,1},{... | collective-permute-start | bytes 1572872 | tf_op jit(solution)/shard_map/ppermute | solution.py:39
  103.9 1.9 %collective-permute-start.31 = (bf16[8,256,128]{2,1,0:T(8,128)(2,1)S(1)}, bf16[8,256,128]{2,1,0:T(8,128)(2,1)S(1)}, u32[]{:S(2)}, u32[]{:S(2)}) collective-permute-start(bf16[8,256,128]{2,1,0:T(8,128)(2,1)S(1)} %shard_map.97.refs_0_), channel_id=1, source_target_pairs={{0,6},{1,25},{2,0},{3,27},{4,2},{5,29},{6,4},{7,31},{8,14},{9,1},{... | collective-permute-start | bytes 1572872 | tf_op jit(solution)/shard_map/ppermute | solution.py:39
  105.8 3.9 %collective-permute-done.32.refs_2_ = bf16[8,256,128]{2,1,0:T(8,128)(2,1)S(1)} collective-permute-done((bf16[8,256,128]{2,1,0:T(8,128)(2,1)S(1)}, bf16[8,256,128]{2,1,0:T(8,128)(2,1)S(1)}, u32[]{:S(2)}, u32[]{:S(2)}) %collective-permute-start.32) | collective-permute-done | bytes 524320 | tf_op jit(solution)/shard_map/ppermute | solution.py:39
  110.7 1.7 %collective-permute-start.28 = (bf16[8,256,128]{2,1,0:T(8,128)(2,1)S(1)}, bf16[8,256,128]{2,1,0:T(8,128)(2,1)S(1)}, u32[]{:S(2)}, u32[]{:S(2)}) collective-permute-start(bf16[8,256,128]{2,1,0:T(8,128)(2,1)S(1)} %collective-permute-done.27.refs_3_), channel_id=1, source_target_pairs={{0,6},{1,25},{2,0},{3,27},{4,2},{5,29},{6,4},{7,31},{8,14},{9,1},{... | collective-permute-start | bytes 1572872 | tf_op jit(solution)/shard_map/ppermute | solution.py:39
  112.4 2.9 %collective-permute-done.23.refs_0_ = bf16[8,256,128]{2,1,0:T(8,128)(2,1)S(1)} collective-permute-done((bf16[8,256,128]{2,1,0:T(8,128)(2,1)S(1)}, bf16[8,256,128]{2,1,0:T(8,128)(2,1)S(1)}, u32[]{:S(2)}, u32[]{:S(2)}) %collective-permute-start.23) | collective-permute-done | bytes 524320 | tf_op jit(solution)/shard_map/ppermute | solution.py:39
  115.9 0.9 collective-permute-start.36
  117.3 2.9 %collective-permute-done.28.refs_1_ = bf16[8,256,128]{2,1,0:T(8,128)(2,1)S(1)} collective-permute-done((bf16[8,256,128]{2,1,0:T(8,128)(2,1)S(1)}, bf16[8,256,128]{2,1,0:T(8,128)(2,1)S(1)}, u32[]{:S(2)}, u32[]{:S(2)}) %collective-permute-start.28) | collective-permute-done | bytes 524320 | tf_op jit(solution)/shard_map/ppermute | solution.py:39
  120.2 1.2 collective-permute-start.30
  121.4 3.4 %collective-permute-done.24.refs_0_ = bf16[8,256,128]{2,1,0:T(8,128)(2,1)S(1)} collective-permute-done((bf16[8,256,128]{2,1,0:T(8,128)(2,1)S(1)}, bf16[8,256,128]{2,1,0:T(8,128)(2,1)S(1)}, u32[]{:S(2)}, u32[]{:S(2)}) %collective-permute-start.24) | collective-permute-done | bytes 524320 | tf_op jit(solution)/shard_map/ppermute | solution.py:39
  124.9 1.8 %collective-permute-start.29 = (bf16[8,256,128]{2,1,0:T(8,128)(2,1)S(1)}, bf16[8,256,128]{2,1,0:T(8,128)(2,1)S(1)}, u32[]{:S(2)}, u32[]{:S(2)}) collective-permute-start(bf16[8,256,128]{2,1,0:T(8,128)(2,1)S(1)} %collective-permute-done.24.refs_0_), channel_id=1, source_target_pairs={{0,1},{1,0},{2,3},{3,2},{4,5},{5,4},{6,7},{7,6},{8,9},{9,8},{10,11... | collective-permute-start | bytes 1572872 | tf_op jit(solution)/shard_map/ppermute | solution.py:39
  126.7 1.5 %fusion.1 = (f32[32768]{0:T(1024)}, f32[32768]{0:T(1024)}, f32[32768]{0:T(1024)}) fusion(f32[4,256,128]{2,1,0:T(8,128)S(1)} %get-tuple-element.44.g, f32[]{:T(128)} %bitcast.5, f32[256,128]{1,0:T(8,128)S(1)} %get-tuple-element.48, f32[256,128]{1,0:T(8,128)S(1)} %get-tuple-element.29, f32[32768]{0:T(1024)S(1)} %copy-done.2), kind=kLoop, calls=%fused_computation.6 | loop fusion | flops 491520 | bytes 917508 | tf_op jit(solution)/shard_map/reshape | solution.py:404
  128.1 2.1 %shard_map.99.refs_8_ = bf16[128,256,128]{2,1,0:T(8,128)(2,1)} custom-call(s32[128]{0:T(128)S(1)} %compare_select_fusion.16.t_ref, bf16[8,256,128]{2,1,0:T(8,128)(2,1)S(1)} %shard_map.97.refs_0_, bf16[8,256,128]{2,1,0:T(8,128)(2,1)S(1)} %shard_map.98.refs_1_, bf16[8,256,128]{2,1,0:T(8,128)(2,1)S(1)} %collective-permute-done.37.refs_2_, ...), custom_call_target="tpu_custom_call" | custom-call | flops 4194304 | bytes 4194304 | tf_op jit(solution)/shard_map/pallas_call | solution.py:61
  130.3 3.1 %shard_map.100.refs_4_ = bf16[128,256,128]{2,1,0:T(8,128)(2,1)} custom-call(s32[128]{0:T(128)S(1)} %compare_select_fusion.16.t_ref, bf16[8,256,128]{2,1,0:T(8,128)(2,1)S(1)} %collective-permute-done.23.refs_0_, bf16[8,256,128]{2,1,0:T(8,128)(2,1)S(1)} %collective-permute-done.31.refs_1_, ...), custom_call_target="tpu_custom_call", output_to_operand_aliasing={{}: (9, {})} | custom-call | flops 8388608 | bytes 8388608 | tf_op jit(solution)/shard_map/pallas_call | solution.py:61
  133.4 2.1 %shard_map.101 = bf16[128,256,128]{2,1,0:T(8,128)(2,1)} custom-call(s32[128]{0:T(128)S(1)} %compare_select_fusion.16.t_ref, bf16[8,256,128]{2,1,0:T(8,128)(2,1)S(1)} %collective-permute-done.24.refs_0_, bf16[8,256,128]{2,1,0:T(8,128)(2,1)S(1)} %collective-permute-done.28.refs_1_, ...), custom_call_target="tpu_custom_call", output_to_operand_aliasing={{}: (5, {})} | custom-call | flops 4194304 | bytes 4194304 | tf_op jit(solution)/shard_map/pallas_call | solution.py:61
  (62 shorter events, 8.5 us)
Async XLA Ops:
  4.6 7.3 %collective-permute-start.5 = (bf16[16,256,128]{2,1,0:T(8,128)(2,1)S(1)}, bf16[16,256,128]{2,1,0:T(8,128)(2,1)S(1)}, u32[]{:S(2)}, u32[]{:S(2)}) collective-permute-start(bf16[16,256,128]{2,1,0:T(8,128)(2,1)S(1)} %get-tuple-element.35), channel_id=1, source_target_pairs={{0,1},{1,0},{2,3},{3,2},{4,5},{5,4},{6,7},{7,6},{8,9},{9,8},{10,11... | collective-permute-start | bytes 3145736 | tf_op jit(solution)/shard_map/ppermute | solution.py:39
  6.0 10.4 %collective-permute-start.9 = (bf16[16,256,128]{2,1,0:T(8,128)(2,1)S(1)}, bf16[16,256,128]{2,1,0:T(8,128)(2,1)S(1)}, u32[]{:S(2)}, u32[]{:S(2)}) collective-permute-start(bf16[16,256,128]{2,1,0:T(8,128)(2,1)S(1)} %get-tuple-element.38), channel_id=1, source_target_pairs={{0,1},{1,0},{2,3},{3,2},{4,5},{5,4},{6,7},{7,6},{8,9},{9,8},{10,11... | collective-permute-start | bytes 3145736 | tf_op jit(solution)/shard_map/ppermute | solution.py:39
  6.1 12.0 %collective-permute-start.4 = (bf16[16,256,128]{2,1,0:T(8,128)(2,1)S(1)}, bf16[16,256,128]{2,1,0:T(8,128)(2,1)S(1)}, u32[]{:S(2)}, u32[]{:S(2)}) collective-permute-start(bf16[16,256,128]{2,1,0:T(8,128)(2,1)S(1)} %get-tuple-element.33), channel_id=1, source_target_pairs={{0,1},{1,0},{2,3},{3,2},{4,5},{5,4},{6,7},{7,6},{8,9},{9,8},{10,11... | collective-permute-start | bytes 3145736 | tf_op jit(solution)/shard_map/ppermute | solution.py:39
  12.1 9.0 %collective-permute-start.11 = (bf16[8,256,128]{2,1,0:T(8,128)(2,1)S(1)}, bf16[8,256,128]{2,1,0:T(8,128)(2,1)S(1)}, u32[]{:S(2)}, u32[]{:S(2)}) collective-permute-start(bf16[8,256,128]{2,1,0:T(8,128)(2,1)S(1)} %get-tuple-element.39), channel_id=1, source_target_pairs={{0,6},{1,25},{2,0},{3,27},{4,2},{5,29},{6,4},{7,31},{8,14},{9,1},{... | collective-permute-start | bytes 1572872 | tf_op jit(solution)/shard_map/ppermute | solution.py:39
  15.0 10.1 %collective-permute-start.3 = (bf16[16,256,128]{2,1,0:T(8,128)(2,1)S(1)}, bf16[16,256,128]{2,1,0:T(8,128)(2,1)S(1)}, u32[]{:S(2)}, u32[]{:S(2)}) collective-permute-start(bf16[16,256,128]{2,1,0:T(8,128)(2,1)S(1)} %get-tuple-element.31), channel_id=1, source_target_pairs={{0,1},{1,0},{2,3},{3,2},{4,5},{5,4},{6,7},{7,6},{8,9},{9,8},{10,11... | collective-permute-start | bytes 3145736 | tf_op jit(solution)/shard_map/ppermute | solution.py:39
  15.2 9.7 %collective-permute-start.6 = (bf16[8,256,128]{2,1,0:T(8,128)(2,1)S(1)}, bf16[8,256,128]{2,1,0:T(8,128)(2,1)S(1)}, u32[]{:S(2)}, u32[]{:S(2)}) collective-permute-start(bf16[8,256,128]{2,1,0:T(8,128)(2,1)S(1)} %get-tuple-element.36), channel_id=1, source_target_pairs={{0,2},{1,9},{2,4},{3,11},{4,6},{5,13},{6,0},{7,15},{8,10},{9,17},{... | collective-permute-start | bytes 1572872 | tf_op jit(solution)/shard_map/ppermute | solution.py:39
  16.6 10.2 %collective-permute-start.10 = (bf16[8,256,128]{2,1,0:T(8,128)(2,1)S(1)}, bf16[8,256,128]{2,1,0:T(8,128)(2,1)S(1)}, u32[]{:S(2)}, u32[]{:S(2)}) collective-permute-start(bf16[8,256,128]{2,1,0:T(8,128)(2,1)S(1)} %shard_map.91), channel_id=1, source_target_pairs={{0,6},{1,25},{2,0},{3,27},{4,2},{5,29},{6,4},{7,31},{8,14},{9,1},{... | collective-permute-start | bytes 1572872 | tf_op jit(solution)/shard_map/ppermute | solution.py:39
  18.2 30.4 %copy-start.3 = (s32[129]{0:T(256)S(1)}, s32[129]{0:T(256)}, u32[]{:S(2)}) copy-start(s32[129]{0:T(256)} %param.9) | copy-start | bytes 1552
  18.2 30.5 %copy-start = (f32[1,65536]{1,0:T(1,128)S(1)}, f32[1,65536]{1,0:T(1,128)}, u32[]{:S(2)}) copy-start(f32[1,65536]{1,0:T(1,128)} %param.7) | copy-start | bytes 786436
  18.2 30.4 %copy-start.1 = (f32[1,65536]{1,0:T(1,128)S(1)}, f32[1,65536]{1,0:T(1,128)}, u32[]{:S(2)}) copy-start(f32[1,65536]{1,0:T(1,128)} %param.8) | copy-start | bytes 786436
  18.3 47.2 %copy-start.2 = (f32[32768]{0:T(1024)S(1)}, f32[32768]{0:T(1024)}, u32[]{:S(2)}) copy-start(f32[32768]{0:T(1024)} %param.6) | copy-start | bytes 393220
  18.3 12.1 %collective-permute-start.8 = (bf16[8,256,128]{2,1,0:T(8,128)(2,1)S(1)}, bf16[8,256,128]{2,1,0:T(8,128)(2,1)S(1)}, u32[]{:S(2)}, u32[]{:S(2)}) collective-permute-start(bf16[8,256,128]{2,1,0:T(8,128)(2,1)S(1)} %shard_map.90), channel_id=1, source_target_pairs={{0,2},{1,9},{2,4},{3,11},{4,6},{5,13},{6,0},{7,15},{8,10},{9,17},{... | collective-permute-start | bytes 1572872 | tf_op jit(solution)/shard_map/ppermute | solution.py:39
  21.4 11.0 %collective-permute-start.12 = (bf16[8,256,128]{2,1,0:T(8,128)(2,1)S(1)}, bf16[8,256,128]{2,1,0:T(8,128)(2,1)S(1)}, u32[]{:S(2)}, u32[]{:S(2)}) collective-permute-start(bf16[8,256,128]{2,1,0:T(8,128)(2,1)S(1)} %shard_map.92), channel_id=1, source_target_pairs={{0,6},{1,25},{2,0},{3,27},{4,2},{5,29},{6,4},{7,31},{8,14},{9,1},{... | collective-permute-start | bytes 1572872 | tf_op jit(solution)/shard_map/ppermute | solution.py:39
  25.1 10.9 %collective-permute-start.7 = (bf16[8,256,128]{2,1,0:T(8,128)(2,1)S(1)}, bf16[8,256,128]{2,1,0:T(8,128)(2,1)S(1)}, u32[]{:S(2)}, u32[]{:S(2)}) collective-permute-start(bf16[8,256,128]{2,1,0:T(8,128)(2,1)S(1)} %shard_map.89), channel_id=1, source_target_pairs={{0,2},{1,9},{2,4},{3,11},{4,6},{5,13},{6,0},{7,15},{8,10},{9,17},{... | collective-permute-start | bytes 1572872 | tf_op jit(solution)/shard_map/ppermute | solution.py:39
  36.6 6.8 %collective-permute-start.13 = (bf16[4,256,128]{2,1,0:T(8,128)(2,1)S(1)}, bf16[4,256,128]{2,1,0:T(8,128)(2,1)S(1)}, u32[]{:S(2)}, u32[]{:S(2)}) collective-permute-start(bf16[4,256,128]{2,1,0:T(8,128)(2,1)S(1)} %get-tuple-element.41), channel_id=1, source_target_pairs={{0,8},{1,3},{2,10},{3,5},{4,12},{5,7},{6,14},{7,1},{8,16},{9,11},{... | collective-permute-start | bytes 786440 | tf_op jit(solution)/shard_map/ppermute | solution.py:39
  37.4 9.3 %collective-permute-start.14 = (bf16[4,256,128]{2,1,0:T(8,128)(2,1)S(1)}, bf16[4,256,128]{2,1,0:T(8,128)(2,1)S(1)}, u32[]{:S(2)}, u32[]{:S(2)}) collective-permute-start(bf16[4,256,128]{2,1,0:T(8,128)(2,1)S(1)} %get-tuple-element.42), channel_id=1, source_target_pairs={{0,16},{1,5},{2,18},{3,7},{4,20},{5,1},{6,22},{7,3},{8,24},{9,13},... | collective-permute-start | bytes 786440 | tf_op jit(solution)/shard_map/ppermute | solution.py:39
  39.8 6.9 %collective-permute-start.15 = (bf16[4,256,128]{2,1,0:T(8,128)(2,1)S(1)}, bf16[4,256,128]{2,1,0:T(8,128)(2,1)S(1)}, u32[]{:S(2)}, u32[]{:S(2)}) collective-permute-start(bf16[4,256,128]{2,1,0:T(8,128)(2,1)S(1)} %get-tuple-element.43), channel_id=1, source_target_pairs={{0,24},{1,7},{2,26},{3,1},{4,28},{5,3},{6,30},{7,5},{8,0},{9,15},{... | collective-permute-start | bytes 786440 | tf_op jit(solution)/shard_map/ppermute | solution.py:39
  46.9 23.2 %collective-permute-start.16 = (bf16[4,256,128]{2,1,0:T(8,128)(2,1)S(1)}, bf16[4,256,128]{2,1,0:T(8,128)(2,1)S(1)}, u32[]{:S(2)}, u32[]{:S(2)}) collective-permute-start(bf16[4,256,128]{2,1,0:T(8,128)(2,1)S(1)} %shard_map.94.w), channel_id=1, source_target_pairs={{0,32},{1,33},{2,34},{3,35},{4,36},{5,37},{6,38},{7,39},{8,40},{9,... | collective-permute-start | bytes 786440 | tf_op jit(solution)/shard_map/ppermute | solution.py:39
  49.3 4.6 %collective-permute-start.1 = (bf16[2,128,128]{2,1,0:T(8,128)(2,1)S(1)}, bf16[2,128,128]{2,1,0:T(8,128)(2,1)S(1)}, u32[]{:S(2)}, u32[]{:S(2)}) collective-permute-start(bf16[2,128,128]{2,1,0:T(8,128)(2,1)S(1)} %get-tuple-element.28), channel_id=1, source_target_pairs={{0,1},{1,0},{2,3},{3,2},{4,5},{5,4},{6,7},{7,6},{8,9},{9,8},{10,11... | collective-permute-start | bytes 196616 | tf_op jit(solution)/shard_map/ppermute | solution.py:39
  52.0 13.5 %collective-permute-start = (bf16[2,136,128]{2,1,0:T(8,128)(2,1)S(1)}, bf16[2,136,128]{2,1,0:T(8,128)(2,1)S(1)}, u32[]{:S(2)}, u32[]{:S(2)}) collective-permute-start(bf16[2,136,128]{2,1,0:T(8,128)(2,1)S(1)} %get-tuple-element.27), channel_id=1, source_target_pairs={{0,1},{1,2},{2,3},{3,4},{4,5},{5,6},{6,7},{7,8},{8,9},{9,10},{10,1... | collective-permute-start | bytes 208904 | tf_op jit(solution)/shard_map/ppermute | solution.py:377
  53.9 11.6 %collective-permute-start.2 = (bf16[2,128,128]{2,1,0:T(8,128)(2,1)S(1)}, bf16[2,128,128]{2,1,0:T(8,128)(2,1)S(1)}, u32[]{:S(2)}, u32[]{:S(2)}) collective-permute-start(bf16[2,128,128]{2,1,0:T(8,128)(2,1)S(1)} %collective-permute-done.1.a), channel_id=1, source_target_pairs={{3,1},{5,3},{7,5},{9,7},{11,9},{13,11},{15,13},{17,15},{19,17},{21... | collective-permute-start | bytes 196616 | tf_op jit(solution)/shard_map/ppermute | solution.py:379
  55.2 14.9 %collective-permute-start.17 = (bf16[4,256,128]{2,1,0:T(8,128)(2,1)S(1)}, bf16[4,256,128]{2,1,0:T(8,128)(2,1)S(1)}, u32[]{:S(2)}, u32[]{:S(2)}) collective-permute-start(bf16[4,256,128]{2,1,0:T(8,128)(2,1)S(1)} %shard_map.94.w), channel_id=1, source_target_pairs={{0,64},{1,65},{2,66},{3,67},{4,68},{5,69},{6,70},{7,71},{8,72},{9,... | collective-permute-start | bytes 786440 | tf_op jit(solution)/shard_map/ppermute | solution.py:39
  64.8 9.7 %collective-permute-start.18 = (bf16[4,256,128]{2,1,0:T(8,128)(2,1)S(1)}, bf16[4,256,128]{2,1,0:T(8,128)(2,1)S(1)}, u32[]{:S(2)}, u32[]{:S(2)}) collective-permute-start(bf16[4,256,128]{2,1,0:T(8,128)(2,1)S(1)} %shard_map.94.w), channel_id=1, source_target_pairs={{0,96},{1,97},{2,98},{3,99},{4,100},{5,101},{6,102},{7,103},{8,104... | collective-permute-start | bytes 786440 | tf_op jit(solution)/shard_map/ppermute | solution.py:39
  67.5 12.5 %collective-permute-start.19 = (bf16[4,256,128]{2,1,0:T(8,128)(2,1)S(1)}, bf16[4,256,128]{2,1,0:T(8,128)(2,1)S(1)}, u32[]{:S(2)}, u32[]{:S(2)}) collective-permute-start(bf16[4,256,128]{2,1,0:T(8,128)(2,1)S(1)} %get-tuple-element.45.refs_0_), channel_id=1, source_target_pairs={{0,96},{1,97},{2,98},{3,99},{4,100},{5,101},{6,102},{7,103},{8,104... | collective-permute-start | bytes 786440 | tf_op jit(solution)/shard_map/ppermute | solution.py:39
  67.6 12.4 %collective-permute-start.20 = (bf16[4,256,128]{2,1,0:T(8,128)(2,1)S(1)}, bf16[4,256,128]{2,1,0:T(8,128)(2,1)S(1)}, u32[]{:S(2)}, u32[]{:S(2)}) collective-permute-start(bf16[4,256,128]{2,1,0:T(8,128)(2,1)S(1)} %get-tuple-element.45.refs_0_), channel_id=1, source_target_pairs={{0,64},{1,65},{2,66},{3,67},{4,68},{5,69},{6,70},{7,71},{8,72},{9,... | collective-permute-start | bytes 786440 | tf_op jit(solution)/shard_map/ppermute | solution.py:39
  70.1 11.8 %collective-permute-start.21 = (bf16[4,256,128]{2,1,0:T(8,128)(2,1)S(1)}, bf16[4,256,128]{2,1,0:T(8,128)(2,1)S(1)}, u32[]{:S(2)}, u32[]{:S(2)}) collective-permute-start(bf16[4,256,128]{2,1,0:T(8,128)(2,1)S(1)} %get-tuple-element.45.refs_0_), channel_id=1, source_target_pairs={{0,32},{1,33},{2,34},{3,35},{4,36},{5,37},{6,38},{7,39},{8,40},{9,... | collective-permute-start | bytes 786440 | tf_op jit(solution)/shard_map/ppermute | solution.py:39
  75.8 11.1 %all-to-all-start = ((f32[32,1,128]{2,1,0:T(1,128)}), f32[32,1,128]{2,1,0:T(1,128)S(1)}, u32[]{:S(2)}, u32[]{:S(2)}) async-start(f32[32,1,128]{2,1,0:T(1,128)} %get-tuple-element.46), calls=%async_computation | async-start | bytes 32768 | tf_op jit(solution)/shard_map/all_to_all | solution.py:401
  88.6 7.1 %collective-permute-start.25 = (bf16[4,256,128]{2,1,0:T(8,128)(2,1)S(1)}, bf16[4,256,128]{2,1,0:T(8,128)(2,1)S(1)}, u32[]{:S(2)}, u32[]{:S(2)}) collective-permute-start(bf16[4,256,128]{2,1,0:T(8,128)(2,1)S(1)} %get-tuple-element.49.a), channel_id=1, source_target_pairs={{0,16},{1,5},{2,18},{3,7},{4,20},{5,1},{6,22},{7,3},{8,24},{9,13},... | collective-permute-start | bytes 786440 | tf_op jit(solution)/shard_map/ppermute | solution.py:39
  89.6 8.9 %collective-permute-start.26 = (bf16[4,256,128]{2,1,0:T(8,128)(2,1)S(1)}, bf16[4,256,128]{2,1,0:T(8,128)(2,1)S(1)}, u32[]{:S(2)}, u32[]{:S(2)}) collective-permute-start(bf16[4,256,128]{2,1,0:T(8,128)(2,1)S(1)} %get-tuple-element.49.a), channel_id=1, source_target_pairs={{0,8},{1,3},{2,10},{3,5},{4,12},{5,7},{6,14},{7,1},{8,16},{9,11},{... | collective-permute-start | bytes 786440 | tf_op jit(solution)/shard_map/ppermute | solution.py:39
  90.2 12.7 %collective-permute-start.22 = (bf16[4,256,128]{2,1,0:T(8,128)(2,1)S(1)}, bf16[4,256,128]{2,1,0:T(8,128)(2,1)S(1)}, u32[]{:S(2)}, u32[]{:S(2)}) collective-permute-start(bf16[4,256,128]{2,1,0:T(8,128)(2,1)S(1)} %get-tuple-element.49.a), channel_id=1, source_target_pairs={{0,24},{1,7},{2,26},{3,1},{4,28},{5,3},{6,30},{7,5},{8,0},{9,15},{... | collective-permute-start | bytes 786440 | tf_op jit(solution)/shard_map/ppermute | solution.py:39
  98.6 5.3 %collective-permute-start.38 = (bf16[8,256,128]{2,1,0:T(8,128)(2,1)S(1)}, bf16[8,256,128]{2,1,0:T(8,128)(2,1)S(1)}, u32[]{:S(2)}, u32[]{:S(2)}) collective-permute-start(bf16[8,256,128]{2,1,0:T(8,128)(2,1)S(1)} %shard_map.98.refs_1_), channel_id=1, source_target_pairs={{0,1},{1,0},{2,3},{3,2},{4,5},{5,4},{6,7},{7,6},{8,9},{9,8},{10,11... | collective-permute-start | bytes 1572872 | tf_op jit(solution)/shard_map/ppermute | solution.py:39
  100.2 9.5 %collective-permute-start.32 = (bf16[8,256,128]{2,1,0:T(8,128)(2,1)S(1)}, bf16[8,256,128]{2,1,0:T(8,128)(2,1)S(1)}, u32[]{:S(2)}, u32[]{:S(2)}) collective-permute-start(bf16[8,256,128]{2,1,0:T(8,128)(2,1)S(1)} %shard_map.98.refs_1_), channel_id=1, source_target_pairs={{0,2},{1,9},{2,4},{3,11},{4,6},{5,13},{6,0},{7,15},{8,10},{9,17},{... | collective-permute-start | bytes 1572872 | tf_op jit(solution)/shard_map/ppermute | solution.py:39
  100.2 10.5 %collective-permute-start.27 = (bf16[8,256,128]{2,1,0:T(8,128)(2,1)S(1)}, bf16[8,256,128]{2,1,0:T(8,128)(2,1)S(1)}, u32[]{:S(2)}, u32[]{:S(2)}) collective-permute-start(bf16[8,256,128]{2,1,0:T(8,128)(2,1)S(1)} %shard_map.98.refs_1_), channel_id=1, source_target_pairs={{0,6},{1,25},{2,0},{3,27},{4,2},{5,29},{6,4},{7,31},{8,14},{9,1},{... | collective-permute-start | bytes 1572872 | tf_op jit(solution)/shard_map/ppermute | solution.py:39
  102.9 12.4 %collective-permute-start.23 = (bf16[8,256,128]{2,1,0:T(8,128)(2,1)S(1)}, bf16[8,256,128]{2,1,0:T(8,128)(2,1)S(1)}, u32[]{:S(2)}, u32[]{:S(2)}) collective-permute-start(bf16[8,256,128]{2,1,0:T(8,128)(2,1)S(1)} %shard_map.97.refs_0_), channel_id=1, source_target_pairs={{0,2},{1,9},{2,4},{3,11},{4,6},{5,13},{6,0},{7,15},{8,10},{9,17},{... | collective-permute-start | bytes 1572872 | tf_op jit(solution)/shard_map/ppermute | solution.py:39
  103.2 12.7 %collective-permute-start.37 = (bf16[8,256,128]{2,1,0:T(8,128)(2,1)S(1)}, bf16[8,256,128]{2,1,0:T(8,128)(2,1)S(1)}, u32[]{:S(2)}, u32[]{:S(2)}) collective-permute-start(bf16[8,256,128]{2,1,0:T(8,128)(2,1)S(1)} %shard_map.97.refs_0_), channel_id=1, source_target_pairs={{0,1},{1,0},{2,3},{3,2},{4,5},{5,4},{6,7},{7,6},{8,9},{9,8},{10,11... | collective-permute-start | bytes 1572872 | tf_op jit(solution)/shard_map/ppermute | solution.py:39
  103.9 12.9 %collective-permute-start.31 = (bf16[8,256,128]{2,1,0:T(8,128)(2,1)S(1)}, bf16[8,256,128]{2,1,0:T(8,128)(2,1)S(1)}, u32[]{:S(2)}, u32[]{:S(2)}) collective-permute-start(bf16[8,256,128]{2,1,0:T(8,128)(2,1)S(1)} %shard_map.97.refs_0_), channel_id=1, source_target_pairs={{0,6},{1,25},{2,0},{3,27},{4,2},{5,29},{6,4},{7,31},{8,14},{9,1},{... | collective-permute-start | bytes 1572872 | tf_op jit(solution)/shard_map/ppermute | solution.py:39
  109.7 7.2 %collective-permute-start.35 = (bf16[8,256,128]{2,1,0:T(8,128)(2,1)S(1)}, bf16[8,256,128]{2,1,0:T(8,128)(2,1)S(1)}, u32[]{:S(2)}, u32[]{:S(2)}) collective-permute-start(bf16[8,256,128]{2,1,0:T(8,128)(2,1)S(1)} %collective-permute-done.32.refs_2_), channel_id=1, source_target_pairs={{0,1},{1,0},{2,3},{3,2},{4,5},{5,4},{6,7},{7,6},{8,9},{9,8},{10,11... | collective-permute-start | bytes 1572872 | tf_op jit(solution)/shard_map/ppermute | solution.py:39
  110.7 9.6 %collective-permute-start.28 = (bf16[8,256,128]{2,1,0:T(8,128)(2,1)S(1)}, bf16[8,256,128]{2,1,0:T(8,128)(2,1)S(1)}, u32[]{:S(2)}, u32[]{:S(2)}) collective-permute-start(bf16[8,256,128]{2,1,0:T(8,128)(2,1)S(1)} %collective-permute-done.27.refs_3_), channel_id=1, source_target_pairs={{0,6},{1,25},{2,0},{3,27},{4,2},{5,29},{6,4},{7,31},{8,14},{9,1},{... | collective-permute-start | bytes 1572872 | tf_op jit(solution)/shard_map/ppermute | solution.py:39
  115.3 9.5 %collective-permute-start.24 = (bf16[8,256,128]{2,1,0:T(8,128)(2,1)S(1)}, bf16[8,256,128]{2,1,0:T(8,128)(2,1)S(1)}, u32[]{:S(2)}, u32[]{:S(2)}) collective-permute-start(bf16[8,256,128]{2,1,0:T(8,128)(2,1)S(1)} %collective-permute-done.23.refs_0_), channel_id=1, source_target_pairs={{0,2},{1,9},{2,4},{3,11},{4,6},{5,13},{6,0},{7,15},{8,10},{9,17},{... | collective-permute-start | bytes 1572872 | tf_op jit(solution)/shard_map/ppermute | solution.py:39
  115.9 14.4 %collective-permute-start.36 = (bf16[8,256,128]{2,1,0:T(8,128)(2,1)S(1)}, bf16[8,256,128]{2,1,0:T(8,128)(2,1)S(1)}, u32[]{:S(2)}, u32[]{:S(2)}) collective-permute-start(bf16[8,256,128]{2,1,0:T(8,128)(2,1)S(1)} %collective-permute-done.27.refs_3_), channel_id=1, source_target_pairs={{0,1},{1,0},{2,3},{3,2},{4,5},{5,4},{6,7},{7,6},{8,9},{9,8},{10,11... | collective-permute-start | bytes 1572872 | tf_op jit(solution)/shard_map/ppermute | solution.py:39
  116.8 13.5 %collective-permute-start.33 = (bf16[8,256,128]{2,1,0:T(8,128)(2,1)S(1)}, bf16[8,256,128]{2,1,0:T(8,128)(2,1)S(1)}, u32[]{:S(2)}, u32[]{:S(2)}) collective-permute-start(bf16[8,256,128]{2,1,0:T(8,128)(2,1)S(1)} %collective-permute-done.23.refs_0_), channel_id=1, source_target_pairs={{0,1},{1,0},{2,3},{3,2},{4,5},{5,4},{6,7},{7,6},{8,9},{9,8},{10,11... | collective-permute-start | bytes 1572872 | tf_op jit(solution)/shard_map/ppermute | solution.py:39
  116.9 13.4 %collective-permute-start.34 = (bf16[8,256,128]{2,1,0:T(8,128)(2,1)S(1)}, bf16[8,256,128]{2,1,0:T(8,128)(2,1)S(1)}, u32[]{:S(2)}, u32[]{:S(2)}) collective-permute-start(bf16[8,256,128]{2,1,0:T(8,128)(2,1)S(1)} %collective-permute-done.31.refs_1_), channel_id=1, source_target_pairs={{0,1},{1,0},{2,3},{3,2},{4,5},{5,4},{6,7},{7,6},{8,9},{9,8},{10,11... | collective-permute-start | bytes 1572872 | tf_op jit(solution)/shard_map/ppermute | solution.py:39
  120.2 13.2 %collective-permute-start.30 = (bf16[8,256,128]{2,1,0:T(8,128)(2,1)S(1)}, bf16[8,256,128]{2,1,0:T(8,128)(2,1)S(1)}, u32[]{:S(2)}, u32[]{:S(2)}) collective-permute-start(bf16[8,256,128]{2,1,0:T(8,128)(2,1)S(1)} %collective-permute-done.28.refs_1_), channel_id=1, source_target_pairs={{0,1},{1,0},{2,3},{3,2},{4,5},{5,4},{6,7},{7,6},{8,9},{9,8},{10,11... | collective-permute-start | bytes 1572872 | tf_op jit(solution)/shard_map/ppermute | solution.py:39
  124.9 8.5 %collective-permute-start.29 = (bf16[8,256,128]{2,1,0:T(8,128)(2,1)S(1)}, bf16[8,256,128]{2,1,0:T(8,128)(2,1)S(1)}, u32[]{:S(2)}, u32[]{:S(2)}) collective-permute-start(bf16[8,256,128]{2,1,0:T(8,128)(2,1)S(1)} %collective-permute-done.24.refs_0_), channel_id=1, source_target_pairs={{0,1},{1,0},{2,3},{3,2},{4,5},{5,4},{6,7},{7,6},{8,9},{9,8},{10,11... | collective-permute-start | bytes 1572872 | tf_op jit(solution)/shard_map/ppermute | solution.py:39
